TPU v7x, 128 devices: a whole 4x4x4 slice. The times are simulated.
128 devices in a mesh: dp: 32 (over x, y, core), group: 4 (over z).
Axes of the slice: x: 4, y: 4, z: 4, core: 2. Of those that a mesh axis runs over, the one named last changes fastest.
Arguments:
- images: bfloat16 [16384, 512], P(('dp', 'group')), may hold values from -1 to 1
- texts: bfloat16 [16384, 512], P(('dp', 'group')), may hold values from -1 to 1
- log_scale: float32 [], replicated, may hold values from 2 to 2.7
Outputs:
- grad_images: bfloat16 [16384, 512], P(('dp', 'group'))
- grad_texts: bfloat16 [16384, 512], P(('dp', 'group'))
- loss: float32 [], replicated
- grad_scale: float32 [], replicated
All inputs are finite; a program needn't handle non-finite values.
Results may differ from a plain program's by a relative error of at most 0.0013.
The roundings to bfloat16 on the way count: a program that leaves them out, or rounds other values in their place, can miss the bound.
Values may be sent and summed in bfloat16 or wider, within the bound.
No kernel may reach another device: no remote copies, remote signals or barrier semaphores. Data moves between devices by JAX's collectives and lax.ppermute only.
A program may use at most 128 MiB of HBM per device.

v0:
```python
import functools

import jax
import jax.numpy as jnp
from jax import lax
from jax.experimental import pallas as pl
from jax.experimental.pallas import tpu as pltpu
from jax.sharding import Mesh
from jax.sharding import PartitionSpec as P


ALL = ("x", "y", "c", "z")
F32, BF16, F16 = jnp.float32, jnp.bfloat16, jnp.float16
LOG2E = 1.4426950408889634
LN2 = 0.6931471805599453
OFFSETS = (1, 3, 2)
ROWS = 128
DOWN = 2.0**-11
STEP = 2.0**8
TINY = 6.2e-5


def turn(value, shift, first):
    pairs = []
    for y in range(4):
        for c in range(2):
            for z in range(4):
                if (c == 0) == first:
                    to = ((y + shift) % 4, c, z)
                else:
                    to = (y, c, (z + shift) % 4)
                pairs.append(((y * 2 + c) * 4 + z, (to[0] * 2 + to[1]) * 4 + to[2]))
    return lax.ppermute(value, ("y", "c", "z"), pairs)


def along_x(value, shift):
    return lax.ppermute(value, "x", [(i, (i + shift) % 4) for i in range(4)])


def other_core(value):
    return lax.ppermute(value, "c", [(0, 1), (1, 0)])


def everyone(value, move):
    got = {0: value}
    for d in OFFSETS:
        got[d] = move(value, d)
    return [got[d] for d in range(4)]


LINES = [[(y * 2) * 4 + z for y in range(4)] for z in range(4)] + [
    [(y * 2 + 1) * 4 + z for z in range(4)] for y in range(4)
]
NT = (((1,), (1,)), ((), ()))
TN = (((0,), (0,)), ((), ()))


def call(kernel, outs, *args, smem=(), scratch=()):
    return pl.pallas_call(
        kernel,
        out_shape=outs,
        in_specs=[
            pl.BlockSpec(memory_space=pltpu.SMEM if i in smem else pltpu.VMEM) for i in range(len(args))
        ],
        out_specs=jax.tree.map(lambda _: pl.BlockSpec(memory_space=pltpu.VMEM), outs),
        scratch_shapes=scratch,
        compiler_params=pltpu.CompilerParams(vmem_limit_bytes=16 << 20),
    )(*args)


def out(shape, dtype=F32):
    return pltpu.VMEM(shape, dtype)


def places():
    y, z, on_y = lax.axis_index("y"), lax.axis_index("z"), lax.axis_index("c") == 0
    return jnp.where(on_y, y, z), jnp.where(on_y, z, y), lax.axis_index("x")


def turn_kernel(axis, a_ref, o_ref):
    here = places()[axis]
    for d in range(4):
        at = pl.multiple_of(lax.rem(here - d + 4, 4) * 128, 128)
        o_ref[128 * d : 128 * (d + 1), :] = a_ref[pl.ds(at, 128), :]


def join_kernel(a0, a1, a2, a3, o_ref):
    for k, a in enumerate((a0, a1, a2, a3)):
        o_ref[128 * k : 128 * (k + 1), :] = a[...]


def lined_up(value):
    copies = jnp.broadcast_to(value[None], (4, ROWS, value.shape[1]))
    got = lax.all_to_all(copies, ("y", "c", "z"), 0, 0, axis_index_groups=LINES, tiled=True)
    return call(functools.partial(turn_kernel, 0), out((512, 512), BF16), got.reshape(512, -1))


def peak(ref):
    tall = jnp.max(jnp.abs(ref[...].astype(F32)), axis=0, keepdims=True)
    return jnp.broadcast_to(jnp.max(tall, axis=1, keepdims=True), (1, 128))


def logits_kernel(first, s_ref, im_ref, t0_ref, t1_ref, l_ref, rows_ref, cols_ref, top_scr, sum_scr, mean_scr):
    s2 = s_ref[0, 0]
    for h, t_ref in enumerate((t0_ref, t1_ref)):
        l_ref[:, 512 * h : 512 * (h + 1)] = s2 * lax.dot_general(
            im_ref[...], t_ref[...], NT, preferred_element_type=F32
        )

    def tops(i, col_tops):
        here = pl.ds(pl.multiple_of(i * 64, 64), 64)
        row_top, new = None, []
        for k in range(8):
            part = l_ref[here, 128 * k : 128 * (k + 1)]
            row_top = part if row_top is None else jnp.maximum(row_top, part)
            new.append(jnp.maximum(col_tops[k], jnp.max(part.reshape(8, 8, 128), axis=0)))
        top_scr[here, :] = row_top
        return tuple(new)

    col_tops = lax.fori_loop(0, 8, tops, tuple(l_ref[0:8, 128 * k : 128 * (k + 1)] for k in range(8)))

    def sums(i, carry):
        here = pl.ds(pl.multiple_of(i * 64, 64), 64)
        row_top = top_scr[here, :]
        row_sum = row_mean = jnp.zeros((64, 128), F32)
        new = []
        for k in range(8):
            part = l_ref[here, 128 * k : 128 * (k + 1)]
            e = jnp.exp2(part - row_top)
            row_sum = row_sum + e
            row_mean = row_mean + e * part
            part = part.reshape(8, 8, 128)
            e = jnp.exp2(part - col_tops[k][None])
            new.append((carry[k][0] + jnp.sum(e, axis=0), carry[k][1] + jnp.sum(e * part, axis=0)))
        sum_scr[here, :] = row_sum
        mean_scr[here, :] = row_mean
        return tuple(new)

    zero = jnp.zeros((8, 128), F32)
    col_sums = lax.fori_loop(0, 8, sums, ((zero, zero),) * 8)
    for k in range(8):
        at = slice(128 * k, 128 * (k + 1))
        top = jnp.max(col_tops[k], axis=0, keepdims=True)
        e = jnp.exp2(col_tops[k] - top)
        cols_ref[0:1, at] = top
        cols_ref[1:2, at] = jnp.sum(e * col_sums[k][0], axis=0, keepdims=True)
        cols_ref[2:3, at] = jnp.sum(e * col_sums[k][1], axis=0, keepdims=True)
    for j in range(4):
        at = slice(128 * j, 128 * (j + 1))
        tops_here = top_scr[at, :].T
        top = jnp.max(tops_here, axis=0, keepdims=True)
        e = jnp.exp2(tops_here - top)
        total = jnp.sum(e * sum_scr[at, :].T, axis=0, keepdims=True)
        rows_ref[j : j + 1, :] = top + jnp.log2(total)
        rows_ref[4 + j : 5 + j, :] = jnp.sum(e * mean_scr[at, :].T, axis=0, keepdims=True) / total
    rows_ref[8:9, :] = peak(im_ref)
    if first:
        rows_ref[9:10, :] = jnp.maximum(peak(t0_ref), peak(t1_ref))
        block = l_ref[0:128, 0:128]
        rows_ref[10:11, :] = jnp.sum(jnp.where(eye(), block, 0.0), axis=0, keepdims=True)


def eye():
    shape = (128, 128)
    return lax.broadcasted_iota(jnp.int32, shape, 0) == lax.broadcasted_iota(jnp.int32, shape, 1)


def logits_of(k, s2, im, t0, t1):
    return call(
        functools.partial(logits_kernel, k == 0),
        (out((512, 1024)), out((16, 128)), out((8, 1024))),
        s2, im, t0, t1,
        smem=(0,),
        scratch=[pltpu.VMEM((512, 128), F32)] * 3,
    )


def merge(parts):
    top = functools.reduce(jnp.maximum, [p[0] for p in parts])
    es = [jnp.exp2(p[0] - top) for p in parts]
    total = sum(es)
    mean = sum(e * p[1] for e, p in zip(es, parts)) / total
    return top + jnp.log2(total), mean


def greatest(values):
    return functools.reduce(jnp.maximum, values)


def row_at(back_second, back_first):
    first, second, _ = places()
    return lax.rem(second - back_second + 4, 4) * 4 + lax.rem(first - back_first + 4, 4)


def start_kernel(r0, r1, r2, r3, c0, c1, c2, c3, all_ref, col_ref, scr):
    rs, cs = (r0, r1, r2, r3), (c0, c1, c2, c3)
    for k, r in enumerate(rs):
        for j in range(4):
            at = row_at(k, j)
            scr[pl.ds(at, 1), :] = r[j : j + 1, :]
            scr[pl.ds(16 + at, 1), :] = r[4 + j : 5 + j, :]
    scr[32:33, :] = r0[10:11, :]
    scr[33:34, :] = r0[9:10, :]
    scr[34:40, :] = jnp.zeros((6, 128), F32)
    message = scr[...]
    for k in range(16):
        all_ref[40 * k : 40 * (k + 1), :] = message
    top = greatest([c[0:1, :] for c in cs])
    es = [jnp.exp2(c[0:1, :] - top) for c in cs]
    total = sum(e * c[1:2, :] for e, c in zip(es, cs))
    mean = sum(e * c[2:3, :] for e, c in zip(es, cs)) / total
    lse = top + jnp.log2(total)
    for k in range(8):
        col_ref[k : k + 1, :] = lse[:, 128 * k : 128 * (k + 1)]
        col_ref[8 + k : 9 + k, :] = mean[:, 128 * k : 128 * (k + 1)]
    col_ref[16:17, :] = greatest([r[8:9, :] for r in rs])
    col_ref[17:24, :] = jnp.zeros((7, 128), F32)


def rolled(v, d, group):
    if d == 0:
        return v
    n = v.shape[0]
    size = n // group
    quarter = size // 4
    pieces = []
    for g in range(group):
        at = g * size
        pieces += [v[at + size - d * quarter : at + size, :], v[at : at + size - d * quarter, :]]
    return jnp.concatenate(pieces, axis=0)


def middle_kernel(b0, b1, col_ref):
    swapped = [jnp.concatenate([b1[k + 4 : k + 8, :], b1[k : k + 4, :]], axis=0) for k in (0, 8)]
    lse, mean = merge([(b0[0:8, :], b0[8:16, :]), swapped])
    col_ref[0:8, :] = lse
    col_ref[8:16, :] = mean
    col_ref[16:24, :] = jnp.maximum(b0[16:24, :], b1[16:24, :])


def pieces_of(value):
    left, pieces = value * DOWN, []
    for _ in range(4):
        head = left.astype(BF16).astype(F32)
        head = jnp.where(jnp.abs(head) < TINY, 0.0, head)
        pieces.append(head)
        left = (left - head) * STEP
    return pieces


def value_of(pieces):
    total = pieces[3]
    for p in (pieces[2], pieces[1], pieces[0]):
        total = p + total * (1.0 / STEP)
    return total * (1.0 / DOWN)


def encoded(first, second):
    lane = lax.broadcasted_iota(jnp.int32, (1, 512), 1) % 256
    value = jnp.where(lane % 64 < 32, first, second)
    row = jnp.zeros((1, 512), F32)
    for p, piece in enumerate(pieces_of(value)):
        row = jnp.where(lane // 64 == p, piece, row)
    return row


def tail(row, at, half):
    shape = (8, 512)
    here = lax.broadcasted_iota(jnp.int32, shape, 0) == at
    if half is not None:
        here = here & (lax.broadcasted_iota(jnp.int32, shape, 1) // 256 == half)
    return jnp.where(here, jnp.broadcast_to(row, shape), 0.0)


def total_of(v):
    return jnp.sum(jnp.sum(v, axis=0, keepdims=True), axis=1, keepdims=True)


def end_kernel(s_ref, a_ref, b0, b1, b2, b3, row_ref, col_ref, codes_ref, unit_ref, back_ref, scr):
    rs = [a_ref[40 * k : 40 * (k + 1), :] for k in range(16)]
    lse, mean = merge([(r[0:16, :], r[16:32, :]) for r in rs])
    scr[...] = lse + 1.0
    for k in range(4):
        for j in range(4):
            row_ref[4 * k + j : 4 * k + j + 1, :] = scr[pl.ds(row_at(k, j), 1), :]
    diagonal = total_of(sum(r[32:33, :] for r in rs)) * LN2
    text_peak = greatest([r[33:34, :] for r in rs])
    codes_ref[1:2, :] = encoded(total_of(lse) * LN2 - 2.0 * diagonal, 0.5 * LN2 * total_of(mean) - diagonal)
    cs = (b0, b1, b2, b3)
    lse, mean = merge([(rolled(c[0:8, :], d, 2), rolled(c[8:16, :], d, 2)) for d, c in enumerate(cs)])
    for k in range(8):
        col_ref[:, 128 * k : 128 * (k + 1)] = lse[k : k + 1, :] + 1.0
    image_peak = greatest([c[16:17, :] for c in cs])
    codes_ref[0:1, :] = encoded(total_of(lse) * LN2, 0.5 * LN2 * total_of(mean))
    scale = s_ref[0, 0] * LN2
    for k, top in enumerate((text_peak, image_peak)):
        unit = 4.0 / jnp.maximum(top, 1e-30)
        unit_ref[k : k + 1, :] = unit
        back = scale / unit
        back_ref[k : k + 1, :] = jnp.concatenate([back] * 4, axis=1)


def image_kernel(which, l_ref, row_ref, col_ref, unit_ref, codes_ref, t0_ref, t1_ref, w_ref, g_ref):
    for j in range(4):
        at = slice(128 * j, 128 * (j + 1))
        row = row_ref[4 * which + j : 4 * which + j + 1, :]
        row = jnp.broadcast_to(row, (128, 128)).T
        for k in range(8):
            to = slice(128 * k, 128 * (k + 1))
            part = l_ref[at, to]
            w = jnp.exp2(part - row) + jnp.exp2(part - col_ref[:, to])
            if which == 0 and j == 0 and k == 0:
                w = w - jnp.where(eye(), 1.0, 0.0)
            w_ref[at, to] = w.astype(BF16)
    g = jnp.dot(w_ref[:, 0:512], t0_ref[...], preferred_element_type=F32)
    g = g + jnp.dot(w_ref[:, 512:1024], t1_ref[...], preferred_element_type=F32)
    g = g * unit_ref[0:1, 0:1]
    for k in range(4):
        g_ref[136 * k : 136 * k + 128, :] = g[128 * k : 128 * (k + 1), :]
        g_ref[136 * k + 128 : 136 * (k + 1), :] = tail(codes_ref[0:1, :], 4 * (k % 2) + which, k // 2)


def text_kernel(w0, w1, w2, w3, i0, i1, i2, i3, unit_ref, codes_ref, g0_ref, g1_ref):
    for h, g_ref in enumerate((g0_ref, g1_ref)):
        at = slice(512 * h, 512 * (h + 1))
        g = None
        for w, i in zip((w0, w1, w2, w3), (i0, i1, i2, i3)):
            part = lax.dot_general(w[:, at], i[...], TN, preferred_element_type=F32)
            g = part if g is None else g + part
        g = g * unit_ref[1:2, 0:1]
        for k in range(4):
            g_ref[136 * k : 136 * k + 128, :] = g[128 * k : 128 * (k + 1), :]
            g_ref[136 * k + 128 : 136 * (k + 1), :] = tail(codes_ref[1:2, :], 2 * k + h, 0)


def decode_kernel(i_ref, t_ref, loss_ref, grad_ref):
    rows = jnp.sum(i_ref[...] + t_ref[...], axis=0, keepdims=True)
    rows = rows[:, 0:256] + rows[:, 256:512]
    pair_total = ROWS * 128
    for v, (ref, count) in enumerate(((loss_ref, 2.0 * pair_total), (grad_ref, float(pair_total)))):
        ref[...] = value_of([rows[:, 64 * p + 32 * v : 64 * p + 32 * v + 1] for p in range(4)]) / count


def group(value, k):
    return value[136 * k : 136 * (k + 1)]


def program(images, texts, log_scale):
    s2 = jnp.reshape(jnp.exp(log_scale) * LOG2E, (1, 1))
    line = lined_up(images)
    chunks = everyone(line, lambda v, d: turn(v, d, False))
    t0 = call(join_kernel, out((512, 512), BF16), *everyone(texts, along_x))
    t1 = other_core(t0)
    parts = [None] * 4
    for k in (0, 1, 3, 2):
        parts[k] = logits_of(k, s2, chunks[k], t0, t1)
    ls = [p[0] for p in parts]
    rows, cols = call(
        start_kernel,
        (out((640, 128)), out((24, 128))),
        *[p[1] for p in parts], *[p[2] for p in parts],
        scratch=[pltpu.VMEM((40, 128), F32)],
    )
    rows = lax.all_to_all(rows.reshape(16, 40, 128), ("y", "z"), 0, 0, tiled=True).reshape(640, 128)
    other = other_core(cols)
    cols = call(middle_kernel, out((24, 128)), cols, other)
    cols = everyone(cols, along_x)
    row_lse, col_lse, codes, unit, back = call(
        end_kernel,
        (out((16, 128)), out((1, 1024)), out((2, 512)), out((2, 128)), out((2, 512))),
        s2, rows, *cols,
        smem=(0,),
        scratch=[pltpu.VMEM((16, 128), F32)],
    )
    ws, gs, sent = {}, {}, {}
    for k in (2, 1, 3, 0):
        ws[k], gs[k] = call(
            functools.partial(image_kernel, k),
            (out((512, 1024), BF16), out((544, 512))),
            ls[k], row_lse, col_lse, unit, codes, t0, t1,
        )
        if k:
            sent[k] = turn(gs[k].astype(F16), 4 - k, False)
    g0, g1 = call(
        text_kernel,
        (out((544, 512)), out((544, 512))),
        *[ws[k] for k in range(4)], *chunks, unit, codes,
    )
    swap = other_core(g1.astype(F16))
    moved = []
    for k in (2, 1, 3):
        moved.append(along_x((group(g0, k) + group(swap, k).astype(F32)).astype(F16), 4 - k))
    gt = group(g0, 0) + sum(m.astype(F32) for m in [group(swap, 0)] + moved)
    sums = [group(gs[0], k) + sum(group(m, k).astype(F32) for m in sent.values()) for k in range(4)]
    moved = []
    for k in (2, 1, 3):
        moved.append(turn(sums[k].astype(F16), 4 - k, True))
    gi = sums[0] + sum(m.astype(F32) for m in moved)
    loss, grad_scale = call(decode_kernel, (out((1, 1)), out((1, 1))), gi[128:], gt[128:])
    grad_images = (gi[0:128] * back[0:1, :]).astype(BF16)
    grad_texts = (gt[0:128] * back[1:2, :]).astype(BF16)
    return grad_images, grad_texts, jnp.reshape(loss, ()), jnp.reshape(grad_scale, ())


def solution(mesh):
    split = Mesh(mesh.devices.reshape(4, 4, 2, mesh.shape["group"]), ALL)
    placed = (P(ALL, None), P(ALL, None), P())
    return jax.shard_map(
        program,
        mesh=split,
        in_specs=placed,
        out_specs=(P(ALL, None), P(ALL, None), P(), P()),
        check_vma=False,
    )
```

profile of v0, /device:TPU:0, one launch (start us, length us, event | category | flops | bytes accessed | tf_op | source)
XLA Modules:
  0.0 103.0 jit_solution(12028536887134498575)
XLA Ops:
  0.6 1.8 %broadcast_in_dim.2 = bf16[4,128,512]{2,1,0:T(8,128)(2,1)} broadcast(bf16[128,512]{1,0:T(8,128)(2,1)} %param.3), dimensions={1,2} | broadcast | bytes 655360 | tf_op jit(solution)/shard_map/broadcast_in_dim | solution.py:93
  2.4 4.6 %all-to-all-start = ((bf16[4,128,512]{2,1,0:T(8,128)(2,1)}), bf16[4,128,512]{2,1,0:T(8,128)(2,1)S(1)}, u32[]{:S(2)}, u32[]{:S(2)}) async-start(bf16[4,128,512]{2,1,0:T(8,128)(2,1)} %broadcast_in_dim.2), calls=%async_computation | async-start | bytes 1048576 | tf_op jit(solution)/shard_map/all_to_all | solution.py:94
  7.0 3.0 %collective-permute-start.1 = (bf16[128,512]{1,0:T(8,128)(2,1)S(1)}, bf16[128,512]{1,0:T(8,128)(2,1)S(1)}, u32[]{:S(2)}, u32[]{:S(2)}) collective-permute-start(bf16[128,512]{1,0:T(8,128)(2,1)S(1)} %copy-done.9), channel_id=1, source_target_pairs={{0,64},{32,96},{64,0},{96,32},{1,65},{33,97},{65,1},{97,33},{2,66}... | collective-permute-start | bytes 393224 | tf_op jit(solution)/shard_map/ppermute | solution.py:37
  10.0 0.6 collective-permute-start
  10.6 2.6 %collective-permute-start.2 = (bf16[128,512]{1,0:T(8,128)(2,1)S(1)}, bf16[128,512]{1,0:T(8,128)(2,1)S(1)}, u32[]{:S(2)}, u32[]{:S(2)}) collective-permute-start(bf16[128,512]{1,0:T(8,128)(2,1)S(1)} %copy-done.9), channel_id=1, source_target_pairs={{0,96},{32,0},{64,32},{96,64},{1,97},{33,1},{65,33},{97,65},{2,98}... | collective-permute-start | bytes 393224 | tf_op jit(solution)/shard_map/ppermute | solution.py:37
  13.3 1.6 %collective-permute-done.1.a2 = bf16[128,512]{1,0:T(8,128)(2,1)S(1)} collective-permute-done((bf16[128,512]{1,0:T(8,128)(2,1)S(1)}, bf16[128,512]{1,0:T(8,128)(2,1)S(1)}, u32[]{:S(2)}, u32[]{:S(2)}) %collective-permute-start.1) | collective-permute-done | bytes 131104 | tf_op jit(solution)/shard_map/ppermute | solution.py:37
  14.9 2.3 %collective-permute-done.a1 = bf16[128,512]{1,0:T(8,128)(2,1)S(1)} collective-permute-done((bf16[128,512]{1,0:T(8,128)(2,1)S(1)}, bf16[128,512]{1,0:T(8,128)(2,1)S(1)}, u32[]{:S(2)}, u32[]{:S(2)}) %collective-permute-start) | collective-permute-done | bytes 131104 | tf_op jit(solution)/shard_map/ppermute | solution.py:37
  17.3 0.1 collective-permute-start.3
  17.4 0.0 all-to-all-done
  17.4 0.1 shard_map.66.im_ref.i0
  17.4 3.5 %collective-permute-start.6 = (bf16[512,512]{1,0:T(8,128)(2,1)S(1)}, bf16[512,512]{1,0:T(8,128)(2,1)S(1)}, u32[]{:S(2)}, u32[]{:S(2)}) collective-permute-start(bf16[512,512]{1,0:T(8,128)(2,1)S(1)} %shard_map.66.im_ref.i0), channel_id=1, source_target_pairs={{0,3},{1,0},{2,1},{3,2},{4,28},{5,29},{6,30},{7,31},{8,11},{9,8},{... | collective-permute-start | bytes 1572872 | tf_op jit(solution)/shard_map/ppermute | solution.py:33
  20.9 0.5 collective-permute-start.5
  21.4 1.0 collective-permute-start.4
  23.1 2.2 %shard_map.68 = (f32[512,1024]{1,0:T(8,128)S(1)}, f32[16,128]{1,0:T(8,128)S(1)}, f32[8,1024]{1,0:T(8,128)S(1)}) custom-call(f32[1,1]{1,0:T(1,128)} %bitcast.s_ref, bf16[512,512]{1,0:T(8,128)(2,1)S(1)} %shard_map.66.im_ref.i0, bf16[512,512]{1,0:T(8,128)(2,1)S(1)} %shard_map.67.t0_ref, bf16[512,512]{1,0:T(8,128)(2,1)S(1)} %collective-permute-done.3.t1_ref), custom_call_target="tpu_custom_call" | custom-call | tf_op jit(solution)/shard_map/pallas_call | solution.py:59
  25.3 1.3 %copy-done = f32[512,1024]{1,0:T(8,128)} copy-done((f32[512,1024]{1,0:T(8,128)}, f32[512,1024]{1,0:T(8,128)S(1)}, u32[]{:S(2)}) %copy-start) | copy-done | bytes 2097176
  26.6 6.6 %collective-permute-done.6.im_ref.i3 = bf16[512,512]{1,0:T(8,128)(2,1)S(1)} collective-permute-done((bf16[512,512]{1,0:T(8,128)(2,1)S(1)}, bf16[512,512]{1,0:T(8,128)(2,1)S(1)}, u32[]{:S(2)}, u32[]{:S(2)}) %collective-permute-start.6) | collective-permute-done | bytes 524320 | tf_op jit(solution)/shard_map/ppermute | solution.py:33
  33.2 2.1 %shard_map.71 = (f32[512,1024]{1,0:T(8,128)S(1)}, f32[16,128]{1,0:T(8,128)S(1)}, f32[8,1024]{1,0:T(8,128)S(1)}) custom-call(f32[1,1]{1,0:T(1,128)} %bitcast.s_ref, bf16[512,512]{1,0:T(8,128)(2,1)S(1)} %collective-permute-done.6.im_ref.i3, bf16[512,512]{1,0:T(8,128)(2,1)S(1)} %shard_map.67.t0_ref, bf16[512,512]{1,0:T(8,128)(2,1)S(1)} %collective-permute-done.3.t1_ref), custom_call_target="tpu_custom_call" | custom-call | tf_op jit(solution)/shard_map/pallas_call | solution.py:59
  35.3 1.4 %copy-done.4 = f32[512,1024]{1,0:T(8,128)} copy-done((f32[512,1024]{1,0:T(8,128)}, f32[512,1024]{1,0:T(8,128)S(1)}, u32[]{:S(2)}) %copy-start.4) | copy-done | bytes 2097176
  36.7 2.1 %shard_map.70 = (f32[512,1024]{1,0:T(8,128)S(1)}, f32[16,128]{1,0:T(8,128)S(1)}, f32[8,1024]{1,0:T(8,128)S(1)}) custom-call(f32[1,1]{1,0:T(1,128)} %bitcast.s_ref, bf16[512,512]{1,0:T(8,128)(2,1)S(1)} %collective-permute-done.5.im_ref.i2, bf16[512,512]{1,0:T(8,128)(2,1)S(1)} %shard_map.67.t0_ref, bf16[512,512]{1,0:T(8,128)(2,1)S(1)} %collective-permute-done.3.t1_ref), custom_call_target="tpu_custom_call" | custom-call | tf_op jit(solution)/shard_map/pallas_call | solution.py:59
  38.8 1.3 %copy-done.2 = f32[512,1024]{1,0:T(8,128)} copy-done((f32[512,1024]{1,0:T(8,128)}, f32[512,1024]{1,0:T(8,128)S(1)}, u32[]{:S(2)}) %copy-start.2) | copy-done | bytes 2097176
  40.1 2.1 %shard_map.69 = (f32[512,1024]{1,0:T(8,128)S(1)}, f32[16,128]{1,0:T(8,128)S(1)}, f32[8,1024]{1,0:T(8,128)S(1)}) custom-call(f32[1,1]{1,0:T(1,128)} %bitcast.s_ref, bf16[512,512]{1,0:T(8,128)(2,1)S(1)} %collective-permute-done.4.im_ref.i1, bf16[512,512]{1,0:T(8,128)(2,1)S(1)} %shard_map.67.t0_ref, bf16[512,512]{1,0:T(8,128)(2,1)S(1)} %collective-permute-done.3.t1_ref), custom_call_target="tpu_custom_call" | custom-call | tf_op jit(solution)/shard_map/pallas_call | solution.py:59
  42.2 1.4 %copy-done.6 = f32[512,1024]{1,0:T(8,128)} copy-done((f32[512,1024]{1,0:T(8,128)}, f32[512,1024]{1,0:T(8,128)S(1)}, u32[]{:S(2)}) %copy-start.6) | copy-done | bytes 2097176
  43.6 0.1 shard_map.72
  43.7 0.7 copy-done.8
  44.5 7.9 %all-to-all-start.1 = ((f32[16,40,128]{2,1,0:T(8,128)}), f32[16,40,128]{2,1,0:T(8,128)S(1)}, u32[]{:S(2)}, u32[]{:S(2)}) async-start(f32[16,40,128]{2,1,0:T(8,128)} %bitcast.10), calls=%async_computation.1 | async-start | bytes 655360 | tf_op jit(solution)/shard_map/all_to_all | solution.py:364
  52.4 0.1 collective-permute-start.7
  52.5 1.2 %collective-permute-done.7.b1 = f32[24,128]{1,0:T(8,128)S(1)} collective-permute-done((f32[24,128]{1,0:T(8,128)S(1)}, f32[24,128]{1,0:T(8,128)S(1)}, u32[]{:S(2)}, u32[]{:S(2)}) %collective-permute-start.7) | collective-permute-done | bytes 12320 | tf_op jit(solution)/shard_map/ppermute | solution.py:41
  53.7 3.0 %collective-permute-start.10 = (f32[24,128]{1,0:T(8,128)S(1)}, f32[24,128]{1,0:T(8,128)S(1)}, u32[]{:S(2)}, u32[]{:S(2)}) collective-permute-start(f32[24,128]{1,0:T(8,128)S(1)} %shard_map.73.b0), channel_id=1, source_target_pairs={{0,96},{32,0},{64,32},{96,64},{1,97},{33,1},{65,33},{97,65},{2,98}... | collective-permute-start | bytes 36872 | tf_op jit(solution)/shard_map/ppermute | solution.py:37
  56.7 0.9 collective-permute-start.8
  57.6 0.5 collective-permute-done.10.b3
  58.1 3.8 %collective-permute-done.9.b2 = f32[24,128]{1,0:T(8,128)S(1)} collective-permute-done((f32[24,128]{1,0:T(8,128)S(1)}, f32[24,128]{1,0:T(8,128)S(1)}, u32[]{:S(2)}, u32[]{:S(2)}) %collective-permute-start.9) | collective-permute-done | bytes 12320 | tf_op jit(solution)/shard_map/ppermute | solution.py:37
  61.9 0.2 shard_map.74
  62.1 1.6 %copy-done.5 = f32[512,1024]{1,0:T(8,128)S(1)} copy-done((f32[512,1024]{1,0:T(8,128)S(1)}, f32[512,1024]{1,0:T(8,128)}, u32[]{:S(2)}) %copy-start.5) | copy-done | bytes 2097176
  63.7 1.2 %shard_map.78 = (bf16[512,1024]{1,0:T(8,128)(2,1)S(1)}, f32[544,512]{1,0:T(8,128)S(1)}) custom-call(f32[512,1024]{1,0:T(8,128)S(1)} %copy-done.5, f32[16,128]{1,0:T(8,128)S(1)} %get-tuple-element.46.row_ref, f32[1,1024]{1,0:T(1,128)S(1)} %get-tuple-element.47.col_ref, f32[2,128]{1,0:T(2,128)S(1)} %get-tuple-element.48.unit_ref, ...), custom_call_target="tpu_custom_call" | custom-call | tf_op jit(solution)/shard_map/pallas_call | solution.py:59
  64.9 0.4 copy-done.7
  65.3 1.2 %shard_map.77 = (bf16[512,1024]{1,0:T(8,128)(2,1)S(1)}, f32[544,512]{1,0:T(8,128)S(1)}) custom-call(f32[512,1024]{1,0:T(8,128)S(1)} %copy-done.7, f32[16,128]{1,0:T(8,128)S(1)} %get-tuple-element.46.row_ref, f32[1,1024]{1,0:T(1,128)S(1)} %get-tuple-element.47.col_ref, f32[2,128]{1,0:T(2,128)S(1)} %get-tuple-element.48.unit_ref, ...), custom_call_target="tpu_custom_call" | custom-call | tf_op jit(solution)/shard_map/pallas_call | solution.py:59
  66.5 0.4 copy-done.3
  66.9 1.2 %shard_map.76 = (bf16[512,1024]{1,0:T(8,128)(2,1)S(1)}, f32[544,512]{1,0:T(8,128)S(1)}) custom-call(f32[512,1024]{1,0:T(8,128)S(1)} %copy-done.3, f32[16,128]{1,0:T(8,128)S(1)} %get-tuple-element.46.row_ref, f32[1,1024]{1,0:T(1,128)S(1)} %get-tuple-element.47.col_ref, f32[2,128]{1,0:T(2,128)S(1)} %get-tuple-element.48.unit_ref, ...), custom_call_target="tpu_custom_call" | custom-call | tf_op jit(solution)/shard_map/pallas_call | solution.py:59
  68.1 0.4 copy-done.1
  68.4 1.2 %shard_map.75 = (bf16[512,1024]{1,0:T(8,128)(2,1)S(1)}, f32[544,512]{1,0:T(8,128)S(1)}) custom-call(f32[512,1024]{1,0:T(8,128)S(1)} %copy-done.1, f32[16,128]{1,0:T(8,128)S(1)} %get-tuple-element.46.row_ref, f32[1,1024]{1,0:T(1,128)S(1)} %get-tuple-element.47.col_ref, f32[2,128]{1,0:T(2,128)S(1)} %get-tuple-element.48.unit_ref, ...), custom_call_target="tpu_custom_call" | custom-call | tf_op jit(solution)/shard_map/pallas_call | solution.py:59
  69.6 2.4 %shard_map.79 = (f32[544,512]{1,0:T(8,128)S(1)}, f32[544,512]{1,0:T(8,128)S(1)}) custom-call(bf16[512,1024]{1,0:T(8,128)(2,1)S(1)} %get-tuple-element.58.w0, bf16[512,1024]{1,0:T(8,128)(2,1)S(1)} %get-tuple-element.59.w1, bf16[512,1024]{1,0:T(8,128)(2,1)S(1)} %get-tuple-element.60.w2, bf16[512,1024]{1,0:T(8,128)(2,1)S(1)} %get-tuple-element.61.w3, ...), custom_call_target="tpu_custom_call" | custom-call | tf_op jit(solution)/shard_map/pallas_call | solution.py:59
  72.0 0.1 convert_element_type.124
  72.1 0.1 collective-permute-start.17
  72.2 0.1 convert_element_type.106
  72.4 0.1 convert_element_type.102
  72.5 3.4 %collective-permute-start.11 = (f16[544,512]{1,0:T(8,128)(2,1)S(1)}, f16[544,512]{1,0:T(8,128)(2,1)S(1)}, u32[]{:S(2)}, u32[]{:S(2)}) collective-permute-start(f16[544,512]{1,0:T(8,128)(2,1)S(1)} %convert_element_type.102), channel_id=1, source_target_pairs={{0,2},{1,3},{2,0},{3,1},{4,20},{5,21},{6,22},{7,23},{8,10},{9,11},... | collective-permute-start | bytes 1671176 | tf_op jit(solution)/shard_map/ppermute | solution.py:33
  75.9 0.1 convert_element_type.104
  76.0 1.2 %collective-permute-start.12 = (f16[544,512]{1,0:T(8,128)(2,1)S(1)}, f16[544,512]{1,0:T(8,128)(2,1)S(1)}, u32[]{:S(2)}, u32[]{:S(2)}) collective-permute-start(f16[544,512]{1,0:T(8,128)(2,1)S(1)} %convert_element_type.104), channel_id=1, source_target_pairs={{0,3},{1,0},{2,1},{3,2},{4,28},{5,29},{6,30},{7,31},{8,11},{9,8},{... | collective-permute-start | bytes 1671176 | tf_op jit(solution)/shard_map/ppermute | solution.py:33
  77.2 0.9 collective-permute-start.13
  78.1 0.1 add_convert_fusion.2
  78.2 2.1 %collective-permute-start.18 = (f16[136,512]{1,0:T(8,128)(2,1)S(1)}, f16[136,512]{1,0:T(8,128)(2,1)S(1)}, u32[]{:S(2)}, u32[]{:S(2)}) collective-permute-start(f16[136,512]{1,0:T(8,128)(2,1)S(1)} %get-tuple-element.69), channel_id=1, source_target_pairs={{0,64},{32,96},{64,0},{96,32},{1,65},{33,97},{65,1},{97,33},{2,66}... | collective-permute-start | bytes 417800 | tf_op jit(solution)/shard_map/ppermute | solution.py:37
  80.4 3.3 %collective-permute-done.11 = f16[544,512]{1,0:T(8,128)(2,1)S(1)} collective-permute-done((f16[544,512]{1,0:T(8,128)(2,1)S(1)}, f16[544,512]{1,0:T(8,128)(2,1)S(1)}, u32[]{:S(2)}, u32[]{:S(2)}) %collective-permute-start.11) | collective-permute-done | bytes 557088 | tf_op jit(solution)/shard_map/ppermute | solution.py:33
  83.7 2.3 %collective-permute-start.19 = (f16[136,512]{1,0:T(8,128)(2,1)S(1)}, f16[136,512]{1,0:T(8,128)(2,1)S(1)}, u32[]{:S(2)}, u32[]{:S(2)}) collective-permute-start(f16[136,512]{1,0:T(8,128)(2,1)S(1)} %get-tuple-element.71), channel_id=1, source_target_pairs={{0,96},{32,0},{64,32},{96,64},{1,97},{33,1},{65,33},{97,65},{2,98}... | collective-permute-start | bytes 417800 | tf_op jit(solution)/shard_map/ppermute | solution.py:37
  86.0 4.0 %collective-permute-done.12 = f16[544,512]{1,0:T(8,128)(2,1)S(1)} collective-permute-done((f16[544,512]{1,0:T(8,128)(2,1)S(1)}, f16[544,512]{1,0:T(8,128)(2,1)S(1)}, u32[]{:S(2)}, u32[]{:S(2)}) %collective-permute-start.12) | collective-permute-done | bytes 557088 | tf_op jit(solution)/shard_map/ppermute | solution.py:33
  90.0 0.2 add_convert_fusion.5
  90.2 3.1 %collective-permute-start.14 = (f16[136,512]{1,0:T(8,128)(2,1)S(1)}, f16[136,512]{1,0:T(8,128)(2,1)S(1)}, u32[]{:S(2)}, u32[]{:S(2)}) collective-permute-start(f16[136,512]{1,0:T(8,128)(2,1)S(1)} %get-tuple-element.66), channel_id=1, source_target_pairs={{0,16},{1,17},{2,18},{3,19},{4,6},{5,7},{6,4},{7,5},{8,24},{9,25},... | collective-permute-start | bytes 417800 | tf_op jit(solution)/shard_map/ppermute | solution.py:33
  93.3 0.6 collective-permute-start.16
  93.8 2.7 %collective-permute-start.15 = (f16[136,512]{1,0:T(8,128)(2,1)S(1)}, f16[136,512]{1,0:T(8,128)(2,1)S(1)}, u32[]{:S(2)}, u32[]{:S(2)}) collective-permute-start(f16[136,512]{1,0:T(8,128)(2,1)S(1)} %get-tuple-element.68), channel_id=1, source_target_pairs={{0,24},{1,25},{2,26},{3,27},{4,7},{5,4},{6,5},{7,6},{8,0},{9,1},{1... | collective-permute-start | bytes 417800 | tf_op jit(solution)/shard_map/ppermute | solution.py:33
  96.5 0.1 add_add_fusion
  96.6 0.7 fusion
  97.3 2.2 %collective-permute-done.16 = f16[136,512]{1,0:T(8,128)(2,1)S(1)} collective-permute-done((f16[136,512]{1,0:T(8,128)(2,1)S(1)}, f16[136,512]{1,0:T(8,128)(2,1)S(1)}, u32[]{:S(2)}, u32[]{:S(2)}) %collective-permute-start.16) | collective-permute-done | bytes 139296 | tf_op jit(solution)/shard_map/ppermute | solution.py:33
  99.5 0.1 add_add_fusion.1
  99.7 0.7 fusion.1
  100.4 0.3 shard_map.80
  (31 shorter events, 0.1 us)
Async XLA Ops:
  0.6 6.4 %copy-start.9 = (bf16[128,512]{1,0:T(8,128)(2,1)S(1)}, bf16[128,512]{1,0:T(8,128)(2,1)}, u32[]{:S(2)}) copy-start(bf16[128,512]{1,0:T(8,128)(2,1)} %a0.1) | copy-start | bytes 393220
  2.4 14.9 %all-to-all-start = ((bf16[4,128,512]{2,1,0:T(8,128)(2,1)}), bf16[4,128,512]{2,1,0:T(8,128)(2,1)S(1)}, u32[]{:S(2)}, u32[]{:S(2)}) async-start(bf16[4,128,512]{2,1,0:T(8,128)(2,1)} %broadcast_in_dim.2), calls=%async_computation | async-start | bytes 1048576 | tf_op jit(solution)/shard_map/all_to_all | solution.py:94
  7.0 7.9 %collective-permute-start.1 = (bf16[128,512]{1,0:T(8,128)(2,1)S(1)}, bf16[128,512]{1,0:T(8,128)(2,1)S(1)}, u32[]{:S(2)}, u32[]{:S(2)}) collective-permute-start(bf16[128,512]{1,0:T(8,128)(2,1)S(1)} %copy-done.9), channel_id=1, source_target_pairs={{0,64},{32,96},{64,0},{96,32},{1,65},{33,97},{65,1},{97,33},{2,66}... | collective-permute-start | bytes 393224 | tf_op jit(solution)/shard_map/ppermute | solution.py:37
  10.0 7.2 %collective-permute-start = (bf16[128,512]{1,0:T(8,128)(2,1)S(1)}, bf16[128,512]{1,0:T(8,128)(2,1)S(1)}, u32[]{:S(2)}, u32[]{:S(2)}) collective-permute-start(bf16[128,512]{1,0:T(8,128)(2,1)S(1)} %copy-done.9), channel_id=1, source_target_pairs={{0,32},{32,64},{64,96},{96,0},{1,33},{33,65},{65,97},{97,1},{2,34}... | collective-permute-start | bytes 393224 | tf_op jit(solution)/shard_map/ppermute | solution.py:37
  10.6 6.6 %collective-permute-start.2 = (bf16[128,512]{1,0:T(8,128)(2,1)S(1)}, bf16[128,512]{1,0:T(8,128)(2,1)S(1)}, u32[]{:S(2)}, u32[]{:S(2)}) collective-permute-start(bf16[128,512]{1,0:T(8,128)(2,1)S(1)} %copy-done.9), channel_id=1, source_target_pairs={{0,96},{32,0},{64,32},{96,64},{1,97},{33,1},{65,33},{97,65},{2,98}... | collective-permute-start | bytes 393224 | tf_op jit(solution)/shard_map/ppermute | solution.py:37
  17.3 5.8 %collective-permute-start.3 = (bf16[512,512]{1,0:T(8,128)(2,1)S(1)}, bf16[512,512]{1,0:T(8,128)(2,1)S(1)}, u32[]{:S(2)}, u32[]{:S(2)}) collective-permute-start(bf16[512,512]{1,0:T(8,128)(2,1)S(1)} %shard_map.67.t0_ref), channel_id=1, source_target_pairs={{0,4},{4,0},{1,5},{5,1},{2,6},{6,2},{3,7},{7,3},{8,12},{12,8},{9,1... | collective-permute-start | bytes 1572872 | tf_op jit(solution)/shard_map/ppermute | solution.py:41
  17.4 15.8 %collective-permute-start.6 = (bf16[512,512]{1,0:T(8,128)(2,1)S(1)}, bf16[512,512]{1,0:T(8,128)(2,1)S(1)}, u32[]{:S(2)}, u32[]{:S(2)}) collective-permute-start(bf16[512,512]{1,0:T(8,128)(2,1)S(1)} %shard_map.66.im_ref.i0), channel_id=1, source_target_pairs={{0,3},{1,0},{2,1},{3,2},{4,28},{5,29},{6,30},{7,31},{8,11},{9,8},{... | collective-permute-start | bytes 1572872 | tf_op jit(solution)/shard_map/ppermute | solution.py:33
  20.9 15.8 %collective-permute-start.5 = (bf16[512,512]{1,0:T(8,128)(2,1)S(1)}, bf16[512,512]{1,0:T(8,128)(2,1)S(1)}, u32[]{:S(2)}, u32[]{:S(2)}) collective-permute-start(bf16[512,512]{1,0:T(8,128)(2,1)S(1)} %shard_map.66.im_ref.i0), channel_id=1, source_target_pairs={{0,2},{1,3},{2,0},{3,1},{4,20},{5,21},{6,22},{7,23},{8,10},{9,11},... | collective-permute-start | bytes 1572872 | tf_op jit(solution)/shard_map/ppermute | solution.py:33
  21.4 18.7 %collective-permute-start.4 = (bf16[512,512]{1,0:T(8,128)(2,1)S(1)}, bf16[512,512]{1,0:T(8,128)(2,1)S(1)}, u32[]{:S(2)}, u32[]{:S(2)}) collective-permute-start(bf16[512,512]{1,0:T(8,128)(2,1)S(1)} %shard_map.66.im_ref.i0), channel_id=1, source_target_pairs={{0,1},{1,2},{2,3},{3,0},{4,12},{5,13},{6,14},{7,15},{8,9},{9,10},{... | collective-permute-start | bytes 1572872 | tf_op jit(solution)/shard_map/ppermute | solution.py:33
  25.3 1.3 %copy-start = (f32[512,1024]{1,0:T(8,128)}, f32[512,1024]{1,0:T(8,128)S(1)}, u32[]{:S(2)}) copy-start(f32[512,1024]{1,0:T(8,128)S(1)} %get-tuple-element.35.l_ref) | copy-start | bytes 6291460
  35.3 1.4 %copy-start.4 = (f32[512,1024]{1,0:T(8,128)}, f32[512,1024]{1,0:T(8,128)S(1)}, u32[]{:S(2)}) copy-start(f32[512,1024]{1,0:T(8,128)S(1)} %get-tuple-element.55.l_ref) | copy-start | bytes 6291460
  38.8 1.3 %copy-start.2 = (f32[512,1024]{1,0:T(8,128)}, f32[512,1024]{1,0:T(8,128)S(1)}, u32[]{:S(2)}) copy-start(f32[512,1024]{1,0:T(8,128)S(1)} %get-tuple-element.51.l_ref) | copy-start | bytes 6291460
  42.2 1.4 %copy-start.6 = (f32[512,1024]{1,0:T(8,128)}, f32[512,1024]{1,0:T(8,128)S(1)}, u32[]{:S(2)}) copy-start(f32[512,1024]{1,0:T(8,128)S(1)} %get-tuple-element.53.l_ref) | copy-start | bytes 6291460
  43.7 0.8 copy-start.8
  44.5 17.4 %all-to-all-start.1 = ((f32[16,40,128]{2,1,0:T(8,128)}), f32[16,40,128]{2,1,0:T(8,128)S(1)}, u32[]{:S(2)}, u32[]{:S(2)}) async-start(f32[16,40,128]{2,1,0:T(8,128)} %bitcast.10), calls=%async_computation.1 | async-start | bytes 655360 | tf_op jit(solution)/shard_map/all_to_all | solution.py:364
  52.4 1.3 %collective-permute-start.7 = (f32[24,128]{1,0:T(8,128)S(1)}, f32[24,128]{1,0:T(8,128)S(1)}, u32[]{:S(2)}, u32[]{:S(2)}) collective-permute-start(f32[24,128]{1,0:T(8,128)S(1)} %get-tuple-element.45.b0), channel_id=1, source_target_pairs={{0,4},{4,0},{1,5},{5,1},{2,6},{6,2},{3,7},{7,3},{8,12},{12,8},{9,1... | collective-permute-start | bytes 36872 | tf_op jit(solution)/shard_map/ppermute | solution.py:41
  53.7 4.4 %collective-permute-start.10 = (f32[24,128]{1,0:T(8,128)S(1)}, f32[24,128]{1,0:T(8,128)S(1)}, u32[]{:S(2)}, u32[]{:S(2)}) collective-permute-start(f32[24,128]{1,0:T(8,128)S(1)} %shard_map.73.b0), channel_id=1, source_target_pairs={{0,96},{32,0},{64,32},{96,64},{1,97},{33,1},{65,33},{97,65},{2,98}... | collective-permute-start | bytes 36872 | tf_op jit(solution)/shard_map/ppermute | solution.py:37
  56.7 5.2 %collective-permute-start.9 = (f32[24,128]{1,0:T(8,128)S(1)}, f32[24,128]{1,0:T(8,128)S(1)}, u32[]{:S(2)}, u32[]{:S(2)}) collective-permute-start(f32[24,128]{1,0:T(8,128)S(1)} %shard_map.73.b0), channel_id=1, source_target_pairs={{0,64},{32,96},{64,0},{96,32},{1,65},{33,97},{65,1},{97,33},{2,66}... | collective-permute-start | bytes 36872 | tf_op jit(solution)/shard_map/ppermute | solution.py:37
  56.7 5.2 %collective-permute-start.8 = (f32[24,128]{1,0:T(8,128)S(1)}, f32[24,128]{1,0:T(8,128)S(1)}, u32[]{:S(2)}, u32[]{:S(2)}) collective-permute-start(f32[24,128]{1,0:T(8,128)S(1)} %shard_map.73.b0), channel_id=1, source_target_pairs={{0,32},{32,64},{64,96},{96,0},{1,33},{33,65},{65,97},{97,1},{2,34}... | collective-permute-start | bytes 36872 | tf_op jit(solution)/shard_map/ppermute | solution.py:37
  62.1 1.6 %copy-start.5 = (f32[512,1024]{1,0:T(8,128)S(1)}, f32[512,1024]{1,0:T(8,128)}, u32[]{:S(2)}) copy-start(f32[512,1024]{1,0:T(8,128)} %copy-done.4) | copy-start | bytes 6291460
  63.7 1.6 %copy-start.7 = (f32[512,1024]{1,0:T(8,128)S(1)}, f32[512,1024]{1,0:T(8,128)}, u32[]{:S(2)}) copy-start(f32[512,1024]{1,0:T(8,128)} %copy-done.6) | copy-start | bytes 6291460
  65.3 1.6 %copy-start.3 = (f32[512,1024]{1,0:T(8,128)S(1)}, f32[512,1024]{1,0:T(8,128)}, u32[]{:S(2)}) copy-start(f32[512,1024]{1,0:T(8,128)} %copy-done.2) | copy-start | bytes 6291460
  66.9 1.6 %copy-start.1 = (f32[512,1024]{1,0:T(8,128)S(1)}, f32[512,1024]{1,0:T(8,128)}, u32[]{:S(2)}) copy-start(f32[512,1024]{1,0:T(8,128)} %copy-done) | copy-start | bytes 6291460
  72.1 6.0 %collective-permute-start.17 = (f16[544,512]{1,0:T(8,128)(2,1)S(1)}, f16[544,512]{1,0:T(8,128)(2,1)S(1)}, u32[]{:S(2)}, u32[]{:S(2)}) collective-permute-start(f16[544,512]{1,0:T(8,128)(2,1)S(1)} %convert_element_type.124), channel_id=1, source_target_pairs={{0,4},{4,0},{1,5},{5,1},{2,6},{6,2},{3,7},{7,3},{8,12},{12,8},{9,1... | collective-permute-start | bytes 1671176 | tf_op jit(solution)/shard_map/ppermute | solution.py:41
  72.5 11.2 %collective-permute-start.11 = (f16[544,512]{1,0:T(8,128)(2,1)S(1)}, f16[544,512]{1,0:T(8,128)(2,1)S(1)}, u32[]{:S(2)}, u32[]{:S(2)}) collective-permute-start(f16[544,512]{1,0:T(8,128)(2,1)S(1)} %convert_element_type.102), channel_id=1, source_target_pairs={{0,2},{1,3},{2,0},{3,1},{4,20},{5,21},{6,22},{7,23},{8,10},{9,11},... | collective-permute-start | bytes 1671176 | tf_op jit(solution)/shard_map/ppermute | solution.py:33
  76.0 14.0 %collective-permute-start.12 = (f16[544,512]{1,0:T(8,128)(2,1)S(1)}, f16[544,512]{1,0:T(8,128)(2,1)S(1)}, u32[]{:S(2)}, u32[]{:S(2)}) collective-permute-start(f16[544,512]{1,0:T(8,128)(2,1)S(1)} %convert_element_type.104), channel_id=1, source_target_pairs={{0,3},{1,0},{2,1},{3,2},{4,28},{5,29},{6,30},{7,31},{8,11},{9,8},{... | collective-permute-start | bytes 1671176 | tf_op jit(solution)/shard_map/ppermute | solution.py:33
  77.2 12.7 %collective-permute-start.13 = (f16[544,512]{1,0:T(8,128)(2,1)S(1)}, f16[544,512]{1,0:T(8,128)(2,1)S(1)}, u32[]{:S(2)}, u32[]{:S(2)}) collective-permute-start(f16[544,512]{1,0:T(8,128)(2,1)S(1)} %convert_element_type.106), channel_id=1, source_target_pairs={{0,1},{1,2},{2,3},{3,0},{4,12},{5,13},{6,14},{7,15},{8,9},{9,10},{... | collective-permute-start | bytes 1671176 | tf_op jit(solution)/shard_map/ppermute | solution.py:33
  78.2 15.6 %collective-permute-start.18 = (f16[136,512]{1,0:T(8,128)(2,1)S(1)}, f16[136,512]{1,0:T(8,128)(2,1)S(1)}, u32[]{:S(2)}, u32[]{:S(2)}) collective-permute-start(f16[136,512]{1,0:T(8,128)(2,1)S(1)} %get-tuple-element.69), channel_id=1, source_target_pairs={{0,64},{32,96},{64,0},{96,32},{1,65},{33,97},{65,1},{97,33},{2,66}... | collective-permute-start | bytes 417800 | tf_op jit(solution)/shard_map/ppermute | solution.py:37
  80.4 16.2 %collective-permute-start.20 = (f16[136,512]{1,0:T(8,128)(2,1)S(1)}, f16[136,512]{1,0:T(8,128)(2,1)S(1)}, u32[]{:S(2)}, u32[]{:S(2)}) collective-permute-start(f16[136,512]{1,0:T(8,128)(2,1)S(1)} %get-tuple-element.70), channel_id=1, source_target_pairs={{0,32},{32,64},{64,96},{96,0},{1,33},{33,65},{65,97},{97,1},{2,34}... | collective-permute-start | bytes 417800 | tf_op jit(solution)/shard_map/ppermute | solution.py:37
  83.7 12.8 %collective-permute-start.19 = (f16[136,512]{1,0:T(8,128)(2,1)S(1)}, f16[136,512]{1,0:T(8,128)(2,1)S(1)}, u32[]{:S(2)}, u32[]{:S(2)}) collective-permute-start(f16[136,512]{1,0:T(8,128)(2,1)S(1)} %get-tuple-element.71), channel_id=1, source_target_pairs={{0,96},{32,0},{64,32},{96,64},{1,97},{33,1},{65,33},{97,65},{2,98}... | collective-permute-start | bytes 417800 | tf_op jit(solution)/shard_map/ppermute | solution.py:37
  90.2 7.1 %collective-permute-start.14 = (f16[136,512]{1,0:T(8,128)(2,1)S(1)}, f16[136,512]{1,0:T(8,128)(2,1)S(1)}, u32[]{:S(2)}, u32[]{:S(2)}) collective-permute-start(f16[136,512]{1,0:T(8,128)(2,1)S(1)} %get-tuple-element.66), channel_id=1, source_target_pairs={{0,16},{1,17},{2,18},{3,19},{4,6},{5,7},{6,4},{7,5},{8,24},{9,25},... | collective-permute-start | bytes 417800 | tf_op jit(solution)/shard_map/ppermute | solution.py:33
  93.3 6.3 %collective-permute-start.16 = (f16[136,512]{1,0:T(8,128)(2,1)S(1)}, f16[136,512]{1,0:T(8,128)(2,1)S(1)}, u32[]{:S(2)}, u32[]{:S(2)}) collective-permute-start(f16[136,512]{1,0:T(8,128)(2,1)S(1)} %get-tuple-element.67), channel_id=1, source_target_pairs={{0,8},{1,9},{2,10},{3,11},{4,5},{5,6},{6,7},{7,4},{8,16},{9,17},{1... | collective-permute-start | bytes 417800 | tf_op jit(solution)/shard_map/ppermute | solution.py:33
  93.8 5.7 %collective-permute-start.15 = (f16[136,512]{1,0:T(8,128)(2,1)S(1)}, f16[136,512]{1,0:T(8,128)(2,1)S(1)}, u32[]{:S(2)}, u32[]{:S(2)}) collective-permute-start(f16[136,512]{1,0:T(8,128)(2,1)S(1)} %get-tuple-element.68), channel_id=1, source_target_pairs={{0,24},{1,25},{2,26},{3,27},{4,7},{5,4},{6,5},{7,6},{8,0},{9,1},{1... | collective-permute-start | bytes 417800 | tf_op jit(solution)/shard_map/ppermute | solution.py:33
where the time goes:
time: 104 us; the launch traced here: 103 us
  starting transfers between devices  44.1 us (42%)
  waiting for transfers between devices  25.6 us (25%)
  Pallas kernels  16.3 us (16%)
  local copies, waits for them, and re-layouts  10.8 us (10%)
  between operations  3.88 us (4%)
  other arithmetic  2.36 us (2%)
    ppermute x9, starting transfers between devices, turn(): return lax.ppermute(value, ('y', 'c', 'z'), pairs)  16.8 us
    pallas_call x15, Pallas kernels, call(): pl.pallas_call(kernel, out_shape=outs, in_specs=[pl.BlockSpec(memory_spac...  16.3 us
    ppermute x9, waiting for transfers between devices, turn(): return lax.ppermute(value, ('y', 'c', 'z'), pairs)  16.2 us
    ppermute x9, starting transfers between devices, along_x(): return lax.ppermute(value, 'x', [(i, (i + shift) % 4) for i in range(4)])  14.6 us
    unnamed x20, local copies, waits for them, and re-layouts  8.96 us
    ppermute x9, waiting for transfers between devices, along_x(): return lax.ppermute(value, 'x', [(i, (i + shift) % 4) for i in range(4)])  8.22 us
    all_to_all x1, starting transfers between devices, program(): lax.all_to_all(rows.reshape(16, 40, 128), ('y', 'z'), 0, 0, tiled=True)  7.95 us
    all_to_all x1, starting transfers between devices, lined_up(): lax.all_to_all(copies, ('y', 'c', 'z'), 0, 0, axis_index_groups=LINES, ti...  4.57 us
  transfers between devices with their start and end apart: 23, of which 9 were waited for; matrix products, arithmetic and copies ran while one was open for 1% of the time, Pallas kernels for 6%

commit v1 on v0

--- a/solution.py
+++ b/solution.py
@@ -48,9 +48,6 @@
     return [got[d] for d in range(4)]
 
 
-LINES = [[(y * 2) * 4 + z for y in range(4)] for z in range(4)] + [
-    [(y * 2 + 1) * 4 + z for z in range(4)] for y in range(4)
-]
 NT = (((1,), (1,)), ((), ()))
 TN = (((0,), (0,)), ((), ()))
 
@@ -72,40 +69,35 @@
     return pltpu.VMEM(shape, dtype)
 
 
+def join_kernel(a0, a1, a2, a3, o_ref):
+    for k, a in enumerate((a0, a1, a2, a3)):
+        o_ref[128 * k : 128 * (k + 1), :] = a[...]
+
+
+def joined(values):
+    return call(join_kernel, out((512, 512), BF16), *values)
+
+
 def places():
     y, z, on_y = lax.axis_index("y"), lax.axis_index("z"), lax.axis_index("c") == 0
     return jnp.where(on_y, y, z), jnp.where(on_y, z, y), lax.axis_index("x")
 
 
-def turn_kernel(axis, a_ref, o_ref):
-    here = places()[axis]
-    for d in range(4):
-        at = pl.multiple_of(lax.rem(here - d + 4, 4) * 128, 128)
-        o_ref[128 * d : 128 * (d + 1), :] = a_ref[pl.ds(at, 128), :]
-
-
-def join_kernel(a0, a1, a2, a3, o_ref):
-    for k, a in enumerate((a0, a1, a2, a3)):
-        o_ref[128 * k : 128 * (k + 1), :] = a[...]
-
-
-def lined_up(value):
-    copies = jnp.broadcast_to(value[None], (4, ROWS, value.shape[1]))
-    got = lax.all_to_all(copies, ("y", "c", "z"), 0, 0, axis_index_groups=LINES, tiled=True)
-    return call(functools.partial(turn_kernel, 0), out((512, 512), BF16), got.reshape(512, -1))
-
-
 def peak(ref):
     tall = jnp.max(jnp.abs(ref[...].astype(F32)), axis=0, keepdims=True)
     return jnp.broadcast_to(jnp.max(tall, axis=1, keepdims=True), (1, 128))
 
 
-def logits_kernel(first, s_ref, im_ref, t0_ref, t1_ref, l_ref, rows_ref, cols_ref, top_scr, sum_scr, mean_scr):
-    s2 = s_ref[0, 0]
-    for h, t_ref in enumerate((t0_ref, t1_ref)):
+def logits_into(l_ref, s2, im_ref, t_refs):
+    for h, t_ref in enumerate(t_refs):
         l_ref[:, 512 * h : 512 * (h + 1)] = s2 * lax.dot_general(
             im_ref[...], t_ref[...], NT, preferred_element_type=F32
         )
+
+
+def logits_kernel(first, s_ref, im_ref, t0_ref, t1_ref, rows_ref, cols_ref, l_ref, top_scr, sum_scr, mean_scr):
+    s2 = s_ref[0, 0]
+    logits_into(l_ref, s2, im_ref, (t0_ref, t1_ref))
 
     def tops(i, col_tops):
         here = pl.ds(pl.multiple_of(i * 64, 64), 64)
@@ -168,10 +160,10 @@
 def logits_of(k, s2, im, t0, t1):
     return call(
         functools.partial(logits_kernel, k == 0),
-        (out((512, 1024)), out((16, 128)), out((8, 1024))),
+        (out((16, 128)), out((8, 1024))),
         s2, im, t0, t1,
         smem=(0,),
-        scratch=[pltpu.VMEM((512, 128), F32)] * 3,
+        scratch=[pltpu.VMEM((512, 1024), F32)] + [pltpu.VMEM((512, 128), F32)] * 3,
     )
 
 
@@ -230,12 +222,12 @@
     return jnp.concatenate(pieces, axis=0)
 
 
-def middle_kernel(b0, b1, col_ref):
-    swapped = [jnp.concatenate([b1[k + 4 : k + 8, :], b1[k : k + 4, :]], axis=0) for k in (0, 8)]
-    lse, mean = merge([(b0[0:8, :], b0[8:16, :]), swapped])
+def middle_kernel(b0, b1, b2, b3, col_ref):
+    cs = (b0, b1, b2, b3)
+    lse, mean = merge([(rolled(c[0:8, :], d, 2), rolled(c[8:16, :], d, 2)) for d, c in enumerate(cs)])
     col_ref[0:8, :] = lse
     col_ref[8:16, :] = mean
-    col_ref[16:24, :] = jnp.maximum(b0[16:24, :], b1[16:24, :])
+    col_ref[16:24, :] = greatest([c[16:24, :] for c in cs])
 
 
 def pieces_of(value):
@@ -276,7 +268,7 @@
     return jnp.sum(jnp.sum(v, axis=0, keepdims=True), axis=1, keepdims=True)
 
 
-def end_kernel(s_ref, a_ref, b0, b1, b2, b3, row_ref, col_ref, codes_ref, unit_ref, back_ref, scr):
+def end_kernel(s_ref, a_ref, b0, b1, row_ref, col_ref, codes_ref, unit_ref, back_ref, scr):
     rs = [a_ref[40 * k : 40 * (k + 1), :] for k in range(16)]
     lse, mean = merge([(r[0:16, :], r[16:32, :]) for r in rs])
     scr[...] = lse + 1.0
@@ -286,11 +278,11 @@
     diagonal = total_of(sum(r[32:33, :] for r in rs)) * LN2
     text_peak = greatest([r[33:34, :] for r in rs])
     codes_ref[1:2, :] = encoded(total_of(lse) * LN2 - 2.0 * diagonal, 0.5 * LN2 * total_of(mean) - diagonal)
-    cs = (b0, b1, b2, b3)
-    lse, mean = merge([(rolled(c[0:8, :], d, 2), rolled(c[8:16, :], d, 2)) for d, c in enumerate(cs)])
+    swapped = [jnp.concatenate([b1[k + 4 : k + 8, :], b1[k : k + 4, :]], axis=0) for k in (0, 8)]
+    lse, mean = merge([(b0[0:8, :], b0[8:16, :]), swapped])
     for k in range(8):
         col_ref[:, 128 * k : 128 * (k + 1)] = lse[k : k + 1, :] + 1.0
-    image_peak = greatest([c[16:17, :] for c in cs])
+    image_peak = jnp.maximum(b0[16:17, :], b1[16:17, :])
     codes_ref[0:1, :] = encoded(total_of(lse) * LN2, 0.5 * LN2 * total_of(mean))
     scale = s_ref[0, 0] * LN2
     for k, top in enumerate((text_peak, image_peak)):
@@ -300,7 +292,8 @@
         back_ref[k : k + 1, :] = jnp.concatenate([back] * 4, axis=1)
 
 
-def image_kernel(which, l_ref, row_ref, col_ref, unit_ref, codes_ref, t0_ref, t1_ref, w_ref, g_ref):
+def image_kernel(which, s_ref, im_ref, row_ref, col_ref, unit_ref, codes_ref, t0_ref, t1_ref, w_ref, g_ref, l_ref):
+    logits_into(l_ref, s_ref[0, 0], im_ref, (t0_ref, t1_ref))
     for j in range(4):
         at = slice(128 * j, 128 * (j + 1))
         row = row_ref[4 * which + j : 4 * which + j + 1, :]
@@ -347,24 +340,25 @@
 
 def program(images, texts, log_scale):
     s2 = jnp.reshape(jnp.exp(log_scale) * LOG2E, (1, 1))
-    line = lined_up(images)
+    line = everyone(images, lambda v, d: turn(v, d, True))
+    line = joined(line)
     chunks = everyone(line, lambda v, d: turn(v, d, False))
-    t0 = call(join_kernel, out((512, 512), BF16), *everyone(texts, along_x))
+    t0 = everyone(texts, along_x)
+    t0 = joined(t0)
     t1 = other_core(t0)
     parts = [None] * 4
     for k in (0, 1, 3, 2):
         parts[k] = logits_of(k, s2, chunks[k], t0, t1)
-    ls = [p[0] for p in parts]
     rows, cols = call(
         start_kernel,
-        (out((640, 128)), out((24, 128))),
-        *[p[1] for p in parts], *[p[2] for p in parts],
+        (jax.ShapeDtypeStruct((640, 128), F32), out((24, 128))),
+        *[p[0] for p in parts], *[p[1] for p in parts],
         scratch=[pltpu.VMEM((40, 128), F32)],
     )
+    cols = everyone(cols, along_x)
     rows = lax.all_to_all(rows.reshape(16, 40, 128), ("y", "z"), 0, 0, tiled=True).reshape(640, 128)
-    other = other_core(cols)
-    cols = call(middle_kernel, out((24, 128)), cols, other)
-    cols = everyone(cols, along_x)
+    cols = call(middle_kernel, out((24, 128)), *cols)
+    cols = [cols, other_core(cols)]
     row_lse, col_lse, codes, unit, back = call(
         end_kernel,
         (out((16, 128)), out((1, 1024)), out((2, 512)), out((2, 128)), out((2, 512))),
@@ -377,7 +371,9 @@
         ws[k], gs[k] = call(
             functools.partial(image_kernel, k),
             (out((512, 1024), BF16), out((544, 512))),
-            ls[k], row_lse, col_lse, unit, codes, t0, t1,
+            s2, chunks[k], row_lse, col_lse, unit, codes, t0, t1,
+            smem=(0,),
+            scratch=[pltpu.VMEM((512, 1024), F32)],
         )
         if k:
             sent[k] = turn(gs[k].astype(F16), 4 - k, False)

time: 104 us -> 93.1 us (0.90)
  local copies, waits for them, and re-layouts: 10.8 us -> 1.65 us
  starting transfers between devices: 44.1 us -> 40.2 us
  Pallas kernels: 16.3 us -> 17.8 us
    unnamed x20 -> x6, local copies, waits for them, and re-layouts: 8.96 us -> 1.64 us
    all_to_all x1 -> x0, starting transfers between devices: 4.57 us -> none  [lined_up(): lax.all_to_all(copies, ('y', 'c', 'z'), 0, 0, axis_index_groups=LINES, ti...]
    ppermute x9 -> x12, starting transfers between devices: 16.8 us -> 20.8 us  [turn(): return lax.ppermute(value, ('y', 'c', 'z'), pairs)]
    ppermute x9, waiting for transfers between devices: 8.22 us -> 6.03 us  [along_x(): return lax.ppermute(value, 'x', [(i, (i + shift) % 4) for i in range(4)])]
    all_to_all x1, starting transfers between devices: 7.95 us -> 5.89 us  [program(): lax.all_to_all(rows.reshape(16, 40, 128), ('y', 'z'), 0, 0, tiled=True)]
    broadcast_in_dim x1 -> x0, local copies, waits for them, and re-layouts: 1.79 us -> none  [lined_up(): copies = jnp.broadcast_to(value[None], (4, ROWS, value.shape[1]))]
    pallas_call x15, Pallas kernels: 16.3 us -> 17.8 us  [call(): pl.pallas_call(kernel, out_shape=outs, in_specs=[pl.BlockSpec(memory_spac...]
    all_to_all x1, waiting for transfers between devices: 0.01 us -> 1.45 us  [program(): lax.all_to_all(rows.reshape(16, 40, 128), ('y', 'z'), 0, 0, tiled=True)]
  transfers between devices with their start and end apart: 23 -> 25, of which waited for: 9 -> 13; matrix products, arithmetic and copies ran while one was open for 1% -> 2% of each run, Pallas kernels for 6% -> 15%
where the time goes in v1:
time: 93.1 us; the launch traced here: 92.1 us
  starting transfers between devices  40.2 us (43%)
  waiting for transfers between devices  26.2 us (28%)
  Pallas kernels  17.8 us (19%)
  between operations  3.87 us (4%)
  other arithmetic  2.41 us (3%)
  local copies, waits for them, and re-layouts  1.65 us (2%)
    ppermute x12, starting transfers between devices, turn(): return lax.ppermute(value, ('y', 'c', 'z'), pairs)  20.8 us
    pallas_call x15, Pallas kernels, call(): pl.pallas_call(kernel, out_shape=outs, in_specs=[pl.BlockSpec(memory_spac...  17.8 us
    ppermute x12, waiting for transfers between devices, turn(): return lax.ppermute(value, ('y', 'c', 'z'), pairs)  17.6 us
    ppermute x9, starting transfers between devices, along_x(): return lax.ppermute(value, 'x', [(i, (i + shift) % 4) for i in range(4)])  13.2 us
    ppermute x9, waiting for transfers between devices, along_x(): return lax.ppermute(value, 'x', [(i, (i + shift) % 4) for i in range(4)])  6.03 us
    all_to_all x1, starting transfers between devices, program(): lax.all_to_all(rows.reshape(16, 40, 128), ('y', 'z'), 0, 0, tiled=True)  5.89 us
  transfers between devices with their start and end apart: 25, of which 13 were waited for; matrix products, arithmetic and copies ran while one was open for 2% of the time, Pallas kernels for 15%

profile of v1, /device:TPU:0, one launch (start us, length us, event | category | flops | bytes accessed | tf_op | source)
XLA Modules:
  0.0 92.1 jit_solution(8802206339905911324)
XLA Ops:
  0.6 1.7 %collective-permute-start.3 = (bf16[128,512]{1,0:T(8,128)(2,1)}, bf16[128,512]{1,0:T(8,128)(2,1)S(1)}, u32[]{:S(2)}, u32[]{:S(2)}) collective-permute-start(bf16[128,512]{1,0:T(8,128)(2,1)} %a0.3), channel_id=1, source_target_pairs={{0,32},{32,64},{64,96},{96,0},{1,33},{33,65},{65,97},{97,1},{2,34}... | collective-permute-start | bytes 393224 | tf_op jit(solution)/shard_map/ppermute | solution.py:37
  2.3 2.7 %collective-permute-start.4 = (bf16[128,512]{1,0:T(8,128)(2,1)}, bf16[128,512]{1,0:T(8,128)(2,1)S(1)}, u32[]{:S(2)}, u32[]{:S(2)}) collective-permute-start(bf16[128,512]{1,0:T(8,128)(2,1)} %a0.3), channel_id=1, source_target_pairs={{0,64},{32,96},{64,0},{96,32},{1,65},{33,97},{65,1},{97,33},{2,66}... | collective-permute-start | bytes 393224 | tf_op jit(solution)/shard_map/ppermute | solution.py:37
  5.0 1.4 %collective-permute-start.5 = (bf16[128,512]{1,0:T(8,128)(2,1)}, bf16[128,512]{1,0:T(8,128)(2,1)S(1)}, u32[]{:S(2)}, u32[]{:S(2)}) collective-permute-start(bf16[128,512]{1,0:T(8,128)(2,1)} %a0.3), channel_id=1, source_target_pairs={{0,96},{32,0},{64,32},{96,64},{1,97},{33,1},{65,33},{97,65},{2,98}... | collective-permute-start | bytes 393224 | tf_op jit(solution)/shard_map/ppermute | solution.py:37
  6.5 1.6 %collective-permute-start = (bf16[128,512]{1,0:T(8,128)(2,1)}, bf16[128,512]{1,0:T(8,128)(2,1)S(1)}, u32[]{:S(2)}, u32[]{:S(2)}) collective-permute-start(bf16[128,512]{1,0:T(8,128)(2,1)} %a0.2), channel_id=1, source_target_pairs={{0,8},{1,9},{2,10},{3,11},{4,5},{5,6},{6,7},{7,4},{8,16},{9,17},{1... | collective-permute-start | bytes 393224 | tf_op jit(solution)/shard_map/ppermute | solution.py:33
  8.0 2.9 %collective-permute-start.1 = (bf16[128,512]{1,0:T(8,128)(2,1)}, bf16[128,512]{1,0:T(8,128)(2,1)S(1)}, u32[]{:S(2)}, u32[]{:S(2)}) collective-permute-start(bf16[128,512]{1,0:T(8,128)(2,1)} %a0.2), channel_id=1, source_target_pairs={{0,16},{1,17},{2,18},{3,19},{4,6},{5,7},{6,4},{7,5},{8,24},{9,25},... | collective-permute-start | bytes 393224 | tf_op jit(solution)/shard_map/ppermute | solution.py:33
  10.9 0.0 collective-permute-done.3.a1
  10.9 1.3 %collective-permute-start.2 = (bf16[128,512]{1,0:T(8,128)(2,1)}, bf16[128,512]{1,0:T(8,128)(2,1)S(1)}, u32[]{:S(2)}, u32[]{:S(2)}) collective-permute-start(bf16[128,512]{1,0:T(8,128)(2,1)} %a0.2), channel_id=1, source_target_pairs={{0,24},{1,25},{2,26},{3,27},{4,7},{5,4},{6,5},{7,6},{8,0},{9,1},{1... | collective-permute-start | bytes 393224 | tf_op jit(solution)/shard_map/ppermute | solution.py:33
  12.3 0.0 collective-permute-done.5.a3
  12.3 0.9 copy-done.1
  13.2 0.1 collective-permute-start.6
  13.4 2.1 %collective-permute-done.1.a2 = bf16[128,512]{1,0:T(8,128)(2,1)S(1)} collective-permute-done((bf16[128,512]{1,0:T(8,128)(2,1)}, bf16[128,512]{1,0:T(8,128)(2,1)S(1)}, u32[]{:S(2)}, u32[]{:S(2)}) %collective-permute-start.1) | collective-permute-done | bytes 131104 | tf_op jit(solution)/shard_map/ppermute | solution.py:33
  15.5 0.6 collective-permute-done.2.a3
  16.2 2.0 %collective-permute-start.7 = (bf16[512,512]{1,0:T(8,128)(2,1)S(1)}, bf16[512,512]{1,0:T(8,128)(2,1)S(1)}, u32[]{:S(2)}, u32[]{:S(2)}) collective-permute-start(bf16[512,512]{1,0:T(8,128)(2,1)S(1)} %shard_map.66.im_ref.i0), channel_id=1, source_target_pairs={{0,1},{1,2},{2,3},{3,0},{4,12},{5,13},{6,14},{7,15},{8,9},{9,10},{... | collective-permute-start | bytes 1572872 | tf_op jit(solution)/shard_map/ppermute | solution.py:33
  18.2 3.6 %collective-permute-start.8 = (bf16[512,512]{1,0:T(8,128)(2,1)S(1)}, bf16[512,512]{1,0:T(8,128)(2,1)S(1)}, u32[]{:S(2)}, u32[]{:S(2)}) collective-permute-start(bf16[512,512]{1,0:T(8,128)(2,1)S(1)} %shard_map.66.im_ref.i0), channel_id=1, source_target_pairs={{0,2},{1,3},{2,0},{3,1},{4,20},{5,21},{6,22},{7,23},{8,10},{9,11},... | collective-permute-start | bytes 1572872 | tf_op jit(solution)/shard_map/ppermute | solution.py:33
  21.7 1.0 %collective-permute-start.9 = (bf16[512,512]{1,0:T(8,128)(2,1)S(1)}, bf16[512,512]{1,0:T(8,128)(2,1)S(1)}, u32[]{:S(2)}, u32[]{:S(2)}) collective-permute-start(bf16[512,512]{1,0:T(8,128)(2,1)S(1)} %shard_map.66.im_ref.i0), channel_id=1, source_target_pairs={{0,3},{1,0},{2,1},{3,2},{4,28},{5,29},{6,30},{7,31},{8,11},{9,8},{... | collective-permute-start | bytes 1572872 | tf_op jit(solution)/shard_map/ppermute | solution.py:33
  23.4 2.2 %shard_map.68 = (f32[16,128]{1,0:T(8,128)S(1)}, f32[8,1024]{1,0:T(8,128)S(1)}) custom-call(f32[1,1]{1,0:T(1,128)} %bitcast.s_ref, bf16[512,512]{1,0:T(8,128)(2,1)S(1)} %shard_map.66.im_ref.i0, bf16[512,512]{1,0:T(8,128)(2,1)S(1)} %shard_map.67.t0_ref, bf16[512,512]{1,0:T(8,128)(2,1)S(1)} %collective-permute-done.6.t1_ref), custom_call_target="tpu_custom_call" | custom-call | tf_op jit(solution)/shard_map/pallas_call | solution.py:56
  25.6 1.8 %collective-permute-done.7.im_ref.i1 = bf16[512,512]{1,0:T(8,128)(2,1)S(1)} collective-permute-done((bf16[512,512]{1,0:T(8,128)(2,1)S(1)}, bf16[512,512]{1,0:T(8,128)(2,1)S(1)}, u32[]{:S(2)}, u32[]{:S(2)}) %collective-permute-start.7) | collective-permute-done | bytes 524320 | tf_op jit(solution)/shard_map/ppermute | solution.py:33
  27.4 2.1 %shard_map.69 = (f32[16,128]{1,0:T(8,128)S(1)}, f32[8,1024]{1,0:T(8,128)S(1)}) custom-call(f32[1,1]{1,0:T(1,128)} %bitcast.s_ref, bf16[512,512]{1,0:T(8,128)(2,1)S(1)} %collective-permute-done.7.im_ref.i1, bf16[512,512]{1,0:T(8,128)(2,1)S(1)} %shard_map.67.t0_ref, bf16[512,512]{1,0:T(8,128)(2,1)S(1)} %collective-permute-done.6.t1_ref), custom_call_target="tpu_custom_call" | custom-call | tf_op jit(solution)/shard_map/pallas_call | solution.py:56
  29.5 5.0 %collective-permute-done.8.im_ref.i2 = bf16[512,512]{1,0:T(8,128)(2,1)S(1)} collective-permute-done((bf16[512,512]{1,0:T(8,128)(2,1)S(1)}, bf16[512,512]{1,0:T(8,128)(2,1)S(1)}, u32[]{:S(2)}, u32[]{:S(2)}) %collective-permute-start.8) | collective-permute-done | bytes 524320 | tf_op jit(solution)/shard_map/ppermute | solution.py:33
  34.5 2.1 %shard_map.70 = (f32[16,128]{1,0:T(8,128)S(1)}, f32[8,1024]{1,0:T(8,128)S(1)}) custom-call(f32[1,1]{1,0:T(1,128)} %bitcast.s_ref, bf16[512,512]{1,0:T(8,128)(2,1)S(1)} %collective-permute-done.8.im_ref.i2, bf16[512,512]{1,0:T(8,128)(2,1)S(1)} %shard_map.67.t0_ref, bf16[512,512]{1,0:T(8,128)(2,1)S(1)} %collective-permute-done.6.t1_ref), custom_call_target="tpu_custom_call" | custom-call | tf_op jit(solution)/shard_map/pallas_call | solution.py:56
  36.6 2.1 %shard_map.71 = (f32[16,128]{1,0:T(8,128)S(1)}, f32[8,1024]{1,0:T(8,128)S(1)}) custom-call(f32[1,1]{1,0:T(1,128)} %bitcast.s_ref, bf16[512,512]{1,0:T(8,128)(2,1)S(1)} %collective-permute-done.9.im_ref.i3, bf16[512,512]{1,0:T(8,128)(2,1)S(1)} %shard_map.67.t0_ref, bf16[512,512]{1,0:T(8,128)(2,1)S(1)} %collective-permute-done.6.t1_ref), custom_call_target="tpu_custom_call" | custom-call | tf_op jit(solution)/shard_map/pallas_call | solution.py:56
  38.7 0.1 shard_map.72
  38.8 0.7 copy-done
  39.5 5.9 %all-to-all-start = ((f32[16,40,128]{2,1,0:T(8,128)}), f32[16,40,128]{2,1,0:T(8,128)S(1)}, u32[]{:S(2)}, u32[]{:S(2)}) async-start(f32[16,40,128]{2,1,0:T(8,128)} %bitcast.8), calls=%async_computation | async-start | bytes 655360 | tf_op jit(solution)/shard_map/all_to_all | solution.py:359
  45.4 0.7 collective-permute-start.10
  46.1 1.7 %collective-permute-start.11 = (f32[24,128]{1,0:T(8,128)S(1)}, f32[24,128]{1,0:T(8,128)S(1)}, u32[]{:S(2)}, u32[]{:S(2)}) collective-permute-start(f32[24,128]{1,0:T(8,128)S(1)} %get-tuple-element.40.b0), channel_id=1, source_target_pairs={{0,64},{32,96},{64,0},{96,32},{1,65},{33,97},{65,1},{97,33},{2,66}... | collective-permute-start | bytes 36872 | tf_op jit(solution)/shard_map/ppermute | solution.py:37
  47.8 1.0 %collective-permute-start.12 = (f32[24,128]{1,0:T(8,128)S(1)}, f32[24,128]{1,0:T(8,128)S(1)}, u32[]{:S(2)}, u32[]{:S(2)}) collective-permute-start(f32[24,128]{1,0:T(8,128)S(1)} %get-tuple-element.40.b0), channel_id=1, source_target_pairs={{0,96},{32,0},{64,32},{96,64},{1,97},{33,1},{65,33},{97,65},{2,98}... | collective-permute-start | bytes 36872 | tf_op jit(solution)/shard_map/ppermute | solution.py:37
  48.9 1.5 %collective-permute-done.10.b1 = f32[24,128]{1,0:T(8,128)S(1)} collective-permute-done((f32[24,128]{1,0:T(8,128)S(1)}, f32[24,128]{1,0:T(8,128)S(1)}, u32[]{:S(2)}, u32[]{:S(2)}) %collective-permute-start.10) | collective-permute-done | bytes 12320 | tf_op jit(solution)/shard_map/ppermute | solution.py:37
  50.4 0.9 collective-permute-done.11.b2
  51.3 0.2 collective-permute-done.12.b3
  51.5 0.1 collective-permute-start.13
  51.6 1.2 %collective-permute-done.13.b1 = f32[24,128]{1,0:T(8,128)S(1)} collective-permute-done((f32[24,128]{1,0:T(8,128)S(1)}, f32[24,128]{1,0:T(8,128)S(1)}, u32[]{:S(2)}, u32[]{:S(2)}) %collective-permute-start.13) | collective-permute-done | bytes 12320 | tf_op jit(solution)/shard_map/ppermute | solution.py:41
  52.8 1.4 %all-to-all-done = f32[16,40,128]{2,1,0:T(8,128)S(1)} async-done(((f32[16,40,128]{2,1,0:T(8,128)}), f32[16,40,128]{2,1,0:T(8,128)S(1)}, u32[]{:S(2)}, u32[]{:S(2)}) %all-to-all-start) | async-done | bytes 327712 | tf_op jit(solution)/shard_map/all_to_all | solution.py:359
  54.3 0.2 shard_map.74
  54.4 1.6 %shard_map.78 = (bf16[512,1024]{1,0:T(8,128)(2,1)S(1)}, f32[544,512]{1,0:T(8,128)S(1)}) custom-call(f32[1,1]{1,0:T(1,128)} %bitcast.s_ref, bf16[512,512]{1,0:T(8,128)(2,1)S(1)} %collective-permute-done.9.im_ref.i3, f32[16,128]{1,0:T(8,128)S(1)} %get-tuple-element.41.row_ref, f32[1,1024]{1,0:T(1,128)S(1)} %get-tuple-element.42.col_ref, ...), custom_call_target="tpu_custom_call" | custom-call | tf_op jit(solution)/shard_map/pallas_call | solution.py:56
  56.0 0.1 convert_element_type.106
  56.1 0.5 collective-permute-start.16
  56.6 1.6 %shard_map.77 = (bf16[512,1024]{1,0:T(8,128)(2,1)S(1)}, f32[544,512]{1,0:T(8,128)S(1)}) custom-call(f32[1,1]{1,0:T(1,128)} %bitcast.s_ref, bf16[512,512]{1,0:T(8,128)(2,1)S(1)} %collective-permute-done.7.im_ref.i1, f32[16,128]{1,0:T(8,128)S(1)} %get-tuple-element.41.row_ref, f32[1,1024]{1,0:T(1,128)S(1)} %get-tuple-element.42.col_ref, ...), custom_call_target="tpu_custom_call" | custom-call | tf_op jit(solution)/shard_map/pallas_call | solution.py:56
  58.2 0.1 convert_element_type.104
  58.3 3.1 %collective-permute-start.15 = (f16[544,512]{1,0:T(8,128)(2,1)S(1)}, f16[544,512]{1,0:T(8,128)(2,1)S(1)}, u32[]{:S(2)}, u32[]{:S(2)}) collective-permute-start(f16[544,512]{1,0:T(8,128)(2,1)S(1)} %convert_element_type.104), channel_id=1, source_target_pairs={{0,3},{1,0},{2,1},{3,2},{4,28},{5,29},{6,30},{7,31},{8,11},{9,8},{... | collective-permute-start | bytes 1671176 | tf_op jit(solution)/shard_map/ppermute | solution.py:33
  61.4 1.6 %shard_map.76 = (bf16[512,1024]{1,0:T(8,128)(2,1)S(1)}, f32[544,512]{1,0:T(8,128)S(1)}) custom-call(f32[1,1]{1,0:T(1,128)} %bitcast.s_ref, bf16[512,512]{1,0:T(8,128)(2,1)S(1)} %collective-permute-done.8.im_ref.i2, f32[16,128]{1,0:T(8,128)S(1)} %get-tuple-element.41.row_ref, f32[1,1024]{1,0:T(1,128)S(1)} %get-tuple-element.42.col_ref, ...), custom_call_target="tpu_custom_call" | custom-call | tf_op jit(solution)/shard_map/pallas_call | solution.py:56
  62.9 0.1 convert_element_type.102
  63.0 0.8 collective-permute-start.14
  63.8 1.6 %shard_map.75 = (bf16[512,1024]{1,0:T(8,128)(2,1)S(1)}, f32[544,512]{1,0:T(8,128)S(1)}) custom-call(f32[1,1]{1,0:T(1,128)} %bitcast.s_ref, bf16[512,512]{1,0:T(8,128)(2,1)S(1)} %shard_map.66.im_ref.i0, f32[16,128]{1,0:T(8,128)S(1)} %get-tuple-element.41.row_ref, f32[1,1024]{1,0:T(1,128)S(1)} %get-tuple-element.42.col_ref, ...), custom_call_target="tpu_custom_call" | custom-call | tf_op jit(solution)/shard_map/pallas_call | solution.py:56
  65.4 2.4 %shard_map.79 = (f32[544,512]{1,0:T(8,128)S(1)}, f32[544,512]{1,0:T(8,128)S(1)}) custom-call(bf16[512,1024]{1,0:T(8,128)(2,1)S(1)} %get-tuple-element.50.w0, bf16[512,1024]{1,0:T(8,128)(2,1)S(1)} %get-tuple-element.51.w1, bf16[512,1024]{1,0:T(8,128)(2,1)S(1)} %get-tuple-element.52.w2, bf16[512,1024]{1,0:T(8,128)(2,1)S(1)} %get-tuple-element.53.w3, ...), custom_call_target="tpu_custom_call" | custom-call | tf_op jit(solution)/shard_map/pallas_call | solution.py:56
  67.8 0.1 convert_element_type.124
  67.9 0.1 collective-permute-start.20
  68.0 6.4 %collective-permute-done.15 = f16[544,512]{1,0:T(8,128)(2,1)S(1)} collective-permute-done((f16[544,512]{1,0:T(8,128)(2,1)S(1)}, f16[544,512]{1,0:T(8,128)(2,1)S(1)}, u32[]{:S(2)}, u32[]{:S(2)}) %collective-permute-start.15) | collective-permute-done | bytes 557088 | tf_op jit(solution)/shard_map/ppermute | solution.py:33
  74.4 0.3 add_convert_fusion.5
  74.7 0.5 collective-permute-start.19
  75.2 2.8 %collective-permute-start.18 = (f16[136,512]{1,0:T(8,128)(2,1)S(1)}, f16[136,512]{1,0:T(8,128)(2,1)S(1)}, u32[]{:S(2)}, u32[]{:S(2)}) collective-permute-start(f16[136,512]{1,0:T(8,128)(2,1)S(1)} %get-tuple-element.60), channel_id=1, source_target_pairs={{0,24},{1,25},{2,26},{3,27},{4,7},{5,4},{6,5},{7,6},{8,0},{9,1},{1... | collective-permute-start | bytes 417800 | tf_op jit(solution)/shard_map/ppermute | solution.py:33
  78.0 0.7 collective-permute-start.17
  78.7 0.1 add_convert_fusion.2
  78.9 1.8 %collective-permute-start.23 = (f16[136,512]{1,0:T(8,128)(2,1)S(1)}, f16[136,512]{1,0:T(8,128)(2,1)S(1)}, u32[]{:S(2)}, u32[]{:S(2)}) collective-permute-start(f16[136,512]{1,0:T(8,128)(2,1)S(1)} %get-tuple-element.62), channel_id=1, source_target_pairs={{0,32},{32,64},{64,96},{96,0},{1,33},{33,65},{65,97},{97,1},{2,34}... | collective-permute-start | bytes 417800 | tf_op jit(solution)/shard_map/ppermute | solution.py:37
  80.7 1.5 %collective-permute-start.22 = (f16[136,512]{1,0:T(8,128)(2,1)S(1)}, f16[136,512]{1,0:T(8,128)(2,1)S(1)}, u32[]{:S(2)}, u32[]{:S(2)}) collective-permute-start(f16[136,512]{1,0:T(8,128)(2,1)S(1)} %get-tuple-element.63), channel_id=1, source_target_pairs={{0,96},{32,0},{64,32},{96,64},{1,97},{33,1},{65,33},{97,65},{2,98}... | collective-permute-start | bytes 417800 | tf_op jit(solution)/shard_map/ppermute | solution.py:37
  82.2 0.7 collective-permute-start.21
  82.8 1.7 %collective-permute-done.17 = f16[136,512]{1,0:T(8,128)(2,1)S(1)} collective-permute-done((f16[136,512]{1,0:T(8,128)(2,1)S(1)}, f16[136,512]{1,0:T(8,128)(2,1)S(1)}, u32[]{:S(2)}, u32[]{:S(2)}) %collective-permute-start.17) | collective-permute-done | bytes 139296 | tf_op jit(solution)/shard_map/ppermute | solution.py:33
  84.5 0.1 add_add_fusion.1
  84.7 0.7 fusion.1
  85.4 1.3 %collective-permute-done.23 = f16[136,512]{1,0:T(8,128)(2,1)S(1)} collective-permute-done((f16[136,512]{1,0:T(8,128)(2,1)S(1)}, f16[136,512]{1,0:T(8,128)(2,1)S(1)}, u32[]{:S(2)}, u32[]{:S(2)}) %collective-permute-start.23) | collective-permute-done | bytes 139296 | tf_op jit(solution)/shard_map/ppermute | solution.py:37
  86.7 2.0 %collective-permute-done.21 = f16[136,512]{1,0:T(8,128)(2,1)S(1)} collective-permute-done((f16[136,512]{1,0:T(8,128)(2,1)S(1)}, f16[136,512]{1,0:T(8,128)(2,1)S(1)}, u32[]{:S(2)}, u32[]{:S(2)}) %collective-permute-start.21) | collective-permute-done | bytes 139296 | tf_op jit(solution)/shard_map/ppermute | solution.py:37
  88.7 0.1 add_add_fusion
  88.8 0.7 fusion
  89.5 0.3 shard_map.80
  (20 shorter events, 0.1 us)
Async XLA Ops:
  0.6 10.3 %collective-permute-start.3 = (bf16[128,512]{1,0:T(8,128)(2,1)}, bf16[128,512]{1,0:T(8,128)(2,1)S(1)}, u32[]{:S(2)}, u32[]{:S(2)}) collective-permute-start(bf16[128,512]{1,0:T(8,128)(2,1)} %a0.3), channel_id=1, source_target_pairs={{0,32},{32,64},{64,96},{96,0},{1,33},{33,65},{65,97},{97,1},{2,34}... | collective-permute-start | bytes 393224 | tf_op jit(solution)/shard_map/ppermute | solution.py:37
  2.3 10.0 %collective-permute-start.4 = (bf16[128,512]{1,0:T(8,128)(2,1)}, bf16[128,512]{1,0:T(8,128)(2,1)S(1)}, u32[]{:S(2)}, u32[]{:S(2)}) collective-permute-start(bf16[128,512]{1,0:T(8,128)(2,1)} %a0.3), channel_id=1, source_target_pairs={{0,64},{32,96},{64,0},{96,32},{1,65},{33,97},{65,1},{97,33},{2,66}... | collective-permute-start | bytes 393224 | tf_op jit(solution)/shard_map/ppermute | solution.py:37
  5.0 7.3 %collective-permute-start.5 = (bf16[128,512]{1,0:T(8,128)(2,1)}, bf16[128,512]{1,0:T(8,128)(2,1)S(1)}, u32[]{:S(2)}, u32[]{:S(2)}) collective-permute-start(bf16[128,512]{1,0:T(8,128)(2,1)} %a0.3), channel_id=1, source_target_pairs={{0,96},{32,0},{64,32},{96,64},{1,97},{33,1},{65,33},{97,65},{2,98}... | collective-permute-start | bytes 393224 | tf_op jit(solution)/shard_map/ppermute | solution.py:37
  6.5 6.9 %collective-permute-start = (bf16[128,512]{1,0:T(8,128)(2,1)}, bf16[128,512]{1,0:T(8,128)(2,1)S(1)}, u32[]{:S(2)}, u32[]{:S(2)}) collective-permute-start(bf16[128,512]{1,0:T(8,128)(2,1)} %a0.2), channel_id=1, source_target_pairs={{0,8},{1,9},{2,10},{3,11},{4,5},{5,6},{6,7},{7,4},{8,16},{9,17},{1... | collective-permute-start | bytes 393224 | tf_op jit(solution)/shard_map/ppermute | solution.py:33
  8.0 7.5 %collective-permute-start.1 = (bf16[128,512]{1,0:T(8,128)(2,1)}, bf16[128,512]{1,0:T(8,128)(2,1)S(1)}, u32[]{:S(2)}, u32[]{:S(2)}) collective-permute-start(bf16[128,512]{1,0:T(8,128)(2,1)} %a0.2), channel_id=1, source_target_pairs={{0,16},{1,17},{2,18},{3,19},{4,6},{5,7},{6,4},{7,5},{8,24},{9,25},... | collective-permute-start | bytes 393224 | tf_op jit(solution)/shard_map/ppermute | solution.py:33
  10.9 5.2 %collective-permute-start.2 = (bf16[128,512]{1,0:T(8,128)(2,1)}, bf16[128,512]{1,0:T(8,128)(2,1)S(1)}, u32[]{:S(2)}, u32[]{:S(2)}) collective-permute-start(bf16[128,512]{1,0:T(8,128)(2,1)} %a0.2), channel_id=1, source_target_pairs={{0,24},{1,25},{2,26},{3,27},{4,7},{5,4},{6,5},{7,6},{8,0},{9,1},{1... | collective-permute-start | bytes 393224 | tf_op jit(solution)/shard_map/ppermute | solution.py:33
  12.3 0.9 copy-start.1
  13.2 2.9 %copy-start.2 = (bf16[128,512]{1,0:T(8,128)(2,1)S(1)}, bf16[128,512]{1,0:T(8,128)(2,1)}, u32[]{:S(2)}) copy-start(bf16[128,512]{1,0:T(8,128)(2,1)} %a0.2) | copy-start | bytes 393220
  13.2 10.2 %collective-permute-start.6 = (bf16[512,512]{1,0:T(8,128)(2,1)S(1)}, bf16[512,512]{1,0:T(8,128)(2,1)S(1)}, u32[]{:S(2)}, u32[]{:S(2)}) collective-permute-start(bf16[512,512]{1,0:T(8,128)(2,1)S(1)} %shard_map.67.t0_ref), channel_id=1, source_target_pairs={{0,4},{4,0},{1,5},{5,1},{2,6},{6,2},{3,7},{7,3},{8,12},{12,8},{9,1... | collective-permute-start | bytes 1572872 | tf_op jit(solution)/shard_map/ppermute | solution.py:41
  16.2 11.3 %collective-permute-start.7 = (bf16[512,512]{1,0:T(8,128)(2,1)S(1)}, bf16[512,512]{1,0:T(8,128)(2,1)S(1)}, u32[]{:S(2)}, u32[]{:S(2)}) collective-permute-start(bf16[512,512]{1,0:T(8,128)(2,1)S(1)} %shard_map.66.im_ref.i0), channel_id=1, source_target_pairs={{0,1},{1,2},{2,3},{3,0},{4,12},{5,13},{6,14},{7,15},{8,9},{9,10},{... | collective-permute-start | bytes 1572872 | tf_op jit(solution)/shard_map/ppermute | solution.py:33
  18.2 16.4 %collective-permute-start.8 = (bf16[512,512]{1,0:T(8,128)(2,1)S(1)}, bf16[512,512]{1,0:T(8,128)(2,1)S(1)}, u32[]{:S(2)}, u32[]{:S(2)}) collective-permute-start(bf16[512,512]{1,0:T(8,128)(2,1)S(1)} %shard_map.66.im_ref.i0), channel_id=1, source_target_pairs={{0,2},{1,3},{2,0},{3,1},{4,20},{5,21},{6,22},{7,23},{8,10},{9,11},... | collective-permute-start | bytes 1572872 | tf_op jit(solution)/shard_map/ppermute | solution.py:33
  21.7 14.9 %collective-permute-start.9 = (bf16[512,512]{1,0:T(8,128)(2,1)S(1)}, bf16[512,512]{1,0:T(8,128)(2,1)S(1)}, u32[]{:S(2)}, u32[]{:S(2)}) collective-permute-start(bf16[512,512]{1,0:T(8,128)(2,1)S(1)} %shard_map.66.im_ref.i0), channel_id=1, source_target_pairs={{0,3},{1,0},{2,1},{3,2},{4,28},{5,29},{6,30},{7,31},{8,11},{9,8},{... | collective-permute-start | bytes 1572872 | tf_op jit(solution)/shard_map/ppermute | solution.py:33
  38.8 0.7 copy-start
  39.5 14.7 %all-to-all-start = ((f32[16,40,128]{2,1,0:T(8,128)}), f32[16,40,128]{2,1,0:T(8,128)S(1)}, u32[]{:S(2)}, u32[]{:S(2)}) async-start(f32[16,40,128]{2,1,0:T(8,128)} %bitcast.8), calls=%async_computation | async-start | bytes 655360 | tf_op jit(solution)/shard_map/all_to_all | solution.py:359
  45.4 5.0 %collective-permute-start.10 = (f32[24,128]{1,0:T(8,128)S(1)}, f32[24,128]{1,0:T(8,128)S(1)}, u32[]{:S(2)}, u32[]{:S(2)}) collective-permute-start(f32[24,128]{1,0:T(8,128)S(1)} %get-tuple-element.40.b0), channel_id=1, source_target_pairs={{0,32},{32,64},{64,96},{96,0},{1,33},{33,65},{65,97},{97,1},{2,34}... | collective-permute-start | bytes 36872 | tf_op jit(solution)/shard_map/ppermute | solution.py:37
  46.1 5.2 %collective-permute-start.11 = (f32[24,128]{1,0:T(8,128)S(1)}, f32[24,128]{1,0:T(8,128)S(1)}, u32[]{:S(2)}, u32[]{:S(2)}) collective-permute-start(f32[24,128]{1,0:T(8,128)S(1)} %get-tuple-element.40.b0), channel_id=1, source_target_pairs={{0,64},{32,96},{64,0},{96,32},{1,65},{33,97},{65,1},{97,33},{2,66}... | collective-permute-start | bytes 36872 | tf_op jit(solution)/shard_map/ppermute | solution.py:37
  47.8 3.7 %collective-permute-start.12 = (f32[24,128]{1,0:T(8,128)S(1)}, f32[24,128]{1,0:T(8,128)S(1)}, u32[]{:S(2)}, u32[]{:S(2)}) collective-permute-start(f32[24,128]{1,0:T(8,128)S(1)} %get-tuple-element.40.b0), channel_id=1, source_target_pairs={{0,96},{32,0},{64,32},{96,64},{1,97},{33,1},{65,33},{97,65},{2,98}... | collective-permute-start | bytes 36872 | tf_op jit(solution)/shard_map/ppermute | solution.py:37
  51.5 1.3 %collective-permute-start.13 = (f32[24,128]{1,0:T(8,128)S(1)}, f32[24,128]{1,0:T(8,128)S(1)}, u32[]{:S(2)}, u32[]{:S(2)}) collective-permute-start(f32[24,128]{1,0:T(8,128)S(1)} %shard_map.73.b0), channel_id=1, source_target_pairs={{0,4},{4,0},{1,5},{5,1},{2,6},{6,2},{3,7},{7,3},{8,12},{12,8},{9,1... | collective-permute-start | bytes 36872 | tf_op jit(solution)/shard_map/ppermute | solution.py:41
  56.1 11.9 %collective-permute-start.16 = (f16[544,512]{1,0:T(8,128)(2,1)S(1)}, f16[544,512]{1,0:T(8,128)(2,1)S(1)}, u32[]{:S(2)}, u32[]{:S(2)}) collective-permute-start(f16[544,512]{1,0:T(8,128)(2,1)S(1)} %convert_element_type.106), channel_id=1, source_target_pairs={{0,1},{1,2},{2,3},{3,0},{4,12},{5,13},{6,14},{7,15},{8,9},{9,10},{... | collective-permute-start | bytes 1671176 | tf_op jit(solution)/shard_map/ppermute | solution.py:33
  58.3 16.1 %collective-permute-start.15 = (f16[544,512]{1,0:T(8,128)(2,1)S(1)}, f16[544,512]{1,0:T(8,128)(2,1)S(1)}, u32[]{:S(2)}, u32[]{:S(2)}) collective-permute-start(f16[544,512]{1,0:T(8,128)(2,1)S(1)} %convert_element_type.104), channel_id=1, source_target_pairs={{0,3},{1,0},{2,1},{3,2},{4,28},{5,29},{6,30},{7,31},{8,11},{9,8},{... | collective-permute-start | bytes 1671176 | tf_op jit(solution)/shard_map/ppermute | solution.py:33
  63.0 11.3 %collective-permute-start.14 = (f16[544,512]{1,0:T(8,128)(2,1)S(1)}, f16[544,512]{1,0:T(8,128)(2,1)S(1)}, u32[]{:S(2)}, u32[]{:S(2)}) collective-permute-start(f16[544,512]{1,0:T(8,128)(2,1)S(1)} %convert_element_type.102), channel_id=1, source_target_pairs={{0,2},{1,3},{2,0},{3,1},{4,20},{5,21},{6,22},{7,23},{8,10},{9,11},... | collective-permute-start | bytes 1671176 | tf_op jit(solution)/shard_map/ppermute | solution.py:33
  67.9 10.8 %collective-permute-start.20 = (f16[544,512]{1,0:T(8,128)(2,1)S(1)}, f16[544,512]{1,0:T(8,128)(2,1)S(1)}, u32[]{:S(2)}, u32[]{:S(2)}) collective-permute-start(f16[544,512]{1,0:T(8,128)(2,1)S(1)} %convert_element_type.124), channel_id=1, source_target_pairs={{0,4},{4,0},{1,5},{5,1},{2,6},{6,2},{3,7},{7,3},{8,12},{12,8},{9,1... | collective-permute-start | bytes 1671176 | tf_op jit(solution)/shard_map/ppermute | solution.py:41
  74.7 7.5 %collective-permute-start.19 = (f16[136,512]{1,0:T(8,128)(2,1)S(1)}, f16[136,512]{1,0:T(8,128)(2,1)S(1)}, u32[]{:S(2)}, u32[]{:S(2)}) collective-permute-start(f16[136,512]{1,0:T(8,128)(2,1)S(1)} %get-tuple-element.59), channel_id=1, source_target_pairs={{0,8},{1,9},{2,10},{3,11},{4,5},{5,6},{6,7},{7,4},{8,16},{9,17},{1... | collective-permute-start | bytes 417800 | tf_op jit(solution)/shard_map/ppermute | solution.py:33
  75.2 7.7 %collective-permute-start.18 = (f16[136,512]{1,0:T(8,128)(2,1)S(1)}, f16[136,512]{1,0:T(8,128)(2,1)S(1)}, u32[]{:S(2)}, u32[]{:S(2)}) collective-permute-start(f16[136,512]{1,0:T(8,128)(2,1)S(1)} %get-tuple-element.60), channel_id=1, source_target_pairs={{0,24},{1,25},{2,26},{3,27},{4,7},{5,4},{6,5},{7,6},{8,0},{9,1},{1... | collective-permute-start | bytes 417800 | tf_op jit(solution)/shard_map/ppermute | solution.py:33
  78.0 6.6 %collective-permute-start.17 = (f16[136,512]{1,0:T(8,128)(2,1)S(1)}, f16[136,512]{1,0:T(8,128)(2,1)S(1)}, u32[]{:S(2)}, u32[]{:S(2)}) collective-permute-start(f16[136,512]{1,0:T(8,128)(2,1)S(1)} %get-tuple-element.58), channel_id=1, source_target_pairs={{0,16},{1,17},{2,18},{3,19},{4,6},{5,7},{6,4},{7,5},{8,24},{9,25},... | collective-permute-start | bytes 417800 | tf_op jit(solution)/shard_map/ppermute | solution.py:33
  78.9 7.8 %collective-permute-start.23 = (f16[136,512]{1,0:T(8,128)(2,1)S(1)}, f16[136,512]{1,0:T(8,128)(2,1)S(1)}, u32[]{:S(2)}, u32[]{:S(2)}) collective-permute-start(f16[136,512]{1,0:T(8,128)(2,1)S(1)} %get-tuple-element.62), channel_id=1, source_target_pairs={{0,32},{32,64},{64,96},{96,0},{1,33},{33,65},{65,97},{97,1},{2,34}... | collective-permute-start | bytes 417800 | tf_op jit(solution)/shard_map/ppermute | solution.py:37
  80.7 6.0 %collective-permute-start.22 = (f16[136,512]{1,0:T(8,128)(2,1)S(1)}, f16[136,512]{1,0:T(8,128)(2,1)S(1)}, u32[]{:S(2)}, u32[]{:S(2)}) collective-permute-start(f16[136,512]{1,0:T(8,128)(2,1)S(1)} %get-tuple-element.63), channel_id=1, source_target_pairs={{0,96},{32,0},{64,32},{96,64},{1,97},{33,1},{65,33},{97,65},{2,98}... | collective-permute-start | bytes 417800 | tf_op jit(solution)/shard_map/ppermute | solution.py:37
  82.2 6.6 %collective-permute-start.21 = (f16[136,512]{1,0:T(8,128)(2,1)S(1)}, f16[136,512]{1,0:T(8,128)(2,1)S(1)}, u32[]{:S(2)}, u32[]{:S(2)}) collective-permute-start(f16[136,512]{1,0:T(8,128)(2,1)S(1)} %get-tuple-element.61), channel_id=1, source_target_pairs={{0,64},{32,96},{64,0},{96,32},{1,65},{33,97},{65,1},{97,33},{2,66}... | collective-permute-start | bytes 417800 | tf_op jit(solution)/shard_map/ppermute | solution.py:37

commit v2 on v1

--- a/solution.py
+++ b/solution.py
@@ -69,6 +69,14 @@
     return pltpu.VMEM(shape, dtype)
 
 
+def hold_kernel(a_ref, o_ref):
+    o_ref[...] = a_ref[...]
+
+
+def held(value):
+    return call(hold_kernel, out((ROWS, 512), BF16), value)
+
+
 def join_kernel(a0, a1, a2, a3, o_ref):
     for k, a in enumerate((a0, a1, a2, a3)):
         o_ref[128 * k : 128 * (k + 1), :] = a[...]
@@ -109,7 +117,9 @@
         top_scr[here, :] = row_top
         return tuple(new)
 
-    col_tops = lax.fori_loop(0, 8, tops, tuple(l_ref[0:8, 128 * k : 128 * (k + 1)] for k in range(8)))
+    col_tops = lax.fori_loop(
+        0, 8, tops, tuple(l_ref[0:8, 128 * k : 128 * (k + 1)] for k in range(8)), unroll=True
+    )
 
     def sums(i, carry):
         here = pl.ds(pl.multiple_of(i * 64, 64), 64)
@@ -129,7 +139,7 @@
         return tuple(new)
 
     zero = jnp.zeros((8, 128), F32)
-    col_sums = lax.fori_loop(0, 8, sums, ((zero, zero),) * 8)
+    col_sums = lax.fori_loop(0, 8, sums, ((zero, zero),) * 8, unroll=True)
     for k in range(8):
         at = slice(128 * k, 128 * (k + 1))
         top = jnp.max(col_tops[k], axis=0, keepdims=True)
@@ -184,9 +194,8 @@
     return lax.rem(second - back_second + 4, 4) * 4 + lax.rem(first - back_first + 4, 4)
 
 
-def start_kernel(r0, r1, r2, r3, c0, c1, c2, c3, all_ref, col_ref, scr):
-    rs, cs = (r0, r1, r2, r3), (c0, c1, c2, c3)
-    for k, r in enumerate(rs):
+def row_kernel(r0, r1, r2, r3, all_ref, scr):
+    for k, r in enumerate((r0, r1, r2, r3)):
         for j in range(4):
             at = row_at(k, j)
             scr[pl.ds(at, 1), :] = r[j : j + 1, :]
@@ -197,6 +206,10 @@
     message = scr[...]
     for k in range(16):
         all_ref[40 * k : 40 * (k + 1), :] = message
+
+
+def col_kernel(r0, r1, r2, r3, c0, c1, c2, c3, col_ref):
+    rs, cs = (r0, r1, r2, r3), (c0, c1, c2, c3)
     top = greatest([c[0:1, :] for c in cs])
     es = [jnp.exp2(c[0:1, :] - top) for c in cs]
     total = sum(e * c[1:2, :] for e, c in zip(es, cs))
@@ -313,21 +326,26 @@
         g_ref[136 * k + 128 : 136 * (k + 1), :] = tail(codes_ref[0:1, :], 4 * (k % 2) + which, k // 2)
 
 
-def text_kernel(w0, w1, w2, w3, i0, i1, i2, i3, unit_ref, codes_ref, g0_ref, g1_ref):
-    for h, g_ref in enumerate((g0_ref, g1_ref)):
-        at = slice(512 * h, 512 * (h + 1))
-        g = None
-        for w, i in zip((w0, w1, w2, w3), (i0, i1, i2, i3)):
-            part = lax.dot_general(w[:, at], i[...], TN, preferred_element_type=F32)
-            g = part if g is None else g + part
-        g = g * unit_ref[1:2, 0:1]
-        for k in range(4):
-            g_ref[136 * k : 136 * k + 128, :] = g[128 * k : 128 * (k + 1), :]
-            g_ref[136 * k + 128 : 136 * (k + 1), :] = tail(codes_ref[1:2, :], 2 * k + h, 0)
-
-
-def decode_kernel(i_ref, t_ref, loss_ref, grad_ref):
-    rows = jnp.sum(i_ref[...] + t_ref[...], axis=0, keepdims=True)
+def text_kernel(h, w0, w1, w2, w3, i0, i1, i2, i3, unit_ref, codes_ref, g_ref):
+    at = slice(512 * h, 512 * (h + 1))
+    g = None
+    for w, i in zip((w0, w1, w2, w3), (i0, i1, i2, i3)):
+        part = lax.dot_general(w[:, at], i[...], TN, preferred_element_type=F32)
+        g = part if g is None else g + part
+    g = g * unit_ref[1:2, 0:1]
+    for k in range(4):
+        g_ref[136 * k : 136 * k + 128, :] = g[128 * k : 128 * (k + 1), :]
+        g_ref[136 * k + 128 : 136 * (k + 1), :] = tail(codes_ref[1:2, :], 2 * k + h, 0)
+
+
+def texts_end_kernel(g_ref, back_ref, o_ref, tail_ref):
+    o_ref[...] = (g_ref[0:128, :] * back_ref[1:2, :]).astype(BF16)
+    tail_ref[...] = g_ref[128:136, :]
+
+
+def images_end_kernel(g_ref, t_ref, back_ref, o_ref, loss_ref, grad_ref):
+    o_ref[...] = (g_ref[0:128, :] * back_ref[0:1, :]).astype(BF16)
+    rows = jnp.sum(g_ref[128:136, :] + t_ref[...], axis=0, keepdims=True)
     rows = rows[:, 0:256] + rows[:, 256:512]
     pair_total = ROWS * 128
     for v, (ref, count) in enumerate(((loss_ref, 2.0 * pair_total), (grad_ref, float(pair_total)))):
@@ -340,20 +358,18 @@
 
 def program(images, texts, log_scale):
     s2 = jnp.reshape(jnp.exp(log_scale) * LOG2E, (1, 1))
-    line = everyone(images, lambda v, d: turn(v, d, True))
+    line = [held(images)] + everyone(images, lambda v, d: turn(v, d, True))[1:]
     line = joined(line)
     chunks = everyone(line, lambda v, d: turn(v, d, False))
-    t0 = everyone(texts, along_x)
+    t0 = [held(texts)] + everyone(texts, along_x)[1:]
     t0 = joined(t0)
     t1 = other_core(t0)
     parts = [None] * 4
     for k in (0, 1, 3, 2):
         parts[k] = logits_of(k, s2, chunks[k], t0, t1)
-    rows, cols = call(
-        start_kernel,
-        (jax.ShapeDtypeStruct((640, 128), F32), out((24, 128))),
-        *[p[0] for p in parts], *[p[1] for p in parts],
-        scratch=[pltpu.VMEM((40, 128), F32)],
+    cols = call(col_kernel, out((24, 128)), *[p[0] for p in parts], *[p[1] for p in parts])
+    rows = call(
+        row_kernel, jax.ShapeDtypeStruct((640, 128), F32), *[p[0] for p in parts], scratch=[pltpu.VMEM((40, 128), F32)]
     )
     cols = everyone(cols, along_x)
     rows = lax.all_to_all(rows.reshape(16, 40, 128), ("y", "z"), 0, 0, tiled=True).reshape(640, 128)
@@ -377,11 +393,14 @@
         )
         if k:
             sent[k] = turn(gs[k].astype(F16), 4 - k, False)
-    g0, g1 = call(
-        text_kernel,
-        (out((544, 512)), out((544, 512))),
-        *[ws[k] for k in range(4)], *chunks, unit, codes,
-    )
+    g0, g1 = [
+        call(
+            functools.partial(text_kernel, h),
+            out((544, 512)),
+            *[ws[k] for k in range(4)], *chunks, unit, codes,
+        )
+        for h in range(2)
+    ]
     swap = other_core(g1.astype(F16))
     moved = []
     for k in (2, 1, 3):
@@ -392,9 +411,16 @@
     for k in (2, 1, 3):
         moved.append(turn(sums[k].astype(F16), 4 - k, True))
     gi = sums[0] + sum(m.astype(F32) for m in moved)
-    loss, grad_scale = call(decode_kernel, (out((1, 1)), out((1, 1))), gi[128:], gt[128:])
-    grad_images = (gi[0:128] * back[0:1, :]).astype(BF16)
-    grad_texts = (gt[0:128] * back[1:2, :]).astype(BF16)
+    grad_texts, gt_tail = call(
+        texts_end_kernel,
+        (jax.ShapeDtypeStruct((ROWS, 512), BF16), out((8, 512))),
+        gt, back,
+    )
+    grad_images, loss, grad_scale = call(
+        images_end_kernel,
+        (jax.ShapeDtypeStruct((ROWS, 512), BF16),) + (jax.ShapeDtypeStruct((1, 1), F32),) * 2,
+        gi, gt_tail, back,
+    )
     return grad_images, grad_texts, jnp.reshape(loss, ()), jnp.reshape(grad_scale, ())
 
 

time: 93.1 us -> 95.1 us (1.021)
  local copies, waits for them, and re-layouts: 1.65 us -> 6.63 us
  between operations: 3.87 us -> 1.58 us
  other arithmetic: 2.41 us -> 1.08 us
  starting transfers between devices: 40.2 us -> 41.3 us
    unnamed x6 -> x18, local copies, waits for them, and re-layouts: 1.64 us -> 6.63 us
    ppermute x12, waiting for transfers between devices: 17.6 us -> 21.1 us  [turn(): return lax.ppermute(value, ('y', 'c', 'z'), pairs)]
    ppermute x12, starting transfers between devices: 20.8 us -> 22.6 us  [turn(): return lax.ppermute(value, ('y', 'c', 'z'), pairs)]
    ppermute x9, waiting for transfers between devices: 6.03 us -> 4.44 us  [along_x(): return lax.ppermute(value, 'x', [(i, (i + shift) % 4) for i in range(4)])]
    ppermute x9, starting transfers between devices: 13.2 us -> 11.7 us  [along_x(): return lax.ppermute(value, 'x', [(i, (i + shift) % 4) for i in range(4)])]
    all_to_all x1, waiting for transfers between devices: 1.45 us -> 0.01 us  [program(): lax.all_to_all(rows.reshape(16, 40, 128), ('y', 'z'), 0, 0, tiled=True)]
    convert_element_type x2 -> x0, other arithmetic: 1.35 us -> none  [the longest x1 0.68 us: program(): grad_texts = (gt[0:128] * back[1:2, :]).astype(BF16)]
    pallas_call x15 -> x20, Pallas kernels: 17.8 us -> 17.3 us  [call(): pl.pallas_call(kernel, out_shape=outs, in_specs=[pl.BlockSpec(memory_spac...]
  transfers between devices with their start and end apart: 25 -> 25, of which waited for: 13 -> 9; matrix products, arithmetic and copies ran while one was open for 2% -> 1% of each run, Pallas kernels for 15% -> 7%
where the time goes in v2:
time: 95.1 us; the launch traced here: 94.6 us
  starting transfers between devices  41.3 us (43%)
  waiting for transfers between devices  26.7 us (28%)
  Pallas kernels  17.3 us (18%)
  local copies, waits for them, and re-layouts  6.63 us (7%)
  between operations  1.58 us (2%)
  other arithmetic  1.08 us (1%)
    ppermute x12, starting transfers between devices, turn(): return lax.ppermute(value, ('y', 'c', 'z'), pairs)  22.6 us
    ppermute x12, waiting for transfers between devices, turn(): return lax.ppermute(value, ('y', 'c', 'z'), pairs)  21.1 us
    pallas_call x20, Pallas kernels, call(): pl.pallas_call(kernel, out_shape=outs, in_specs=[pl.BlockSpec(memory_spac...  17.3 us
    ppermute x9, starting transfers between devices, along_x(): return lax.ppermute(value, 'x', [(i, (i + shift) % 4) for i in range(4)])  11.7 us
    unnamed x18, local copies, waits for them, and re-layouts  6.63 us
    all_to_all x1, starting transfers between devices, program(): lax.all_to_all(rows.reshape(16, 40, 128), ('y', 'z'), 0, 0, tiled=True)  6.49 us
    ppermute x9, waiting for transfers between devices, along_x(): return lax.ppermute(value, 'x', [(i, (i + shift) % 4) for i in range(4)])  4.44 us
  transfers between devices with their start and end apart: 25, of which 9 were waited for; matrix products, arithmetic and copies ran while one was open for 1% of the time, Pallas kernels for 7%

profile of v2, /device:TPU:0, one launch (start us, length us, event | category | flops | bytes accessed | tf_op | source)
XLA Modules:
  0.0 94.6 jit_solution(9427364286890644020)
XLA Ops:
  0.6 1.7 %collective-permute-start.3 = (bf16[128,512]{1,0:T(8,128)(2,1)}, bf16[128,512]{1,0:T(8,128)(2,1)S(1)}, u32[]{:S(2)}, u32[]{:S(2)}) collective-permute-start(bf16[128,512]{1,0:T(8,128)(2,1)} %a_ref.3), channel_id=1, source_target_pairs={{0,32},{32,64},{64,96},{96,0},{1,33},{33,65},{65,97},{97,1},{2,34}... | collective-permute-start | bytes 393224 | tf_op jit(solution)/shard_map/ppermute | solution.py:37
  2.3 1.6 %collective-permute-start.5 = (bf16[128,512]{1,0:T(8,128)(2,1)}, bf16[128,512]{1,0:T(8,128)(2,1)S(1)}, u32[]{:S(2)}, u32[]{:S(2)}) collective-permute-start(bf16[128,512]{1,0:T(8,128)(2,1)} %a_ref.3), channel_id=1, source_target_pairs={{0,96},{32,0},{64,32},{96,64},{1,97},{33,1},{65,33},{97,65},{2,98}... | collective-permute-start | bytes 393224 | tf_op jit(solution)/shard_map/ppermute | solution.py:37
  3.9 1.9 %collective-permute-start.4 = (bf16[128,512]{1,0:T(8,128)(2,1)}, bf16[128,512]{1,0:T(8,128)(2,1)S(1)}, u32[]{:S(2)}, u32[]{:S(2)}) collective-permute-start(bf16[128,512]{1,0:T(8,128)(2,1)} %a_ref.3), channel_id=1, source_target_pairs={{0,64},{32,96},{64,0},{96,32},{1,65},{33,97},{65,1},{97,33},{2,66}... | collective-permute-start | bytes 393224 | tf_op jit(solution)/shard_map/ppermute | solution.py:37
  5.9 1.6 %collective-permute-start = (bf16[128,512]{1,0:T(8,128)(2,1)}, bf16[128,512]{1,0:T(8,128)(2,1)S(1)}, u32[]{:S(2)}, u32[]{:S(2)}) collective-permute-start(bf16[128,512]{1,0:T(8,128)(2,1)} %a_ref.2), channel_id=1, source_target_pairs={{0,8},{1,9},{2,10},{3,11},{4,5},{5,6},{6,7},{7,4},{8,16},{9,17},{1... | collective-permute-start | bytes 393224 | tf_op jit(solution)/shard_map/ppermute | solution.py:33
  7.4 1.7 %collective-permute-start.2 = (bf16[128,512]{1,0:T(8,128)(2,1)}, bf16[128,512]{1,0:T(8,128)(2,1)S(1)}, u32[]{:S(2)}, u32[]{:S(2)}) collective-permute-start(bf16[128,512]{1,0:T(8,128)(2,1)} %a_ref.2), channel_id=1, source_target_pairs={{0,24},{1,25},{2,26},{3,27},{4,7},{5,4},{6,5},{7,6},{8,0},{9,1},{1... | collective-permute-start | bytes 393224 | tf_op jit(solution)/shard_map/ppermute | solution.py:33
  9.1 2.0 %collective-permute-start.1 = (bf16[128,512]{1,0:T(8,128)(2,1)}, bf16[128,512]{1,0:T(8,128)(2,1)S(1)}, u32[]{:S(2)}, u32[]{:S(2)}) collective-permute-start(bf16[128,512]{1,0:T(8,128)(2,1)} %a_ref.2), channel_id=1, source_target_pairs={{0,16},{1,17},{2,18},{3,19},{4,6},{5,7},{6,4},{7,5},{8,24},{9,25},... | collective-permute-start | bytes 393224 | tf_op jit(solution)/shard_map/ppermute | solution.py:33
  11.1 0.9 copy-done.2
  12.0 0.9 copy-done.1
  13.0 0.1 collective-permute-start.6
  13.1 2.6 %collective-permute-done.1.a2 = bf16[128,512]{1,0:T(8,128)(2,1)S(1)} collective-permute-done((bf16[128,512]{1,0:T(8,128)(2,1)}, bf16[128,512]{1,0:T(8,128)(2,1)S(1)}, u32[]{:S(2)}, u32[]{:S(2)}) %collective-permute-start.1) | collective-permute-done | bytes 131104 | tf_op jit(solution)/shard_map/ppermute | solution.py:33
  15.8 4.1 %collective-permute-start.9 = (bf16[512,512]{1,0:T(8,128)(2,1)S(1)}, bf16[512,512]{1,0:T(8,128)(2,1)S(1)}, u32[]{:S(2)}, u32[]{:S(2)}) collective-permute-start(bf16[512,512]{1,0:T(8,128)(2,1)S(1)} %shard_map.67.im_ref.i0), channel_id=1, source_target_pairs={{0,3},{1,0},{2,1},{3,2},{4,28},{5,29},{6,30},{7,31},{8,11},{9,8},{... | collective-permute-start | bytes 1572872 | tf_op jit(solution)/shard_map/ppermute | solution.py:33
  19.9 1.3 %collective-permute-start.7 = (bf16[512,512]{1,0:T(8,128)(2,1)S(1)}, bf16[512,512]{1,0:T(8,128)(2,1)S(1)}, u32[]{:S(2)}, u32[]{:S(2)}) collective-permute-start(bf16[512,512]{1,0:T(8,128)(2,1)S(1)} %shard_map.67.im_ref.i0), channel_id=1, source_target_pairs={{0,1},{1,2},{2,3},{3,0},{4,12},{5,13},{6,14},{7,15},{8,9},{9,10},{... | collective-permute-start | bytes 1572872 | tf_op jit(solution)/shard_map/ppermute | solution.py:33
  21.9 1.7 %shard_map.70 = (f32[16,128]{1,0:T(8,128)S(1)}, f32[8,1024]{1,0:T(8,128)S(1)}) custom-call(f32[1,1]{1,0:T(1,128)} %bitcast.s_ref, bf16[512,512]{1,0:T(8,128)(2,1)S(1)} %shard_map.67.im_ref.i0, bf16[512,512]{1,0:T(8,128)(2,1)S(1)} %shard_map.69.t0_ref, bf16[512,512]{1,0:T(8,128)(2,1)S(1)} %collective-permute-done.6.t1_ref), custom_call_target="tpu_custom_call" | custom-call | tf_op jit(solution)/shard_map/pallas_call | solution.py:56
  23.6 8.6 %collective-permute-done.9.im_ref.i3 = bf16[512,512]{1,0:T(8,128)(2,1)S(1)} collective-permute-done((bf16[512,512]{1,0:T(8,128)(2,1)S(1)}, bf16[512,512]{1,0:T(8,128)(2,1)S(1)}, u32[]{:S(2)}, u32[]{:S(2)}) %collective-permute-start.9) | collective-permute-done | bytes 524320 | tf_op jit(solution)/shard_map/ppermute | solution.py:33
  32.2 1.6 %shard_map.73 = (f32[16,128]{1,0:T(8,128)S(1)}, f32[8,1024]{1,0:T(8,128)S(1)}) custom-call(f32[1,1]{1,0:T(1,128)} %bitcast.s_ref, bf16[512,512]{1,0:T(8,128)(2,1)S(1)} %collective-permute-done.9.im_ref.i3, bf16[512,512]{1,0:T(8,128)(2,1)S(1)} %shard_map.69.t0_ref, bf16[512,512]{1,0:T(8,128)(2,1)S(1)} %collective-permute-done.6.t1_ref), custom_call_target="tpu_custom_call" | custom-call | tf_op jit(solution)/shard_map/pallas_call | solution.py:56
  33.8 0.6 copy-done.3
  34.4 1.6 %shard_map.72 = (f32[16,128]{1,0:T(8,128)S(1)}, f32[8,1024]{1,0:T(8,128)S(1)}) custom-call(f32[1,1]{1,0:T(1,128)} %bitcast.s_ref, bf16[512,512]{1,0:T(8,128)(2,1)S(1)} %collective-permute-done.8.im_ref.i2, bf16[512,512]{1,0:T(8,128)(2,1)S(1)} %shard_map.69.t0_ref, bf16[512,512]{1,0:T(8,128)(2,1)S(1)} %collective-permute-done.6.t1_ref), custom_call_target="tpu_custom_call" | custom-call | tf_op jit(solution)/shard_map/pallas_call | solution.py:56
  36.0 0.6 copy-done.5
  36.7 1.6 %shard_map.71 = (f32[16,128]{1,0:T(8,128)S(1)}, f32[8,1024]{1,0:T(8,128)S(1)}) custom-call(f32[1,1]{1,0:T(1,128)} %bitcast.s_ref, bf16[512,512]{1,0:T(8,128)(2,1)S(1)} %collective-permute-done.7.im_ref.i1, bf16[512,512]{1,0:T(8,128)(2,1)S(1)} %shard_map.69.t0_ref, bf16[512,512]{1,0:T(8,128)(2,1)S(1)} %collective-permute-done.6.t1_ref), custom_call_target="tpu_custom_call" | custom-call | tf_op jit(solution)/shard_map/pallas_call | solution.py:56
  38.2 0.6 copy-done.7
  38.9 0.1 shard_map.74
  38.9 0.7 copy-done
  39.6 6.5 %all-to-all-start = ((f32[16,40,128]{2,1,0:T(8,128)}), f32[16,40,128]{2,1,0:T(8,128)S(1)}, u32[]{:S(2)}, u32[]{:S(2)}) async-start(f32[16,40,128]{2,1,0:T(8,128)} %bitcast.6), calls=%async_computation | async-start | bytes 655360 | tf_op jit(solution)/shard_map/all_to_all | solution.py:375
  46.1 0.7 copy-done.4
  46.9 0.8 copy-done.6
  47.7 0.8 copy-done.8
  48.4 2.0 %collective-permute-start.12 = (f32[24,128]{1,0:T(8,128)S(1)}, f32[24,128]{1,0:T(8,128)S(1)}, u32[]{:S(2)}, u32[]{:S(2)}) collective-permute-start(f32[24,128]{1,0:T(8,128)S(1)} %shard_map.75.b0), channel_id=1, source_target_pairs={{0,96},{32,0},{64,32},{96,64},{1,97},{33,1},{65,33},{97,65},{2,98}... | collective-permute-start | bytes 36872 | tf_op jit(solution)/shard_map/ppermute | solution.py:37
  50.5 0.7 collective-permute-start.11
  51.2 0.5 collective-permute-start.10
  51.6 0.6 collective-permute-done.12.b3
  52.2 3.4 %collective-permute-done.11.b2 = f32[24,128]{1,0:T(8,128)S(1)} collective-permute-done((f32[24,128]{1,0:T(8,128)S(1)}, f32[24,128]{1,0:T(8,128)S(1)}, u32[]{:S(2)}, u32[]{:S(2)}) %collective-permute-start.11) | collective-permute-done | bytes 12320 | tf_op jit(solution)/shard_map/ppermute | solution.py:37
  55.7 0.4 collective-permute-done.10.b1
  56.1 0.3 collective-permute-start.13
  56.4 1.2 %collective-permute-done.13.b1 = f32[24,128]{1,0:T(8,128)S(1)} collective-permute-done((f32[24,128]{1,0:T(8,128)S(1)}, f32[24,128]{1,0:T(8,128)S(1)}, u32[]{:S(2)}, u32[]{:S(2)}) %collective-permute-start.13) | collective-permute-done | bytes 12320 | tf_op jit(solution)/shard_map/ppermute | solution.py:41
  57.5 0.2 shard_map.77
  57.7 1.6 %shard_map.81 = (bf16[512,1024]{1,0:T(8,128)(2,1)S(1)}, f32[544,512]{1,0:T(8,128)S(1)}) custom-call(f32[1,1]{1,0:T(1,128)} %bitcast.s_ref, bf16[512,512]{1,0:T(8,128)(2,1)S(1)} %collective-permute-done.9.im_ref.i3, f32[16,128]{1,0:T(8,128)S(1)} %get-tuple-element.38.row_ref, f32[1,1024]{1,0:T(1,128)S(1)} %get-tuple-element.39.col_ref, ...), custom_call_target="tpu_custom_call" | custom-call | tf_op jit(solution)/shard_map/pallas_call | solution.py:56
  59.3 1.6 %shard_map.80 = (bf16[512,1024]{1,0:T(8,128)(2,1)S(1)}, f32[544,512]{1,0:T(8,128)S(1)}) custom-call(f32[1,1]{1,0:T(1,128)} %bitcast.s_ref, bf16[512,512]{1,0:T(8,128)(2,1)S(1)} %collective-permute-done.7.im_ref.i1, f32[16,128]{1,0:T(8,128)S(1)} %get-tuple-element.38.row_ref, f32[1,1024]{1,0:T(1,128)S(1)} %get-tuple-element.39.col_ref, ...), custom_call_target="tpu_custom_call" | custom-call | tf_op jit(solution)/shard_map/pallas_call | solution.py:56
  60.9 1.6 %shard_map.79 = (bf16[512,1024]{1,0:T(8,128)(2,1)S(1)}, f32[544,512]{1,0:T(8,128)S(1)}) custom-call(f32[1,1]{1,0:T(1,128)} %bitcast.s_ref, bf16[512,512]{1,0:T(8,128)(2,1)S(1)} %collective-permute-done.8.im_ref.i2, f32[16,128]{1,0:T(8,128)S(1)} %get-tuple-element.38.row_ref, f32[1,1024]{1,0:T(1,128)S(1)} %get-tuple-element.39.col_ref, ...), custom_call_target="tpu_custom_call" | custom-call | tf_op jit(solution)/shard_map/pallas_call | solution.py:56
  62.5 1.6 %shard_map.78 = (bf16[512,1024]{1,0:T(8,128)(2,1)S(1)}, f32[544,512]{1,0:T(8,128)S(1)}) custom-call(f32[1,1]{1,0:T(1,128)} %bitcast.s_ref, bf16[512,512]{1,0:T(8,128)(2,1)S(1)} %shard_map.67.im_ref.i0, f32[16,128]{1,0:T(8,128)S(1)} %get-tuple-element.38.row_ref, f32[1,1024]{1,0:T(1,128)S(1)} %get-tuple-element.39.col_ref, ...), custom_call_target="tpu_custom_call" | custom-call | tf_op jit(solution)/shard_map/pallas_call | solution.py:56
  64.0 1.3 %shard_map.83 = f32[544,512]{1,0:T(8,128)S(1)} custom-call(bf16[512,1024]{1,0:T(8,128)(2,1)S(1)} %get-tuple-element.46.w0, bf16[512,1024]{1,0:T(8,128)(2,1)S(1)} %get-tuple-element.47.w1, bf16[512,1024]{1,0:T(8,128)(2,1)S(1)} %get-tuple-element.48.w2, bf16[512,1024]{1,0:T(8,128)(2,1)S(1)} %get-tuple-element.49.w3, bf16[512,512]{1,0:T(8,128)(2,1)S(1)} %shard_map.67.im_ref.i0, ...), custom_call_target="tpu_custom_call" | custom-call | tf_op jit(solution)/shard_map/pallas_call | solution.py:56
  65.3 0.1 convert_element_type.117
  65.4 0.2 collective-permute-start.20
  65.7 0.1 convert_element_type.100
  65.8 2.0 %collective-permute-start.16 = (f16[544,512]{1,0:T(8,128)(2,1)S(1)}, f16[544,512]{1,0:T(8,128)(2,1)S(1)}, u32[]{:S(2)}, u32[]{:S(2)}) collective-permute-start(f16[544,512]{1,0:T(8,128)(2,1)S(1)} %convert_element_type.100), channel_id=1, source_target_pairs={{0,1},{1,2},{2,3},{3,0},{4,12},{5,13},{6,14},{7,15},{8,9},{9,10},{... | collective-permute-start | bytes 1671176 | tf_op jit(solution)/shard_map/ppermute | solution.py:33
  67.8 0.1 convert_element_type.98
  67.9 1.4 %collective-permute-start.15 = (f16[544,512]{1,0:T(8,128)(2,1)S(1)}, f16[544,512]{1,0:T(8,128)(2,1)S(1)}, u32[]{:S(2)}, u32[]{:S(2)}) collective-permute-start(f16[544,512]{1,0:T(8,128)(2,1)S(1)} %convert_element_type.98), channel_id=1, source_target_pairs={{0,3},{1,0},{2,1},{3,2},{4,28},{5,29},{6,30},{7,31},{8,11},{9,8},{... | collective-permute-start | bytes 1671176 | tf_op jit(solution)/shard_map/ppermute | solution.py:33
  69.3 0.1 convert_element_type.96
  69.4 2.3 %collective-permute-start.14 = (f16[544,512]{1,0:T(8,128)(2,1)S(1)}, f16[544,512]{1,0:T(8,128)(2,1)S(1)}, u32[]{:S(2)}, u32[]{:S(2)}) collective-permute-start(f16[544,512]{1,0:T(8,128)(2,1)S(1)} %convert_element_type.96), channel_id=1, source_target_pairs={{0,2},{1,3},{2,0},{3,1},{4,20},{5,21},{6,22},{7,23},{8,10},{9,11},... | collective-permute-start | bytes 1671176 | tf_op jit(solution)/shard_map/ppermute | solution.py:33
  71.7 1.3 %shard_map.82 = f32[544,512]{1,0:T(8,128)S(1)} custom-call(bf16[512,1024]{1,0:T(8,128)(2,1)S(1)} %get-tuple-element.46.w0, bf16[512,1024]{1,0:T(8,128)(2,1)S(1)} %get-tuple-element.47.w1, bf16[512,1024]{1,0:T(8,128)(2,1)S(1)} %get-tuple-element.48.w2, bf16[512,1024]{1,0:T(8,128)(2,1)S(1)} %get-tuple-element.49.w3, bf16[512,512]{1,0:T(8,128)(2,1)S(1)} %shard_map.67.im_ref.i0, ...), custom_call_target="tpu_custom_call" | custom-call | tf_op jit(solution)/shard_map/pallas_call | solution.py:56
  73.0 0.2 fusion.2
  73.2 1.7 %collective-permute-start.21 = (f16[136,512]{1,0:T(8,128)(2,1)S(1)}, f16[136,512]{1,0:T(8,128)(2,1)S(1)}, u32[]{:S(2)}, u32[]{:S(2)}) collective-permute-start(f16[136,512]{1,0:T(8,128)(2,1)S(1)} %get-tuple-element.59), channel_id=1, source_target_pairs={{0,64},{32,96},{64,0},{96,32},{1,65},{33,97},{65,1},{97,33},{2,66}... | collective-permute-start | bytes 417800 | tf_op jit(solution)/shard_map/ppermute | solution.py:37
  74.8 0.1 collective-permute-start.23
  74.9 1.7 %collective-permute-done.16 = f16[544,512]{1,0:T(8,128)(2,1)S(1)} collective-permute-done((f16[544,512]{1,0:T(8,128)(2,1)S(1)}, f16[544,512]{1,0:T(8,128)(2,1)S(1)}, u32[]{:S(2)}, u32[]{:S(2)}) %collective-permute-start.16) | collective-permute-done | bytes 557088 | tf_op jit(solution)/shard_map/ppermute | solution.py:33
  76.6 1.5 %collective-permute-start.22 = (f16[136,512]{1,0:T(8,128)(2,1)S(1)}, f16[136,512]{1,0:T(8,128)(2,1)S(1)}, u32[]{:S(2)}, u32[]{:S(2)}) collective-permute-start(f16[136,512]{1,0:T(8,128)(2,1)S(1)} %get-tuple-element.61), channel_id=1, source_target_pairs={{0,96},{32,0},{64,32},{96,64},{1,97},{33,1},{65,33},{97,65},{2,98}... | collective-permute-start | bytes 417800 | tf_op jit(solution)/shard_map/ppermute | solution.py:37
  78.1 5.8 %collective-permute-done.14 = f16[544,512]{1,0:T(8,128)(2,1)S(1)} collective-permute-done((f16[544,512]{1,0:T(8,128)(2,1)S(1)}, f16[544,512]{1,0:T(8,128)(2,1)S(1)}, u32[]{:S(2)}, u32[]{:S(2)}) %collective-permute-start.14) | collective-permute-done | bytes 557088 | tf_op jit(solution)/shard_map/ppermute | solution.py:33
  83.9 0.2 add_convert_fusion.2
  84.2 3.1 %collective-permute-start.17 = (f16[136,512]{1,0:T(8,128)(2,1)S(1)}, f16[136,512]{1,0:T(8,128)(2,1)S(1)}, u32[]{:S(2)}, u32[]{:S(2)}) collective-permute-start(f16[136,512]{1,0:T(8,128)(2,1)S(1)} %get-tuple-element.56), channel_id=1, source_target_pairs={{0,16},{1,17},{2,18},{3,19},{4,6},{5,7},{6,4},{7,5},{8,24},{9,25},... | collective-permute-start | bytes 417800 | tf_op jit(solution)/shard_map/ppermute | solution.py:33
  87.2 0.6 collective-permute-start.19
  87.8 2.7 %collective-permute-start.18 = (f16[136,512]{1,0:T(8,128)(2,1)S(1)}, f16[136,512]{1,0:T(8,128)(2,1)S(1)}, u32[]{:S(2)}, u32[]{:S(2)}) collective-permute-start(f16[136,512]{1,0:T(8,128)(2,1)S(1)} %get-tuple-element.58), channel_id=1, source_target_pairs={{0,24},{1,25},{2,26},{3,27},{4,7},{5,4},{6,5},{7,6},{8,0},{9,1},{1... | collective-permute-start | bytes 417800 | tf_op jit(solution)/shard_map/ppermute | solution.py:33
  90.5 0.1 slice_add_fusion.3.g_ref
  90.6 0.7 shard_map.84
  91.3 2.2 %collective-permute-done.19 = f16[136,512]{1,0:T(8,128)(2,1)S(1)} collective-permute-done((f16[136,512]{1,0:T(8,128)(2,1)S(1)}, f16[136,512]{1,0:T(8,128)(2,1)S(1)}, u32[]{:S(2)}, u32[]{:S(2)}) %collective-permute-start.19) | collective-permute-done | bytes 139296 | tf_op jit(solution)/shard_map/ppermute | solution.py:33
  93.5 0.2 add_add_fusion.g_ref
  93.7 0.9 shard_map.85
  (32 shorter events, 0.2 us)
Async XLA Ops:
  0.6 8.5 %collective-permute-start.3 = (bf16[128,512]{1,0:T(8,128)(2,1)}, bf16[128,512]{1,0:T(8,128)(2,1)S(1)}, u32[]{:S(2)}, u32[]{:S(2)}) collective-permute-start(bf16[128,512]{1,0:T(8,128)(2,1)} %a_ref.3), channel_id=1, source_target_pairs={{0,32},{32,64},{64,96},{96,0},{1,33},{33,65},{65,97},{97,1},{2,34}... | collective-permute-start | bytes 393224 | tf_op jit(solution)/shard_map/ppermute | solution.py:37
  2.3 10.7 %collective-permute-start.5 = (bf16[128,512]{1,0:T(8,128)(2,1)}, bf16[128,512]{1,0:T(8,128)(2,1)S(1)}, u32[]{:S(2)}, u32[]{:S(2)}) collective-permute-start(bf16[128,512]{1,0:T(8,128)(2,1)} %a_ref.3), channel_id=1, source_target_pairs={{0,96},{32,0},{64,32},{96,64},{1,97},{33,1},{65,33},{97,65},{2,98}... | collective-permute-start | bytes 393224 | tf_op jit(solution)/shard_map/ppermute | solution.py:37
  3.9 9.0 %collective-permute-start.4 = (bf16[128,512]{1,0:T(8,128)(2,1)}, bf16[128,512]{1,0:T(8,128)(2,1)S(1)}, u32[]{:S(2)}, u32[]{:S(2)}) collective-permute-start(bf16[128,512]{1,0:T(8,128)(2,1)} %a_ref.3), channel_id=1, source_target_pairs={{0,64},{32,96},{64,0},{96,32},{1,65},{33,97},{65,1},{97,33},{2,66}... | collective-permute-start | bytes 393224 | tf_op jit(solution)/shard_map/ppermute | solution.py:37
  5.9 7.3 %collective-permute-start = (bf16[128,512]{1,0:T(8,128)(2,1)}, bf16[128,512]{1,0:T(8,128)(2,1)S(1)}, u32[]{:S(2)}, u32[]{:S(2)}) collective-permute-start(bf16[128,512]{1,0:T(8,128)(2,1)} %a_ref.2), channel_id=1, source_target_pairs={{0,8},{1,9},{2,10},{3,11},{4,5},{5,6},{6,7},{7,4},{8,16},{9,17},{1... | collective-permute-start | bytes 393224 | tf_op jit(solution)/shard_map/ppermute | solution.py:33
  7.4 5.7 %collective-permute-start.2 = (bf16[128,512]{1,0:T(8,128)(2,1)}, bf16[128,512]{1,0:T(8,128)(2,1)S(1)}, u32[]{:S(2)}, u32[]{:S(2)}) collective-permute-start(bf16[128,512]{1,0:T(8,128)(2,1)} %a_ref.2), channel_id=1, source_target_pairs={{0,24},{1,25},{2,26},{3,27},{4,7},{5,4},{6,5},{7,6},{8,0},{9,1},{1... | collective-permute-start | bytes 393224 | tf_op jit(solution)/shard_map/ppermute | solution.py:33
  9.1 6.7 %collective-permute-start.1 = (bf16[128,512]{1,0:T(8,128)(2,1)}, bf16[128,512]{1,0:T(8,128)(2,1)S(1)}, u32[]{:S(2)}, u32[]{:S(2)}) collective-permute-start(bf16[128,512]{1,0:T(8,128)(2,1)} %a_ref.2), channel_id=1, source_target_pairs={{0,16},{1,17},{2,18},{3,19},{4,6},{5,7},{6,4},{7,5},{8,24},{9,25},... | collective-permute-start | bytes 393224 | tf_op jit(solution)/shard_map/ppermute | solution.py:33
  11.1 0.9 copy-start.2
  12.0 0.9 copy-start.1
  13.0 8.9 %collective-permute-start.6 = (bf16[512,512]{1,0:T(8,128)(2,1)S(1)}, bf16[512,512]{1,0:T(8,128)(2,1)S(1)}, u32[]{:S(2)}, u32[]{:S(2)}) collective-permute-start(bf16[512,512]{1,0:T(8,128)(2,1)S(1)} %shard_map.69.t0_ref), channel_id=1, source_target_pairs={{0,4},{4,0},{1,5},{5,1},{2,6},{6,2},{3,7},{7,3},{8,12},{12,8},{9,1... | collective-permute-start | bytes 1572872 | tf_op jit(solution)/shard_map/ppermute | solution.py:41
  15.8 16.4 %collective-permute-start.9 = (bf16[512,512]{1,0:T(8,128)(2,1)S(1)}, bf16[512,512]{1,0:T(8,128)(2,1)S(1)}, u32[]{:S(2)}, u32[]{:S(2)}) collective-permute-start(bf16[512,512]{1,0:T(8,128)(2,1)S(1)} %shard_map.67.im_ref.i0), channel_id=1, source_target_pairs={{0,3},{1,0},{2,1},{3,2},{4,28},{5,29},{6,30},{7,31},{8,11},{9,8},{... | collective-permute-start | bytes 1572872 | tf_op jit(solution)/shard_map/ppermute | solution.py:33
  19.9 14.5 %collective-permute-start.8 = (bf16[512,512]{1,0:T(8,128)(2,1)S(1)}, bf16[512,512]{1,0:T(8,128)(2,1)S(1)}, u32[]{:S(2)}, u32[]{:S(2)}) collective-permute-start(bf16[512,512]{1,0:T(8,128)(2,1)S(1)} %shard_map.67.im_ref.i0), channel_id=1, source_target_pairs={{0,2},{1,3},{2,0},{3,1},{4,20},{5,21},{6,22},{7,23},{8,10},{9,11},... | collective-permute-start | bytes 1572872 | tf_op jit(solution)/shard_map/ppermute | solution.py:33
  19.9 16.7 %collective-permute-start.7 = (bf16[512,512]{1,0:T(8,128)(2,1)S(1)}, bf16[512,512]{1,0:T(8,128)(2,1)S(1)}, u32[]{:S(2)}, u32[]{:S(2)}) collective-permute-start(bf16[512,512]{1,0:T(8,128)(2,1)S(1)} %shard_map.67.im_ref.i0), channel_id=1, source_target_pairs={{0,1},{1,2},{2,3},{3,0},{4,12},{5,13},{6,14},{7,15},{8,9},{9,10},{... | collective-permute-start | bytes 1572872 | tf_op jit(solution)/shard_map/ppermute | solution.py:33
  33.8 0.6 copy-start.3
  36.0 0.6 copy-start.5
  38.2 0.6 copy-start.7
  38.9 0.7 copy-start
  39.6 17.9 %all-to-all-start = ((f32[16,40,128]{2,1,0:T(8,128)}), f32[16,40,128]{2,1,0:T(8,128)S(1)}, u32[]{:S(2)}, u32[]{:S(2)}) async-start(f32[16,40,128]{2,1,0:T(8,128)} %bitcast.6), calls=%async_computation | async-start | bytes 655360 | tf_op jit(solution)/shard_map/all_to_all | solution.py:375
  46.1 0.8 copy-start.4
  46.9 0.8 copy-start.6
  47.7 0.8 copy-start.8
  48.4 3.8 %collective-permute-start.12 = (f32[24,128]{1,0:T(8,128)S(1)}, f32[24,128]{1,0:T(8,128)S(1)}, u32[]{:S(2)}, u32[]{:S(2)}) collective-permute-start(f32[24,128]{1,0:T(8,128)S(1)} %shard_map.75.b0), channel_id=1, source_target_pairs={{0,96},{32,0},{64,32},{96,64},{1,97},{33,1},{65,33},{97,65},{2,98}... | collective-permute-start | bytes 36872 | tf_op jit(solution)/shard_map/ppermute | solution.py:37
  50.5 5.2 %collective-permute-start.11 = (f32[24,128]{1,0:T(8,128)S(1)}, f32[24,128]{1,0:T(8,128)S(1)}, u32[]{:S(2)}, u32[]{:S(2)}) collective-permute-start(f32[24,128]{1,0:T(8,128)S(1)} %shard_map.75.b0), channel_id=1, source_target_pairs={{0,64},{32,96},{64,0},{96,32},{1,65},{33,97},{65,1},{97,33},{2,66}... | collective-permute-start | bytes 36872 | tf_op jit(solution)/shard_map/ppermute | solution.py:37
  51.2 4.9 %collective-permute-start.10 = (f32[24,128]{1,0:T(8,128)S(1)}, f32[24,128]{1,0:T(8,128)S(1)}, u32[]{:S(2)}, u32[]{:S(2)}) collective-permute-start(f32[24,128]{1,0:T(8,128)S(1)} %shard_map.75.b0), channel_id=1, source_target_pairs={{0,32},{32,64},{64,96},{96,0},{1,33},{33,65},{65,97},{97,1},{2,34}... | collective-permute-start | bytes 36872 | tf_op jit(solution)/shard_map/ppermute | solution.py:37
  56.1 1.4 %collective-permute-start.13 = (f32[24,128]{1,0:T(8,128)S(1)}, f32[24,128]{1,0:T(8,128)S(1)}, u32[]{:S(2)}, u32[]{:S(2)}) collective-permute-start(f32[24,128]{1,0:T(8,128)S(1)} %shard_map.76.b0), channel_id=1, source_target_pairs={{0,4},{4,0},{1,5},{5,1},{2,6},{6,2},{3,7},{7,3},{8,12},{12,8},{9,1... | collective-permute-start | bytes 36872 | tf_op jit(solution)/shard_map/ppermute | solution.py:41
  65.4 7.6 %collective-permute-start.20 = (f16[544,512]{1,0:T(8,128)(2,1)S(1)}, f16[544,512]{1,0:T(8,128)(2,1)S(1)}, u32[]{:S(2)}, u32[]{:S(2)}) collective-permute-start(f16[544,512]{1,0:T(8,128)(2,1)S(1)} %convert_element_type.117), channel_id=1, source_target_pairs={{0,4},{4,0},{1,5},{5,1},{2,6},{6,2},{3,7},{7,3},{8,12},{12,8},{9,1... | collective-permute-start | bytes 1671176 | tf_op jit(solution)/shard_map/ppermute | solution.py:41
  65.8 10.8 %collective-permute-start.16 = (f16[544,512]{1,0:T(8,128)(2,1)S(1)}, f16[544,512]{1,0:T(8,128)(2,1)S(1)}, u32[]{:S(2)}, u32[]{:S(2)}) collective-permute-start(f16[544,512]{1,0:T(8,128)(2,1)S(1)} %convert_element_type.100), channel_id=1, source_target_pairs={{0,1},{1,2},{2,3},{3,0},{4,12},{5,13},{6,14},{7,15},{8,9},{9,10},{... | collective-permute-start | bytes 1671176 | tf_op jit(solution)/shard_map/ppermute | solution.py:33
  67.9 10.2 %collective-permute-start.15 = (f16[544,512]{1,0:T(8,128)(2,1)S(1)}, f16[544,512]{1,0:T(8,128)(2,1)S(1)}, u32[]{:S(2)}, u32[]{:S(2)}) collective-permute-start(f16[544,512]{1,0:T(8,128)(2,1)S(1)} %convert_element_type.98), channel_id=1, source_target_pairs={{0,3},{1,0},{2,1},{3,2},{4,28},{5,29},{6,30},{7,31},{8,11},{9,8},{... | collective-permute-start | bytes 1671176 | tf_op jit(solution)/shard_map/ppermute | solution.py:33
  69.4 14.5 %collective-permute-start.14 = (f16[544,512]{1,0:T(8,128)(2,1)S(1)}, f16[544,512]{1,0:T(8,128)(2,1)S(1)}, u32[]{:S(2)}, u32[]{:S(2)}) collective-permute-start(f16[544,512]{1,0:T(8,128)(2,1)S(1)} %convert_element_type.96), channel_id=1, source_target_pairs={{0,2},{1,3},{2,0},{3,1},{4,20},{5,21},{6,22},{7,23},{8,10},{9,11},... | collective-permute-start | bytes 1671176 | tf_op jit(solution)/shard_map/ppermute | solution.py:33
  73.2 14.6 %collective-permute-start.21 = (f16[136,512]{1,0:T(8,128)(2,1)S(1)}, f16[136,512]{1,0:T(8,128)(2,1)S(1)}, u32[]{:S(2)}, u32[]{:S(2)}) collective-permute-start(f16[136,512]{1,0:T(8,128)(2,1)S(1)} %get-tuple-element.59), channel_id=1, source_target_pairs={{0,64},{32,96},{64,0},{96,32},{1,65},{33,97},{65,1},{97,33},{2,66}... | collective-permute-start | bytes 417800 | tf_op jit(solution)/shard_map/ppermute | solution.py:37
  74.8 15.6 %collective-permute-start.23 = (f16[136,512]{1,0:T(8,128)(2,1)S(1)}, f16[136,512]{1,0:T(8,128)(2,1)S(1)}, u32[]{:S(2)}, u32[]{:S(2)}) collective-permute-start(f16[136,512]{1,0:T(8,128)(2,1)S(1)} %get-tuple-element.60), channel_id=1, source_target_pairs={{0,32},{32,64},{64,96},{96,0},{1,33},{33,65},{65,97},{97,1},{2,34}... | collective-permute-start | bytes 417800 | tf_op jit(solution)/shard_map/ppermute | solution.py:37
  76.6 13.9 %collective-permute-start.22 = (f16[136,512]{1,0:T(8,128)(2,1)S(1)}, f16[136,512]{1,0:T(8,128)(2,1)S(1)}, u32[]{:S(2)}, u32[]{:S(2)}) collective-permute-start(f16[136,512]{1,0:T(8,128)(2,1)S(1)} %get-tuple-element.61), channel_id=1, source_target_pairs={{0,96},{32,0},{64,32},{96,64},{1,97},{33,1},{65,33},{97,65},{2,98}... | collective-permute-start | bytes 417800 | tf_op jit(solution)/shard_map/ppermute | solution.py:37
  84.2 7.1 %collective-permute-start.17 = (f16[136,512]{1,0:T(8,128)(2,1)S(1)}, f16[136,512]{1,0:T(8,128)(2,1)S(1)}, u32[]{:S(2)}, u32[]{:S(2)}) collective-permute-start(f16[136,512]{1,0:T(8,128)(2,1)S(1)} %get-tuple-element.56), channel_id=1, source_target_pairs={{0,16},{1,17},{2,18},{3,19},{4,6},{5,7},{6,4},{7,5},{8,24},{9,25},... | collective-permute-start | bytes 417800 | tf_op jit(solution)/shard_map/ppermute | solution.py:33
  87.2 6.3 %collective-permute-start.19 = (f16[136,512]{1,0:T(8,128)(2,1)S(1)}, f16[136,512]{1,0:T(8,128)(2,1)S(1)}, u32[]{:S(2)}, u32[]{:S(2)}) collective-permute-start(f16[136,512]{1,0:T(8,128)(2,1)S(1)} %get-tuple-element.57), channel_id=1, source_target_pairs={{0,8},{1,9},{2,10},{3,11},{4,5},{5,6},{6,7},{7,4},{8,16},{9,17},{1... | collective-permute-start | bytes 417800 | tf_op jit(solution)/shard_map/ppermute | solution.py:33
  87.8 5.7 %collective-permute-start.18 = (f16[136,512]{1,0:T(8,128)(2,1)S(1)}, f16[136,512]{1,0:T(8,128)(2,1)S(1)}, u32[]{:S(2)}, u32[]{:S(2)}) collective-permute-start(f16[136,512]{1,0:T(8,128)(2,1)S(1)} %get-tuple-element.58), channel_id=1, source_target_pairs={{0,24},{1,25},{2,26},{3,27},{4,7},{5,4},{6,5},{7,6},{8,0},{9,1},{1... | collective-permute-start | bytes 417800 | tf_op jit(solution)/shard_map/ppermute | solution.py:33

commit v3 on v2

--- a/solution.py
+++ b/solution.py
@@ -69,17 +69,33 @@
     return pltpu.VMEM(shape, dtype)
 
 
-def hold_kernel(a_ref, o_ref):
-    o_ref[...] = a_ref[...]
-
-
-def held(value):
-    return call(hold_kernel, out((ROWS, 512), BF16), value)
-
-
-def join_kernel(a0, a1, a2, a3, o_ref):
-    for k, a in enumerate((a0, a1, a2, a3)):
-        o_ref[128 * k : 128 * (k + 1), :] = a[...]
+def hold_kernel(a_ref, b_ref, a_out, b_out, sems):
+    copies = [
+        pltpu.make_async_copy(ref, o_ref, sems.at[k])
+        for k, (ref, o_ref) in enumerate(((a_ref, a_out), (b_ref, b_out)))
+    ]
+    for copy in copies:
+        copy.start()
+    for copy in copies:
+        copy.wait()
+
+
+def held(a, b):
+    return pl.pallas_call(
+        hold_kernel,
+        out_shape=(out(a.shape, BF16), out(b.shape, BF16)),
+        in_specs=[pl.BlockSpec(memory_space=pl.ANY)] * 2,
+        out_specs=(pl.BlockSpec(memory_space=pltpu.VMEM),) * 2,
+        scratch_shapes=[pltpu.SemaphoreType.DMA((2,))],
+        name="hold",
+    )(a, b)
+
+
+def join_kernel(*refs):
+    o_ref, at = refs[-1], 0
+    for a in refs[:-1]:
+        o_ref[at : at + a.shape[0], :] = a[...]
+        at += a.shape[0]
 
 
 def joined(values):
@@ -358,10 +374,17 @@
 
 def program(images, texts, log_scale):
     s2 = jnp.reshape(jnp.exp(log_scale) * LOG2E, (1, 1))
-    line = [held(images)] + everyone(images, lambda v, d: turn(v, d, True))[1:]
+    own_images, own_texts = held(images, texts)
+    line = [own_images] + everyone(images, lambda v, d: turn(v, d, True))[1:]
     line = joined(line)
-    chunks = everyone(line, lambda v, d: turn(v, d, False))
-    t0 = [held(texts)] + everyone(texts, along_x)[1:]
+    chunks = [line, None, None, None]
+    for d in (1, 3):
+        chunks[d] = turn(line, d, False)
+    halves = []
+    for d, part in ((1, chunks[1][0:256]), (3, chunks[3][256:512])):
+        halves.append(turn(part, d, False))
+    chunks[2] = joined(halves)
+    t0 = [own_texts] + everyone(texts, along_x)[1:]
     t0 = joined(t0)
     t1 = other_core(t0)
     parts = [None] * 4
@@ -391,8 +414,14 @@
             smem=(0,),
             scratch=[pltpu.VMEM((512, 1024), F32)],
         )
-        if k:
-            sent[k] = turn(gs[k].astype(F16), 4 - k, False)
+        if k == 2:
+            for d, part in ((3, gs[k][0:272]), (1, gs[k][272:544])):
+                sent[d] = turn(part.astype(F16), d, False).astype(F32)
+        elif k:
+            mine = [gs[k][0:272], gs[k][272:544]]
+            mine[k // 2] = mine[k // 2] + sent.pop(4 - k)
+            mine = jnp.concatenate([m.astype(F16) for m in mine], axis=0)
+            sent[k + 4] = turn(mine, 4 - k, False)
     g0, g1 = [
         call(
             functools.partial(text_kernel, h),

time: 95.1 us -> 92.3 us (0.971)
  waiting for transfers between devices: 26.7 us -> 18.2 us
  starting transfers between devices: 41.3 us -> 44.3 us
  local copies, waits for them, and re-layouts: 6.63 us -> 7.99 us
  Pallas kernels: 17.3 us -> 18.3 us
    ppermute x12 -> x14, waiting for transfers between devices: 21.1 us -> 8.31 us  [turn(): return lax.ppermute(value, ('y', 'c', 'z'), pairs)]
    ppermute x9, waiting for transfers between devices: 4.44 us -> 8.69 us  [along_x(): return lax.ppermute(value, 'x', [(i, (i + shift) % 4) for i in range(4)])]
    ppermute x12 -> x14, starting transfers between devices: 22.6 us -> 25.6 us  [turn(): return lax.ppermute(value, ('y', 'c', 'z'), pairs)]
    slice x0 -> x3, local copies, waits for them, and re-layouts: none -> 1.55 us  [the longest x1 0.73 us: program(): chunks[3][256:512]]
    ppermute x9, starting transfers between devices: 11.7 us -> 13.2 us  [along_x(): return lax.ppermute(value, 'x', [(i, (i + shift) % 4) for i in range(4)])]
    all_to_all x1, starting transfers between devices: 6.49 us -> 5.06 us  [program(): lax.all_to_all(rows.reshape(16, 40, 128), ('y', 'z'), 0, 0, tiled=True)]
    pallas_call x0 -> x1, Pallas kernels: none -> 0.98 us  [held(): pl.pallas_call(hold_kernel, out_shape=(out(a.shape, BF16), out(b.shape, B...]
    unnamed x18 -> x20, local copies, waits for them, and re-layouts: 6.63 us -> 6.44 us
  transfers between devices with their start and end apart: 25 -> 27, of which waited for: 9 -> 13; matrix products, arithmetic and copies ran while one was open for 1% -> 3% of each run, Pallas kernels for 7% -> 15%
where the time goes in v3:
time: 92.3 us; the launch traced here: 91.7 us
  starting transfers between devices  44.3 us (48%)
  Pallas kernels  18.3 us (20%)
  waiting for transfers between devices  18.2 us (20%)
  local copies, waits for them, and re-layouts  7.99 us (9%)
  between operations  1.61 us (2%)
  other arithmetic  1.39 us (2%)
    ppermute x14, starting transfers between devices, turn(): return lax.ppermute(value, ('y', 'c', 'z'), pairs)  25.6 us
    pallas_call x19, Pallas kernels, call(): pl.pallas_call(kernel, out_shape=outs, in_specs=[pl.BlockSpec(memory_spac...  17.3 us
    ppermute x9, starting transfers between devices, along_x(): return lax.ppermute(value, 'x', [(i, (i + shift) % 4) for i in range(4)])  13.2 us
    ppermute x9, waiting for transfers between devices, along_x(): return lax.ppermute(value, 'x', [(i, (i + shift) % 4) for i in range(4)])  8.69 us
    ppermute x14, waiting for transfers between devices, turn(): return lax.ppermute(value, ('y', 'c', 'z'), pairs)  8.31 us
    unnamed x20, local copies, waits for them, and re-layouts  6.44 us
    all_to_all x1, starting transfers between devices, program(): lax.all_to_all(rows.reshape(16, 40, 128), ('y', 'z'), 0, 0, tiled=True)  5.06 us
  transfers between devices with their start and end apart: 27, of which 13 were waited for; matrix products, arithmetic and copies ran while one was open for 3% of the time, Pallas kernels for 15%

profile of v3, /device:TPU:0, one launch (start us, length us, event | category | flops | bytes accessed | tf_op | source)
XLA Modules:
  0.0 91.7 jit_solution(12585830138898820986)
XLA Ops:
  0.6 1.8 %collective-permute-start = (bf16[128,512]{1,0:T(8,128)(2,1)}, bf16[128,512]{1,0:T(8,128)(2,1)S(1)}, u32[]{:S(2)}, u32[]{:S(2)}) collective-permute-start(bf16[128,512]{1,0:T(8,128)(2,1)} %a_ref.1), channel_id=1, source_target_pairs={{0,8},{1,9},{2,10},{3,11},{4,5},{5,6},{6,7},{7,4},{8,16},{9,17},{1... | collective-permute-start | bytes 393224 | tf_op jit(solution)/shard_map/ppermute | solution.py:33
  2.4 1.5 %collective-permute-start.2 = (bf16[128,512]{1,0:T(8,128)(2,1)}, bf16[128,512]{1,0:T(8,128)(2,1)S(1)}, u32[]{:S(2)}, u32[]{:S(2)}) collective-permute-start(bf16[128,512]{1,0:T(8,128)(2,1)} %a_ref.1), channel_id=1, source_target_pairs={{0,24},{1,25},{2,26},{3,27},{4,7},{5,4},{6,5},{7,6},{8,0},{9,1},{1... | collective-permute-start | bytes 393224 | tf_op jit(solution)/shard_map/ppermute | solution.py:33
  3.9 2.1 %collective-permute-start.1 = (bf16[128,512]{1,0:T(8,128)(2,1)}, bf16[128,512]{1,0:T(8,128)(2,1)S(1)}, u32[]{:S(2)}, u32[]{:S(2)}) collective-permute-start(bf16[128,512]{1,0:T(8,128)(2,1)} %a_ref.1), channel_id=1, source_target_pairs={{0,16},{1,17},{2,18},{3,19},{4,6},{5,7},{6,4},{7,5},{8,24},{9,25},... | collective-permute-start | bytes 393224 | tf_op jit(solution)/shard_map/ppermute | solution.py:33
  6.0 1.0 %hold.1 = (bf16[128,512]{1,0:T(8,128)(2,1)S(1)}, bf16[128,512]{1,0:T(8,128)(2,1)S(1)}) custom-call(bf16[128,512]{1,0:T(8,128)(2,1)} %a_ref.1, bf16[128,512]{1,0:T(8,128)(2,1)} %b_ref.1), custom_call_target="tpu_custom_call" | custom-call | tf_op jit(solution)/shard_map/hold/pallas_call | solution.py:84
  7.1 0.5 collective-permute-done.2.refs_3_
  7.6 3.1 %collective-permute-done.1.refs_2_ = bf16[128,512]{1,0:T(8,128)(2,1)S(1)} collective-permute-done((bf16[128,512]{1,0:T(8,128)(2,1)}, bf16[128,512]{1,0:T(8,128)(2,1)S(1)}, u32[]{:S(2)}, u32[]{:S(2)}) %collective-permute-start.1) | collective-permute-done | bytes 131104 | tf_op jit(solution)/shard_map/ppermute | solution.py:33
  10.7 4.2 %collective-permute-start.9 = (bf16[512,512]{1,0:T(8,128)(2,1)S(1)}, bf16[512,512]{1,0:T(8,128)(2,1)S(1)}, u32[]{:S(2)}, u32[]{:S(2)}) collective-permute-start(bf16[512,512]{1,0:T(8,128)(2,1)S(1)} %shard_map.66.im_ref.i0), channel_id=1, source_target_pairs={{0,3},{1,0},{2,1},{3,2},{4,28},{5,29},{6,30},{7,31},{8,11},{9,8},{... | collective-permute-start | bytes 1572872 | tf_op jit(solution)/shard_map/ppermute | solution.py:33
  14.9 1.5 %collective-permute-start.3 = (bf16[128,512]{1,0:T(8,128)(2,1)S(1)}, bf16[128,512]{1,0:T(8,128)(2,1)S(1)}, u32[]{:S(2)}, u32[]{:S(2)}) collective-permute-start(bf16[128,512]{1,0:T(8,128)(2,1)S(1)} %copy-done.9), channel_id=1, source_target_pairs={{0,32},{32,64},{64,96},{96,0},{1,33},{33,65},{65,97},{97,1},{2,34}... | collective-permute-start | bytes 393224 | tf_op jit(solution)/shard_map/ppermute | solution.py:37
  16.4 1.7 %collective-permute-start.5 = (bf16[128,512]{1,0:T(8,128)(2,1)S(1)}, bf16[128,512]{1,0:T(8,128)(2,1)S(1)}, u32[]{:S(2)}, u32[]{:S(2)}) collective-permute-start(bf16[128,512]{1,0:T(8,128)(2,1)S(1)} %copy-done.9), channel_id=1, source_target_pairs={{0,96},{32,0},{64,32},{96,64},{1,97},{33,1},{65,33},{97,65},{2,98}... | collective-permute-start | bytes 393224 | tf_op jit(solution)/shard_map/ppermute | solution.py:37
  18.1 1.8 %collective-permute-start.4 = (bf16[128,512]{1,0:T(8,128)(2,1)S(1)}, bf16[128,512]{1,0:T(8,128)(2,1)S(1)}, u32[]{:S(2)}, u32[]{:S(2)}) collective-permute-start(bf16[128,512]{1,0:T(8,128)(2,1)S(1)} %copy-done.9), channel_id=1, source_target_pairs={{0,64},{32,96},{64,0},{96,32},{1,65},{33,97},{65,1},{97,33},{2,66}... | collective-permute-start | bytes 393224 | tf_op jit(solution)/shard_map/ppermute | solution.py:37
  19.9 2.5 %collective-permute-done.3.refs_1_ = bf16[128,512]{1,0:T(8,128)(2,1)S(1)} collective-permute-done((bf16[128,512]{1,0:T(8,128)(2,1)S(1)}, bf16[128,512]{1,0:T(8,128)(2,1)S(1)}, u32[]{:S(2)}, u32[]{:S(2)}) %collective-permute-start.3) | collective-permute-done | bytes 131104 | tf_op jit(solution)/shard_map/ppermute | solution.py:37
  22.5 2.1 %collective-permute-done.4.refs_2_ = bf16[128,512]{1,0:T(8,128)(2,1)S(1)} collective-permute-done((bf16[128,512]{1,0:T(8,128)(2,1)S(1)}, bf16[128,512]{1,0:T(8,128)(2,1)S(1)}, u32[]{:S(2)}, u32[]{:S(2)}) %collective-permute-start.4) | collective-permute-done | bytes 131104 | tf_op jit(solution)/shard_map/ppermute | solution.py:37
  24.7 0.7 slice.117
  25.5 3.2 %collective-permute-start.10 = (bf16[256,512]{1,0:T(8,128)(2,1)}, bf16[256,512]{1,0:T(8,128)(2,1)S(1)}, u32[]{:S(2)}, u32[]{:S(2)}) collective-permute-start(bf16[256,512]{1,0:T(8,128)(2,1)} %slice.117), channel_id=1, source_target_pairs={{0,3},{1,0},{2,1},{3,2},{4,28},{5,29},{6,30},{7,31},{8,11},{9,8},{... | collective-permute-start | bytes 786440 | tf_op jit(solution)/shard_map/ppermute | solution.py:33
  28.7 0.7 slice.116
  30.1 1.7 %shard_map.68 = (f32[16,128]{1,0:T(8,128)S(1)}, f32[8,1024]{1,0:T(8,128)S(1)}) custom-call(f32[1,1]{1,0:T(1,128)} %bitcast.s_ref, bf16[512,512]{1,0:T(8,128)(2,1)S(1)} %shard_map.66.im_ref.i0, bf16[512,512]{1,0:T(8,128)(2,1)S(1)} %shard_map.67.t0_ref, bf16[512,512]{1,0:T(8,128)(2,1)S(1)} %collective-permute-done.6.t1_ref), custom_call_target="tpu_custom_call" | custom-call | tf_op jit(solution)/shard_map/pallas_call | solution.py:56
  31.8 1.6 %shard_map.72 = (f32[16,128]{1,0:T(8,128)S(1)}, f32[8,1024]{1,0:T(8,128)S(1)}) custom-call(f32[1,1]{1,0:T(1,128)} %bitcast.s_ref, bf16[512,512]{1,0:T(8,128)(2,1)S(1)} %collective-permute-done.9.im_ref.i3, bf16[512,512]{1,0:T(8,128)(2,1)S(1)} %shard_map.67.t0_ref, bf16[512,512]{1,0:T(8,128)(2,1)S(1)} %collective-permute-done.6.t1_ref), custom_call_target="tpu_custom_call" | custom-call | tf_op jit(solution)/shard_map/pallas_call | solution.py:56
  33.4 0.6 copy-done.3
  34.0 1.6 %shard_map.69 = (f32[16,128]{1,0:T(8,128)S(1)}, f32[8,1024]{1,0:T(8,128)S(1)}) custom-call(f32[1,1]{1,0:T(1,128)} %bitcast.s_ref, bf16[512,512]{1,0:T(8,128)(2,1)S(1)} %collective-permute-done.7.im_ref.i1, bf16[512,512]{1,0:T(8,128)(2,1)S(1)} %shard_map.67.t0_ref, bf16[512,512]{1,0:T(8,128)(2,1)S(1)} %collective-permute-done.6.t1_ref), custom_call_target="tpu_custom_call" | custom-call | tf_op jit(solution)/shard_map/pallas_call | solution.py:56
  35.6 0.6 copy-done.5
  36.2 1.0 %collective-permute-done.8.refs_0_ = bf16[256,512]{1,0:T(8,128)(2,1)S(1)} collective-permute-done((bf16[256,512]{1,0:T(8,128)(2,1)}, bf16[256,512]{1,0:T(8,128)(2,1)S(1)}, u32[]{:S(2)}, u32[]{:S(2)}) %collective-permute-start.8) | collective-permute-done | bytes 262176 | tf_op jit(solution)/shard_map/ppermute | solution.py:33
  37.2 0.7 copy-done.1
  37.9 0.9 %copy-done.2 = bf16[256,512]{1,0:T(8,128)(2,1)S(1)} copy-done((bf16[256,512]{1,0:T(8,128)(2,1)S(1)}, bf16[256,512]{1,0:T(8,128)(2,1)}, u32[]{:S(2)}) %copy-start.2) | copy-done | bytes 262168
  38.9 1.6 %shard_map.71 = (f32[16,128]{1,0:T(8,128)S(1)}, f32[8,1024]{1,0:T(8,128)S(1)}) custom-call(f32[1,1]{1,0:T(1,128)} %bitcast.s_ref, bf16[512,512]{1,0:T(8,128)(2,1)S(1)} %shard_map.70.im_ref.i2, bf16[512,512]{1,0:T(8,128)(2,1)S(1)} %shard_map.67.t0_ref, bf16[512,512]{1,0:T(8,128)(2,1)S(1)} %collective-permute-done.6.t1_ref), custom_call_target="tpu_custom_call" | custom-call | tf_op jit(solution)/shard_map/pallas_call | solution.py:56
  40.5 0.6 copy-done.7
  41.2 0.7 copy-done
  41.9 5.1 %all-to-all-start = ((f32[16,40,128]{2,1,0:T(8,128)}), f32[16,40,128]{2,1,0:T(8,128)S(1)}, u32[]{:S(2)}, u32[]{:S(2)}) async-start(f32[16,40,128]{2,1,0:T(8,128)} %bitcast.6), calls=%async_computation | async-start | bytes 655360 | tf_op jit(solution)/shard_map/all_to_all | solution.py:398
  47.0 0.7 copy-done.4
  47.7 0.8 copy-done.6
  48.5 0.8 copy-done.8
  49.3 1.6 %collective-permute-start.13 = (f32[24,128]{1,0:T(8,128)S(1)}, f32[24,128]{1,0:T(8,128)S(1)}, u32[]{:S(2)}, u32[]{:S(2)}) collective-permute-start(f32[24,128]{1,0:T(8,128)S(1)} %shard_map.74.b0), channel_id=1, source_target_pairs={{0,96},{32,0},{64,32},{96,64},{1,97},{33,1},{65,33},{97,65},{2,98}... | collective-permute-start | bytes 36872 | tf_op jit(solution)/shard_map/ppermute | solution.py:37
  50.9 0.8 collective-permute-start.12
  51.7 0.9 collective-permute-start.11
  52.6 0.5 collective-permute-done.13.b3
  53.0 3.1 %collective-permute-done.12.b2 = f32[24,128]{1,0:T(8,128)S(1)} collective-permute-done((f32[24,128]{1,0:T(8,128)S(1)}, f32[24,128]{1,0:T(8,128)S(1)}, u32[]{:S(2)}, u32[]{:S(2)}) %collective-permute-start.12) | collective-permute-done | bytes 12320 | tf_op jit(solution)/shard_map/ppermute | solution.py:37
  56.1 0.5 collective-permute-done.11.b1
  56.6 0.3 collective-permute-start.14
  56.9 1.2 %collective-permute-done.14.b1 = f32[24,128]{1,0:T(8,128)S(1)} collective-permute-done((f32[24,128]{1,0:T(8,128)S(1)}, f32[24,128]{1,0:T(8,128)S(1)}, u32[]{:S(2)}, u32[]{:S(2)}) %collective-permute-start.14) | collective-permute-done | bytes 12320 | tf_op jit(solution)/shard_map/ppermute | solution.py:41
  58.0 0.2 shard_map.76
  58.2 1.6 %shard_map.79 = (bf16[512,1024]{1,0:T(8,128)(2,1)S(1)}, f32[544,512]{1,0:T(8,128)S(1)}) custom-call(f32[1,1]{1,0:T(1,128)} %bitcast.s_ref, bf16[512,512]{1,0:T(8,128)(2,1)S(1)} %shard_map.70.im_ref.i2, f32[16,128]{1,0:T(8,128)S(1)} %get-tuple-element.42.row_ref, f32[1,1024]{1,0:T(1,128)S(1)} %get-tuple-element.43.col_ref, ...), custom_call_target="tpu_custom_call" | custom-call | tf_op jit(solution)/shard_map/pallas_call | solution.py:56
  60.0 2.0 %collective-permute-start.17 = (f16[272,512]{1,0:T(8,128)(2,1)S(1)}, f16[272,512]{1,0:T(8,128)(2,1)S(1)}, u32[]{:S(2)}, u32[]{:S(2)}) collective-permute-start(f16[272,512]{1,0:T(8,128)(2,1)S(1)} %get-tuple-element.71), channel_id=1, source_target_pairs={{0,1},{1,2},{2,3},{3,0},{4,12},{5,13},{6,14},{7,15},{8,9},{9,10},{... | collective-permute-start | bytes 835592 | tf_op jit(solution)/shard_map/ppermute | solution.py:33
  62.0 1.3 %collective-permute-start.15 = (f16[272,512]{1,0:T(8,128)(2,1)S(1)}, f16[272,512]{1,0:T(8,128)(2,1)S(1)}, u32[]{:S(2)}, u32[]{:S(2)}) collective-permute-start(f16[272,512]{1,0:T(8,128)(2,1)S(1)} %get-tuple-element.70), channel_id=1, source_target_pairs={{0,3},{1,0},{2,1},{3,2},{4,28},{5,29},{6,30},{7,31},{8,11},{9,8},{... | collective-permute-start | bytes 835592 | tf_op jit(solution)/shard_map/ppermute | solution.py:33
  63.3 1.6 %shard_map.80 = (bf16[512,1024]{1,0:T(8,128)(2,1)S(1)}, f32[544,512]{1,0:T(8,128)S(1)}) custom-call(f32[1,1]{1,0:T(1,128)} %bitcast.s_ref, bf16[512,512]{1,0:T(8,128)(2,1)S(1)} %collective-permute-done.9.im_ref.i3, f32[16,128]{1,0:T(8,128)S(1)} %get-tuple-element.42.row_ref, f32[1,1024]{1,0:T(1,128)S(1)} %get-tuple-element.43.col_ref, ...), custom_call_target="tpu_custom_call" | custom-call | tf_op jit(solution)/shard_map/pallas_call | solution.py:56
  64.9 1.6 %shard_map.78 = (bf16[512,1024]{1,0:T(8,128)(2,1)S(1)}, f32[544,512]{1,0:T(8,128)S(1)}) custom-call(f32[1,1]{1,0:T(1,128)} %bitcast.s_ref, bf16[512,512]{1,0:T(8,128)(2,1)S(1)} %collective-permute-done.7.im_ref.i1, f32[16,128]{1,0:T(8,128)S(1)} %get-tuple-element.42.row_ref, f32[1,1024]{1,0:T(1,128)S(1)} %get-tuple-element.43.col_ref, ...), custom_call_target="tpu_custom_call" | custom-call | tf_op jit(solution)/shard_map/pallas_call | solution.py:56
  66.5 1.6 %shard_map.77 = (bf16[512,1024]{1,0:T(8,128)(2,1)S(1)}, f32[544,512]{1,0:T(8,128)S(1)}) custom-call(f32[1,1]{1,0:T(1,128)} %bitcast.s_ref, bf16[512,512]{1,0:T(8,128)(2,1)S(1)} %shard_map.66.im_ref.i0, f32[16,128]{1,0:T(8,128)S(1)} %get-tuple-element.42.row_ref, f32[1,1024]{1,0:T(1,128)S(1)} %get-tuple-element.43.col_ref, ...), custom_call_target="tpu_custom_call" | custom-call | tf_op jit(solution)/shard_map/pallas_call | solution.py:56
  68.1 1.3 %shard_map.82 = f32[544,512]{1,0:T(8,128)S(1)} custom-call(bf16[512,1024]{1,0:T(8,128)(2,1)S(1)} %get-tuple-element.50.w0, bf16[512,1024]{1,0:T(8,128)(2,1)S(1)} %get-tuple-element.51.w1, bf16[512,1024]{1,0:T(8,128)(2,1)S(1)} %get-tuple-element.52.w2, bf16[512,1024]{1,0:T(8,128)(2,1)S(1)} %get-tuple-element.53.w3, bf16[512,512]{1,0:T(8,128)(2,1)S(1)} %shard_map.66.im_ref.i0, ...), custom_call_target="tpu_custom_call" | custom-call | tf_op jit(solution)/shard_map/pallas_call | solution.py:56
  69.6 0.2 slice_convert_fusion
  69.9 1.6 %collective-permute-start.18 = (f16[544,512]{1,0:T(8,128)(2,1)S(1)}, f16[544,512]{1,0:T(8,128)(2,1)S(1)}, u32[]{:S(2)}, u32[]{:S(2)}) collective-permute-start(f16[544,512]{1,0:T(8,128)(2,1)S(1)} %pad_maximum_fusion.1), channel_id=1, source_target_pairs={{0,1},{1,2},{2,3},{3,0},{4,12},{5,13},{6,14},{7,15},{8,9},{9,10},{... | collective-permute-start | bytes 1671176 | tf_op jit(solution)/shard_map/ppermute | solution.py:33
  71.5 0.2 add_convert_fusion.1
  71.8 1.8 %collective-permute-start.16 = (f16[544,512]{1,0:T(8,128)(2,1)S(1)}, f16[544,512]{1,0:T(8,128)(2,1)S(1)}, u32[]{:S(2)}, u32[]{:S(2)}) collective-permute-start(f16[544,512]{1,0:T(8,128)(2,1)S(1)} %pad_maximum_fusion), channel_id=1, source_target_pairs={{0,3},{1,0},{2,1},{3,2},{4,28},{5,29},{6,30},{7,31},{8,11},{9,8},{... | collective-permute-start | bytes 1671176 | tf_op jit(solution)/shard_map/ppermute | solution.py:33
  73.6 1.3 %shard_map.81 = f32[544,512]{1,0:T(8,128)S(1)} custom-call(bf16[512,1024]{1,0:T(8,128)(2,1)S(1)} %get-tuple-element.50.w0, bf16[512,1024]{1,0:T(8,128)(2,1)S(1)} %get-tuple-element.51.w1, bf16[512,1024]{1,0:T(8,128)(2,1)S(1)} %get-tuple-element.52.w2, bf16[512,1024]{1,0:T(8,128)(2,1)S(1)} %get-tuple-element.53.w3, bf16[512,512]{1,0:T(8,128)(2,1)S(1)} %shard_map.66.im_ref.i0, ...), custom_call_target="tpu_custom_call" | custom-call | tf_op jit(solution)/shard_map/pallas_call | solution.py:56
  74.9 0.2 fusion.2
  75.1 1.6 %collective-permute-start.23 = (f16[136,512]{1,0:T(8,128)(2,1)S(1)}, f16[136,512]{1,0:T(8,128)(2,1)S(1)}, u32[]{:S(2)}, u32[]{:S(2)}) collective-permute-start(f16[136,512]{1,0:T(8,128)(2,1)S(1)} %get-tuple-element.63), channel_id=1, source_target_pairs={{0,64},{32,96},{64,0},{96,32},{1,65},{33,97},{65,1},{97,33},{2,66}... | collective-permute-start | bytes 417800 | tf_op jit(solution)/shard_map/ppermute | solution.py:37
  76.7 0.5 collective-permute-start.25
  77.1 2.8 %collective-permute-start.24 = (f16[136,512]{1,0:T(8,128)(2,1)S(1)}, f16[136,512]{1,0:T(8,128)(2,1)S(1)}, u32[]{:S(2)}, u32[]{:S(2)}) collective-permute-start(f16[136,512]{1,0:T(8,128)(2,1)S(1)} %get-tuple-element.65), channel_id=1, source_target_pairs={{0,96},{32,0},{64,32},{96,64},{1,97},{33,1},{65,33},{97,65},{2,98}... | collective-permute-start | bytes 417800 | tf_op jit(solution)/shard_map/ppermute | solution.py:37
  79.9 0.8 collective-permute-done.18
  80.7 0.7 collective-permute-done.16
  81.4 0.2 add_convert_fusion.4
  81.6 2.9 %collective-permute-start.19 = (f16[136,512]{1,0:T(8,128)(2,1)S(1)}, f16[136,512]{1,0:T(8,128)(2,1)S(1)}, u32[]{:S(2)}, u32[]{:S(2)}) collective-permute-start(f16[136,512]{1,0:T(8,128)(2,1)S(1)} %get-tuple-element.60), channel_id=1, source_target_pairs={{0,16},{1,17},{2,18},{3,19},{4,6},{5,7},{6,4},{7,5},{8,24},{9,25},... | collective-permute-start | bytes 417800 | tf_op jit(solution)/shard_map/ppermute | solution.py:33
  84.4 0.6 collective-permute-start.21
  85.0 2.7 %collective-permute-start.20 = (f16[136,512]{1,0:T(8,128)(2,1)S(1)}, f16[136,512]{1,0:T(8,128)(2,1)S(1)}, u32[]{:S(2)}, u32[]{:S(2)}) collective-permute-start(f16[136,512]{1,0:T(8,128)(2,1)S(1)} %get-tuple-element.62), channel_id=1, source_target_pairs={{0,24},{1,25},{2,26},{3,27},{4,7},{5,4},{6,5},{7,6},{8,0},{9,1},{1... | collective-permute-start | bytes 417800 | tf_op jit(solution)/shard_map/ppermute | solution.py:33
  87.8 0.7 shard_map.83
  88.4 2.2 %collective-permute-done.21 = f16[136,512]{1,0:T(8,128)(2,1)S(1)} collective-permute-done((f16[136,512]{1,0:T(8,128)(2,1)S(1)}, f16[136,512]{1,0:T(8,128)(2,1)S(1)}, u32[]{:S(2)}, u32[]{:S(2)}) %collective-permute-start.21) | collective-permute-done | bytes 139296 | tf_op jit(solution)/shard_map/ppermute | solution.py:33
  90.8 0.9 shard_map.84
  (43 shorter events, 1.3 us)
Async XLA Ops:
  0.6 14.3 %copy-start.9 = (bf16[128,512]{1,0:T(8,128)(2,1)S(1)}, bf16[128,512]{1,0:T(8,128)(2,1)}, u32[]{:S(2)}) copy-start(bf16[128,512]{1,0:T(8,128)(2,1)} %b_ref.1) | copy-start | bytes 393220
  0.6 6.5 %collective-permute-start = (bf16[128,512]{1,0:T(8,128)(2,1)}, bf16[128,512]{1,0:T(8,128)(2,1)S(1)}, u32[]{:S(2)}, u32[]{:S(2)}) collective-permute-start(bf16[128,512]{1,0:T(8,128)(2,1)} %a_ref.1), channel_id=1, source_target_pairs={{0,8},{1,9},{2,10},{3,11},{4,5},{5,6},{6,7},{7,4},{8,16},{9,17},{1... | collective-permute-start | bytes 393224 | tf_op jit(solution)/shard_map/ppermute | solution.py:33
  2.4 5.2 %collective-permute-start.2 = (bf16[128,512]{1,0:T(8,128)(2,1)}, bf16[128,512]{1,0:T(8,128)(2,1)S(1)}, u32[]{:S(2)}, u32[]{:S(2)}) collective-permute-start(bf16[128,512]{1,0:T(8,128)(2,1)} %a_ref.1), channel_id=1, source_target_pairs={{0,24},{1,25},{2,26},{3,27},{4,7},{5,4},{6,5},{7,6},{8,0},{9,1},{1... | collective-permute-start | bytes 393224 | tf_op jit(solution)/shard_map/ppermute | solution.py:33
  3.9 6.7 %collective-permute-start.1 = (bf16[128,512]{1,0:T(8,128)(2,1)}, bf16[128,512]{1,0:T(8,128)(2,1)S(1)}, u32[]{:S(2)}, u32[]{:S(2)}) collective-permute-start(bf16[128,512]{1,0:T(8,128)(2,1)} %a_ref.1), channel_id=1, source_target_pairs={{0,16},{1,17},{2,18},{3,19},{4,6},{5,7},{6,4},{7,5},{8,24},{9,25},... | collective-permute-start | bytes 393224 | tf_op jit(solution)/shard_map/ppermute | solution.py:33
  10.7 14.1 %collective-permute-start.9 = (bf16[512,512]{1,0:T(8,128)(2,1)S(1)}, bf16[512,512]{1,0:T(8,128)(2,1)S(1)}, u32[]{:S(2)}, u32[]{:S(2)}) collective-permute-start(bf16[512,512]{1,0:T(8,128)(2,1)S(1)} %shard_map.66.im_ref.i0), channel_id=1, source_target_pairs={{0,3},{1,0},{2,1},{3,2},{4,28},{5,29},{6,30},{7,31},{8,11},{9,8},{... | collective-permute-start | bytes 1572872 | tf_op jit(solution)/shard_map/ppermute | solution.py:33
  14.9 13.8 %collective-permute-start.7 = (bf16[512,512]{1,0:T(8,128)(2,1)S(1)}, bf16[512,512]{1,0:T(8,128)(2,1)S(1)}, u32[]{:S(2)}, u32[]{:S(2)}) collective-permute-start(bf16[512,512]{1,0:T(8,128)(2,1)S(1)} %shard_map.66.im_ref.i0), channel_id=1, source_target_pairs={{0,1},{1,2},{2,3},{3,0},{4,12},{5,13},{6,14},{7,15},{8,9},{9,10},{... | collective-permute-start | bytes 1572872 | tf_op jit(solution)/shard_map/ppermute | solution.py:33
  14.9 7.6 %collective-permute-start.3 = (bf16[128,512]{1,0:T(8,128)(2,1)S(1)}, bf16[128,512]{1,0:T(8,128)(2,1)S(1)}, u32[]{:S(2)}, u32[]{:S(2)}) collective-permute-start(bf16[128,512]{1,0:T(8,128)(2,1)S(1)} %copy-done.9), channel_id=1, source_target_pairs={{0,32},{32,64},{64,96},{96,0},{1,33},{33,65},{65,97},{97,1},{2,34}... | collective-permute-start | bytes 393224 | tf_op jit(solution)/shard_map/ppermute | solution.py:37
  16.4 6.1 %collective-permute-start.5 = (bf16[128,512]{1,0:T(8,128)(2,1)S(1)}, bf16[128,512]{1,0:T(8,128)(2,1)S(1)}, u32[]{:S(2)}, u32[]{:S(2)}) collective-permute-start(bf16[128,512]{1,0:T(8,128)(2,1)S(1)} %copy-done.9), channel_id=1, source_target_pairs={{0,96},{32,0},{64,32},{96,64},{1,97},{33,1},{65,33},{97,65},{2,98}... | collective-permute-start | bytes 393224 | tf_op jit(solution)/shard_map/ppermute | solution.py:37
  18.1 6.5 %collective-permute-start.4 = (bf16[128,512]{1,0:T(8,128)(2,1)S(1)}, bf16[128,512]{1,0:T(8,128)(2,1)S(1)}, u32[]{:S(2)}, u32[]{:S(2)}) collective-permute-start(bf16[128,512]{1,0:T(8,128)(2,1)S(1)} %copy-done.9), channel_id=1, source_target_pairs={{0,64},{32,96},{64,0},{96,32},{1,65},{33,97},{65,1},{97,33},{2,66}... | collective-permute-start | bytes 393224 | tf_op jit(solution)/shard_map/ppermute | solution.py:37
  24.6 5.5 %collective-permute-start.6 = (bf16[512,512]{1,0:T(8,128)(2,1)S(1)}, bf16[512,512]{1,0:T(8,128)(2,1)S(1)}, u32[]{:S(2)}, u32[]{:S(2)}) collective-permute-start(bf16[512,512]{1,0:T(8,128)(2,1)S(1)} %shard_map.67.t0_ref), channel_id=1, source_target_pairs={{0,4},{4,0},{1,5},{5,1},{2,6},{6,2},{3,7},{7,3},{8,12},{12,8},{9,1... | collective-permute-start | bytes 1572872 | tf_op jit(solution)/shard_map/ppermute | solution.py:41
  25.5 10.8 %collective-permute-start.10 = (bf16[256,512]{1,0:T(8,128)(2,1)}, bf16[256,512]{1,0:T(8,128)(2,1)S(1)}, u32[]{:S(2)}, u32[]{:S(2)}) collective-permute-start(bf16[256,512]{1,0:T(8,128)(2,1)} %slice.117), channel_id=1, source_target_pairs={{0,3},{1,0},{2,1},{3,2},{4,28},{5,29},{6,30},{7,31},{8,11},{9,8},{... | collective-permute-start | bytes 786440 | tf_op jit(solution)/shard_map/ppermute | solution.py:33
  29.4 7.8 %collective-permute-start.8 = (bf16[256,512]{1,0:T(8,128)(2,1)}, bf16[256,512]{1,0:T(8,128)(2,1)S(1)}, u32[]{:S(2)}, u32[]{:S(2)}) collective-permute-start(bf16[256,512]{1,0:T(8,128)(2,1)} %slice.116), channel_id=1, source_target_pairs={{0,1},{1,2},{2,3},{3,0},{4,12},{5,13},{6,14},{7,15},{8,9},{9,10},{... | collective-permute-start | bytes 786440 | tf_op jit(solution)/shard_map/ppermute | solution.py:33
  33.4 0.6 copy-start.3
  35.6 0.6 copy-start.5
  37.2 0.7 copy-start.1
  37.9 0.9 %copy-start.2 = (bf16[256,512]{1,0:T(8,128)(2,1)S(1)}, bf16[256,512]{1,0:T(8,128)(2,1)}, u32[]{:S(2)}) copy-start(bf16[256,512]{1,0:T(8,128)(2,1)} %copy-done.1) | copy-start | bytes 786436
  40.5 0.6 copy-start.7
  41.2 0.7 copy-start
  41.9 16.2 %all-to-all-start = ((f32[16,40,128]{2,1,0:T(8,128)}), f32[16,40,128]{2,1,0:T(8,128)S(1)}, u32[]{:S(2)}, u32[]{:S(2)}) async-start(f32[16,40,128]{2,1,0:T(8,128)} %bitcast.6), calls=%async_computation | async-start | bytes 655360 | tf_op jit(solution)/shard_map/all_to_all | solution.py:398
  46.9 0.8 copy-start.4
  47.7 0.8 copy-start.6
  48.5 0.8 copy-start.8
  49.3 3.8 %collective-permute-start.13 = (f32[24,128]{1,0:T(8,128)S(1)}, f32[24,128]{1,0:T(8,128)S(1)}, u32[]{:S(2)}, u32[]{:S(2)}) collective-permute-start(f32[24,128]{1,0:T(8,128)S(1)} %shard_map.74.b0), channel_id=1, source_target_pairs={{0,96},{32,0},{64,32},{96,64},{1,97},{33,1},{65,33},{97,65},{2,98}... | collective-permute-start | bytes 36872 | tf_op jit(solution)/shard_map/ppermute | solution.py:37
  50.9 5.2 %collective-permute-start.12 = (f32[24,128]{1,0:T(8,128)S(1)}, f32[24,128]{1,0:T(8,128)S(1)}, u32[]{:S(2)}, u32[]{:S(2)}) collective-permute-start(f32[24,128]{1,0:T(8,128)S(1)} %shard_map.74.b0), channel_id=1, source_target_pairs={{0,64},{32,96},{64,0},{96,32},{1,65},{33,97},{65,1},{97,33},{2,66}... | collective-permute-start | bytes 36872 | tf_op jit(solution)/shard_map/ppermute | solution.py:37
  51.7 4.9 %collective-permute-start.11 = (f32[24,128]{1,0:T(8,128)S(1)}, f32[24,128]{1,0:T(8,128)S(1)}, u32[]{:S(2)}, u32[]{:S(2)}) collective-permute-start(f32[24,128]{1,0:T(8,128)S(1)} %shard_map.74.b0), channel_id=1, source_target_pairs={{0,32},{32,64},{64,96},{96,0},{1,33},{33,65},{65,97},{97,1},{2,34}... | collective-permute-start | bytes 36872 | tf_op jit(solution)/shard_map/ppermute | solution.py:37
  56.6 1.4 %collective-permute-start.14 = (f32[24,128]{1,0:T(8,128)S(1)}, f32[24,128]{1,0:T(8,128)S(1)}, u32[]{:S(2)}, u32[]{:S(2)}) collective-permute-start(f32[24,128]{1,0:T(8,128)S(1)} %shard_map.75.b0), channel_id=1, source_target_pairs={{0,4},{4,0},{1,5},{5,1},{2,6},{6,2},{3,7},{7,3},{8,12},{12,8},{9,1... | collective-permute-start | bytes 36872 | tf_op jit(solution)/shard_map/ppermute | solution.py:41
  60.0 9.6 %collective-permute-start.17 = (f16[272,512]{1,0:T(8,128)(2,1)S(1)}, f16[272,512]{1,0:T(8,128)(2,1)S(1)}, u32[]{:S(2)}, u32[]{:S(2)}) collective-permute-start(f16[272,512]{1,0:T(8,128)(2,1)S(1)} %get-tuple-element.71), channel_id=1, source_target_pairs={{0,1},{1,2},{2,3},{3,0},{4,12},{5,13},{6,14},{7,15},{8,9},{9,10},{... | collective-permute-start | bytes 835592 | tf_op jit(solution)/shard_map/ppermute | solution.py:33
  62.0 9.4 %collective-permute-start.15 = (f16[272,512]{1,0:T(8,128)(2,1)S(1)}, f16[272,512]{1,0:T(8,128)(2,1)S(1)}, u32[]{:S(2)}, u32[]{:S(2)}) collective-permute-start(f16[272,512]{1,0:T(8,128)(2,1)S(1)} %get-tuple-element.70), channel_id=1, source_target_pairs={{0,3},{1,0},{2,1},{3,2},{4,28},{5,29},{6,30},{7,31},{8,11},{9,8},{... | collective-permute-start | bytes 835592 | tf_op jit(solution)/shard_map/ppermute | solution.py:33
  69.5 5.4 %collective-permute-start.22 = (f16[544,512]{1,0:T(8,128)(2,1)S(1)}, f16[544,512]{1,0:T(8,128)(2,1)S(1)}, u32[]{:S(2)}, u32[]{:S(2)}) collective-permute-start(f16[544,512]{1,0:T(8,128)(2,1)S(1)} %convert_element_type.109), channel_id=1, source_target_pairs={{0,4},{4,0},{1,5},{5,1},{2,6},{6,2},{3,7},{7,3},{8,12},{12,8},{9,1... | collective-permute-start | bytes 1671176 | tf_op jit(solution)/shard_map/ppermute | solution.py:41
  69.9 10.8 %collective-permute-start.18 = (f16[544,512]{1,0:T(8,128)(2,1)S(1)}, f16[544,512]{1,0:T(8,128)(2,1)S(1)}, u32[]{:S(2)}, u32[]{:S(2)}) collective-permute-start(f16[544,512]{1,0:T(8,128)(2,1)S(1)} %pad_maximum_fusion.1), channel_id=1, source_target_pairs={{0,1},{1,2},{2,3},{3,0},{4,12},{5,13},{6,14},{7,15},{8,9},{9,10},{... | collective-permute-start | bytes 1671176 | tf_op jit(solution)/shard_map/ppermute | solution.py:33
  71.8 9.6 %collective-permute-start.16 = (f16[544,512]{1,0:T(8,128)(2,1)S(1)}, f16[544,512]{1,0:T(8,128)(2,1)S(1)}, u32[]{:S(2)}, u32[]{:S(2)}) collective-permute-start(f16[544,512]{1,0:T(8,128)(2,1)S(1)} %pad_maximum_fusion), channel_id=1, source_target_pairs={{0,3},{1,0},{2,1},{3,2},{4,28},{5,29},{6,30},{7,31},{8,11},{9,8},{... | collective-permute-start | bytes 1671176 | tf_op jit(solution)/shard_map/ppermute | solution.py:33
  75.1 9.9 %collective-permute-start.23 = (f16[136,512]{1,0:T(8,128)(2,1)S(1)}, f16[136,512]{1,0:T(8,128)(2,1)S(1)}, u32[]{:S(2)}, u32[]{:S(2)}) collective-permute-start(f16[136,512]{1,0:T(8,128)(2,1)S(1)} %get-tuple-element.63), channel_id=1, source_target_pairs={{0,64},{32,96},{64,0},{96,32},{1,65},{33,97},{65,1},{97,33},{2,66}... | collective-permute-start | bytes 417800 | tf_op jit(solution)/shard_map/ppermute | solution.py:37
  76.7 11.0 %collective-permute-start.25 = (f16[136,512]{1,0:T(8,128)(2,1)S(1)}, f16[136,512]{1,0:T(8,128)(2,1)S(1)}, u32[]{:S(2)}, u32[]{:S(2)}) collective-permute-start(f16[136,512]{1,0:T(8,128)(2,1)S(1)} %get-tuple-element.64), channel_id=1, source_target_pairs={{0,32},{32,64},{64,96},{96,0},{1,33},{33,65},{65,97},{97,1},{2,34}... | collective-permute-start | bytes 417800 | tf_op jit(solution)/shard_map/ppermute | solution.py:37
  77.1 10.5 %collective-permute-start.24 = (f16[136,512]{1,0:T(8,128)(2,1)S(1)}, f16[136,512]{1,0:T(8,128)(2,1)S(1)}, u32[]{:S(2)}, u32[]{:S(2)}) collective-permute-start(f16[136,512]{1,0:T(8,128)(2,1)S(1)} %get-tuple-element.65), channel_id=1, source_target_pairs={{0,96},{32,0},{64,32},{96,64},{1,97},{33,1},{65,33},{97,65},{2,98}... | collective-permute-start | bytes 417800 | tf_op jit(solution)/shard_map/ppermute | solution.py:37
  81.6 6.9 %collective-permute-start.19 = (f16[136,512]{1,0:T(8,128)(2,1)S(1)}, f16[136,512]{1,0:T(8,128)(2,1)S(1)}, u32[]{:S(2)}, u32[]{:S(2)}) collective-permute-start(f16[136,512]{1,0:T(8,128)(2,1)S(1)} %get-tuple-element.60), channel_id=1, source_target_pairs={{0,16},{1,17},{2,18},{3,19},{4,6},{5,7},{6,4},{7,5},{8,24},{9,25},... | collective-permute-start | bytes 417800 | tf_op jit(solution)/shard_map/ppermute | solution.py:33
  84.4 6.3 %collective-permute-start.21 = (f16[136,512]{1,0:T(8,128)(2,1)S(1)}, f16[136,512]{1,0:T(8,128)(2,1)S(1)}, u32[]{:S(2)}, u32[]{:S(2)}) collective-permute-start(f16[136,512]{1,0:T(8,128)(2,1)S(1)} %get-tuple-element.61), channel_id=1, source_target_pairs={{0,8},{1,9},{2,10},{3,11},{4,5},{5,6},{6,7},{7,4},{8,16},{9,17},{1... | collective-permute-start | bytes 417800 | tf_op jit(solution)/shard_map/ppermute | solution.py:33
  85.0 5.7 %collective-permute-start.20 = (f16[136,512]{1,0:T(8,128)(2,1)S(1)}, f16[136,512]{1,0:T(8,128)(2,1)S(1)}, u32[]{:S(2)}, u32[]{:S(2)}) collective-permute-start(f16[136,512]{1,0:T(8,128)(2,1)S(1)} %get-tuple-element.62), channel_id=1, source_target_pairs={{0,24},{1,25},{2,26},{3,27},{4,7},{5,4},{6,5},{7,6},{8,0},{9,1},{1... | collective-permute-start | bytes 417800 | tf_op jit(solution)/shard_map/ppermute | solution.py:33

commit v4 on v3

--- a/solution.py
+++ b/solution.py
@@ -91,11 +91,9 @@
     )(a, b)
 
 
-def join_kernel(*refs):
-    o_ref, at = refs[-1], 0
-    for a in refs[:-1]:
-        o_ref[at : at + a.shape[0], :] = a[...]
-        at += a.shape[0]
+def join_kernel(a0, a1, a2, a3, o_ref):
+    for k, a in enumerate((a0, a1, a2, a3)):
+        o_ref[128 * k : 128 * (k + 1), :] = a[...]
 
 
 def joined(values):
@@ -377,13 +375,7 @@
     own_images, own_texts = held(images, texts)
     line = [own_images] + everyone(images, lambda v, d: turn(v, d, True))[1:]
     line = joined(line)
-    chunks = [line, None, None, None]
-    for d in (1, 3):
-        chunks[d] = turn(line, d, False)
-    halves = []
-    for d, part in ((1, chunks[1][0:256]), (3, chunks[3][256:512])):
-        halves.append(turn(part, d, False))
-    chunks[2] = joined(halves)
+    chunks = everyone(line, lambda v, d: turn(v, d, False))
     t0 = [own_texts] + everyone(texts, along_x)[1:]
     t0 = joined(t0)
     t1 = other_core(t0)
@@ -414,14 +406,8 @@
             smem=(0,),
             scratch=[pltpu.VMEM((512, 1024), F32)],
         )
-        if k == 2:
-            for d, part in ((3, gs[k][0:272]), (1, gs[k][272:544])):
-                sent[d] = turn(part.astype(F16), d, False).astype(F32)
-        elif k:
-            mine = [gs[k][0:272], gs[k][272:544]]
-            mine[k // 2] = mine[k // 2] + sent.pop(4 - k)
-            mine = jnp.concatenate([m.astype(F16) for m in mine], axis=0)
-            sent[k + 4] = turn(mine, 4 - k, False)
+        if k:
+            sent[k] = turn(gs[k].astype(F16), 4 - k, False)
     g0, g1 = [
         call(
             functools.partial(text_kernel, h),

time: 92.3 us -> 95.1 us (1.030)
  waiting for transfers between devices: 18.2 us -> 27.5 us
  local copies, waits for them, and re-layouts: 7.99 us -> 4.81 us
  starting transfers between devices: 44.3 us -> 41.4 us
    ppermute x14 -> x12, waiting for transfers between devices: 8.31 us -> 21.9 us  [turn(): return lax.ppermute(value, ('y', 'c', 'z'), pairs)]
    ppermute x9, waiting for transfers between devices: 8.69 us -> 4.43 us  [along_x(): return lax.ppermute(value, 'x', [(i, (i + shift) % 4) for i in range(4)])]
    ppermute x14 -> x12, starting transfers between devices: 25.6 us -> 22.6 us  [turn(): return lax.ppermute(value, ('y', 'c', 'z'), pairs)]
    unnamed x20 -> x14, local copies, waits for them, and re-layouts: 6.44 us -> 4.81 us
    slice x3 -> x0, local copies, waits for them, and re-layouts: 1.55 us -> none  [the longest x1 0.73 us: program(): chunks[3][256:512]]
    ppermute x9, starting transfers between devices: 13.2 us -> 11.7 us  [along_x(): return lax.ppermute(value, 'x', [(i, (i + shift) % 4) for i in range(4)])]
    all_to_all x1, starting transfers between devices: 5.06 us -> 6.49 us  [program(): lax.all_to_all(rows.reshape(16, 40, 128), ('y', 'z'), 0, 0, tiled=True)]
    pallas_call x19 -> x18, Pallas kernels: 17.3 us -> 17.2 us  [call(): pl.pallas_call(kernel, out_shape=outs, in_specs=[pl.BlockSpec(memory_spac...]
  transfers between devices with their start and end apart: 27 -> 25, of which waited for: 13 -> 10; matrix products, arithmetic and copies ran while one was open for 3% -> 1% of each run, Pallas kernels for 15% -> 8%
where the time goes in v4:
time: 95.1 us; the launch traced here: 94.6 us
  starting transfers between devices  41.4 us (44%)
  waiting for transfers between devices  27.5 us (29%)
  Pallas kernels  18.2 us (19%)
  local copies, waits for them, and re-layouts  4.81 us (5%)
  between operations  1.56 us (2%)
  other arithmetic  1.08 us (1%)
    ppermute x12, starting transfers between devices, turn(): return lax.ppermute(value, ('y', 'c', 'z'), pairs)  22.6 us
    ppermute x12, waiting for transfers between devices, turn(): return lax.ppermute(value, ('y', 'c', 'z'), pairs)  21.9 us
    pallas_call x18, Pallas kernels, call(): pl.pallas_call(kernel, out_shape=outs, in_specs=[pl.BlockSpec(memory_spac...  17.2 us
    ppermute x9, starting transfers between devices, along_x(): return lax.ppermute(value, 'x', [(i, (i + shift) % 4) for i in range(4)])  11.7 us
    all_to_all x1, starting transfers between devices, program(): lax.all_to_all(rows.reshape(16, 40, 128), ('y', 'z'), 0, 0, tiled=True)  6.49 us
    unnamed x14, local copies, waits for them, and re-layouts  4.81 us
    ppermute x9, waiting for transfers between devices, along_x(): return lax.ppermute(value, 'x', [(i, (i + shift) % 4) for i in range(4)])  4.43 us
  transfers between devices with their start and end apart: 25, of which 10 were waited for; matrix products, arithmetic and copies ran while one was open for 1% of the time, Pallas kernels for 8%

profile of v4, /device:TPU:0, one launch (start us, length us, event | category | flops | bytes accessed | tf_op | source)
XLA Modules:
  0.0 94.6 jit_solution(8447707611375220147)
XLA Ops:
  0.6 1.7 %collective-permute-start.3 = (bf16[128,512]{1,0:T(8,128)(2,1)}, bf16[128,512]{1,0:T(8,128)(2,1)S(1)}, u32[]{:S(2)}, u32[]{:S(2)}) collective-permute-start(bf16[128,512]{1,0:T(8,128)(2,1)} %b_ref.1), channel_id=1, source_target_pairs={{0,32},{32,64},{64,96},{96,0},{1,33},{33,65},{65,97},{97,1},{2,34}... | collective-permute-start | bytes 393224 | tf_op jit(solution)/shard_map/ppermute | solution.py:37
  2.3 1.6 %collective-permute-start.5 = (bf16[128,512]{1,0:T(8,128)(2,1)}, bf16[128,512]{1,0:T(8,128)(2,1)S(1)}, u32[]{:S(2)}, u32[]{:S(2)}) collective-permute-start(bf16[128,512]{1,0:T(8,128)(2,1)} %b_ref.1), channel_id=1, source_target_pairs={{0,96},{32,0},{64,32},{96,64},{1,97},{33,1},{65,33},{97,65},{2,98}... | collective-permute-start | bytes 393224 | tf_op jit(solution)/shard_map/ppermute | solution.py:37
  3.9 1.9 %collective-permute-start.4 = (bf16[128,512]{1,0:T(8,128)(2,1)}, bf16[128,512]{1,0:T(8,128)(2,1)S(1)}, u32[]{:S(2)}, u32[]{:S(2)}) collective-permute-start(bf16[128,512]{1,0:T(8,128)(2,1)} %b_ref.1), channel_id=1, source_target_pairs={{0,64},{32,96},{64,0},{96,32},{1,65},{33,97},{65,1},{97,33},{2,66}... | collective-permute-start | bytes 393224 | tf_op jit(solution)/shard_map/ppermute | solution.py:37
  5.9 1.6 %collective-permute-start = (bf16[128,512]{1,0:T(8,128)(2,1)}, bf16[128,512]{1,0:T(8,128)(2,1)S(1)}, u32[]{:S(2)}, u32[]{:S(2)}) collective-permute-start(bf16[128,512]{1,0:T(8,128)(2,1)} %a_ref.1), channel_id=1, source_target_pairs={{0,8},{1,9},{2,10},{3,11},{4,5},{5,6},{6,7},{7,4},{8,16},{9,17},{1... | collective-permute-start | bytes 393224 | tf_op jit(solution)/shard_map/ppermute | solution.py:33
  7.4 1.7 %collective-permute-start.2 = (bf16[128,512]{1,0:T(8,128)(2,1)}, bf16[128,512]{1,0:T(8,128)(2,1)S(1)}, u32[]{:S(2)}, u32[]{:S(2)}) collective-permute-start(bf16[128,512]{1,0:T(8,128)(2,1)} %a_ref.1), channel_id=1, source_target_pairs={{0,24},{1,25},{2,26},{3,27},{4,7},{5,4},{6,5},{7,6},{8,0},{9,1},{1... | collective-permute-start | bytes 393224 | tf_op jit(solution)/shard_map/ppermute | solution.py:33
  9.1 2.0 %collective-permute-start.1 = (bf16[128,512]{1,0:T(8,128)(2,1)}, bf16[128,512]{1,0:T(8,128)(2,1)S(1)}, u32[]{:S(2)}, u32[]{:S(2)}) collective-permute-start(bf16[128,512]{1,0:T(8,128)(2,1)} %a_ref.1), channel_id=1, source_target_pairs={{0,16},{1,17},{2,18},{3,19},{4,6},{5,7},{6,4},{7,5},{8,24},{9,25},... | collective-permute-start | bytes 393224 | tf_op jit(solution)/shard_map/ppermute | solution.py:33
  11.1 1.0 %hold.1 = (bf16[128,512]{1,0:T(8,128)(2,1)S(1)}, bf16[128,512]{1,0:T(8,128)(2,1)S(1)}) custom-call(bf16[128,512]{1,0:T(8,128)(2,1)} %a_ref.1, bf16[128,512]{1,0:T(8,128)(2,1)} %b_ref.1), custom_call_target="tpu_custom_call" | custom-call | tf_op jit(solution)/shard_map/hold/pallas_call | solution.py:84
  12.1 0.1 collective-permute-start.6
  12.3 0.4 collective-permute-done.2.a3
  12.6 3.2 %collective-permute-done.1.a2 = bf16[128,512]{1,0:T(8,128)(2,1)S(1)} collective-permute-done((bf16[128,512]{1,0:T(8,128)(2,1)}, bf16[128,512]{1,0:T(8,128)(2,1)S(1)}, u32[]{:S(2)}, u32[]{:S(2)}) %collective-permute-start.1) | collective-permute-done | bytes 131104 | tf_op jit(solution)/shard_map/ppermute | solution.py:33
  15.8 4.1 %collective-permute-start.9 = (bf16[512,512]{1,0:T(8,128)(2,1)S(1)}, bf16[512,512]{1,0:T(8,128)(2,1)S(1)}, u32[]{:S(2)}, u32[]{:S(2)}) collective-permute-start(bf16[512,512]{1,0:T(8,128)(2,1)S(1)} %shard_map.66.im_ref.i0), channel_id=1, source_target_pairs={{0,3},{1,0},{2,1},{3,2},{4,28},{5,29},{6,30},{7,31},{8,11},{9,8},{... | collective-permute-start | bytes 1572872 | tf_op jit(solution)/shard_map/ppermute | solution.py:33
  19.9 1.3 %collective-permute-start.7 = (bf16[512,512]{1,0:T(8,128)(2,1)S(1)}, bf16[512,512]{1,0:T(8,128)(2,1)S(1)}, u32[]{:S(2)}, u32[]{:S(2)}) collective-permute-start(bf16[512,512]{1,0:T(8,128)(2,1)S(1)} %shard_map.66.im_ref.i0), channel_id=1, source_target_pairs={{0,1},{1,2},{2,3},{3,0},{4,12},{5,13},{6,14},{7,15},{8,9},{9,10},{... | collective-permute-start | bytes 1572872 | tf_op jit(solution)/shard_map/ppermute | solution.py:33
  21.9 1.7 %shard_map.68 = (f32[16,128]{1,0:T(8,128)S(1)}, f32[8,1024]{1,0:T(8,128)S(1)}) custom-call(f32[1,1]{1,0:T(1,128)} %bitcast.s_ref, bf16[512,512]{1,0:T(8,128)(2,1)S(1)} %shard_map.66.im_ref.i0, bf16[512,512]{1,0:T(8,128)(2,1)S(1)} %shard_map.67.t0_ref, bf16[512,512]{1,0:T(8,128)(2,1)S(1)} %collective-permute-done.6.t1_ref), custom_call_target="tpu_custom_call" | custom-call | tf_op jit(solution)/shard_map/pallas_call | solution.py:56
  23.6 8.6 %collective-permute-done.9.im_ref.i3 = bf16[512,512]{1,0:T(8,128)(2,1)S(1)} collective-permute-done((bf16[512,512]{1,0:T(8,128)(2,1)S(1)}, bf16[512,512]{1,0:T(8,128)(2,1)S(1)}, u32[]{:S(2)}, u32[]{:S(2)}) %collective-permute-start.9) | collective-permute-done | bytes 524320 | tf_op jit(solution)/shard_map/ppermute | solution.py:33
  32.2 1.6 %shard_map.71 = (f32[16,128]{1,0:T(8,128)S(1)}, f32[8,1024]{1,0:T(8,128)S(1)}) custom-call(f32[1,1]{1,0:T(1,128)} %bitcast.s_ref, bf16[512,512]{1,0:T(8,128)(2,1)S(1)} %collective-permute-done.9.im_ref.i3, bf16[512,512]{1,0:T(8,128)(2,1)S(1)} %shard_map.67.t0_ref, bf16[512,512]{1,0:T(8,128)(2,1)S(1)} %collective-permute-done.6.t1_ref), custom_call_target="tpu_custom_call" | custom-call | tf_op jit(solution)/shard_map/pallas_call | solution.py:56
  33.8 0.6 copy-done.1
  34.5 1.6 %shard_map.70 = (f32[16,128]{1,0:T(8,128)S(1)}, f32[8,1024]{1,0:T(8,128)S(1)}) custom-call(f32[1,1]{1,0:T(1,128)} %bitcast.s_ref, bf16[512,512]{1,0:T(8,128)(2,1)S(1)} %collective-permute-done.8.im_ref.i2, bf16[512,512]{1,0:T(8,128)(2,1)S(1)} %shard_map.67.t0_ref, bf16[512,512]{1,0:T(8,128)(2,1)S(1)} %collective-permute-done.6.t1_ref), custom_call_target="tpu_custom_call" | custom-call | tf_op jit(solution)/shard_map/pallas_call | solution.py:56
  36.0 0.6 copy-done.3
  36.7 1.6 %shard_map.69 = (f32[16,128]{1,0:T(8,128)S(1)}, f32[8,1024]{1,0:T(8,128)S(1)}) custom-call(f32[1,1]{1,0:T(1,128)} %bitcast.s_ref, bf16[512,512]{1,0:T(8,128)(2,1)S(1)} %collective-permute-done.7.im_ref.i1, bf16[512,512]{1,0:T(8,128)(2,1)S(1)} %shard_map.67.t0_ref, bf16[512,512]{1,0:T(8,128)(2,1)S(1)} %collective-permute-done.6.t1_ref), custom_call_target="tpu_custom_call" | custom-call | tf_op jit(solution)/shard_map/pallas_call | solution.py:56
  38.3 0.6 copy-done.5
  38.9 0.1 shard_map.72
  38.9 0.7 copy-done
  39.6 6.5 %all-to-all-start = ((f32[16,40,128]{2,1,0:T(8,128)}), f32[16,40,128]{2,1,0:T(8,128)S(1)}, u32[]{:S(2)}, u32[]{:S(2)}) async-start(f32[16,40,128]{2,1,0:T(8,128)} %bitcast.6), calls=%async_computation | async-start | bytes 655360 | tf_op jit(solution)/shard_map/all_to_all | solution.py:390
  46.2 0.7 copy-done.2
  46.9 0.8 copy-done.4
  47.7 0.8 copy-done.6
  48.5 2.0 %collective-permute-start.12 = (f32[24,128]{1,0:T(8,128)S(1)}, f32[24,128]{1,0:T(8,128)S(1)}, u32[]{:S(2)}, u32[]{:S(2)}) collective-permute-start(f32[24,128]{1,0:T(8,128)S(1)} %shard_map.73.b0), channel_id=1, source_target_pairs={{0,96},{32,0},{64,32},{96,64},{1,97},{33,1},{65,33},{97,65},{2,98}... | collective-permute-start | bytes 36872 | tf_op jit(solution)/shard_map/ppermute | solution.py:37
  50.5 0.7 collective-permute-start.11
  51.2 0.5 collective-permute-start.10
  51.7 0.6 collective-permute-done.12.b3
  52.2 3.4 %collective-permute-done.11.b2 = f32[24,128]{1,0:T(8,128)S(1)} collective-permute-done((f32[24,128]{1,0:T(8,128)S(1)}, f32[24,128]{1,0:T(8,128)S(1)}, u32[]{:S(2)}, u32[]{:S(2)}) %collective-permute-start.11) | collective-permute-done | bytes 12320 | tf_op jit(solution)/shard_map/ppermute | solution.py:37
  55.7 0.4 collective-permute-done.10.b1
  56.1 0.3 collective-permute-start.13
  56.4 1.2 %collective-permute-done.13.b1 = f32[24,128]{1,0:T(8,128)S(1)} collective-permute-done((f32[24,128]{1,0:T(8,128)S(1)}, f32[24,128]{1,0:T(8,128)S(1)}, u32[]{:S(2)}, u32[]{:S(2)}) %collective-permute-start.13) | collective-permute-done | bytes 12320 | tf_op jit(solution)/shard_map/ppermute | solution.py:41
  57.5 0.2 shard_map.75
  57.7 1.6 %shard_map.79 = (bf16[512,1024]{1,0:T(8,128)(2,1)S(1)}, f32[544,512]{1,0:T(8,128)S(1)}) custom-call(f32[1,1]{1,0:T(1,128)} %bitcast.s_ref, bf16[512,512]{1,0:T(8,128)(2,1)S(1)} %collective-permute-done.9.im_ref.i3, f32[16,128]{1,0:T(8,128)S(1)} %get-tuple-element.42.row_ref, f32[1,1024]{1,0:T(1,128)S(1)} %get-tuple-element.43.col_ref, ...), custom_call_target="tpu_custom_call" | custom-call | tf_op jit(solution)/shard_map/pallas_call | solution.py:56
  59.3 1.6 %shard_map.78 = (bf16[512,1024]{1,0:T(8,128)(2,1)S(1)}, f32[544,512]{1,0:T(8,128)S(1)}) custom-call(f32[1,1]{1,0:T(1,128)} %bitcast.s_ref, bf16[512,512]{1,0:T(8,128)(2,1)S(1)} %collective-permute-done.7.im_ref.i1, f32[16,128]{1,0:T(8,128)S(1)} %get-tuple-element.42.row_ref, f32[1,1024]{1,0:T(1,128)S(1)} %get-tuple-element.43.col_ref, ...), custom_call_target="tpu_custom_call" | custom-call | tf_op jit(solution)/shard_map/pallas_call | solution.py:56
  60.9 1.6 %shard_map.77 = (bf16[512,1024]{1,0:T(8,128)(2,1)S(1)}, f32[544,512]{1,0:T(8,128)S(1)}) custom-call(f32[1,1]{1,0:T(1,128)} %bitcast.s_ref, bf16[512,512]{1,0:T(8,128)(2,1)S(1)} %collective-permute-done.8.im_ref.i2, f32[16,128]{1,0:T(8,128)S(1)} %get-tuple-element.42.row_ref, f32[1,1024]{1,0:T(1,128)S(1)} %get-tuple-element.43.col_ref, ...), custom_call_target="tpu_custom_call" | custom-call | tf_op jit(solution)/shard_map/pallas_call | solution.py:56
  62.5 1.6 %shard_map.76 = (bf16[512,1024]{1,0:T(8,128)(2,1)S(1)}, f32[544,512]{1,0:T(8,128)S(1)}) custom-call(f32[1,1]{1,0:T(1,128)} %bitcast.s_ref, bf16[512,512]{1,0:T(8,128)(2,1)S(1)} %shard_map.66.im_ref.i0, f32[16,128]{1,0:T(8,128)S(1)} %get-tuple-element.42.row_ref, f32[1,1024]{1,0:T(1,128)S(1)} %get-tuple-element.43.col_ref, ...), custom_call_target="tpu_custom_call" | custom-call | tf_op jit(solution)/shard_map/pallas_call | solution.py:56
  64.0 1.3 %shard_map.81 = f32[544,512]{1,0:T(8,128)S(1)} custom-call(bf16[512,1024]{1,0:T(8,128)(2,1)S(1)} %get-tuple-element.50.w0, bf16[512,1024]{1,0:T(8,128)(2,1)S(1)} %get-tuple-element.51.w1, bf16[512,1024]{1,0:T(8,128)(2,1)S(1)} %get-tuple-element.52.w2, bf16[512,1024]{1,0:T(8,128)(2,1)S(1)} %get-tuple-element.53.w3, bf16[512,512]{1,0:T(8,128)(2,1)S(1)} %shard_map.66.im_ref.i0, ...), custom_call_target="tpu_custom_call" | custom-call | tf_op jit(solution)/shard_map/pallas_call | solution.py:56
  65.3 0.1 convert_element_type.117
  65.4 0.2 collective-permute-start.20
  65.7 0.1 convert_element_type.100
  65.8 2.0 %collective-permute-start.16 = (f16[544,512]{1,0:T(8,128)(2,1)S(1)}, f16[544,512]{1,0:T(8,128)(2,1)S(1)}, u32[]{:S(2)}, u32[]{:S(2)}) collective-permute-start(f16[544,512]{1,0:T(8,128)(2,1)S(1)} %convert_element_type.100), channel_id=1, source_target_pairs={{0,1},{1,2},{2,3},{3,0},{4,12},{5,13},{6,14},{7,15},{8,9},{9,10},{... | collective-permute-start | bytes 1671176 | tf_op jit(solution)/shard_map/ppermute | solution.py:33
  67.8 0.1 convert_element_type.98
  67.9 1.4 %collective-permute-start.15 = (f16[544,512]{1,0:T(8,128)(2,1)S(1)}, f16[544,512]{1,0:T(8,128)(2,1)S(1)}, u32[]{:S(2)}, u32[]{:S(2)}) collective-permute-start(f16[544,512]{1,0:T(8,128)(2,1)S(1)} %convert_element_type.98), channel_id=1, source_target_pairs={{0,3},{1,0},{2,1},{3,2},{4,28},{5,29},{6,30},{7,31},{8,11},{9,8},{... | collective-permute-start | bytes 1671176 | tf_op jit(solution)/shard_map/ppermute | solution.py:33
  69.3 0.1 convert_element_type.96
  69.4 2.3 %collective-permute-start.14 = (f16[544,512]{1,0:T(8,128)(2,1)S(1)}, f16[544,512]{1,0:T(8,128)(2,1)S(1)}, u32[]{:S(2)}, u32[]{:S(2)}) collective-permute-start(f16[544,512]{1,0:T(8,128)(2,1)S(1)} %convert_element_type.96), channel_id=1, source_target_pairs={{0,2},{1,3},{2,0},{3,1},{4,20},{5,21},{6,22},{7,23},{8,10},{9,11},... | collective-permute-start | bytes 1671176 | tf_op jit(solution)/shard_map/ppermute | solution.py:33
  71.7 1.3 %shard_map.80 = f32[544,512]{1,0:T(8,128)S(1)} custom-call(bf16[512,1024]{1,0:T(8,128)(2,1)S(1)} %get-tuple-element.50.w0, bf16[512,1024]{1,0:T(8,128)(2,1)S(1)} %get-tuple-element.51.w1, bf16[512,1024]{1,0:T(8,128)(2,1)S(1)} %get-tuple-element.52.w2, bf16[512,1024]{1,0:T(8,128)(2,1)S(1)} %get-tuple-element.53.w3, bf16[512,512]{1,0:T(8,128)(2,1)S(1)} %shard_map.66.im_ref.i0, ...), custom_call_target="tpu_custom_call" | custom-call | tf_op jit(solution)/shard_map/pallas_call | solution.py:56
  73.0 0.2 fusion.2
  73.2 1.7 %collective-permute-start.21 = (f16[136,512]{1,0:T(8,128)(2,1)S(1)}, f16[136,512]{1,0:T(8,128)(2,1)S(1)}, u32[]{:S(2)}, u32[]{:S(2)}) collective-permute-start(f16[136,512]{1,0:T(8,128)(2,1)S(1)} %get-tuple-element.63), channel_id=1, source_target_pairs={{0,64},{32,96},{64,0},{96,32},{1,65},{33,97},{65,1},{97,33},{2,66}... | collective-permute-start | bytes 417800 | tf_op jit(solution)/shard_map/ppermute | solution.py:37
  74.9 0.1 collective-permute-start.23
  74.9 1.7 %collective-permute-done.16 = f16[544,512]{1,0:T(8,128)(2,1)S(1)} collective-permute-done((f16[544,512]{1,0:T(8,128)(2,1)S(1)}, f16[544,512]{1,0:T(8,128)(2,1)S(1)}, u32[]{:S(2)}, u32[]{:S(2)}) %collective-permute-start.16) | collective-permute-done | bytes 557088 | tf_op jit(solution)/shard_map/ppermute | solution.py:33
  76.6 1.5 %collective-permute-start.22 = (f16[136,512]{1,0:T(8,128)(2,1)S(1)}, f16[136,512]{1,0:T(8,128)(2,1)S(1)}, u32[]{:S(2)}, u32[]{:S(2)}) collective-permute-start(f16[136,512]{1,0:T(8,128)(2,1)S(1)} %get-tuple-element.65), channel_id=1, source_target_pairs={{0,96},{32,0},{64,32},{96,64},{1,97},{33,1},{65,33},{97,65},{2,98}... | collective-permute-start | bytes 417800 | tf_op jit(solution)/shard_map/ppermute | solution.py:37
  78.1 5.8 %collective-permute-done.14 = f16[544,512]{1,0:T(8,128)(2,1)S(1)} collective-permute-done((f16[544,512]{1,0:T(8,128)(2,1)S(1)}, f16[544,512]{1,0:T(8,128)(2,1)S(1)}, u32[]{:S(2)}, u32[]{:S(2)}) %collective-permute-start.14) | collective-permute-done | bytes 557088 | tf_op jit(solution)/shard_map/ppermute | solution.py:33
  83.9 0.2 add_convert_fusion.2
  84.2 3.1 %collective-permute-start.17 = (f16[136,512]{1,0:T(8,128)(2,1)S(1)}, f16[136,512]{1,0:T(8,128)(2,1)S(1)}, u32[]{:S(2)}, u32[]{:S(2)}) collective-permute-start(f16[136,512]{1,0:T(8,128)(2,1)S(1)} %get-tuple-element.60), channel_id=1, source_target_pairs={{0,16},{1,17},{2,18},{3,19},{4,6},{5,7},{6,4},{7,5},{8,24},{9,25},... | collective-permute-start | bytes 417800 | tf_op jit(solution)/shard_map/ppermute | solution.py:33
  87.2 0.6 collective-permute-start.19
  87.8 2.7 %collective-permute-start.18 = (f16[136,512]{1,0:T(8,128)(2,1)S(1)}, f16[136,512]{1,0:T(8,128)(2,1)S(1)}, u32[]{:S(2)}, u32[]{:S(2)}) collective-permute-start(f16[136,512]{1,0:T(8,128)(2,1)S(1)} %get-tuple-element.62), channel_id=1, source_target_pairs={{0,24},{1,25},{2,26},{3,27},{4,7},{5,4},{6,5},{7,6},{8,0},{9,1},{1... | collective-permute-start | bytes 417800 | tf_op jit(solution)/shard_map/ppermute | solution.py:33
  90.5 0.1 slice_add_fusion.3.g_ref
  90.6 0.7 shard_map.82
  91.3 2.2 %collective-permute-done.19 = f16[136,512]{1,0:T(8,128)(2,1)S(1)} collective-permute-done((f16[136,512]{1,0:T(8,128)(2,1)S(1)}, f16[136,512]{1,0:T(8,128)(2,1)S(1)}, u32[]{:S(2)}, u32[]{:S(2)}) %collective-permute-start.19) | collective-permute-done | bytes 139296 | tf_op jit(solution)/shard_map/ppermute | solution.py:33
  93.5 0.2 add_add_fusion.g_ref
  93.7 0.9 shard_map.83
  (27 shorter events, 0.2 us)
Async XLA Ops:
  0.6 8.5 %collective-permute-start.3 = (bf16[128,512]{1,0:T(8,128)(2,1)}, bf16[128,512]{1,0:T(8,128)(2,1)S(1)}, u32[]{:S(2)}, u32[]{:S(2)}) collective-permute-start(bf16[128,512]{1,0:T(8,128)(2,1)} %b_ref.1), channel_id=1, source_target_pairs={{0,32},{32,64},{64,96},{96,0},{1,33},{33,65},{65,97},{97,1},{2,34}... | collective-permute-start | bytes 393224 | tf_op jit(solution)/shard_map/ppermute | solution.py:37
  2.3 9.8 %collective-permute-start.5 = (bf16[128,512]{1,0:T(8,128)(2,1)}, bf16[128,512]{1,0:T(8,128)(2,1)S(1)}, u32[]{:S(2)}, u32[]{:S(2)}) collective-permute-start(bf16[128,512]{1,0:T(8,128)(2,1)} %b_ref.1), channel_id=1, source_target_pairs={{0,96},{32,0},{64,32},{96,64},{1,97},{33,1},{65,33},{97,65},{2,98}... | collective-permute-start | bytes 393224 | tf_op jit(solution)/shard_map/ppermute | solution.py:37
  3.9 8.2 %collective-permute-start.4 = (bf16[128,512]{1,0:T(8,128)(2,1)}, bf16[128,512]{1,0:T(8,128)(2,1)S(1)}, u32[]{:S(2)}, u32[]{:S(2)}) collective-permute-start(bf16[128,512]{1,0:T(8,128)(2,1)} %b_ref.1), channel_id=1, source_target_pairs={{0,64},{32,96},{64,0},{96,32},{1,65},{33,97},{65,1},{97,33},{2,66}... | collective-permute-start | bytes 393224 | tf_op jit(solution)/shard_map/ppermute | solution.py:37
  5.9 6.4 %collective-permute-start = (bf16[128,512]{1,0:T(8,128)(2,1)}, bf16[128,512]{1,0:T(8,128)(2,1)S(1)}, u32[]{:S(2)}, u32[]{:S(2)}) collective-permute-start(bf16[128,512]{1,0:T(8,128)(2,1)} %a_ref.1), channel_id=1, source_target_pairs={{0,8},{1,9},{2,10},{3,11},{4,5},{5,6},{6,7},{7,4},{8,16},{9,17},{1... | collective-permute-start | bytes 393224 | tf_op jit(solution)/shard_map/ppermute | solution.py:33
  7.4 5.2 %collective-permute-start.2 = (bf16[128,512]{1,0:T(8,128)(2,1)}, bf16[128,512]{1,0:T(8,128)(2,1)S(1)}, u32[]{:S(2)}, u32[]{:S(2)}) collective-permute-start(bf16[128,512]{1,0:T(8,128)(2,1)} %a_ref.1), channel_id=1, source_target_pairs={{0,24},{1,25},{2,26},{3,27},{4,7},{5,4},{6,5},{7,6},{8,0},{9,1},{1... | collective-permute-start | bytes 393224 | tf_op jit(solution)/shard_map/ppermute | solution.py:33
  9.1 6.7 %collective-permute-start.1 = (bf16[128,512]{1,0:T(8,128)(2,1)}, bf16[128,512]{1,0:T(8,128)(2,1)S(1)}, u32[]{:S(2)}, u32[]{:S(2)}) collective-permute-start(bf16[128,512]{1,0:T(8,128)(2,1)} %a_ref.1), channel_id=1, source_target_pairs={{0,16},{1,17},{2,18},{3,19},{4,6},{5,7},{6,4},{7,5},{8,24},{9,25},... | collective-permute-start | bytes 393224 | tf_op jit(solution)/shard_map/ppermute | solution.py:33
  12.1 9.7 %collective-permute-start.6 = (bf16[512,512]{1,0:T(8,128)(2,1)S(1)}, bf16[512,512]{1,0:T(8,128)(2,1)S(1)}, u32[]{:S(2)}, u32[]{:S(2)}) collective-permute-start(bf16[512,512]{1,0:T(8,128)(2,1)S(1)} %shard_map.67.t0_ref), channel_id=1, source_target_pairs={{0,4},{4,0},{1,5},{5,1},{2,6},{6,2},{3,7},{7,3},{8,12},{12,8},{9,1... | collective-permute-start | bytes 1572872 | tf_op jit(solution)/shard_map/ppermute | solution.py:41
  15.8 16.4 %collective-permute-start.9 = (bf16[512,512]{1,0:T(8,128)(2,1)S(1)}, bf16[512,512]{1,0:T(8,128)(2,1)S(1)}, u32[]{:S(2)}, u32[]{:S(2)}) collective-permute-start(bf16[512,512]{1,0:T(8,128)(2,1)S(1)} %shard_map.66.im_ref.i0), channel_id=1, source_target_pairs={{0,3},{1,0},{2,1},{3,2},{4,28},{5,29},{6,30},{7,31},{8,11},{9,8},{... | collective-permute-start | bytes 1572872 | tf_op jit(solution)/shard_map/ppermute | solution.py:33
  19.9 14.5 %collective-permute-start.8 = (bf16[512,512]{1,0:T(8,128)(2,1)S(1)}, bf16[512,512]{1,0:T(8,128)(2,1)S(1)}, u32[]{:S(2)}, u32[]{:S(2)}) collective-permute-start(bf16[512,512]{1,0:T(8,128)(2,1)S(1)} %shard_map.66.im_ref.i0), channel_id=1, source_target_pairs={{0,2},{1,3},{2,0},{3,1},{4,20},{5,21},{6,22},{7,23},{8,10},{9,11},... | collective-permute-start | bytes 1572872 | tf_op jit(solution)/shard_map/ppermute | solution.py:33
  19.9 16.7 %collective-permute-start.7 = (bf16[512,512]{1,0:T(8,128)(2,1)S(1)}, bf16[512,512]{1,0:T(8,128)(2,1)S(1)}, u32[]{:S(2)}, u32[]{:S(2)}) collective-permute-start(bf16[512,512]{1,0:T(8,128)(2,1)S(1)} %shard_map.66.im_ref.i0), channel_id=1, source_target_pairs={{0,1},{1,2},{2,3},{3,0},{4,12},{5,13},{6,14},{7,15},{8,9},{9,10},{... | collective-permute-start | bytes 1572872 | tf_op jit(solution)/shard_map/ppermute | solution.py:33
  33.8 0.6 copy-start.1
  36.0 0.6 copy-start.3
  38.2 0.6 copy-start.5
  38.9 0.7 copy-start
  39.6 17.9 %all-to-all-start = ((f32[16,40,128]{2,1,0:T(8,128)}), f32[16,40,128]{2,1,0:T(8,128)S(1)}, u32[]{:S(2)}, u32[]{:S(2)}) async-start(f32[16,40,128]{2,1,0:T(8,128)} %bitcast.6), calls=%async_computation | async-start | bytes 655360 | tf_op jit(solution)/shard_map/all_to_all | solution.py:390
  46.1 0.8 copy-start.2
  46.9 0.8 copy-start.4
  47.7 0.8 copy-start.6
  48.5 3.8 %collective-permute-start.12 = (f32[24,128]{1,0:T(8,128)S(1)}, f32[24,128]{1,0:T(8,128)S(1)}, u32[]{:S(2)}, u32[]{:S(2)}) collective-permute-start(f32[24,128]{1,0:T(8,128)S(1)} %shard_map.73.b0), channel_id=1, source_target_pairs={{0,96},{32,0},{64,32},{96,64},{1,97},{33,1},{65,33},{97,65},{2,98}... | collective-permute-start | bytes 36872 | tf_op jit(solution)/shard_map/ppermute | solution.py:37
  50.5 5.2 %collective-permute-start.11 = (f32[24,128]{1,0:T(8,128)S(1)}, f32[24,128]{1,0:T(8,128)S(1)}, u32[]{:S(2)}, u32[]{:S(2)}) collective-permute-start(f32[24,128]{1,0:T(8,128)S(1)} %shard_map.73.b0), channel_id=1, source_target_pairs={{0,64},{32,96},{64,0},{96,32},{1,65},{33,97},{65,1},{97,33},{2,66}... | collective-permute-start | bytes 36872 | tf_op jit(solution)/shard_map/ppermute | solution.py:37
  51.2 4.9 %collective-permute-start.10 = (f32[24,128]{1,0:T(8,128)S(1)}, f32[24,128]{1,0:T(8,128)S(1)}, u32[]{:S(2)}, u32[]{:S(2)}) collective-permute-start(f32[24,128]{1,0:T(8,128)S(1)} %shard_map.73.b0), channel_id=1, source_target_pairs={{0,32},{32,64},{64,96},{96,0},{1,33},{33,65},{65,97},{97,1},{2,34}... | collective-permute-start | bytes 36872 | tf_op jit(solution)/shard_map/ppermute | solution.py:37
  56.1 1.4 %collective-permute-start.13 = (f32[24,128]{1,0:T(8,128)S(1)}, f32[24,128]{1,0:T(8,128)S(1)}, u32[]{:S(2)}, u32[]{:S(2)}) collective-permute-start(f32[24,128]{1,0:T(8,128)S(1)} %shard_map.74.b0), channel_id=1, source_target_pairs={{0,4},{4,0},{1,5},{5,1},{2,6},{6,2},{3,7},{7,3},{8,12},{12,8},{9,1... | collective-permute-start | bytes 36872 | tf_op jit(solution)/shard_map/ppermute | solution.py:41
  65.4 7.6 %collective-permute-start.20 = (f16[544,512]{1,0:T(8,128)(2,1)S(1)}, f16[544,512]{1,0:T(8,128)(2,1)S(1)}, u32[]{:S(2)}, u32[]{:S(2)}) collective-permute-start(f16[544,512]{1,0:T(8,128)(2,1)S(1)} %convert_element_type.117), channel_id=1, source_target_pairs={{0,4},{4,0},{1,5},{5,1},{2,6},{6,2},{3,7},{7,3},{8,12},{12,8},{9,1... | collective-permute-start | bytes 1671176 | tf_op jit(solution)/shard_map/ppermute | solution.py:41
  65.8 10.8 %collective-permute-start.16 = (f16[544,512]{1,0:T(8,128)(2,1)S(1)}, f16[544,512]{1,0:T(8,128)(2,1)S(1)}, u32[]{:S(2)}, u32[]{:S(2)}) collective-permute-start(f16[544,512]{1,0:T(8,128)(2,1)S(1)} %convert_element_type.100), channel_id=1, source_target_pairs={{0,1},{1,2},{2,3},{3,0},{4,12},{5,13},{6,14},{7,15},{8,9},{9,10},{... | collective-permute-start | bytes 1671176 | tf_op jit(solution)/shard_map/ppermute | solution.py:33
  67.9 10.2 %collective-permute-start.15 = (f16[544,512]{1,0:T(8,128)(2,1)S(1)}, f16[544,512]{1,0:T(8,128)(2,1)S(1)}, u32[]{:S(2)}, u32[]{:S(2)}) collective-permute-start(f16[544,512]{1,0:T(8,128)(2,1)S(1)} %convert_element_type.98), channel_id=1, source_target_pairs={{0,3},{1,0},{2,1},{3,2},{4,28},{5,29},{6,30},{7,31},{8,11},{9,8},{... | collective-permute-start | bytes 1671176 | tf_op jit(solution)/shard_map/ppermute | solution.py:33
  69.4 14.6 %collective-permute-start.14 = (f16[544,512]{1,0:T(8,128)(2,1)S(1)}, f16[544,512]{1,0:T(8,128)(2,1)S(1)}, u32[]{:S(2)}, u32[]{:S(2)}) collective-permute-start(f16[544,512]{1,0:T(8,128)(2,1)S(1)} %convert_element_type.96), channel_id=1, source_target_pairs={{0,2},{1,3},{2,0},{3,1},{4,20},{5,21},{6,22},{7,23},{8,10},{9,11},... | collective-permute-start | bytes 1671176 | tf_op jit(solution)/shard_map/ppermute | solution.py:33
  73.2 14.6 %collective-permute-start.21 = (f16[136,512]{1,0:T(8,128)(2,1)S(1)}, f16[136,512]{1,0:T(8,128)(2,1)S(1)}, u32[]{:S(2)}, u32[]{:S(2)}) collective-permute-start(f16[136,512]{1,0:T(8,128)(2,1)S(1)} %get-tuple-element.63), channel_id=1, source_target_pairs={{0,64},{32,96},{64,0},{96,32},{1,65},{33,97},{65,1},{97,33},{2,66}... | collective-permute-start | bytes 417800 | tf_op jit(solution)/shard_map/ppermute | solution.py:37
  74.9 15.6 %collective-permute-start.23 = (f16[136,512]{1,0:T(8,128)(2,1)S(1)}, f16[136,512]{1,0:T(8,128)(2,1)S(1)}, u32[]{:S(2)}, u32[]{:S(2)}) collective-permute-start(f16[136,512]{1,0:T(8,128)(2,1)S(1)} %get-tuple-element.64), channel_id=1, source_target_pairs={{0,32},{32,64},{64,96},{96,0},{1,33},{33,65},{65,97},{97,1},{2,34}... | collective-permute-start | bytes 417800 | tf_op jit(solution)/shard_map/ppermute | solution.py:37
  76.6 13.9 %collective-permute-start.22 = (f16[136,512]{1,0:T(8,128)(2,1)S(1)}, f16[136,512]{1,0:T(8,128)(2,1)S(1)}, u32[]{:S(2)}, u32[]{:S(2)}) collective-permute-start(f16[136,512]{1,0:T(8,128)(2,1)S(1)} %get-tuple-element.65), channel_id=1, source_target_pairs={{0,96},{32,0},{64,32},{96,64},{1,97},{33,1},{65,33},{97,65},{2,98}... | collective-permute-start | bytes 417800 | tf_op jit(solution)/shard_map/ppermute | solution.py:37
  84.2 7.1 %collective-permute-start.17 = (f16[136,512]{1,0:T(8,128)(2,1)S(1)}, f16[136,512]{1,0:T(8,128)(2,1)S(1)}, u32[]{:S(2)}, u32[]{:S(2)}) collective-permute-start(f16[136,512]{1,0:T(8,128)(2,1)S(1)} %get-tuple-element.60), channel_id=1, source_target_pairs={{0,16},{1,17},{2,18},{3,19},{4,6},{5,7},{6,4},{7,5},{8,24},{9,25},... | collective-permute-start | bytes 417800 | tf_op jit(solution)/shard_map/ppermute | solution.py:33
  87.2 6.3 %collective-permute-start.19 = (f16[136,512]{1,0:T(8,128)(2,1)S(1)}, f16[136,512]{1,0:T(8,128)(2,1)S(1)}, u32[]{:S(2)}, u32[]{:S(2)}) collective-permute-start(f16[136,512]{1,0:T(8,128)(2,1)S(1)} %get-tuple-element.61), channel_id=1, source_target_pairs={{0,8},{1,9},{2,10},{3,11},{4,5},{5,6},{6,7},{7,4},{8,16},{9,17},{1... | collective-permute-start | bytes 417800 | tf_op jit(solution)/shard_map/ppermute | solution.py:33
  87.8 5.7 %collective-permute-start.18 = (f16[136,512]{1,0:T(8,128)(2,1)S(1)}, f16[136,512]{1,0:T(8,128)(2,1)S(1)}, u32[]{:S(2)}, u32[]{:S(2)}) collective-permute-start(f16[136,512]{1,0:T(8,128)(2,1)S(1)} %get-tuple-element.62), channel_id=1, source_target_pairs={{0,24},{1,25},{2,26},{3,27},{4,7},{5,4},{6,5},{7,6},{8,0},{9,1},{1... | collective-permute-start | bytes 417800 | tf_op jit(solution)/shard_map/ppermute | solution.py:33

commit v5 on v2

--- a/solution.py
+++ b/solution.py
@@ -103,9 +103,14 @@
         )
 
 
-def logits_kernel(first, s_ref, im_ref, t0_ref, t1_ref, rows_ref, cols_ref, l_ref, top_scr, sum_scr, mean_scr):
-    s2 = s_ref[0, 0]
-    logits_into(l_ref, s2, im_ref, (t0_ref, t1_ref))
+def logits_kernel(k, *refs):
+    first, keep = k == 0, k != 2
+    s_ref, im_ref, t0_ref, t1_ref, rows_ref, cols_ref = refs[:6]
+    l_ref, top_scr, sum_scr, mean_scr = refs[7:11] if keep else refs[6:10]
+    logits_into(l_ref, s_ref[0, 0], im_ref, (t0_ref, t1_ref))
+    if keep:
+        copy = pltpu.make_async_copy(l_ref, refs[6], refs[11])
+        copy.start()
 
     def tops(i, col_tops):
         here = pl.ds(pl.multiple_of(i * 64, 64), 64)
@@ -160,6 +165,8 @@
         rows_ref[9:10, :] = jnp.maximum(peak(t0_ref), peak(t1_ref))
         block = l_ref[0:128, 0:128]
         rows_ref[10:11, :] = jnp.sum(jnp.where(eye(), block, 0.0), axis=0, keepdims=True)
+    if keep:
+        copy.wait()
 
 
 def eye():
@@ -168,13 +175,20 @@
 
 
 def logits_of(k, s2, im, t0, t1):
-    return call(
-        functools.partial(logits_kernel, k == 0),
-        (out((16, 128)), out((8, 1024))),
-        s2, im, t0, t1,
-        smem=(0,),
-        scratch=[pltpu.VMEM((512, 1024), F32)] + [pltpu.VMEM((512, 128), F32)] * 3,
-    )
+    keep = k != 2
+    vmem = pl.BlockSpec(memory_space=pltpu.VMEM)
+    got = pl.pallas_call(
+        functools.partial(logits_kernel, k),
+        out_shape=(out((16, 128)), out((8, 1024))) + ((pltpu.HBM((512, 1024), F32),) if keep else ()),
+        in_specs=[pl.BlockSpec(memory_space=pltpu.SMEM)] + [vmem] * 3,
+        out_specs=(vmem, vmem) + ((pl.BlockSpec(memory_space=pltpu.HBM),) if keep else ()),
+        scratch_shapes=[pltpu.VMEM((512, 1024), F32)]
+        + [pltpu.VMEM((512, 128), F32)] * 3
+        + ([pltpu.SemaphoreType.DMA] if keep else []),
+        compiler_params=pltpu.CompilerParams(vmem_limit_bytes=16 << 20),
+        name="logits",
+    )(s2, im, t0, t1)
+    return got if keep else (*got, im)
 
 
 def merge(parts):
@@ -305,8 +319,10 @@
         back_ref[k : k + 1, :] = jnp.concatenate([back] * 4, axis=1)
 
 
-def image_kernel(which, s_ref, im_ref, row_ref, col_ref, unit_ref, codes_ref, t0_ref, t1_ref, w_ref, g_ref, l_ref):
-    logits_into(l_ref, s_ref[0, 0], im_ref, (t0_ref, t1_ref))
+def image_kernel(which, s_ref, l_ref, row_ref, col_ref, unit_ref, codes_ref, t0_ref, t1_ref, w_ref, g_ref, *scr):
+    if scr:
+        logits_into(scr[0], s_ref[0, 0], l_ref, (t0_ref, t1_ref))
+        l_ref = scr[0]
     for j in range(4):
         at = slice(128 * j, 128 * (j + 1))
         row = row_ref[4 * which + j : 4 * which + j + 1, :]
@@ -387,9 +403,10 @@
         ws[k], gs[k] = call(
             functools.partial(image_kernel, k),
             (out((512, 1024), BF16), out((544, 512))),
-            s2, chunks[k], row_lse, col_lse, unit, codes, t0, t1,
+            s2, chunks[k] if k == 2 else pltpu.with_memory_space_constraint(parts[k][2], pltpu.VMEM),
+            row_lse, col_lse, unit, codes, t0, t1,
             smem=(0,),
-            scratch=[pltpu.VMEM((512, 1024), F32)],
+            scratch=[pltpu.VMEM((512, 1024), F32)] if k == 2 else (),
         )
         if k:
             sent[k] = turn(gs[k].astype(F16), 4 - k, False)

time: 95.1 us -> 97.4 us (1.024)
  local copies, waits for them, and re-layouts: 6.63 us -> 9.04 us
  waiting for transfers between devices: 26.7 us -> 24.9 us
    pallas_call x0 -> x4, Pallas kernels: none -> 8.57 us  [logits_of(): pl.pallas_call(functools.partial(logits_kernel, k), out_shape=(out((16, 1...]
    pallas_call x20 -> x16, Pallas kernels: 17.3 us -> 9.64 us  [call(): pl.pallas_call(kernel, out_shape=outs, in_specs=[pl.BlockSpec(memory_spac...]
    unnamed x18 -> x24, local copies, waits for them, and re-layouts: 6.63 us -> 9.04 us
    ppermute x12, waiting for transfers between devices: 21.1 us -> 19.3 us  [turn(): return lax.ppermute(value, ('y', 'c', 'z'), pairs)]
    ppermute x12, starting transfers between devices: 22.6 us -> 24.3 us  [turn(): return lax.ppermute(value, ('y', 'c', 'z'), pairs)]
  transfers between devices with their start and end apart: 25 -> 25, of which waited for: 9 -> 10; matrix products, arithmetic and copies ran while one was open for 1% -> 1% of each run, Pallas kernels for 7% -> 9%
where the time goes in v5:
time: 97.4 us; the launch traced here: 96.7 us
  starting transfers between devices  41.8 us (43%)
  waiting for transfers between devices  24.9 us (26%)
  Pallas kernels  18.2 us (19%)
  local copies, waits for them, and re-layouts  9.04 us (9%)
  between operations  1.62 us (2%)
  other arithmetic  1.12 us (1%)
    ppermute x12, starting transfers between devices, turn(): return lax.ppermute(value, ('y', 'c', 'z'), pairs)  24.3 us
    ppermute x12, waiting for transfers between devices, turn(): return lax.ppermute(value, ('y', 'c', 'z'), pairs)  19.3 us
    ppermute x9, starting transfers between devices, along_x(): return lax.ppermute(value, 'x', [(i, (i + shift) % 4) for i in range(4)])  11 us
    pallas_call x16, Pallas kernels, call(): pl.pallas_call(kernel, out_shape=outs, in_specs=[pl.BlockSpec(memory_spac...  9.64 us
    unnamed x24, local copies, waits for them, and re-layouts  9.04 us
    pallas_call x4, Pallas kernels, logits_of(): pl.pallas_call(functools.partial(logits_kernel, k), out_shape=(out((16, 1...  8.57 us
    all_to_all x1, starting transfers between devices, program(): lax.all_to_all(rows.reshape(16, 40, 128), ('y', 'z'), 0, 0, tiled=True)  5.88 us
    ppermute x9, waiting for transfers between devices, along_x(): return lax.ppermute(value, 'x', [(i, (i + shift) % 4) for i in range(4)])  4.44 us
  transfers between devices with their start and end apart: 25, of which 10 were waited for; matrix products, arithmetic and copies ran while one was open for 1% of the time, Pallas kernels for 9%

profile of v5, /device:TPU:0, one launch (start us, length us, event | category | flops | bytes accessed | tf_op | source)
XLA Modules:
  0.0 96.7 jit_solution(10052491406215548434)
XLA Ops:
  0.6 1.7 %collective-permute-start.3 = (bf16[128,512]{1,0:T(8,128)(2,1)}, bf16[128,512]{1,0:T(8,128)(2,1)S(1)}, u32[]{:S(2)}, u32[]{:S(2)}) collective-permute-start(bf16[128,512]{1,0:T(8,128)(2,1)} %a_ref.3), channel_id=1, source_target_pairs={{0,32},{32,64},{64,96},{96,0},{1,33},{33,65},{65,97},{97,1},{2,34}... | collective-permute-start | bytes 393224 | tf_op jit(solution)/shard_map/ppermute | solution.py:37
  2.3 1.6 %collective-permute-start.5 = (bf16[128,512]{1,0:T(8,128)(2,1)}, bf16[128,512]{1,0:T(8,128)(2,1)S(1)}, u32[]{:S(2)}, u32[]{:S(2)}) collective-permute-start(bf16[128,512]{1,0:T(8,128)(2,1)} %a_ref.3), channel_id=1, source_target_pairs={{0,96},{32,0},{64,32},{96,64},{1,97},{33,1},{65,33},{97,65},{2,98}... | collective-permute-start | bytes 393224 | tf_op jit(solution)/shard_map/ppermute | solution.py:37
  3.9 1.9 %collective-permute-start.4 = (bf16[128,512]{1,0:T(8,128)(2,1)}, bf16[128,512]{1,0:T(8,128)(2,1)S(1)}, u32[]{:S(2)}, u32[]{:S(2)}) collective-permute-start(bf16[128,512]{1,0:T(8,128)(2,1)} %a_ref.3), channel_id=1, source_target_pairs={{0,64},{32,96},{64,0},{96,32},{1,65},{33,97},{65,1},{97,33},{2,66}... | collective-permute-start | bytes 393224 | tf_op jit(solution)/shard_map/ppermute | solution.py:37
  5.9 1.6 %collective-permute-start = (bf16[128,512]{1,0:T(8,128)(2,1)}, bf16[128,512]{1,0:T(8,128)(2,1)S(1)}, u32[]{:S(2)}, u32[]{:S(2)}) collective-permute-start(bf16[128,512]{1,0:T(8,128)(2,1)} %a_ref.2), channel_id=1, source_target_pairs={{0,8},{1,9},{2,10},{3,11},{4,5},{5,6},{6,7},{7,4},{8,16},{9,17},{1... | collective-permute-start | bytes 393224 | tf_op jit(solution)/shard_map/ppermute | solution.py:33
  7.4 1.7 %collective-permute-start.2 = (bf16[128,512]{1,0:T(8,128)(2,1)}, bf16[128,512]{1,0:T(8,128)(2,1)S(1)}, u32[]{:S(2)}, u32[]{:S(2)}) collective-permute-start(bf16[128,512]{1,0:T(8,128)(2,1)} %a_ref.2), channel_id=1, source_target_pairs={{0,24},{1,25},{2,26},{3,27},{4,7},{5,4},{6,5},{7,6},{8,0},{9,1},{1... | collective-permute-start | bytes 393224 | tf_op jit(solution)/shard_map/ppermute | solution.py:33
  9.1 2.0 %collective-permute-start.1 = (bf16[128,512]{1,0:T(8,128)(2,1)}, bf16[128,512]{1,0:T(8,128)(2,1)S(1)}, u32[]{:S(2)}, u32[]{:S(2)}) collective-permute-start(bf16[128,512]{1,0:T(8,128)(2,1)} %a_ref.2), channel_id=1, source_target_pairs={{0,16},{1,17},{2,18},{3,19},{4,6},{5,7},{6,4},{7,5},{8,24},{9,25},... | collective-permute-start | bytes 393224 | tf_op jit(solution)/shard_map/ppermute | solution.py:33
  11.1 0.9 copy-done.5
  12.0 0.9 copy-done.4
  13.1 2.6 %collective-permute-done.1.a2 = bf16[128,512]{1,0:T(8,128)(2,1)S(1)} collective-permute-done((bf16[128,512]{1,0:T(8,128)(2,1)}, bf16[128,512]{1,0:T(8,128)(2,1)S(1)}, u32[]{:S(2)}, u32[]{:S(2)}) %collective-permute-start.1) | collective-permute-done | bytes 131104 | tf_op jit(solution)/shard_map/ppermute | solution.py:33
  15.8 4.0 %collective-permute-start.8 = (bf16[512,512]{1,0:T(8,128)(2,1)S(1)}, bf16[512,512]{1,0:T(8,128)(2,1)S(1)}, u32[]{:S(2)}, u32[]{:S(2)}) collective-permute-start(bf16[512,512]{1,0:T(8,128)(2,1)S(1)} %shard_map.67.refs_1_.i0), channel_id=1, source_target_pairs={{0,2},{1,3},{2,0},{3,1},{4,20},{5,21},{6,22},{7,23},{8,10},{9,11},... | collective-permute-start | bytes 1572872 | tf_op jit(solution)/shard_map/ppermute | solution.py:33
  19.8 1.0 %collective-permute-start.7 = (bf16[512,512]{1,0:T(8,128)(2,1)S(1)}, bf16[512,512]{1,0:T(8,128)(2,1)S(1)}, u32[]{:S(2)}, u32[]{:S(2)}) collective-permute-start(bf16[512,512]{1,0:T(8,128)(2,1)S(1)} %shard_map.67.refs_1_.i0), channel_id=1, source_target_pairs={{0,1},{1,2},{2,3},{3,0},{4,12},{5,13},{6,14},{7,15},{8,9},{9,10},{... | collective-permute-start | bytes 1572872 | tf_op jit(solution)/shard_map/ppermute | solution.py:33
  20.8 2.2 %collective-permute-start.9 = (bf16[512,512]{1,0:T(8,128)(2,1)S(1)}, bf16[512,512]{1,0:T(8,128)(2,1)S(1)}, u32[]{:S(2)}, u32[]{:S(2)}) collective-permute-start(bf16[512,512]{1,0:T(8,128)(2,1)S(1)} %shard_map.67.refs_1_.i0), channel_id=1, source_target_pairs={{0,3},{1,0},{2,1},{3,2},{4,28},{5,29},{6,30},{7,31},{8,11},{9,8},{... | collective-permute-start | bytes 1572872 | tf_op jit(solution)/shard_map/ppermute | solution.py:33
  23.7 2.4 %logits.4 = (f32[16,128]{1,0:T(8,128)S(1)}, f32[8,1024]{1,0:T(8,128)S(1)}, f32[512,1024]{1,0:T(8,128)}) custom-call(f32[1,1]{1,0:T(1,128)} %bitcast.refs_0_.s_ref, bf16[512,512]{1,0:T(8,128)(2,1)S(1)} %shard_map.67.refs_1_.i0, bf16[512,512]{1,0:T(8,128)(2,1)S(1)} %shard_map.69.refs_2_.t0_ref, bf16[512,512]{1,0:T(8,128)(2,1)S(1)} %collective-permute-done.6.refs_3_.t1_ref), custom_call_target="tpu_custom_call" | custom-call | tf_op jit(solution)/shard_map/logits/pallas_call | solution.py:180
  26.1 0.9 collective-permute-done.8.refs_1_.l_ref.i2
  27.0 1.6 %logits.6 = (f32[16,128]{1,0:T(8,128)S(1)}, f32[8,1024]{1,0:T(8,128)S(1)}) custom-call(f32[1,1]{1,0:T(1,128)} %bitcast.refs_0_.s_ref, bf16[512,512]{1,0:T(8,128)(2,1)S(1)} %collective-permute-done.8.refs_1_.l_ref.i2, bf16[512,512]{1,0:T(8,128)(2,1)S(1)} %shard_map.69.refs_2_.t0_ref, bf16[512,512]{1,0:T(8,128)(2,1)S(1)} %collective-permute-done.6.refs_3_.t1_ref), custom_call_target="tpu_custom_call" | custom-call | tf_op jit(solution)/shard_map/logits/pallas_call | solution.py:180
  28.6 0.6 copy-done.6
  29.2 3.3 %collective-permute-done.7.refs_1_.i1 = bf16[512,512]{1,0:T(8,128)(2,1)S(1)} collective-permute-done((bf16[512,512]{1,0:T(8,128)(2,1)S(1)}, bf16[512,512]{1,0:T(8,128)(2,1)S(1)}, u32[]{:S(2)}, u32[]{:S(2)}) %collective-permute-start.7) | collective-permute-done | bytes 524320 | tf_op jit(solution)/shard_map/ppermute | solution.py:33
  32.6 2.3 %logits.5 = (f32[16,128]{1,0:T(8,128)S(1)}, f32[8,1024]{1,0:T(8,128)S(1)}, f32[512,1024]{1,0:T(8,128)}) custom-call(f32[1,1]{1,0:T(1,128)} %bitcast.refs_0_.s_ref, bf16[512,512]{1,0:T(8,128)(2,1)S(1)} %collective-permute-done.7.refs_1_.i1, bf16[512,512]{1,0:T(8,128)(2,1)S(1)} %shard_map.69.refs_2_.t0_ref, ...), custom_call_target="tpu_custom_call" | custom-call | tf_op jit(solution)/shard_map/logits/pallas_call | solution.py:180
  34.9 0.6 copy-done.8
  35.5 2.3 %logits.7 = (f32[16,128]{1,0:T(8,128)S(1)}, f32[8,1024]{1,0:T(8,128)S(1)}, f32[512,1024]{1,0:T(8,128)}) custom-call(f32[1,1]{1,0:T(1,128)} %bitcast.refs_0_.s_ref, bf16[512,512]{1,0:T(8,128)(2,1)S(1)} %collective-permute-done.9.refs_1_.i3, bf16[512,512]{1,0:T(8,128)(2,1)S(1)} %shard_map.69.refs_2_.t0_ref, ...), custom_call_target="tpu_custom_call" | custom-call | tf_op jit(solution)/shard_map/logits/pallas_call | solution.py:180
  37.8 0.6 copy-done.10
  38.5 0.7 copy-done.3
  39.2 5.9 %all-to-all-start = ((f32[16,40,128]{2,1,0:T(8,128)}), f32[16,40,128]{2,1,0:T(8,128)S(1)}, u32[]{:S(2)}, u32[]{:S(2)}) async-start(f32[16,40,128]{2,1,0:T(8,128)} %bitcast.6), calls=%async_computation | async-start | bytes 655360 | tf_op jit(solution)/shard_map/all_to_all | solution.py:391
  45.1 0.7 copy-done.7
  45.8 0.8 copy-done.9
  46.6 0.8 copy-done.11
  47.4 2.0 %collective-permute-start.12 = (f32[24,128]{1,0:T(8,128)S(1)}, f32[24,128]{1,0:T(8,128)S(1)}, u32[]{:S(2)}, u32[]{:S(2)}) collective-permute-start(f32[24,128]{1,0:T(8,128)S(1)} %shard_map.71.b0), channel_id=1, source_target_pairs={{0,96},{32,0},{64,32},{96,64},{1,97},{33,1},{65,33},{97,65},{2,98}... | collective-permute-start | bytes 36872 | tf_op jit(solution)/shard_map/ppermute | solution.py:37
  49.4 0.7 collective-permute-start.11
  50.1 0.5 collective-permute-start.10
  50.6 0.6 collective-permute-done.12.b3
  51.1 3.5 %collective-permute-done.11.b2 = f32[24,128]{1,0:T(8,128)S(1)} collective-permute-done((f32[24,128]{1,0:T(8,128)S(1)}, f32[24,128]{1,0:T(8,128)S(1)}, u32[]{:S(2)}, u32[]{:S(2)}) %collective-permute-start.11) | collective-permute-done | bytes 12320 | tf_op jit(solution)/shard_map/ppermute | solution.py:37
  54.6 0.4 collective-permute-done.10.b1
  55.0 0.3 collective-permute-start.13
  55.3 1.2 %collective-permute-done.13.b1 = f32[24,128]{1,0:T(8,128)S(1)} collective-permute-done((f32[24,128]{1,0:T(8,128)S(1)}, f32[24,128]{1,0:T(8,128)S(1)}, u32[]{:S(2)}, u32[]{:S(2)}) %collective-permute-start.13) | collective-permute-done | bytes 12320 | tf_op jit(solution)/shard_map/ppermute | solution.py:41
  56.5 0.2 shard_map.73
  56.7 1.6 %shard_map.75 = (bf16[512,1024]{1,0:T(8,128)(2,1)S(1)}, f32[544,512]{1,0:T(8,128)S(1)}) custom-call(f32[1,1]{1,0:T(1,128)} %bitcast.refs_0_.s_ref, bf16[512,512]{1,0:T(8,128)(2,1)S(1)} %collective-permute-done.8.refs_1_.l_ref.i2, f32[16,128]{1,0:T(8,128)S(1)} %get-tuple-element.42.row_ref, f32[1,1024]{1,0:T(1,128)S(1)} %get-tuple-element.43.col_ref, ...), custom_call_target="tpu_custom_call" | custom-call | tf_op jit(solution)/shard_map/pallas_call | solution.py:56
  58.3 1.6 %copy-done.2 = f32[512,1024]{1,0:T(8,128)S(1)} copy-done((f32[512,1024]{1,0:T(8,128)S(1)}, f32[512,1024]{1,0:T(8,128)}, u32[]{:S(2)}) %copy-start.2) | copy-done | bytes 2097176
  59.9 1.2 %shard_map.77 = (bf16[512,1024]{1,0:T(8,128)(2,1)S(1)}, f32[544,512]{1,0:T(8,128)S(1)}) custom-call(f32[1,1]{1,0:T(1,128)} %bitcast.refs_0_.s_ref, f32[512,1024]{1,0:T(8,128)S(1)} %copy-done.2, f32[16,128]{1,0:T(8,128)S(1)} %get-tuple-element.42.row_ref, f32[1,1024]{1,0:T(1,128)S(1)} %get-tuple-element.43.col_ref, f32[2,128]{1,0:T(2,128)S(1)} %get-tuple-element.44.unit_ref, ...), custom_call_target="tpu_custom_call" | custom-call | tf_op jit(solution)/shard_map/pallas_call | solution.py:56
  61.0 0.4 copy-done.1
  61.4 1.2 %shard_map.76 = (bf16[512,1024]{1,0:T(8,128)(2,1)S(1)}, f32[544,512]{1,0:T(8,128)S(1)}) custom-call(f32[1,1]{1,0:T(1,128)} %bitcast.refs_0_.s_ref, f32[512,1024]{1,0:T(8,128)S(1)} %copy-done.1, f32[16,128]{1,0:T(8,128)S(1)} %get-tuple-element.42.row_ref, f32[1,1024]{1,0:T(1,128)S(1)} %get-tuple-element.43.col_ref, f32[2,128]{1,0:T(2,128)S(1)} %get-tuple-element.44.unit_ref, ...), custom_call_target="tpu_custom_call" | custom-call | tf_op jit(solution)/shard_map/pallas_call | solution.py:56
  62.6 0.4 copy-done
  63.0 1.2 %shard_map.74 = (bf16[512,1024]{1,0:T(8,128)(2,1)S(1)}, f32[544,512]{1,0:T(8,128)S(1)}) custom-call(f32[1,1]{1,0:T(1,128)} %bitcast.refs_0_.s_ref, f32[512,1024]{1,0:T(8,128)S(1)} %copy-done, f32[16,128]{1,0:T(8,128)S(1)} %get-tuple-element.42.row_ref, f32[1,1024]{1,0:T(1,128)S(1)} %get-tuple-element.43.col_ref, f32[2,128]{1,0:T(2,128)S(1)} %get-tuple-element.44.unit_ref, ...), custom_call_target="tpu_custom_call" | custom-call | tf_op jit(solution)/shard_map/pallas_call | solution.py:56
  64.2 1.3 %shard_map.79 = f32[544,512]{1,0:T(8,128)S(1)} custom-call(bf16[512,1024]{1,0:T(8,128)(2,1)S(1)} %get-tuple-element.52.w0, bf16[512,1024]{1,0:T(8,128)(2,1)S(1)} %get-tuple-element.53.w1, bf16[512,1024]{1,0:T(8,128)(2,1)S(1)} %get-tuple-element.54.w2, bf16[512,1024]{1,0:T(8,128)(2,1)S(1)} %get-tuple-element.55.w3, ...), custom_call_target="tpu_custom_call" | custom-call | tf_op jit(solution)/shard_map/pallas_call | solution.py:56
  65.5 0.1 convert_element_type.117
  65.6 0.2 collective-permute-start.20
  65.9 0.1 convert_element_type.100
  66.0 0.1 convert_element_type.98
  66.1 3.2 %collective-permute-start.15 = (f16[544,512]{1,0:T(8,128)(2,1)S(1)}, f16[544,512]{1,0:T(8,128)(2,1)S(1)}, u32[]{:S(2)}, u32[]{:S(2)}) collective-permute-start(f16[544,512]{1,0:T(8,128)(2,1)S(1)} %convert_element_type.98), channel_id=1, source_target_pairs={{0,3},{1,0},{2,1},{3,2},{4,28},{5,29},{6,30},{7,31},{8,11},{9,8},{... | collective-permute-start | bytes 1671176 | tf_op jit(solution)/shard_map/ppermute | solution.py:33
  69.3 0.1 convert_element_type.96
  69.4 2.4 %collective-permute-start.14 = (f16[544,512]{1,0:T(8,128)(2,1)S(1)}, f16[544,512]{1,0:T(8,128)(2,1)S(1)}, u32[]{:S(2)}, u32[]{:S(2)}) collective-permute-start(f16[544,512]{1,0:T(8,128)(2,1)S(1)} %convert_element_type.96), channel_id=1, source_target_pairs={{0,2},{1,3},{2,0},{3,1},{4,20},{5,21},{6,22},{7,23},{8,10},{9,11},... | collective-permute-start | bytes 1671176 | tf_op jit(solution)/shard_map/ppermute | solution.py:33
  71.8 1.3 %shard_map.78 = f32[544,512]{1,0:T(8,128)S(1)} custom-call(bf16[512,1024]{1,0:T(8,128)(2,1)S(1)} %get-tuple-element.52.w0, bf16[512,1024]{1,0:T(8,128)(2,1)S(1)} %get-tuple-element.53.w1, bf16[512,1024]{1,0:T(8,128)(2,1)S(1)} %get-tuple-element.54.w2, bf16[512,1024]{1,0:T(8,128)(2,1)S(1)} %get-tuple-element.55.w3, ...), custom_call_target="tpu_custom_call" | custom-call | tf_op jit(solution)/shard_map/pallas_call | solution.py:56
  73.1 0.1 fusion.2
  73.2 1.7 %collective-permute-start.21 = (f16[136,512]{1,0:T(8,128)(2,1)S(1)}, f16[136,512]{1,0:T(8,128)(2,1)S(1)}, u32[]{:S(2)}, u32[]{:S(2)}) collective-permute-start(f16[136,512]{1,0:T(8,128)(2,1)S(1)} %get-tuple-element.65), channel_id=1, source_target_pairs={{0,64},{32,96},{64,0},{96,32},{1,65},{33,97},{65,1},{97,33},{2,66}... | collective-permute-start | bytes 417800 | tf_op jit(solution)/shard_map/ppermute | solution.py:37
  75.0 7.3 %collective-permute-done.15 = f16[544,512]{1,0:T(8,128)(2,1)S(1)} collective-permute-done((f16[544,512]{1,0:T(8,128)(2,1)S(1)}, f16[544,512]{1,0:T(8,128)(2,1)S(1)}, u32[]{:S(2)}, u32[]{:S(2)}) %collective-permute-start.15) | collective-permute-done | bytes 557088 | tf_op jit(solution)/shard_map/ppermute | solution.py:33
  82.3 0.8 collective-permute-start.22
  83.1 2.9 %collective-permute-done.16 = f16[544,512]{1,0:T(8,128)(2,1)S(1)} collective-permute-done((f16[544,512]{1,0:T(8,128)(2,1)S(1)}, f16[544,512]{1,0:T(8,128)(2,1)S(1)}, u32[]{:S(2)}, u32[]{:S(2)}) %collective-permute-start.16) | collective-permute-done | bytes 557088 | tf_op jit(solution)/shard_map/ppermute | solution.py:33
  86.0 0.3 add_convert_fusion.2
  86.3 3.1 %collective-permute-start.17 = (f16[136,512]{1,0:T(8,128)(2,1)S(1)}, f16[136,512]{1,0:T(8,128)(2,1)S(1)}, u32[]{:S(2)}, u32[]{:S(2)}) collective-permute-start(f16[136,512]{1,0:T(8,128)(2,1)S(1)} %get-tuple-element.62), channel_id=1, source_target_pairs={{0,16},{1,17},{2,18},{3,19},{4,6},{5,7},{6,4},{7,5},{8,24},{9,25},... | collective-permute-start | bytes 417800 | tf_op jit(solution)/shard_map/ppermute | solution.py:33
  89.4 0.6 collective-permute-start.19
  89.9 2.7 %collective-permute-start.18 = (f16[136,512]{1,0:T(8,128)(2,1)S(1)}, f16[136,512]{1,0:T(8,128)(2,1)S(1)}, u32[]{:S(2)}, u32[]{:S(2)}) collective-permute-start(f16[136,512]{1,0:T(8,128)(2,1)S(1)} %get-tuple-element.64), channel_id=1, source_target_pairs={{0,24},{1,25},{2,26},{3,27},{4,7},{5,4},{6,5},{7,6},{8,0},{9,1},{1... | collective-permute-start | bytes 417800 | tf_op jit(solution)/shard_map/ppermute | solution.py:33
  92.7 0.7 shard_map.80
  93.4 2.2 %collective-permute-done.19 = f16[136,512]{1,0:T(8,128)(2,1)S(1)} collective-permute-done((f16[136,512]{1,0:T(8,128)(2,1)S(1)}, f16[136,512]{1,0:T(8,128)(2,1)S(1)}, u32[]{:S(2)}, u32[]{:S(2)}) %collective-permute-start.19) | collective-permute-done | bytes 139296 | tf_op jit(solution)/shard_map/ppermute | solution.py:33
  95.6 0.2 add_add_fusion.g_ref
  95.8 0.9 shard_map.81
  (38 shorter events, 0.5 us)
Async XLA Ops:
  0.6 8.5 %collective-permute-start.3 = (bf16[128,512]{1,0:T(8,128)(2,1)}, bf16[128,512]{1,0:T(8,128)(2,1)S(1)}, u32[]{:S(2)}, u32[]{:S(2)}) collective-permute-start(bf16[128,512]{1,0:T(8,128)(2,1)} %a_ref.3), channel_id=1, source_target_pairs={{0,32},{32,64},{64,96},{96,0},{1,33},{33,65},{65,97},{97,1},{2,34}... | collective-permute-start | bytes 393224 | tf_op jit(solution)/shard_map/ppermute | solution.py:37
  2.3 10.7 %collective-permute-start.5 = (bf16[128,512]{1,0:T(8,128)(2,1)}, bf16[128,512]{1,0:T(8,128)(2,1)S(1)}, u32[]{:S(2)}, u32[]{:S(2)}) collective-permute-start(bf16[128,512]{1,0:T(8,128)(2,1)} %a_ref.3), channel_id=1, source_target_pairs={{0,96},{32,0},{64,32},{96,64},{1,97},{33,1},{65,33},{97,65},{2,98}... | collective-permute-start | bytes 393224 | tf_op jit(solution)/shard_map/ppermute | solution.py:37
  3.9 9.0 %collective-permute-start.4 = (bf16[128,512]{1,0:T(8,128)(2,1)}, bf16[128,512]{1,0:T(8,128)(2,1)S(1)}, u32[]{:S(2)}, u32[]{:S(2)}) collective-permute-start(bf16[128,512]{1,0:T(8,128)(2,1)} %a_ref.3), channel_id=1, source_target_pairs={{0,64},{32,96},{64,0},{96,32},{1,65},{33,97},{65,1},{97,33},{2,66}... | collective-permute-start | bytes 393224 | tf_op jit(solution)/shard_map/ppermute | solution.py:37
  5.9 7.3 %collective-permute-start = (bf16[128,512]{1,0:T(8,128)(2,1)}, bf16[128,512]{1,0:T(8,128)(2,1)S(1)}, u32[]{:S(2)}, u32[]{:S(2)}) collective-permute-start(bf16[128,512]{1,0:T(8,128)(2,1)} %a_ref.2), channel_id=1, source_target_pairs={{0,8},{1,9},{2,10},{3,11},{4,5},{5,6},{6,7},{7,4},{8,16},{9,17},{1... | collective-permute-start | bytes 393224 | tf_op jit(solution)/shard_map/ppermute | solution.py:33
  7.4 5.7 %collective-permute-start.2 = (bf16[128,512]{1,0:T(8,128)(2,1)}, bf16[128,512]{1,0:T(8,128)(2,1)S(1)}, u32[]{:S(2)}, u32[]{:S(2)}) collective-permute-start(bf16[128,512]{1,0:T(8,128)(2,1)} %a_ref.2), channel_id=1, source_target_pairs={{0,24},{1,25},{2,26},{3,27},{4,7},{5,4},{6,5},{7,6},{8,0},{9,1},{1... | collective-permute-start | bytes 393224 | tf_op jit(solution)/shard_map/ppermute | solution.py:33
  9.1 6.7 %collective-permute-start.1 = (bf16[128,512]{1,0:T(8,128)(2,1)}, bf16[128,512]{1,0:T(8,128)(2,1)S(1)}, u32[]{:S(2)}, u32[]{:S(2)}) collective-permute-start(bf16[128,512]{1,0:T(8,128)(2,1)} %a_ref.2), channel_id=1, source_target_pairs={{0,16},{1,17},{2,18},{3,19},{4,6},{5,7},{6,4},{7,5},{8,24},{9,25},... | collective-permute-start | bytes 393224 | tf_op jit(solution)/shard_map/ppermute | solution.py:33
  11.1 0.9 copy-start.5
  12.0 0.9 copy-start.4
  13.0 10.7 %collective-permute-start.6 = (bf16[512,512]{1,0:T(8,128)(2,1)S(1)}, bf16[512,512]{1,0:T(8,128)(2,1)S(1)}, u32[]{:S(2)}, u32[]{:S(2)}) collective-permute-start(bf16[512,512]{1,0:T(8,128)(2,1)S(1)} %shard_map.69.refs_2_.t0_ref), channel_id=1, source_target_pairs={{0,4},{4,0},{1,5},{5,1},{2,6},{6,2},{3,7},{7,3},{8,12},{12,8},{9,1... | collective-permute-start | bytes 1572872 | tf_op jit(solution)/shard_map/ppermute | solution.py:41
  15.8 11.2 %collective-permute-start.8 = (bf16[512,512]{1,0:T(8,128)(2,1)S(1)}, bf16[512,512]{1,0:T(8,128)(2,1)S(1)}, u32[]{:S(2)}, u32[]{:S(2)}) collective-permute-start(bf16[512,512]{1,0:T(8,128)(2,1)S(1)} %shard_map.67.refs_1_.i0), channel_id=1, source_target_pairs={{0,2},{1,3},{2,0},{3,1},{4,20},{5,21},{6,22},{7,23},{8,10},{9,11},... | collective-permute-start | bytes 1572872 | tf_op jit(solution)/shard_map/ppermute | solution.py:33
  19.8 12.8 %collective-permute-start.7 = (bf16[512,512]{1,0:T(8,128)(2,1)S(1)}, bf16[512,512]{1,0:T(8,128)(2,1)S(1)}, u32[]{:S(2)}, u32[]{:S(2)}) collective-permute-start(bf16[512,512]{1,0:T(8,128)(2,1)S(1)} %shard_map.67.refs_1_.i0), channel_id=1, source_target_pairs={{0,1},{1,2},{2,3},{3,0},{4,12},{5,13},{6,14},{7,15},{8,9},{9,10},{... | collective-permute-start | bytes 1572872 | tf_op jit(solution)/shard_map/ppermute | solution.py:33
  20.8 14.7 %collective-permute-start.9 = (bf16[512,512]{1,0:T(8,128)(2,1)S(1)}, bf16[512,512]{1,0:T(8,128)(2,1)S(1)}, u32[]{:S(2)}, u32[]{:S(2)}) collective-permute-start(bf16[512,512]{1,0:T(8,128)(2,1)S(1)} %shard_map.67.refs_1_.i0), channel_id=1, source_target_pairs={{0,3},{1,0},{2,1},{3,2},{4,28},{5,29},{6,30},{7,31},{8,11},{9,8},{... | collective-permute-start | bytes 1572872 | tf_op jit(solution)/shard_map/ppermute | solution.py:33
  28.6 0.6 copy-start.6
  34.8 0.6 copy-start.8
  37.8 0.6 copy-start.10
  38.5 0.7 copy-start.3
  39.2 17.3 %all-to-all-start = ((f32[16,40,128]{2,1,0:T(8,128)}), f32[16,40,128]{2,1,0:T(8,128)S(1)}, u32[]{:S(2)}, u32[]{:S(2)}) async-start(f32[16,40,128]{2,1,0:T(8,128)} %bitcast.6), calls=%async_computation | async-start | bytes 655360 | tf_op jit(solution)/shard_map/all_to_all | solution.py:391
  45.1 0.8 copy-start.7
  45.8 0.8 copy-start.9
  46.6 0.8 copy-start.11
  47.4 3.8 %collective-permute-start.12 = (f32[24,128]{1,0:T(8,128)S(1)}, f32[24,128]{1,0:T(8,128)S(1)}, u32[]{:S(2)}, u32[]{:S(2)}) collective-permute-start(f32[24,128]{1,0:T(8,128)S(1)} %shard_map.71.b0), channel_id=1, source_target_pairs={{0,96},{32,0},{64,32},{96,64},{1,97},{33,1},{65,33},{97,65},{2,98}... | collective-permute-start | bytes 36872 | tf_op jit(solution)/shard_map/ppermute | solution.py:37
  49.4 5.2 %collective-permute-start.11 = (f32[24,128]{1,0:T(8,128)S(1)}, f32[24,128]{1,0:T(8,128)S(1)}, u32[]{:S(2)}, u32[]{:S(2)}) collective-permute-start(f32[24,128]{1,0:T(8,128)S(1)} %shard_map.71.b0), channel_id=1, source_target_pairs={{0,64},{32,96},{64,0},{96,32},{1,65},{33,97},{65,1},{97,33},{2,66}... | collective-permute-start | bytes 36872 | tf_op jit(solution)/shard_map/ppermute | solution.py:37
  50.1 4.9 %collective-permute-start.10 = (f32[24,128]{1,0:T(8,128)S(1)}, f32[24,128]{1,0:T(8,128)S(1)}, u32[]{:S(2)}, u32[]{:S(2)}) collective-permute-start(f32[24,128]{1,0:T(8,128)S(1)} %shard_map.71.b0), channel_id=1, source_target_pairs={{0,32},{32,64},{64,96},{96,0},{1,33},{33,65},{65,97},{97,1},{2,34}... | collective-permute-start | bytes 36872 | tf_op jit(solution)/shard_map/ppermute | solution.py:37
  55.0 1.4 %collective-permute-start.13 = (f32[24,128]{1,0:T(8,128)S(1)}, f32[24,128]{1,0:T(8,128)S(1)}, u32[]{:S(2)}, u32[]{:S(2)}) collective-permute-start(f32[24,128]{1,0:T(8,128)S(1)} %shard_map.72.b0), channel_id=1, source_target_pairs={{0,4},{4,0},{1,5},{5,1},{2,6},{6,2},{3,7},{7,3},{8,12},{12,8},{9,1... | collective-permute-start | bytes 36872 | tf_op jit(solution)/shard_map/ppermute | solution.py:41
  58.3 1.6 %copy-start.2 = (f32[512,1024]{1,0:T(8,128)S(1)}, f32[512,1024]{1,0:T(8,128)}, u32[]{:S(2)}) copy-start(f32[512,1024]{1,0:T(8,128)} %get-tuple-element.50.l_ref) | copy-start | bytes 6291460
  59.8 1.6 %copy-start.1 = (f32[512,1024]{1,0:T(8,128)S(1)}, f32[512,1024]{1,0:T(8,128)}, u32[]{:S(2)}) copy-start(f32[512,1024]{1,0:T(8,128)} %get-tuple-element.48.l_ref) | copy-start | bytes 6291460
  61.4 1.6 %copy-start = (f32[512,1024]{1,0:T(8,128)S(1)}, f32[512,1024]{1,0:T(8,128)}, u32[]{:S(2)}) copy-start(f32[512,1024]{1,0:T(8,128)} %get-tuple-element.33.l_ref) | copy-start | bytes 6291460
  65.6 7.5 %collective-permute-start.20 = (f16[544,512]{1,0:T(8,128)(2,1)S(1)}, f16[544,512]{1,0:T(8,128)(2,1)S(1)}, u32[]{:S(2)}, u32[]{:S(2)}) collective-permute-start(f16[544,512]{1,0:T(8,128)(2,1)S(1)} %convert_element_type.117), channel_id=1, source_target_pairs={{0,4},{4,0},{1,5},{5,1},{2,6},{6,2},{3,7},{7,3},{8,12},{12,8},{9,1... | collective-permute-start | bytes 1671176 | tf_op jit(solution)/shard_map/ppermute | solution.py:41
  66.1 16.2 %collective-permute-start.15 = (f16[544,512]{1,0:T(8,128)(2,1)S(1)}, f16[544,512]{1,0:T(8,128)(2,1)S(1)}, u32[]{:S(2)}, u32[]{:S(2)}) collective-permute-start(f16[544,512]{1,0:T(8,128)(2,1)S(1)} %convert_element_type.98), channel_id=1, source_target_pairs={{0,3},{1,0},{2,1},{3,2},{4,28},{5,29},{6,30},{7,31},{8,11},{9,8},{... | collective-permute-start | bytes 1671176 | tf_op jit(solution)/shard_map/ppermute | solution.py:33
  69.3 16.7 %collective-permute-start.16 = (f16[544,512]{1,0:T(8,128)(2,1)S(1)}, f16[544,512]{1,0:T(8,128)(2,1)S(1)}, u32[]{:S(2)}, u32[]{:S(2)}) collective-permute-start(f16[544,512]{1,0:T(8,128)(2,1)S(1)} %convert_element_type.100), channel_id=1, source_target_pairs={{0,1},{1,2},{2,3},{3,0},{4,12},{5,13},{6,14},{7,15},{8,9},{9,10},{... | collective-permute-start | bytes 1671176 | tf_op jit(solution)/shard_map/ppermute | solution.py:33
  69.4 16.6 %collective-permute-start.14 = (f16[544,512]{1,0:T(8,128)(2,1)S(1)}, f16[544,512]{1,0:T(8,128)(2,1)S(1)}, u32[]{:S(2)}, u32[]{:S(2)}) collective-permute-start(f16[544,512]{1,0:T(8,128)(2,1)S(1)} %convert_element_type.96), channel_id=1, source_target_pairs={{0,2},{1,3},{2,0},{3,1},{4,20},{5,21},{6,22},{7,23},{8,10},{9,11},... | collective-permute-start | bytes 1671176 | tf_op jit(solution)/shard_map/ppermute | solution.py:33
  73.2 16.7 %collective-permute-start.21 = (f16[136,512]{1,0:T(8,128)(2,1)S(1)}, f16[136,512]{1,0:T(8,128)(2,1)S(1)}, u32[]{:S(2)}, u32[]{:S(2)}) collective-permute-start(f16[136,512]{1,0:T(8,128)(2,1)S(1)} %get-tuple-element.65), channel_id=1, source_target_pairs={{0,64},{32,96},{64,0},{96,32},{1,65},{33,97},{65,1},{97,33},{2,66}... | collective-permute-start | bytes 417800 | tf_op jit(solution)/shard_map/ppermute | solution.py:37
  74.9 17.7 %collective-permute-start.23 = (f16[136,512]{1,0:T(8,128)(2,1)S(1)}, f16[136,512]{1,0:T(8,128)(2,1)S(1)}, u32[]{:S(2)}, u32[]{:S(2)}) collective-permute-start(f16[136,512]{1,0:T(8,128)(2,1)S(1)} %get-tuple-element.66), channel_id=1, source_target_pairs={{0,32},{32,64},{64,96},{96,0},{1,33},{33,65},{65,97},{97,1},{2,34}... | collective-permute-start | bytes 417800 | tf_op jit(solution)/shard_map/ppermute | solution.py:37
  82.3 10.3 %collective-permute-start.22 = (f16[136,512]{1,0:T(8,128)(2,1)S(1)}, f16[136,512]{1,0:T(8,128)(2,1)S(1)}, u32[]{:S(2)}, u32[]{:S(2)}) collective-permute-start(f16[136,512]{1,0:T(8,128)(2,1)S(1)} %get-tuple-element.67), channel_id=1, source_target_pairs={{0,96},{32,0},{64,32},{96,64},{1,97},{33,1},{65,33},{97,65},{2,98}... | collective-permute-start | bytes 417800 | tf_op jit(solution)/shard_map/ppermute | solution.py:37
  86.3 7.1 %collective-permute-start.17 = (f16[136,512]{1,0:T(8,128)(2,1)S(1)}, f16[136,512]{1,0:T(8,128)(2,1)S(1)}, u32[]{:S(2)}, u32[]{:S(2)}) collective-permute-start(f16[136,512]{1,0:T(8,128)(2,1)S(1)} %get-tuple-element.62), channel_id=1, source_target_pairs={{0,16},{1,17},{2,18},{3,19},{4,6},{5,7},{6,4},{7,5},{8,24},{9,25},... | collective-permute-start | bytes 417800 | tf_op jit(solution)/shard_map/ppermute | solution.py:33
  89.4 6.3 %collective-permute-start.19 = (f16[136,512]{1,0:T(8,128)(2,1)S(1)}, f16[136,512]{1,0:T(8,128)(2,1)S(1)}, u32[]{:S(2)}, u32[]{:S(2)}) collective-permute-start(f16[136,512]{1,0:T(8,128)(2,1)S(1)} %get-tuple-element.63), channel_id=1, source_target_pairs={{0,8},{1,9},{2,10},{3,11},{4,5},{5,6},{6,7},{7,4},{8,16},{9,17},{1... | collective-permute-start | bytes 417800 | tf_op jit(solution)/shard_map/ppermute | solution.py:33
  89.9 5.7 %collective-permute-start.18 = (f16[136,512]{1,0:T(8,128)(2,1)S(1)}, f16[136,512]{1,0:T(8,128)(2,1)S(1)}, u32[]{:S(2)}, u32[]{:S(2)}) collective-permute-start(f16[136,512]{1,0:T(8,128)(2,1)S(1)} %get-tuple-element.64), channel_id=1, source_target_pairs={{0,24},{1,25},{2,26},{3,27},{4,7},{5,4},{6,5},{7,6},{8,0},{9,1},{1... | collective-permute-start | bytes 417800 | tf_op jit(solution)/shard_map/ppermute | solution.py:33

commit v6 on v3

--- a/solution.py
+++ b/solution.py
@@ -96,6 +96,14 @@
     for a in refs[:-1]:
         o_ref[at : at + a.shape[0], :] = a[...]
         at += a.shape[0]
+
+
+def half_kernel(at, a_ref, o_ref):
+    o_ref[...] = a_ref[at : at + 256, :]
+
+
+def half(value, at):
+    return call(functools.partial(half_kernel, at), out((256, 512), BF16), value)
 
 
 def joined(values):
@@ -381,7 +389,8 @@
     for d in (1, 3):
         chunks[d] = turn(line, d, False)
     halves = []
-    for d, part in ((1, chunks[1][0:256]), (3, chunks[3][256:512])):
+    for d in (1, 3):
+        part = half(chunks[d], 256 * (d // 2))
         halves.append(turn(part, d, False))
     chunks[2] = joined(halves)
     t0 = [own_texts] + everyone(texts, along_x)[1:]
@@ -414,14 +423,8 @@
             smem=(0,),
             scratch=[pltpu.VMEM((512, 1024), F32)],
         )
-        if k == 2:
-            for d, part in ((3, gs[k][0:272]), (1, gs[k][272:544])):
-                sent[d] = turn(part.astype(F16), d, False).astype(F32)
-        elif k:
-            mine = [gs[k][0:272], gs[k][272:544]]
-            mine[k // 2] = mine[k // 2] + sent.pop(4 - k)
-            mine = jnp.concatenate([m.astype(F16) for m in mine], axis=0)
-            sent[k + 4] = turn(mine, 4 - k, False)
+        if k:
+            sent[k] = turn(gs[k].astype(F16), 4 - k, False)
     g0, g1 = [
         call(
             functools.partial(text_kernel, h),

time: 92.3 us -> 93.7 us (1.015)
  waiting for transfers between devices: 18.2 us -> 23.9 us
  local copies, waits for them, and re-layouts: 7.99 us -> 4.8 us
  starting transfers between devices: 44.3 us -> 42.6 us
    ppermute x14 -> x13, waiting for transfers between devices: 8.31 us -> 14 us  [turn(): return lax.ppermute(value, ('y', 'c', 'z'), pairs)]
    unnamed x20 -> x16, local copies, waits for them, and re-layouts: 6.44 us -> 4.8 us
    slice x3 -> x0, local copies, waits for them, and re-layouts: 1.55 us -> none  [the longest x1 0.73 us: program(): chunks[3][256:512]]
    ppermute x9, starting transfers between devices: 13.2 us -> 11.9 us  [along_x(): return lax.ppermute(value, 'x', [(i, (i + shift) % 4) for i in range(4)])]
    pallas_call x19 -> x21, Pallas kernels: 17.3 us -> 18.2 us  [call(): pl.pallas_call(kernel, out_shape=outs, in_specs=[pl.BlockSpec(memory_spac...]
    ppermute x14 -> x13, starting transfers between devices: 25.6 us -> 24.9 us  [turn(): return lax.ppermute(value, ('y', 'c', 'z'), pairs)]
  transfers between devices with their start and end apart: 27 -> 26, of which waited for: 13 -> 13; matrix products, arithmetic and copies ran while one was open for 3% -> 1% of each run, Pallas kernels for 15% -> 9%
where the time goes in v6:
time: 93.7 us; the launch traced here: 93.1 us
  starting transfers between devices  42.6 us (45%)
  waiting for transfers between devices  23.9 us (26%)
  Pallas kernels  19.2 us (20%)
  local copies, waits for them, and re-layouts  4.8 us (5%)
  between operations  1.58 us (2%)
  other arithmetic  1.08 us (1%)
    ppermute x13, starting transfers between devices, turn(): return lax.ppermute(value, ('y', 'c', 'z'), pairs)  24.9 us
    pallas_call x21, Pallas kernels, call(): pl.pallas_call(kernel, out_shape=outs, in_specs=[pl.BlockSpec(memory_spac...  18.2 us
    ppermute x13, waiting for transfers between devices, turn(): return lax.ppermute(value, ('y', 'c', 'z'), pairs)  14 us
    ppermute x9, starting transfers between devices, along_x(): return lax.ppermute(value, 'x', [(i, (i + shift) % 4) for i in range(4)])  11.9 us
    ppermute x9, waiting for transfers between devices, along_x(): return lax.ppermute(value, 'x', [(i, (i + shift) % 4) for i in range(4)])  8.68 us
    all_to_all x1, starting transfers between devices, program(): lax.all_to_all(rows.reshape(16, 40, 128), ('y', 'z'), 0, 0, tiled=True)  5.16 us
    unnamed x16, local copies, waits for them, and re-layouts  4.8 us
  transfers between devices with their start and end apart: 26, of which 13 were waited for; matrix products, arithmetic and copies ran while one was open for 1% of the time, Pallas kernels for 9%

profile of v6, /device:TPU:0, one launch (start us, length us, event | category | flops | bytes accessed | tf_op | source)
XLA Modules:
  0.0 93.1 jit_solution(12158859241322162655)
XLA Ops:
  0.6 1.8 %collective-permute-start = (bf16[128,512]{1,0:T(8,128)(2,1)}, bf16[128,512]{1,0:T(8,128)(2,1)S(1)}, u32[]{:S(2)}, u32[]{:S(2)}) collective-permute-start(bf16[128,512]{1,0:T(8,128)(2,1)} %a_ref.1), channel_id=1, source_target_pairs={{0,8},{1,9},{2,10},{3,11},{4,5},{5,6},{6,7},{7,4},{8,16},{9,17},{1... | collective-permute-start | bytes 393224 | tf_op jit(solution)/shard_map/ppermute | solution.py:33
  2.4 1.5 %collective-permute-start.2 = (bf16[128,512]{1,0:T(8,128)(2,1)}, bf16[128,512]{1,0:T(8,128)(2,1)S(1)}, u32[]{:S(2)}, u32[]{:S(2)}) collective-permute-start(bf16[128,512]{1,0:T(8,128)(2,1)} %a_ref.1), channel_id=1, source_target_pairs={{0,24},{1,25},{2,26},{3,27},{4,7},{5,4},{6,5},{7,6},{8,0},{9,1},{1... | collective-permute-start | bytes 393224 | tf_op jit(solution)/shard_map/ppermute | solution.py:33
  3.9 2.1 %collective-permute-start.1 = (bf16[128,512]{1,0:T(8,128)(2,1)}, bf16[128,512]{1,0:T(8,128)(2,1)S(1)}, u32[]{:S(2)}, u32[]{:S(2)}) collective-permute-start(bf16[128,512]{1,0:T(8,128)(2,1)} %a_ref.1), channel_id=1, source_target_pairs={{0,16},{1,17},{2,18},{3,19},{4,6},{5,7},{6,4},{7,5},{8,24},{9,25},... | collective-permute-start | bytes 393224 | tf_op jit(solution)/shard_map/ppermute | solution.py:33
  6.0 1.0 %hold.1 = (bf16[128,512]{1,0:T(8,128)(2,1)S(1)}, bf16[128,512]{1,0:T(8,128)(2,1)S(1)}) custom-call(bf16[128,512]{1,0:T(8,128)(2,1)} %a_ref.1, bf16[128,512]{1,0:T(8,128)(2,1)} %b_ref.1), custom_call_target="tpu_custom_call" | custom-call | tf_op jit(solution)/shard_map/hold/pallas_call | solution.py:84
  7.1 0.5 collective-permute-done.2.refs_3_
  7.6 3.1 %collective-permute-done.1.refs_2_ = bf16[128,512]{1,0:T(8,128)(2,1)S(1)} collective-permute-done((bf16[128,512]{1,0:T(8,128)(2,1)}, bf16[128,512]{1,0:T(8,128)(2,1)S(1)}, u32[]{:S(2)}, u32[]{:S(2)}) %collective-permute-start.1) | collective-permute-done | bytes 131104 | tf_op jit(solution)/shard_map/ppermute | solution.py:33
  10.7 4.2 %collective-permute-start.9 = (bf16[512,512]{1,0:T(8,128)(2,1)S(1)}, bf16[512,512]{1,0:T(8,128)(2,1)S(1)}, u32[]{:S(2)}, u32[]{:S(2)}) collective-permute-start(bf16[512,512]{1,0:T(8,128)(2,1)S(1)} %shard_map.66.im_ref.i0), channel_id=1, source_target_pairs={{0,3},{1,0},{2,1},{3,2},{4,28},{5,29},{6,30},{7,31},{8,11},{9,8},{... | collective-permute-start | bytes 1572872 | tf_op jit(solution)/shard_map/ppermute | solution.py:33
  14.9 1.5 %collective-permute-start.3 = (bf16[128,512]{1,0:T(8,128)(2,1)S(1)}, bf16[128,512]{1,0:T(8,128)(2,1)S(1)}, u32[]{:S(2)}, u32[]{:S(2)}) collective-permute-start(bf16[128,512]{1,0:T(8,128)(2,1)S(1)} %copy-done.7), channel_id=1, source_target_pairs={{0,32},{32,64},{64,96},{96,0},{1,33},{33,65},{65,97},{97,1},{2,34}... | collective-permute-start | bytes 393224 | tf_op jit(solution)/shard_map/ppermute | solution.py:37
  16.4 1.7 %collective-permute-start.5 = (bf16[128,512]{1,0:T(8,128)(2,1)S(1)}, bf16[128,512]{1,0:T(8,128)(2,1)S(1)}, u32[]{:S(2)}, u32[]{:S(2)}) collective-permute-start(bf16[128,512]{1,0:T(8,128)(2,1)S(1)} %copy-done.7), channel_id=1, source_target_pairs={{0,96},{32,0},{64,32},{96,64},{1,97},{33,1},{65,33},{97,65},{2,98}... | collective-permute-start | bytes 393224 | tf_op jit(solution)/shard_map/ppermute | solution.py:37
  18.1 1.8 %collective-permute-start.4 = (bf16[128,512]{1,0:T(8,128)(2,1)S(1)}, bf16[128,512]{1,0:T(8,128)(2,1)S(1)}, u32[]{:S(2)}, u32[]{:S(2)}) collective-permute-start(bf16[128,512]{1,0:T(8,128)(2,1)S(1)} %copy-done.7), channel_id=1, source_target_pairs={{0,64},{32,96},{64,0},{96,32},{1,65},{33,97},{65,1},{97,33},{2,66}... | collective-permute-start | bytes 393224 | tf_op jit(solution)/shard_map/ppermute | solution.py:37
  19.9 2.5 %collective-permute-done.3.refs_1_ = bf16[128,512]{1,0:T(8,128)(2,1)S(1)} collective-permute-done((bf16[128,512]{1,0:T(8,128)(2,1)S(1)}, bf16[128,512]{1,0:T(8,128)(2,1)S(1)}, u32[]{:S(2)}, u32[]{:S(2)}) %collective-permute-start.3) | collective-permute-done | bytes 131104 | tf_op jit(solution)/shard_map/ppermute | solution.py:37
  22.5 2.1 %collective-permute-done.4.refs_2_ = bf16[128,512]{1,0:T(8,128)(2,1)S(1)} collective-permute-done((bf16[128,512]{1,0:T(8,128)(2,1)S(1)}, bf16[128,512]{1,0:T(8,128)(2,1)S(1)}, u32[]{:S(2)}, u32[]{:S(2)}) %collective-permute-start.4) | collective-permute-done | bytes 131104 | tf_op jit(solution)/shard_map/ppermute | solution.py:37
  24.8 3.3 %collective-permute-start.10 = (bf16[256,512]{1,0:T(8,128)(2,1)S(1)}, bf16[256,512]{1,0:T(8,128)(2,1)S(1)}, u32[]{:S(2)}, u32[]{:S(2)}) collective-permute-start(bf16[256,512]{1,0:T(8,128)(2,1)S(1)} %shard_map.71), channel_id=1, source_target_pairs={{0,3},{1,0},{2,1},{3,2},{4,28},{5,29},{6,30},{7,31},{8,11},{9,8},{... | collective-permute-start | bytes 786440 | tf_op jit(solution)/shard_map/ppermute | solution.py:33
  28.9 1.7 %shard_map.68 = (f32[16,128]{1,0:T(8,128)S(1)}, f32[8,1024]{1,0:T(8,128)S(1)}) custom-call(f32[1,1]{1,0:T(1,128)} %bitcast.s_ref, bf16[512,512]{1,0:T(8,128)(2,1)S(1)} %shard_map.66.im_ref.i0, bf16[512,512]{1,0:T(8,128)(2,1)S(1)} %shard_map.67.t0_ref, bf16[512,512]{1,0:T(8,128)(2,1)S(1)} %collective-permute-done.6.t1_ref), custom_call_target="tpu_custom_call" | custom-call | tf_op jit(solution)/shard_map/pallas_call | solution.py:56
  30.6 1.6 %shard_map.74 = (f32[16,128]{1,0:T(8,128)S(1)}, f32[8,1024]{1,0:T(8,128)S(1)}) custom-call(f32[1,1]{1,0:T(1,128)} %bitcast.s_ref, bf16[512,512]{1,0:T(8,128)(2,1)S(1)} %collective-permute-done.9.a_ref.im_ref.i3, bf16[512,512]{1,0:T(8,128)(2,1)S(1)} %shard_map.67.t0_ref, bf16[512,512]{1,0:T(8,128)(2,1)S(1)} %collective-permute-done.6.t1_ref), custom_call_target="tpu_custom_call" | custom-call | tf_op jit(solution)/shard_map/pallas_call | solution.py:56
  32.2 0.6 copy-done.1
  32.8 1.6 %shard_map.69 = (f32[16,128]{1,0:T(8,128)S(1)}, f32[8,1024]{1,0:T(8,128)S(1)}) custom-call(f32[1,1]{1,0:T(1,128)} %bitcast.s_ref, bf16[512,512]{1,0:T(8,128)(2,1)S(1)} %collective-permute-done.7.im_ref.a_ref.i1, bf16[512,512]{1,0:T(8,128)(2,1)S(1)} %shard_map.67.t0_ref, bf16[512,512]{1,0:T(8,128)(2,1)S(1)} %collective-permute-done.6.t1_ref), custom_call_target="tpu_custom_call" | custom-call | tf_op jit(solution)/shard_map/pallas_call | solution.py:56
  34.4 0.6 copy-done.3
  35.0 0.9 collective-permute-done.8.refs_0_
  35.9 1.0 %shard_map.72.im_ref.i2 = bf16[512,512]{1,0:T(8,128)(2,1)S(1)} custom-call(bf16[256,512]{1,0:T(8,128)(2,1)} %collective-permute-done.8.refs_0_, bf16[256,512]{1,0:T(8,128)(2,1)S(1)} %collective-permute-done.10.refs_1_), custom_call_target="tpu_custom_call" | custom-call | tf_op jit(solution)/shard_map/pallas_call | solution.py:56
  36.8 1.6 %shard_map.73 = (f32[16,128]{1,0:T(8,128)S(1)}, f32[8,1024]{1,0:T(8,128)S(1)}) custom-call(f32[1,1]{1,0:T(1,128)} %bitcast.s_ref, bf16[512,512]{1,0:T(8,128)(2,1)S(1)} %shard_map.72.im_ref.i2, bf16[512,512]{1,0:T(8,128)(2,1)S(1)} %shard_map.67.t0_ref, bf16[512,512]{1,0:T(8,128)(2,1)S(1)} %collective-permute-done.6.t1_ref), custom_call_target="tpu_custom_call" | custom-call | tf_op jit(solution)/shard_map/pallas_call | solution.py:56
  38.4 0.6 copy-done.5
  39.1 0.7 copy-done
  39.8 5.2 %all-to-all-start = ((f32[16,40,128]{2,1,0:T(8,128)}), f32[16,40,128]{2,1,0:T(8,128)S(1)}, u32[]{:S(2)}, u32[]{:S(2)}) async-start(f32[16,40,128]{2,1,0:T(8,128)} %bitcast.6), calls=%async_computation | async-start | bytes 655360 | tf_op jit(solution)/shard_map/all_to_all | solution.py:407
  45.0 0.7 copy-done.2
  45.8 0.8 copy-done.4
  46.5 0.8 copy-done.6
  47.3 1.6 %collective-permute-start.13 = (f32[24,128]{1,0:T(8,128)S(1)}, f32[24,128]{1,0:T(8,128)S(1)}, u32[]{:S(2)}, u32[]{:S(2)}) collective-permute-start(f32[24,128]{1,0:T(8,128)S(1)} %shard_map.76.b0), channel_id=1, source_target_pairs={{0,96},{32,0},{64,32},{96,64},{1,97},{33,1},{65,33},{97,65},{2,98}... | collective-permute-start | bytes 36872 | tf_op jit(solution)/shard_map/ppermute | solution.py:37
  48.9 0.8 collective-permute-start.12
  49.7 0.9 collective-permute-start.11
  50.6 0.5 collective-permute-done.13.b3
  51.1 3.1 %collective-permute-done.12.b2 = f32[24,128]{1,0:T(8,128)S(1)} collective-permute-done((f32[24,128]{1,0:T(8,128)S(1)}, f32[24,128]{1,0:T(8,128)S(1)}, u32[]{:S(2)}, u32[]{:S(2)}) %collective-permute-start.12) | collective-permute-done | bytes 12320 | tf_op jit(solution)/shard_map/ppermute | solution.py:37
  54.1 0.5 collective-permute-done.11.b1
  54.6 0.3 collective-permute-start.14
  54.9 1.2 %collective-permute-done.14.b1 = f32[24,128]{1,0:T(8,128)S(1)} collective-permute-done((f32[24,128]{1,0:T(8,128)S(1)}, f32[24,128]{1,0:T(8,128)S(1)}, u32[]{:S(2)}, u32[]{:S(2)}) %collective-permute-start.14) | collective-permute-done | bytes 12320 | tf_op jit(solution)/shard_map/ppermute | solution.py:41
  56.1 0.2 shard_map.78
  56.3 1.6 %shard_map.82 = (bf16[512,1024]{1,0:T(8,128)(2,1)S(1)}, f32[544,512]{1,0:T(8,128)S(1)}) custom-call(f32[1,1]{1,0:T(1,128)} %bitcast.s_ref, bf16[512,512]{1,0:T(8,128)(2,1)S(1)} %collective-permute-done.9.a_ref.im_ref.i3, f32[16,128]{1,0:T(8,128)S(1)} %get-tuple-element.42.row_ref, f32[1,1024]{1,0:T(1,128)S(1)} %get-tuple-element.43.col_ref, ...), custom_call_target="tpu_custom_call" | custom-call | tf_op jit(solution)/shard_map/pallas_call | solution.py:56
  57.8 1.6 %shard_map.81 = (bf16[512,1024]{1,0:T(8,128)(2,1)S(1)}, f32[544,512]{1,0:T(8,128)S(1)}) custom-call(f32[1,1]{1,0:T(1,128)} %bitcast.s_ref, bf16[512,512]{1,0:T(8,128)(2,1)S(1)} %collective-permute-done.7.im_ref.a_ref.i1, f32[16,128]{1,0:T(8,128)S(1)} %get-tuple-element.42.row_ref, f32[1,1024]{1,0:T(1,128)S(1)} %get-tuple-element.43.col_ref, ...), custom_call_target="tpu_custom_call" | custom-call | tf_op jit(solution)/shard_map/pallas_call | solution.py:56
  59.4 1.6 %shard_map.80 = (bf16[512,1024]{1,0:T(8,128)(2,1)S(1)}, f32[544,512]{1,0:T(8,128)S(1)}) custom-call(f32[1,1]{1,0:T(1,128)} %bitcast.s_ref, bf16[512,512]{1,0:T(8,128)(2,1)S(1)} %shard_map.72.im_ref.i2, f32[16,128]{1,0:T(8,128)S(1)} %get-tuple-element.42.row_ref, f32[1,1024]{1,0:T(1,128)S(1)} %get-tuple-element.43.col_ref, ...), custom_call_target="tpu_custom_call" | custom-call | tf_op jit(solution)/shard_map/pallas_call | solution.py:56
  61.0 1.6 %shard_map.79 = (bf16[512,1024]{1,0:T(8,128)(2,1)S(1)}, f32[544,512]{1,0:T(8,128)S(1)}) custom-call(f32[1,1]{1,0:T(1,128)} %bitcast.s_ref, bf16[512,512]{1,0:T(8,128)(2,1)S(1)} %shard_map.66.im_ref.i0, f32[16,128]{1,0:T(8,128)S(1)} %get-tuple-element.42.row_ref, f32[1,1024]{1,0:T(1,128)S(1)} %get-tuple-element.43.col_ref, ...), custom_call_target="tpu_custom_call" | custom-call | tf_op jit(solution)/shard_map/pallas_call | solution.py:56
  62.6 1.3 %shard_map.84 = f32[544,512]{1,0:T(8,128)S(1)} custom-call(bf16[512,1024]{1,0:T(8,128)(2,1)S(1)} %get-tuple-element.50.w0, bf16[512,1024]{1,0:T(8,128)(2,1)S(1)} %get-tuple-element.51.w1, bf16[512,1024]{1,0:T(8,128)(2,1)S(1)} %get-tuple-element.52.w2, bf16[512,1024]{1,0:T(8,128)(2,1)S(1)} %get-tuple-element.53.w3, bf16[512,512]{1,0:T(8,128)(2,1)S(1)} %shard_map.66.im_ref.i0, ...), custom_call_target="tpu_custom_call" | custom-call | tf_op jit(solution)/shard_map/pallas_call | solution.py:56
  63.9 0.1 convert_element_type.117
  64.0 0.3 collective-permute-start.21
  64.2 0.1 convert_element_type.100
  64.4 2.0 %collective-permute-start.17 = (f16[544,512]{1,0:T(8,128)(2,1)S(1)}, f16[544,512]{1,0:T(8,128)(2,1)S(1)}, u32[]{:S(2)}, u32[]{:S(2)}) collective-permute-start(f16[544,512]{1,0:T(8,128)(2,1)S(1)} %convert_element_type.100), channel_id=1, source_target_pairs={{0,1},{1,2},{2,3},{3,0},{4,12},{5,13},{6,14},{7,15},{8,9},{9,10},{... | collective-permute-start | bytes 1671176 | tf_op jit(solution)/shard_map/ppermute | solution.py:33
  66.4 0.1 convert_element_type.98
  66.5 1.4 %collective-permute-start.16 = (f16[544,512]{1,0:T(8,128)(2,1)S(1)}, f16[544,512]{1,0:T(8,128)(2,1)S(1)}, u32[]{:S(2)}, u32[]{:S(2)}) collective-permute-start(f16[544,512]{1,0:T(8,128)(2,1)S(1)} %convert_element_type.98), channel_id=1, source_target_pairs={{0,3},{1,0},{2,1},{3,2},{4,28},{5,29},{6,30},{7,31},{8,11},{9,8},{... | collective-permute-start | bytes 1671176 | tf_op jit(solution)/shard_map/ppermute | solution.py:33
  67.8 0.1 convert_element_type.96
  68.0 2.3 %collective-permute-start.15 = (f16[544,512]{1,0:T(8,128)(2,1)S(1)}, f16[544,512]{1,0:T(8,128)(2,1)S(1)}, u32[]{:S(2)}, u32[]{:S(2)}) collective-permute-start(f16[544,512]{1,0:T(8,128)(2,1)S(1)} %convert_element_type.96), channel_id=1, source_target_pairs={{0,2},{1,3},{2,0},{3,1},{4,20},{5,21},{6,22},{7,23},{8,10},{9,11},... | collective-permute-start | bytes 1671176 | tf_op jit(solution)/shard_map/ppermute | solution.py:33
  70.2 1.3 %shard_map.83 = f32[544,512]{1,0:T(8,128)S(1)} custom-call(bf16[512,1024]{1,0:T(8,128)(2,1)S(1)} %get-tuple-element.50.w0, bf16[512,1024]{1,0:T(8,128)(2,1)S(1)} %get-tuple-element.51.w1, bf16[512,1024]{1,0:T(8,128)(2,1)S(1)} %get-tuple-element.52.w2, bf16[512,1024]{1,0:T(8,128)(2,1)S(1)} %get-tuple-element.53.w3, bf16[512,512]{1,0:T(8,128)(2,1)S(1)} %shard_map.66.im_ref.i0, ...), custom_call_target="tpu_custom_call" | custom-call | tf_op jit(solution)/shard_map/pallas_call | solution.py:56
  71.5 0.2 fusion.2
  71.7 1.6 %collective-permute-start.22 = (f16[136,512]{1,0:T(8,128)(2,1)S(1)}, f16[136,512]{1,0:T(8,128)(2,1)S(1)}, u32[]{:S(2)}, u32[]{:S(2)}) collective-permute-start(f16[136,512]{1,0:T(8,128)(2,1)S(1)} %get-tuple-element.63), channel_id=1, source_target_pairs={{0,64},{32,96},{64,0},{96,32},{1,65},{33,97},{65,1},{97,33},{2,66}... | collective-permute-start | bytes 417800 | tf_op jit(solution)/shard_map/ppermute | solution.py:37
  73.3 0.5 collective-permute-start.24
  73.8 1.4 %collective-permute-done.17 = f16[544,512]{1,0:T(8,128)(2,1)S(1)} collective-permute-done((f16[544,512]{1,0:T(8,128)(2,1)S(1)}, f16[544,512]{1,0:T(8,128)(2,1)S(1)}, u32[]{:S(2)}, u32[]{:S(2)}) %collective-permute-start.17) | collective-permute-done | bytes 557088 | tf_op jit(solution)/shard_map/ppermute | solution.py:33
  75.2 1.4 %collective-permute-start.23 = (f16[136,512]{1,0:T(8,128)(2,1)S(1)}, f16[136,512]{1,0:T(8,128)(2,1)S(1)}, u32[]{:S(2)}, u32[]{:S(2)}) collective-permute-start(f16[136,512]{1,0:T(8,128)(2,1)S(1)} %get-tuple-element.65), channel_id=1, source_target_pairs={{0,96},{32,0},{64,32},{96,64},{1,97},{33,1},{65,33},{97,65},{2,98}... | collective-permute-start | bytes 417800 | tf_op jit(solution)/shard_map/ppermute | solution.py:37
  76.6 5.9 %collective-permute-done.15 = f16[544,512]{1,0:T(8,128)(2,1)S(1)} collective-permute-done((f16[544,512]{1,0:T(8,128)(2,1)S(1)}, f16[544,512]{1,0:T(8,128)(2,1)S(1)}, u32[]{:S(2)}, u32[]{:S(2)}) %collective-permute-start.15) | collective-permute-done | bytes 557088 | tf_op jit(solution)/shard_map/ppermute | solution.py:33
  82.5 0.2 add_convert_fusion.2
  82.7 3.0 %collective-permute-start.18 = (f16[136,512]{1,0:T(8,128)(2,1)S(1)}, f16[136,512]{1,0:T(8,128)(2,1)S(1)}, u32[]{:S(2)}, u32[]{:S(2)}) collective-permute-start(f16[136,512]{1,0:T(8,128)(2,1)S(1)} %get-tuple-element.60), channel_id=1, source_target_pairs={{0,16},{1,17},{2,18},{3,19},{4,6},{5,7},{6,4},{7,5},{8,24},{9,25},... | collective-permute-start | bytes 417800 | tf_op jit(solution)/shard_map/ppermute | solution.py:33
  85.8 0.6 collective-permute-start.20
  86.4 2.7 %collective-permute-start.19 = (f16[136,512]{1,0:T(8,128)(2,1)S(1)}, f16[136,512]{1,0:T(8,128)(2,1)S(1)}, u32[]{:S(2)}, u32[]{:S(2)}) collective-permute-start(f16[136,512]{1,0:T(8,128)(2,1)S(1)} %get-tuple-element.62), channel_id=1, source_target_pairs={{0,24},{1,25},{2,26},{3,27},{4,7},{5,4},{6,5},{7,6},{8,0},{9,1},{1... | collective-permute-start | bytes 417800 | tf_op jit(solution)/shard_map/ppermute | solution.py:33
  89.1 0.7 shard_map.85
  89.8 2.2 %collective-permute-done.20 = f16[136,512]{1,0:T(8,128)(2,1)S(1)} collective-permute-done((f16[136,512]{1,0:T(8,128)(2,1)S(1)}, f16[136,512]{1,0:T(8,128)(2,1)S(1)}, u32[]{:S(2)}, u32[]{:S(2)}) %collective-permute-start.20) | collective-permute-done | bytes 139296 | tf_op jit(solution)/shard_map/ppermute | solution.py:33
  92.1 0.2 add_add_fusion.g_ref
  92.2 0.9 shard_map.86
  (34 shorter events, 0.6 us)
Async XLA Ops:
  0.6 14.3 %copy-start.7 = (bf16[128,512]{1,0:T(8,128)(2,1)S(1)}, bf16[128,512]{1,0:T(8,128)(2,1)}, u32[]{:S(2)}) copy-start(bf16[128,512]{1,0:T(8,128)(2,1)} %b_ref.1) | copy-start | bytes 393220
  0.6 6.5 %collective-permute-start = (bf16[128,512]{1,0:T(8,128)(2,1)}, bf16[128,512]{1,0:T(8,128)(2,1)S(1)}, u32[]{:S(2)}, u32[]{:S(2)}) collective-permute-start(bf16[128,512]{1,0:T(8,128)(2,1)} %a_ref.1), channel_id=1, source_target_pairs={{0,8},{1,9},{2,10},{3,11},{4,5},{5,6},{6,7},{7,4},{8,16},{9,17},{1... | collective-permute-start | bytes 393224 | tf_op jit(solution)/shard_map/ppermute | solution.py:33
  2.4 5.2 %collective-permute-start.2 = (bf16[128,512]{1,0:T(8,128)(2,1)}, bf16[128,512]{1,0:T(8,128)(2,1)S(1)}, u32[]{:S(2)}, u32[]{:S(2)}) collective-permute-start(bf16[128,512]{1,0:T(8,128)(2,1)} %a_ref.1), channel_id=1, source_target_pairs={{0,24},{1,25},{2,26},{3,27},{4,7},{5,4},{6,5},{7,6},{8,0},{9,1},{1... | collective-permute-start | bytes 393224 | tf_op jit(solution)/shard_map/ppermute | solution.py:33
  3.9 6.7 %collective-permute-start.1 = (bf16[128,512]{1,0:T(8,128)(2,1)}, bf16[128,512]{1,0:T(8,128)(2,1)S(1)}, u32[]{:S(2)}, u32[]{:S(2)}) collective-permute-start(bf16[128,512]{1,0:T(8,128)(2,1)} %a_ref.1), channel_id=1, source_target_pairs={{0,16},{1,17},{2,18},{3,19},{4,6},{5,7},{6,4},{7,5},{8,24},{9,25},... | collective-permute-start | bytes 393224 | tf_op jit(solution)/shard_map/ppermute | solution.py:33
  10.7 14.1 %collective-permute-start.9 = (bf16[512,512]{1,0:T(8,128)(2,1)S(1)}, bf16[512,512]{1,0:T(8,128)(2,1)S(1)}, u32[]{:S(2)}, u32[]{:S(2)}) collective-permute-start(bf16[512,512]{1,0:T(8,128)(2,1)S(1)} %shard_map.66.im_ref.i0), channel_id=1, source_target_pairs={{0,3},{1,0},{2,1},{3,2},{4,28},{5,29},{6,30},{7,31},{8,11},{9,8},{... | collective-permute-start | bytes 1572872 | tf_op jit(solution)/shard_map/ppermute | solution.py:33
  14.9 13.2 %collective-permute-start.7 = (bf16[512,512]{1,0:T(8,128)(2,1)S(1)}, bf16[512,512]{1,0:T(8,128)(2,1)S(1)}, u32[]{:S(2)}, u32[]{:S(2)}) collective-permute-start(bf16[512,512]{1,0:T(8,128)(2,1)S(1)} %shard_map.66.im_ref.i0), channel_id=1, source_target_pairs={{0,1},{1,2},{2,3},{3,0},{4,12},{5,13},{6,14},{7,15},{8,9},{9,10},{... | collective-permute-start | bytes 1572872 | tf_op jit(solution)/shard_map/ppermute | solution.py:33
  14.9 7.6 %collective-permute-start.3 = (bf16[128,512]{1,0:T(8,128)(2,1)S(1)}, bf16[128,512]{1,0:T(8,128)(2,1)S(1)}, u32[]{:S(2)}, u32[]{:S(2)}) collective-permute-start(bf16[128,512]{1,0:T(8,128)(2,1)S(1)} %copy-done.7), channel_id=1, source_target_pairs={{0,32},{32,64},{64,96},{96,0},{1,33},{33,65},{65,97},{97,1},{2,34}... | collective-permute-start | bytes 393224 | tf_op jit(solution)/shard_map/ppermute | solution.py:37
  16.4 6.1 %collective-permute-start.5 = (bf16[128,512]{1,0:T(8,128)(2,1)S(1)}, bf16[128,512]{1,0:T(8,128)(2,1)S(1)}, u32[]{:S(2)}, u32[]{:S(2)}) collective-permute-start(bf16[128,512]{1,0:T(8,128)(2,1)S(1)} %copy-done.7), channel_id=1, source_target_pairs={{0,96},{32,0},{64,32},{96,64},{1,97},{33,1},{65,33},{97,65},{2,98}... | collective-permute-start | bytes 393224 | tf_op jit(solution)/shard_map/ppermute | solution.py:37
  18.1 6.5 %collective-permute-start.4 = (bf16[128,512]{1,0:T(8,128)(2,1)S(1)}, bf16[128,512]{1,0:T(8,128)(2,1)S(1)}, u32[]{:S(2)}, u32[]{:S(2)}) collective-permute-start(bf16[128,512]{1,0:T(8,128)(2,1)S(1)} %copy-done.7), channel_id=1, source_target_pairs={{0,64},{32,96},{64,0},{96,32},{1,65},{33,97},{65,1},{97,33},{2,66}... | collective-permute-start | bytes 393224 | tf_op jit(solution)/shard_map/ppermute | solution.py:37
  24.6 4.2 %collective-permute-start.6 = (bf16[512,512]{1,0:T(8,128)(2,1)S(1)}, bf16[512,512]{1,0:T(8,128)(2,1)S(1)}, u32[]{:S(2)}, u32[]{:S(2)}) collective-permute-start(bf16[512,512]{1,0:T(8,128)(2,1)S(1)} %shard_map.67.t0_ref), channel_id=1, source_target_pairs={{0,4},{4,0},{1,5},{5,1},{2,6},{6,2},{3,7},{7,3},{8,12},{12,8},{9,1... | collective-permute-start | bytes 1572872 | tf_op jit(solution)/shard_map/ppermute | solution.py:41
  24.8 10.2 %collective-permute-start.10 = (bf16[256,512]{1,0:T(8,128)(2,1)S(1)}, bf16[256,512]{1,0:T(8,128)(2,1)S(1)}, u32[]{:S(2)}, u32[]{:S(2)}) collective-permute-start(bf16[256,512]{1,0:T(8,128)(2,1)S(1)} %shard_map.71), channel_id=1, source_target_pairs={{0,3},{1,0},{2,1},{3,2},{4,28},{5,29},{6,30},{7,31},{8,11},{9,8},{... | collective-permute-start | bytes 786440 | tf_op jit(solution)/shard_map/ppermute | solution.py:33
  28.1 7.8 %collective-permute-start.8 = (bf16[256,512]{1,0:T(8,128)(2,1)S(1)}, bf16[256,512]{1,0:T(8,128)(2,1)}, u32[]{:S(2)}, u32[]{:S(2)}) collective-permute-start(bf16[256,512]{1,0:T(8,128)(2,1)S(1)} %shard_map.70), channel_id=1, source_target_pairs={{0,1},{1,2},{2,3},{3,0},{4,12},{5,13},{6,14},{7,15},{8,9},{9,10},{... | collective-permute-start | bytes 786440 | tf_op jit(solution)/shard_map/ppermute | solution.py:33
  32.2 0.6 copy-start.1
  34.4 0.6 copy-start.3
  38.4 0.6 copy-start.5
  39.1 0.7 copy-start
  39.8 16.3 %all-to-all-start = ((f32[16,40,128]{2,1,0:T(8,128)}), f32[16,40,128]{2,1,0:T(8,128)S(1)}, u32[]{:S(2)}, u32[]{:S(2)}) async-start(f32[16,40,128]{2,1,0:T(8,128)} %bitcast.6), calls=%async_computation | async-start | bytes 655360 | tf_op jit(solution)/shard_map/all_to_all | solution.py:407
  45.0 0.8 copy-start.2
  45.8 0.8 copy-start.4
  46.5 0.8 copy-start.6
  47.3 3.8 %collective-permute-start.13 = (f32[24,128]{1,0:T(8,128)S(1)}, f32[24,128]{1,0:T(8,128)S(1)}, u32[]{:S(2)}, u32[]{:S(2)}) collective-permute-start(f32[24,128]{1,0:T(8,128)S(1)} %shard_map.76.b0), channel_id=1, source_target_pairs={{0,96},{32,0},{64,32},{96,64},{1,97},{33,1},{65,33},{97,65},{2,98}... | collective-permute-start | bytes 36872 | tf_op jit(solution)/shard_map/ppermute | solution.py:37
  48.9 5.2 %collective-permute-start.12 = (f32[24,128]{1,0:T(8,128)S(1)}, f32[24,128]{1,0:T(8,128)S(1)}, u32[]{:S(2)}, u32[]{:S(2)}) collective-permute-start(f32[24,128]{1,0:T(8,128)S(1)} %shard_map.76.b0), channel_id=1, source_target_pairs={{0,64},{32,96},{64,0},{96,32},{1,65},{33,97},{65,1},{97,33},{2,66}... | collective-permute-start | bytes 36872 | tf_op jit(solution)/shard_map/ppermute | solution.py:37
  49.7 4.9 %collective-permute-start.11 = (f32[24,128]{1,0:T(8,128)S(1)}, f32[24,128]{1,0:T(8,128)S(1)}, u32[]{:S(2)}, u32[]{:S(2)}) collective-permute-start(f32[24,128]{1,0:T(8,128)S(1)} %shard_map.76.b0), channel_id=1, source_target_pairs={{0,32},{32,64},{64,96},{96,0},{1,33},{33,65},{65,97},{97,1},{2,34}... | collective-permute-start | bytes 36872 | tf_op jit(solution)/shard_map/ppermute | solution.py:37
  54.6 1.4 %collective-permute-start.14 = (f32[24,128]{1,0:T(8,128)S(1)}, f32[24,128]{1,0:T(8,128)S(1)}, u32[]{:S(2)}, u32[]{:S(2)}) collective-permute-start(f32[24,128]{1,0:T(8,128)S(1)} %shard_map.77.b0), channel_id=1, source_target_pairs={{0,4},{4,0},{1,5},{5,1},{2,6},{6,2},{3,7},{7,3},{8,12},{12,8},{9,1... | collective-permute-start | bytes 36872 | tf_op jit(solution)/shard_map/ppermute | solution.py:41
  64.0 7.5 %collective-permute-start.21 = (f16[544,512]{1,0:T(8,128)(2,1)S(1)}, f16[544,512]{1,0:T(8,128)(2,1)S(1)}, u32[]{:S(2)}, u32[]{:S(2)}) collective-permute-start(f16[544,512]{1,0:T(8,128)(2,1)S(1)} %convert_element_type.117), channel_id=1, source_target_pairs={{0,4},{4,0},{1,5},{5,1},{2,6},{6,2},{3,7},{7,3},{8,12},{12,8},{9,1... | collective-permute-start | bytes 1671176 | tf_op jit(solution)/shard_map/ppermute | solution.py:41
  64.4 10.8 %collective-permute-start.17 = (f16[544,512]{1,0:T(8,128)(2,1)S(1)}, f16[544,512]{1,0:T(8,128)(2,1)S(1)}, u32[]{:S(2)}, u32[]{:S(2)}) collective-permute-start(f16[544,512]{1,0:T(8,128)(2,1)S(1)} %convert_element_type.100), channel_id=1, source_target_pairs={{0,1},{1,2},{2,3},{3,0},{4,12},{5,13},{6,14},{7,15},{8,9},{9,10},{... | collective-permute-start | bytes 1671176 | tf_op jit(solution)/shard_map/ppermute | solution.py:33
  66.5 10.1 %collective-permute-start.16 = (f16[544,512]{1,0:T(8,128)(2,1)S(1)}, f16[544,512]{1,0:T(8,128)(2,1)S(1)}, u32[]{:S(2)}, u32[]{:S(2)}) collective-permute-start(f16[544,512]{1,0:T(8,128)(2,1)S(1)} %convert_element_type.98), channel_id=1, source_target_pairs={{0,3},{1,0},{2,1},{3,2},{4,28},{5,29},{6,30},{7,31},{8,11},{9,8},{... | collective-permute-start | bytes 1671176 | tf_op jit(solution)/shard_map/ppermute | solution.py:33
  68.0 14.6 %collective-permute-start.15 = (f16[544,512]{1,0:T(8,128)(2,1)S(1)}, f16[544,512]{1,0:T(8,128)(2,1)S(1)}, u32[]{:S(2)}, u32[]{:S(2)}) collective-permute-start(f16[544,512]{1,0:T(8,128)(2,1)S(1)} %convert_element_type.96), channel_id=1, source_target_pairs={{0,2},{1,3},{2,0},{3,1},{4,20},{5,21},{6,22},{7,23},{8,10},{9,11},... | collective-permute-start | bytes 1671176 | tf_op jit(solution)/shard_map/ppermute | solution.py:33
  71.7 14.7 %collective-permute-start.22 = (f16[136,512]{1,0:T(8,128)(2,1)S(1)}, f16[136,512]{1,0:T(8,128)(2,1)S(1)}, u32[]{:S(2)}, u32[]{:S(2)}) collective-permute-start(f16[136,512]{1,0:T(8,128)(2,1)S(1)} %get-tuple-element.63), channel_id=1, source_target_pairs={{0,64},{32,96},{64,0},{96,32},{1,65},{33,97},{65,1},{97,33},{2,66}... | collective-permute-start | bytes 417800 | tf_op jit(solution)/shard_map/ppermute | solution.py:37
  73.3 15.7 %collective-permute-start.24 = (f16[136,512]{1,0:T(8,128)(2,1)S(1)}, f16[136,512]{1,0:T(8,128)(2,1)S(1)}, u32[]{:S(2)}, u32[]{:S(2)}) collective-permute-start(f16[136,512]{1,0:T(8,128)(2,1)S(1)} %get-tuple-element.64), channel_id=1, source_target_pairs={{0,32},{32,64},{64,96},{96,0},{1,33},{33,65},{65,97},{97,1},{2,34}... | collective-permute-start | bytes 417800 | tf_op jit(solution)/shard_map/ppermute | solution.py:37
  75.2 13.9 %collective-permute-start.23 = (f16[136,512]{1,0:T(8,128)(2,1)S(1)}, f16[136,512]{1,0:T(8,128)(2,1)S(1)}, u32[]{:S(2)}, u32[]{:S(2)}) collective-permute-start(f16[136,512]{1,0:T(8,128)(2,1)S(1)} %get-tuple-element.65), channel_id=1, source_target_pairs={{0,96},{32,0},{64,32},{96,64},{1,97},{33,1},{65,33},{97,65},{2,98}... | collective-permute-start | bytes 417800 | tf_op jit(solution)/shard_map/ppermute | solution.py:37
  82.7 7.1 %collective-permute-start.18 = (f16[136,512]{1,0:T(8,128)(2,1)S(1)}, f16[136,512]{1,0:T(8,128)(2,1)S(1)}, u32[]{:S(2)}, u32[]{:S(2)}) collective-permute-start(f16[136,512]{1,0:T(8,128)(2,1)S(1)} %get-tuple-element.60), channel_id=1, source_target_pairs={{0,16},{1,17},{2,18},{3,19},{4,6},{5,7},{6,4},{7,5},{8,24},{9,25},... | collective-permute-start | bytes 417800 | tf_op jit(solution)/shard_map/ppermute | solution.py:33
  85.8 6.3 %collective-permute-start.20 = (f16[136,512]{1,0:T(8,128)(2,1)S(1)}, f16[136,512]{1,0:T(8,128)(2,1)S(1)}, u32[]{:S(2)}, u32[]{:S(2)}) collective-permute-start(f16[136,512]{1,0:T(8,128)(2,1)S(1)} %get-tuple-element.61), channel_id=1, source_target_pairs={{0,8},{1,9},{2,10},{3,11},{4,5},{5,6},{6,7},{7,4},{8,16},{9,17},{1... | collective-permute-start | bytes 417800 | tf_op jit(solution)/shard_map/ppermute | solution.py:33
  86.4 5.7 %collective-permute-start.19 = (f16[136,512]{1,0:T(8,128)(2,1)S(1)}, f16[136,512]{1,0:T(8,128)(2,1)S(1)}, u32[]{:S(2)}, u32[]{:S(2)}) collective-permute-start(f16[136,512]{1,0:T(8,128)(2,1)S(1)} %get-tuple-element.62), channel_id=1, source_target_pairs={{0,24},{1,25},{2,26},{3,27},{4,7},{5,4},{6,5},{7,6},{8,0},{9,1},{1... | collective-permute-start | bytes 417800 | tf_op jit(solution)/shard_map/ppermute | solution.py:33

commit v7 on v6

--- a/solution.py
+++ b/solution.py
@@ -128,7 +128,7 @@
 
 
 def logits_kernel(first, s_ref, im_ref, t0_ref, t1_ref, rows_ref, cols_ref, l_ref, top_scr, sum_scr, mean_scr):
-    s2 = s_ref[0, 0]
+    s2, count = s_ref[0, 0], im_ref.shape[0] // 64
     logits_into(l_ref, s2, im_ref, (t0_ref, t1_ref))
 
     def tops(i, col_tops):
@@ -142,7 +142,7 @@
         return tuple(new)
 
     col_tops = lax.fori_loop(
-        0, 8, tops, tuple(l_ref[0:8, 128 * k : 128 * (k + 1)] for k in range(8)), unroll=True
+        0, count, tops, tuple(l_ref[0:8, 128 * k : 128 * (k + 1)] for k in range(8)), unroll=True
     )
 
     def sums(i, carry):
@@ -163,7 +163,7 @@
         return tuple(new)
 
     zero = jnp.zeros((8, 128), F32)
-    col_sums = lax.fori_loop(0, 8, sums, ((zero, zero),) * 8, unroll=True)
+    col_sums = lax.fori_loop(0, count, sums, ((zero, zero),) * 8, unroll=True)
     for k in range(8):
         at = slice(128 * k, 128 * (k + 1))
         top = jnp.max(col_tops[k], axis=0, keepdims=True)
@@ -171,7 +171,7 @@
         cols_ref[0:1, at] = top
         cols_ref[1:2, at] = jnp.sum(e * col_sums[k][0], axis=0, keepdims=True)
         cols_ref[2:3, at] = jnp.sum(e * col_sums[k][1], axis=0, keepdims=True)
-    for j in range(4):
+    for j in range(count // 2):
         at = slice(128 * j, 128 * (j + 1))
         tops_here = top_scr[at, :].T
         top = jnp.max(tops_here, axis=0, keepdims=True)
@@ -197,7 +197,7 @@
         (out((16, 128)), out((8, 1024))),
         s2, im, t0, t1,
         smem=(0,),
-        scratch=[pltpu.VMEM((512, 1024), F32)] + [pltpu.VMEM((512, 128), F32)] * 3,
+        scratch=[pltpu.VMEM((im.shape[0], width), F32) for width in (1024, 128, 128, 128)],
     )
 
 
@@ -218,12 +218,12 @@
     return lax.rem(second - back_second + 4, 4) * 4 + lax.rem(first - back_first + 4, 4)
 
 
-def row_kernel(r0, r1, r2, r3, all_ref, scr):
-    for k, r in enumerate((r0, r1, r2, r3)):
-        for j in range(4):
+def row_kernel(r0, r1, r2, r3, r4, all_ref, scr):
+    for k, r, start, end in ((0, r0, 0, 4), (1, r1, 0, 4), (2, r2, 0, 2), (2, r3, 2, 4), (3, r4, 0, 4)):
+        for j in range(start, end):
             at = row_at(k, j)
-            scr[pl.ds(at, 1), :] = r[j : j + 1, :]
-            scr[pl.ds(16 + at, 1), :] = r[4 + j : 5 + j, :]
+            scr[pl.ds(at, 1), :] = r[j - start : j - start + 1, :]
+            scr[pl.ds(16 + at, 1), :] = r[4 + j - start : 5 + j - start, :]
     scr[32:33, :] = r0[10:11, :]
     scr[33:34, :] = r0[9:10, :]
     scr[34:40, :] = jnp.zeros((6, 128), F32)
@@ -232,8 +232,8 @@
         all_ref[40 * k : 40 * (k + 1), :] = message
 
 
-def col_kernel(r0, r1, r2, r3, c0, c1, c2, c3, col_ref):
-    rs, cs = (r0, r1, r2, r3), (c0, c1, c2, c3)
+def col_kernel(r0, r1, r2, r3, r4, c0, c1, c2, c3, c4, col_ref):
+    rs, cs = (r0, r1, r2, r3, r4), (c0, c1, c2, c3, c4)
     top = greatest([c[0:1, :] for c in cs])
     es = [jnp.exp2(c[0:1, :] - top) for c in cs]
     total = sum(e * c[1:2, :] for e, c in zip(es, cs))
@@ -383,7 +383,7 @@
 def program(images, texts, log_scale):
     s2 = jnp.reshape(jnp.exp(log_scale) * LOG2E, (1, 1))
     own_images, own_texts = held(images, texts)
-    line = [own_images] + everyone(images, lambda v, d: turn(v, d, True))[1:]
+    line = [own_images] + everyone(own_images, lambda v, d: turn(v, d, True))[1:]
     line = joined(line)
     chunks = [line, None, None, None]
     for d in (1, 3):
@@ -393,12 +393,12 @@
         part = half(chunks[d], 256 * (d // 2))
         halves.append(turn(part, d, False))
     chunks[2] = joined(halves)
-    t0 = [own_texts] + everyone(texts, along_x)[1:]
+    t0 = [own_texts] + everyone(own_texts, along_x)[1:]
     t0 = joined(t0)
     t1 = other_core(t0)
-    parts = [None] * 4
-    for k in (0, 1, 3, 2):
-        parts[k] = logits_of(k, s2, chunks[k], t0, t1)
+    parts = []
+    for k, im in (("0", chunks[0]), ("1", chunks[1]), ("2a", halves[0]), ("2b", halves[1]), ("3", chunks[3])):
+        parts.append(logits_of(0 if k == "0" else 1, s2, im, t0, t1))
     cols = call(col_kernel, out((24, 128)), *[p[0] for p in parts], *[p[1] for p in parts])
     rows = call(
         row_kernel, jax.ShapeDtypeStruct((640, 128), F32), *[p[0] for p in parts], scratch=[pltpu.VMEM((40, 128), F32)]

time: 93.7 us -> 95.9 us (1.023)
  starting transfers between devices: 42.6 us -> 40.3 us
  waiting for transfers between devices: 23.9 us -> 25.9 us
  local copies, waits for them, and re-layouts: 4.8 us -> 6.29 us
    ppermute x9, waiting for transfers between devices: 8.68 us -> 10.3 us  [along_x(): return lax.ppermute(value, 'x', [(i, (i + shift) % 4) for i in range(4)])]
    all_to_all x1, starting transfers between devices: 5.16 us -> 3.55 us  [program(): lax.all_to_all(rows.reshape(16, 40, 128), ('y', 'z'), 0, 0, tiled=True)]
    ppermute x13, waiting for transfers between devices: 14 us -> 15.6 us  [turn(): return lax.ppermute(value, ('y', 'c', 'z'), pairs)]
    unnamed x16 -> x32, local copies, waits for them, and re-layouts: 4.8 us -> 6.29 us
    ppermute x3, waiting for transfers between devices: 1.17 us -> 0.01 us  [other_core(): return lax.ppermute(value, 'c', [(0, 1), (1, 0)])]
    pallas_call x21 -> x22, Pallas kernels: 18.2 us -> 18.9 us  [call(): pl.pallas_call(kernel, out_shape=outs, in_specs=[pl.BlockSpec(memory_spac...]
where the time goes in v7:
time: 95.9 us; the launch traced here: 95.2 us
  starting transfers between devices  40.3 us (42%)
  waiting for transfers between devices  25.9 us (27%)
  Pallas kernels  19.9 us (21%)
  local copies, waits for them, and re-layouts  6.29 us (7%)
  between operations  1.65 us (2%)
  other arithmetic  1.06 us (1%)
    ppermute x13, starting transfers between devices, turn(): return lax.ppermute(value, ('y', 'c', 'z'), pairs)  24.1 us
    pallas_call x22, Pallas kernels, call(): pl.pallas_call(kernel, out_shape=outs, in_specs=[pl.BlockSpec(memory_spac...  18.9 us
    ppermute x13, waiting for transfers between devices, turn(): return lax.ppermute(value, ('y', 'c', 'z'), pairs)  15.6 us
    ppermute x9, starting transfers between devices, along_x(): return lax.ppermute(value, 'x', [(i, (i + shift) % 4) for i in range(4)])  11.7 us
    ppermute x9, waiting for transfers between devices, along_x(): return lax.ppermute(value, 'x', [(i, (i + shift) % 4) for i in range(4)])  10.3 us
    unnamed x32, local copies, waits for them, and re-layouts  6.29 us
    all_to_all x1, starting transfers between devices, program(): lax.all_to_all(rows.reshape(16, 40, 128), ('y', 'z'), 0, 0, tiled=True)  3.55 us
  transfers between devices with their start and end apart: 26, of which 13 were waited for; matrix products, arithmetic and copies ran while one was open for 1% of the time, Pallas kernels for 9%

profile of v7, /device:TPU:0, one launch (start us, length us, event | category | flops | bytes accessed | tf_op | source)
XLA Modules:
  0.0 95.2 jit_solution(7418575778308172015)
XLA Ops:
  0.6 1.0 %hold.1 = (bf16[128,512]{1,0:T(8,128)(2,1)S(1)}, bf16[128,512]{1,0:T(8,128)(2,1)S(1)}) custom-call(bf16[128,512]{1,0:T(8,128)(2,1)} %a_ref.1, bf16[128,512]{1,0:T(8,128)(2,1)} %b_ref.1), custom_call_target="tpu_custom_call" | custom-call | tf_op jit(solution)/shard_map/hold/pallas_call | solution.py:84
  1.6 3.2 %collective-permute-start.2 = (bf16[128,512]{1,0:T(8,128)(2,1)S(1)}, bf16[128,512]{1,0:T(8,128)(2,1)S(1)}, u32[]{:S(2)}, u32[]{:S(2)}) collective-permute-start(bf16[128,512]{1,0:T(8,128)(2,1)S(1)} %get-tuple-element.34.refs_0_), channel_id=1, source_target_pairs={{0,24},{1,25},{2,26},{3,27},{4,7},{5,4},{6,5},{7,6},{8,0},{9,1},{1... | collective-permute-start | bytes 393224 | tf_op jit(solution)/shard_map/ppermute | solution.py:33
  4.8 0.6 collective-permute-start.1
  5.4 1.0 %collective-permute-start = (bf16[128,512]{1,0:T(8,128)(2,1)S(1)}, bf16[128,512]{1,0:T(8,128)(2,1)S(1)}, u32[]{:S(2)}, u32[]{:S(2)}) collective-permute-start(bf16[128,512]{1,0:T(8,128)(2,1)S(1)} %get-tuple-element.34.refs_0_), channel_id=1, source_target_pairs={{0,8},{1,9},{2,10},{3,11},{4,5},{5,6},{6,7},{7,4},{8,16},{9,17},{1... | collective-permute-start | bytes 393224 | tf_op jit(solution)/shard_map/ppermute | solution.py:33
  6.4 2.3 %collective-permute-done.2.refs_3_ = bf16[128,512]{1,0:T(8,128)(2,1)S(1)} collective-permute-done((bf16[128,512]{1,0:T(8,128)(2,1)S(1)}, bf16[128,512]{1,0:T(8,128)(2,1)S(1)}, u32[]{:S(2)}, u32[]{:S(2)}) %collective-permute-start.2) | collective-permute-done | bytes 131104 | tf_op jit(solution)/shard_map/ppermute | solution.py:33
  8.7 2.6 %collective-permute-done.1.refs_2_ = bf16[128,512]{1,0:T(8,128)(2,1)S(1)} collective-permute-done((bf16[128,512]{1,0:T(8,128)(2,1)S(1)}, bf16[128,512]{1,0:T(8,128)(2,1)S(1)}, u32[]{:S(2)}, u32[]{:S(2)}) %collective-permute-start.1) | collective-permute-done | bytes 131104 | tf_op jit(solution)/shard_map/ppermute | solution.py:33
  11.4 1.3 %collective-permute-done.refs_1_ = bf16[128,512]{1,0:T(8,128)(2,1)S(1)} collective-permute-done((bf16[128,512]{1,0:T(8,128)(2,1)S(1)}, bf16[128,512]{1,0:T(8,128)(2,1)S(1)}, u32[]{:S(2)}, u32[]{:S(2)}) %collective-permute-start) | collective-permute-done | bytes 131104 | tf_op jit(solution)/shard_map/ppermute | solution.py:33
  12.7 4.1 %collective-permute-start.9 = (bf16[512,512]{1,0:T(8,128)(2,1)S(1)}, bf16[512,512]{1,0:T(8,128)(2,1)S(1)}, u32[]{:S(2)}, u32[]{:S(2)}) collective-permute-start(bf16[512,512]{1,0:T(8,128)(2,1)S(1)} %shard_map.66.im_ref.i0), channel_id=1, source_target_pairs={{0,3},{1,0},{2,1},{3,2},{4,28},{5,29},{6,30},{7,31},{8,11},{9,8},{... | collective-permute-start | bytes 1572872 | tf_op jit(solution)/shard_map/ppermute | solution.py:33
  16.8 2.8 %collective-permute-start.5 = (bf16[128,512]{1,0:T(8,128)(2,1)S(1)}, bf16[128,512]{1,0:T(8,128)(2,1)S(1)}, u32[]{:S(2)}, u32[]{:S(2)}) collective-permute-start(bf16[128,512]{1,0:T(8,128)(2,1)S(1)} %get-tuple-element.35.refs_0_), channel_id=1, source_target_pairs={{0,96},{32,0},{64,32},{96,64},{1,97},{33,1},{65,33},{97,65},{2,98}... | collective-permute-start | bytes 393224 | tf_op jit(solution)/shard_map/ppermute | solution.py:37
  19.6 0.8 collective-permute-start.4
  20.4 0.9 collective-permute-start.3
  21.3 2.2 %collective-permute-done.5.refs_3_ = bf16[128,512]{1,0:T(8,128)(2,1)S(1)} collective-permute-done((bf16[128,512]{1,0:T(8,128)(2,1)S(1)}, bf16[128,512]{1,0:T(8,128)(2,1)S(1)}, u32[]{:S(2)}, u32[]{:S(2)}) %collective-permute-start.5) | collective-permute-done | bytes 131104 | tf_op jit(solution)/shard_map/ppermute | solution.py:37
  23.5 2.6 %collective-permute-done.4.refs_2_ = bf16[128,512]{1,0:T(8,128)(2,1)S(1)} collective-permute-done((bf16[128,512]{1,0:T(8,128)(2,1)S(1)}, bf16[128,512]{1,0:T(8,128)(2,1)S(1)}, u32[]{:S(2)}, u32[]{:S(2)}) %collective-permute-start.4) | collective-permute-done | bytes 131104 | tf_op jit(solution)/shard_map/ppermute | solution.py:37
  26.2 1.3 %collective-permute-done.3.refs_1_ = bf16[128,512]{1,0:T(8,128)(2,1)S(1)} collective-permute-done((bf16[128,512]{1,0:T(8,128)(2,1)S(1)}, bf16[128,512]{1,0:T(8,128)(2,1)S(1)}, u32[]{:S(2)}, u32[]{:S(2)}) %collective-permute-start.3) | collective-permute-done | bytes 131104 | tf_op jit(solution)/shard_map/ppermute | solution.py:37
  27.6 3.3 %collective-permute-start.10 = (bf16[256,512]{1,0:T(8,128)(2,1)S(1)}, bf16[256,512]{1,0:T(8,128)(2,1)S(1)}, u32[]{:S(2)}, u32[]{:S(2)}) collective-permute-start(bf16[256,512]{1,0:T(8,128)(2,1)S(1)} %shard_map.72), channel_id=1, source_target_pairs={{0,3},{1,0},{2,1},{3,2},{4,28},{5,29},{6,30},{7,31},{8,11},{9,8},{... | collective-permute-start | bytes 786440 | tf_op jit(solution)/shard_map/ppermute | solution.py:33
  31.0 0.7 shard_map.70
  32.4 1.7 %shard_map.68 = (f32[16,128]{1,0:T(8,128)S(1)}, f32[8,1024]{1,0:T(8,128)S(1)}) custom-call(f32[1,1]{1,0:T(1,128)} %bitcast.s_ref, bf16[512,512]{1,0:T(8,128)(2,1)S(1)} %shard_map.66.im_ref.i0, bf16[512,512]{1,0:T(8,128)(2,1)S(1)} %shard_map.67.t0_ref, bf16[512,512]{1,0:T(8,128)(2,1)S(1)} %collective-permute-done.6.t1_ref), custom_call_target="tpu_custom_call" | custom-call | tf_op jit(solution)/shard_map/pallas_call | solution.py:56
  34.1 1.6 %shard_map.74 = (f32[16,128]{1,0:T(8,128)S(1)}, f32[8,1024]{1,0:T(8,128)S(1)}) custom-call(f32[1,1]{1,0:T(1,128)} %bitcast.s_ref, bf16[512,512]{1,0:T(8,128)(2,1)S(1)} %collective-permute-done.9.a_ref.im_ref.i3, bf16[512,512]{1,0:T(8,128)(2,1)S(1)} %shard_map.67.t0_ref, bf16[512,512]{1,0:T(8,128)(2,1)S(1)} %collective-permute-done.6.t1_ref), custom_call_target="tpu_custom_call" | custom-call | tf_op jit(solution)/shard_map/pallas_call | solution.py:56
  35.7 1.6 %shard_map.69 = (f32[16,128]{1,0:T(8,128)S(1)}, f32[8,1024]{1,0:T(8,128)S(1)}) custom-call(f32[1,1]{1,0:T(1,128)} %bitcast.s_ref, bf16[512,512]{1,0:T(8,128)(2,1)S(1)} %collective-permute-done.7.im_ref.a_ref.i1, bf16[512,512]{1,0:T(8,128)(2,1)S(1)} %shard_map.67.t0_ref, bf16[512,512]{1,0:T(8,128)(2,1)S(1)} %collective-permute-done.6.t1_ref), custom_call_target="tpu_custom_call" | custom-call | tf_op jit(solution)/shard_map/pallas_call | solution.py:56
  37.3 0.9 shard_map.73
  38.2 1.3 %collective-permute-done.8.im_ref.refs_0_ = bf16[256,512]{1,0:T(8,128)(2,1)S(1)} collective-permute-done((bf16[256,512]{1,0:T(8,128)(2,1)}, bf16[256,512]{1,0:T(8,128)(2,1)S(1)}, u32[]{:S(2)}, u32[]{:S(2)}) %collective-permute-start.8) | collective-permute-done | bytes 262176 | tf_op jit(solution)/shard_map/ppermute | solution.py:33
  39.5 0.9 shard_map.71
  40.4 0.8 shard_map.75
  41.2 3.6 %all-to-all-start = ((f32[16,40,128]{2,1,0:T(8,128)}), f32[16,40,128]{2,1,0:T(8,128)S(1)}, u32[]{:S(2)}, u32[]{:S(2)}) async-start(f32[16,40,128]{2,1,0:T(8,128)} %bitcast.1), calls=%async_computation | async-start | bytes 655360 | tf_op jit(solution)/shard_map/all_to_all | solution.py:407
  44.8 0.7 copy-done.5
  45.5 0.8 copy-done.7
  46.3 0.8 copy-done.9
  47.1 0.7 copy-done.11
  47.8 0.7 copy-done.13
  48.5 0.7 copy-done.15
  49.2 0.6 collective-permute-start.13
  49.8 0.8 collective-permute-start.12
  50.6 0.9 collective-permute-start.11
  51.5 1.5 %collective-permute-done.13.b3 = f32[24,128]{1,0:T(8,128)S(1)} collective-permute-done((f32[24,128]{1,0:T(8,128)S(1)}, f32[24,128]{1,0:T(8,128)S(1)}, u32[]{:S(2)}, u32[]{:S(2)}) %collective-permute-start.13) | collective-permute-done | bytes 12320 | tf_op jit(solution)/shard_map/ppermute | solution.py:37
  53.0 2.2 %collective-permute-done.12.b2 = f32[24,128]{1,0:T(8,128)S(1)} collective-permute-done((f32[24,128]{1,0:T(8,128)S(1)}, f32[24,128]{1,0:T(8,128)S(1)}, u32[]{:S(2)}, u32[]{:S(2)}) %collective-permute-start.12) | collective-permute-done | bytes 12320 | tf_op jit(solution)/shard_map/ppermute | solution.py:37
  55.1 0.5 collective-permute-done.11.b1
  55.6 0.3 collective-permute-start.14
  55.9 0.9 copy-done.1
  56.9 0.9 copy-done.3
  57.9 0.2 shard_map.78
  58.1 1.6 %shard_map.83 = (bf16[512,1024]{1,0:T(8,128)(2,1)S(1)}, f32[544,512]{1,0:T(8,128)S(1)}) custom-call(f32[1,1]{1,0:T(1,128)} %bitcast.s_ref, bf16[512,512]{1,0:T(8,128)(2,1)S(1)} %collective-permute-done.9.a_ref.im_ref.i3, f32[16,128]{1,0:T(8,128)S(1)} %get-tuple-element.46.row_ref, f32[1,1024]{1,0:T(1,128)S(1)} %get-tuple-element.47.col_ref, ...), custom_call_target="tpu_custom_call" | custom-call | tf_op jit(solution)/shard_map/pallas_call | solution.py:56
  59.7 1.6 %shard_map.82 = (bf16[512,1024]{1,0:T(8,128)(2,1)S(1)}, f32[544,512]{1,0:T(8,128)S(1)}) custom-call(f32[1,1]{1,0:T(1,128)} %bitcast.s_ref, bf16[512,512]{1,0:T(8,128)(2,1)S(1)} %collective-permute-done.7.im_ref.a_ref.i1, f32[16,128]{1,0:T(8,128)S(1)} %get-tuple-element.46.row_ref, f32[1,1024]{1,0:T(1,128)S(1)} %get-tuple-element.47.col_ref, ...), custom_call_target="tpu_custom_call" | custom-call | tf_op jit(solution)/shard_map/pallas_call | solution.py:56
  61.2 1.6 %shard_map.79 = (bf16[512,1024]{1,0:T(8,128)(2,1)S(1)}, f32[544,512]{1,0:T(8,128)S(1)}) custom-call(f32[1,1]{1,0:T(1,128)} %bitcast.s_ref, bf16[512,512]{1,0:T(8,128)(2,1)S(1)} %shard_map.66.im_ref.i0, f32[16,128]{1,0:T(8,128)S(1)} %get-tuple-element.46.row_ref, f32[1,1024]{1,0:T(1,128)S(1)} %get-tuple-element.47.col_ref, ...), custom_call_target="tpu_custom_call" | custom-call | tf_op jit(solution)/shard_map/pallas_call | solution.py:56
  62.8 1.6 %shard_map.81 = (bf16[512,1024]{1,0:T(8,128)(2,1)S(1)}, f32[544,512]{1,0:T(8,128)S(1)}) custom-call(f32[1,1]{1,0:T(1,128)} %bitcast.s_ref, bf16[512,512]{1,0:T(8,128)(2,1)S(1)} %shard_map.80.im_ref.i2, f32[16,128]{1,0:T(8,128)S(1)} %get-tuple-element.46.row_ref, f32[1,1024]{1,0:T(1,128)S(1)} %get-tuple-element.47.col_ref, ...), custom_call_target="tpu_custom_call" | custom-call | tf_op jit(solution)/shard_map/pallas_call | solution.py:56
  64.4 1.3 %shard_map.85 = f32[544,512]{1,0:T(8,128)S(1)} custom-call(bf16[512,1024]{1,0:T(8,128)(2,1)S(1)} %get-tuple-element.54.w0, bf16[512,1024]{1,0:T(8,128)(2,1)S(1)} %get-tuple-element.55.w1, bf16[512,1024]{1,0:T(8,128)(2,1)S(1)} %get-tuple-element.56.w2, bf16[512,1024]{1,0:T(8,128)(2,1)S(1)} %get-tuple-element.57.w3, bf16[512,512]{1,0:T(8,128)(2,1)S(1)} %shard_map.66.im_ref.i0, ...), custom_call_target="tpu_custom_call" | custom-call | tf_op jit(solution)/shard_map/pallas_call | solution.py:56
  65.8 0.6 collective-permute-start.21
  66.5 1.9 %collective-permute-start.17 = (f16[544,512]{1,0:T(8,128)(2,1)S(1)}, f16[544,512]{1,0:T(8,128)(2,1)S(1)}, u32[]{:S(2)}, u32[]{:S(2)}) collective-permute-start(f16[544,512]{1,0:T(8,128)(2,1)S(1)} %convert_element_type.100), channel_id=1, source_target_pairs={{0,1},{1,2},{2,3},{3,0},{4,12},{5,13},{6,14},{7,15},{8,9},{9,10},{... | collective-permute-start | bytes 1671176 | tf_op jit(solution)/shard_map/ppermute | solution.py:33
  68.5 1.5 %collective-permute-start.16 = (f16[544,512]{1,0:T(8,128)(2,1)S(1)}, f16[544,512]{1,0:T(8,128)(2,1)S(1)}, u32[]{:S(2)}, u32[]{:S(2)}) collective-permute-start(f16[544,512]{1,0:T(8,128)(2,1)S(1)} %convert_element_type.98), channel_id=1, source_target_pairs={{0,3},{1,0},{2,1},{3,2},{4,28},{5,29},{6,30},{7,31},{8,11},{9,8},{... | collective-permute-start | bytes 1671176 | tf_op jit(solution)/shard_map/ppermute | solution.py:33
  70.1 2.2 %collective-permute-start.15 = (f16[544,512]{1,0:T(8,128)(2,1)S(1)}, f16[544,512]{1,0:T(8,128)(2,1)S(1)}, u32[]{:S(2)}, u32[]{:S(2)}) collective-permute-start(f16[544,512]{1,0:T(8,128)(2,1)S(1)} %convert_element_type.96), channel_id=1, source_target_pairs={{0,2},{1,3},{2,0},{3,1},{4,20},{5,21},{6,22},{7,23},{8,10},{9,11},... | collective-permute-start | bytes 1671176 | tf_op jit(solution)/shard_map/ppermute | solution.py:33
  72.3 1.3 %shard_map.84 = f32[544,512]{1,0:T(8,128)S(1)} custom-call(bf16[512,1024]{1,0:T(8,128)(2,1)S(1)} %get-tuple-element.54.w0, bf16[512,1024]{1,0:T(8,128)(2,1)S(1)} %get-tuple-element.55.w1, bf16[512,1024]{1,0:T(8,128)(2,1)S(1)} %get-tuple-element.56.w2, bf16[512,1024]{1,0:T(8,128)(2,1)S(1)} %get-tuple-element.57.w3, bf16[512,512]{1,0:T(8,128)(2,1)S(1)} %shard_map.66.im_ref.i0, ...), custom_call_target="tpu_custom_call" | custom-call | tf_op jit(solution)/shard_map/pallas_call | solution.py:56
  73.6 0.2 fusion.2
  73.7 1.5 %collective-permute-start.22 = (f16[136,512]{1,0:T(8,128)(2,1)S(1)}, f16[136,512]{1,0:T(8,128)(2,1)S(1)}, u32[]{:S(2)}, u32[]{:S(2)}) collective-permute-start(f16[136,512]{1,0:T(8,128)(2,1)S(1)} %get-tuple-element.67), channel_id=1, source_target_pairs={{0,64},{32,96},{64,0},{96,32},{1,65},{33,97},{65,1},{97,33},{2,66}... | collective-permute-start | bytes 417800 | tf_op jit(solution)/shard_map/ppermute | solution.py:37
  75.2 1.5 %collective-permute-start.24 = (f16[136,512]{1,0:T(8,128)(2,1)S(1)}, f16[136,512]{1,0:T(8,128)(2,1)S(1)}, u32[]{:S(2)}, u32[]{:S(2)}) collective-permute-start(f16[136,512]{1,0:T(8,128)(2,1)S(1)} %get-tuple-element.68), channel_id=1, source_target_pairs={{0,32},{32,64},{64,96},{96,0},{1,33},{33,65},{65,97},{97,1},{2,34}... | collective-permute-start | bytes 417800 | tf_op jit(solution)/shard_map/ppermute | solution.py:37
  76.7 0.6 collective-permute-done.17
  77.3 2.0 %collective-permute-start.23 = (f16[136,512]{1,0:T(8,128)(2,1)S(1)}, f16[136,512]{1,0:T(8,128)(2,1)S(1)}, u32[]{:S(2)}, u32[]{:S(2)}) collective-permute-start(f16[136,512]{1,0:T(8,128)(2,1)S(1)} %get-tuple-element.69), channel_id=1, source_target_pairs={{0,96},{32,0},{64,32},{96,64},{1,97},{33,1},{65,33},{97,65},{2,98}... | collective-permute-start | bytes 417800 | tf_op jit(solution)/shard_map/ppermute | solution.py:37
  79.3 5.2 %collective-permute-done.15 = f16[544,512]{1,0:T(8,128)(2,1)S(1)} collective-permute-done((f16[544,512]{1,0:T(8,128)(2,1)S(1)}, f16[544,512]{1,0:T(8,128)(2,1)S(1)}, u32[]{:S(2)}, u32[]{:S(2)}) %collective-permute-start.15) | collective-permute-done | bytes 557088 | tf_op jit(solution)/shard_map/ppermute | solution.py:33
  84.5 0.2 add_convert_fusion.2
  84.8 3.1 %collective-permute-start.18 = (f16[136,512]{1,0:T(8,128)(2,1)S(1)}, f16[136,512]{1,0:T(8,128)(2,1)S(1)}, u32[]{:S(2)}, u32[]{:S(2)}) collective-permute-start(f16[136,512]{1,0:T(8,128)(2,1)S(1)} %get-tuple-element.64), channel_id=1, source_target_pairs={{0,16},{1,17},{2,18},{3,19},{4,6},{5,7},{6,4},{7,5},{8,24},{9,25},... | collective-permute-start | bytes 417800 | tf_op jit(solution)/shard_map/ppermute | solution.py:33
  87.8 0.6 collective-permute-start.20
  88.4 2.7 %collective-permute-start.19 = (f16[136,512]{1,0:T(8,128)(2,1)S(1)}, f16[136,512]{1,0:T(8,128)(2,1)S(1)}, u32[]{:S(2)}, u32[]{:S(2)}) collective-permute-start(f16[136,512]{1,0:T(8,128)(2,1)S(1)} %get-tuple-element.66), channel_id=1, source_target_pairs={{0,24},{1,25},{2,26},{3,27},{4,7},{5,4},{6,5},{7,6},{8,0},{9,1},{1... | collective-permute-start | bytes 417800 | tf_op jit(solution)/shard_map/ppermute | solution.py:33
  91.2 0.7 shard_map.86
  91.9 2.2 %collective-permute-done.20 = f16[136,512]{1,0:T(8,128)(2,1)S(1)} collective-permute-done((f16[136,512]{1,0:T(8,128)(2,1)S(1)}, f16[136,512]{1,0:T(8,128)(2,1)S(1)}, u32[]{:S(2)}, u32[]{:S(2)}) %collective-permute-start.20) | collective-permute-done | bytes 139296 | tf_op jit(solution)/shard_map/ppermute | solution.py:33
  94.1 0.1 add_add_fusion.g_ref
  94.3 0.9 shard_map.87
  (51 shorter events, 0.9 us)
Async XLA Ops:
  1.6 7.1 %collective-permute-start.2 = (bf16[128,512]{1,0:T(8,128)(2,1)S(1)}, bf16[128,512]{1,0:T(8,128)(2,1)S(1)}, u32[]{:S(2)}, u32[]{:S(2)}) collective-permute-start(bf16[128,512]{1,0:T(8,128)(2,1)S(1)} %get-tuple-element.34.refs_0_), channel_id=1, source_target_pairs={{0,24},{1,25},{2,26},{3,27},{4,7},{5,4},{6,5},{7,6},{8,0},{9,1},{1... | collective-permute-start | bytes 393224 | tf_op jit(solution)/shard_map/ppermute | solution.py:33
  4.8 6.6 %collective-permute-start.1 = (bf16[128,512]{1,0:T(8,128)(2,1)S(1)}, bf16[128,512]{1,0:T(8,128)(2,1)S(1)}, u32[]{:S(2)}, u32[]{:S(2)}) collective-permute-start(bf16[128,512]{1,0:T(8,128)(2,1)S(1)} %get-tuple-element.34.refs_0_), channel_id=1, source_target_pairs={{0,16},{1,17},{2,18},{3,19},{4,6},{5,7},{6,4},{7,5},{8,24},{9,25},... | collective-permute-start | bytes 393224 | tf_op jit(solution)/shard_map/ppermute | solution.py:33
  5.4 7.2 %collective-permute-start = (bf16[128,512]{1,0:T(8,128)(2,1)S(1)}, bf16[128,512]{1,0:T(8,128)(2,1)S(1)}, u32[]{:S(2)}, u32[]{:S(2)}) collective-permute-start(bf16[128,512]{1,0:T(8,128)(2,1)S(1)} %get-tuple-element.34.refs_0_), channel_id=1, source_target_pairs={{0,8},{1,9},{2,10},{3,11},{4,5},{5,6},{6,7},{7,4},{8,16},{9,17},{1... | collective-permute-start | bytes 393224 | tf_op jit(solution)/shard_map/ppermute | solution.py:33
  12.7 14.9 %collective-permute-start.9 = (bf16[512,512]{1,0:T(8,128)(2,1)S(1)}, bf16[512,512]{1,0:T(8,128)(2,1)S(1)}, u32[]{:S(2)}, u32[]{:S(2)}) collective-permute-start(bf16[512,512]{1,0:T(8,128)(2,1)S(1)} %shard_map.66.im_ref.i0), channel_id=1, source_target_pairs={{0,3},{1,0},{2,1},{3,2},{4,28},{5,29},{6,30},{7,31},{8,11},{9,8},{... | collective-permute-start | bytes 1572872 | tf_op jit(solution)/shard_map/ppermute | solution.py:33
  16.8 14.1 %collective-permute-start.7 = (bf16[512,512]{1,0:T(8,128)(2,1)S(1)}, bf16[512,512]{1,0:T(8,128)(2,1)S(1)}, u32[]{:S(2)}, u32[]{:S(2)}) collective-permute-start(bf16[512,512]{1,0:T(8,128)(2,1)S(1)} %shard_map.66.im_ref.i0), channel_id=1, source_target_pairs={{0,1},{1,2},{2,3},{3,0},{4,12},{5,13},{6,14},{7,15},{8,9},{9,10},{... | collective-permute-start | bytes 1572872 | tf_op jit(solution)/shard_map/ppermute | solution.py:33
  16.8 6.7 %collective-permute-start.5 = (bf16[128,512]{1,0:T(8,128)(2,1)S(1)}, bf16[128,512]{1,0:T(8,128)(2,1)S(1)}, u32[]{:S(2)}, u32[]{:S(2)}) collective-permute-start(bf16[128,512]{1,0:T(8,128)(2,1)S(1)} %get-tuple-element.35.refs_0_), channel_id=1, source_target_pairs={{0,96},{32,0},{64,32},{96,64},{1,97},{33,1},{65,33},{97,65},{2,98}... | collective-permute-start | bytes 393224 | tf_op jit(solution)/shard_map/ppermute | solution.py:37
  19.6 6.6 %collective-permute-start.4 = (bf16[128,512]{1,0:T(8,128)(2,1)S(1)}, bf16[128,512]{1,0:T(8,128)(2,1)S(1)}, u32[]{:S(2)}, u32[]{:S(2)}) collective-permute-start(bf16[128,512]{1,0:T(8,128)(2,1)S(1)} %get-tuple-element.35.refs_0_), channel_id=1, source_target_pairs={{0,64},{32,96},{64,0},{96,32},{1,65},{33,97},{65,1},{97,33},{2,66}... | collective-permute-start | bytes 393224 | tf_op jit(solution)/shard_map/ppermute | solution.py:37
  20.4 7.1 %collective-permute-start.3 = (bf16[128,512]{1,0:T(8,128)(2,1)S(1)}, bf16[128,512]{1,0:T(8,128)(2,1)S(1)}, u32[]{:S(2)}, u32[]{:S(2)}) collective-permute-start(bf16[128,512]{1,0:T(8,128)(2,1)S(1)} %get-tuple-element.35.refs_0_), channel_id=1, source_target_pairs={{0,32},{32,64},{64,96},{96,0},{1,33},{33,65},{65,97},{97,1},{2,34}... | collective-permute-start | bytes 393224 | tf_op jit(solution)/shard_map/ppermute | solution.py:37
  27.5 4.8 %collective-permute-start.6 = (bf16[512,512]{1,0:T(8,128)(2,1)S(1)}, bf16[512,512]{1,0:T(8,128)(2,1)S(1)}, u32[]{:S(2)}, u32[]{:S(2)}) collective-permute-start(bf16[512,512]{1,0:T(8,128)(2,1)S(1)} %shard_map.67.t0_ref), channel_id=1, source_target_pairs={{0,4},{4,0},{1,5},{5,1},{2,6},{6,2},{3,7},{7,3},{8,12},{12,8},{9,1... | collective-permute-start | bytes 1572872 | tf_op jit(solution)/shard_map/ppermute | solution.py:41
  27.6 9.6 %collective-permute-start.10 = (bf16[256,512]{1,0:T(8,128)(2,1)S(1)}, bf16[256,512]{1,0:T(8,128)(2,1)S(1)}, u32[]{:S(2)}, u32[]{:S(2)}) collective-permute-start(bf16[256,512]{1,0:T(8,128)(2,1)S(1)} %shard_map.72), channel_id=1, source_target_pairs={{0,3},{1,0},{2,1},{3,2},{4,28},{5,29},{6,30},{7,31},{8,11},{9,8},{... | collective-permute-start | bytes 786440 | tf_op jit(solution)/shard_map/ppermute | solution.py:33
  31.7 7.8 %collective-permute-start.8 = (bf16[256,512]{1,0:T(8,128)(2,1)}, bf16[256,512]{1,0:T(8,128)(2,1)S(1)}, u32[]{:S(2)}, u32[]{:S(2)}) collective-permute-start(bf16[256,512]{1,0:T(8,128)(2,1)} %shard_map.70), channel_id=1, source_target_pairs={{0,1},{1,2},{2,3},{3,0},{4,12},{5,13},{6,14},{7,15},{8,9},{9,10},{... | collective-permute-start | bytes 786440 | tf_op jit(solution)/shard_map/ppermute | solution.py:33
  37.2 3.1 %copy-start.4 = (f32[8,1024]{1,0:T(8,128)}, f32[8,1024]{1,0:T(8,128)S(1)}, u32[]{:S(2)}) copy-start(f32[8,1024]{1,0:T(8,128)S(1)} %get-tuple-element.42.c1) | copy-start | bytes 98308
  37.3 3.1 %copy-start.10 = (f32[16,128]{1,0:T(8,128)}, f32[16,128]{1,0:T(8,128)S(1)}, u32[]{:S(2)}) copy-start(f32[16,128]{1,0:T(8,128)S(1)} %get-tuple-element.37.r1) | copy-start | bytes 24580
  37.3 3.1 %copy-start = (bf16[256,512]{1,0:T(8,128)(2,1)}, bf16[256,512]{1,0:T(8,128)(2,1)S(1)}, u32[]{:S(2)}) copy-start(bf16[256,512]{1,0:T(8,128)(2,1)S(1)} %collective-permute-done.10.im_ref.refs_1_) | copy-start | bytes 786436
  38.2 3.0 %copy-start.12 = (f32[16,128]{1,0:T(8,128)}, f32[16,128]{1,0:T(8,128)S(1)}, u32[]{:S(2)}) copy-start(f32[16,128]{1,0:T(8,128)S(1)} %get-tuple-element.39.r3) | copy-start | bytes 24580
  38.2 3.0 %copy-start.6 = (f32[8,1024]{1,0:T(8,128)}, f32[8,1024]{1,0:T(8,128)S(1)}, u32[]{:S(2)}) copy-start(f32[8,1024]{1,0:T(8,128)S(1)} %get-tuple-element.44.c3) | copy-start | bytes 98308
  39.5 1.8 %copy-start.2 = (bf16[256,512]{1,0:T(8,128)(2,1)}, bf16[256,512]{1,0:T(8,128)(2,1)S(1)}, u32[]{:S(2)}) copy-start(bf16[256,512]{1,0:T(8,128)(2,1)S(1)} %collective-permute-done.8.im_ref.refs_0_) | copy-start | bytes 786436
  40.4 0.8 copy-start.14
  40.4 0.8 copy-start.8
  41.2 16.7 %all-to-all-start = ((f32[16,40,128]{2,1,0:T(8,128)}), f32[16,40,128]{2,1,0:T(8,128)S(1)}, u32[]{:S(2)}, u32[]{:S(2)}) async-start(f32[16,40,128]{2,1,0:T(8,128)} %bitcast.1), calls=%async_computation | async-start | bytes 655360 | tf_op jit(solution)/shard_map/all_to_all | solution.py:407
  44.8 0.8 copy-start.5
  45.5 0.8 copy-start.7
  46.3 0.8 copy-start.9
  47.1 0.7 copy-start.11
  47.8 0.7 copy-start.13
  48.5 0.7 copy-start.15
  49.2 3.8 %collective-permute-start.13 = (f32[24,128]{1,0:T(8,128)S(1)}, f32[24,128]{1,0:T(8,128)S(1)}, u32[]{:S(2)}, u32[]{:S(2)}) collective-permute-start(f32[24,128]{1,0:T(8,128)S(1)} %shard_map.76.b0), channel_id=1, source_target_pairs={{0,96},{32,0},{64,32},{96,64},{1,97},{33,1},{65,33},{97,65},{2,98}... | collective-permute-start | bytes 36872 | tf_op jit(solution)/shard_map/ppermute | solution.py:37
  49.8 5.3 %collective-permute-start.12 = (f32[24,128]{1,0:T(8,128)S(1)}, f32[24,128]{1,0:T(8,128)S(1)}, u32[]{:S(2)}, u32[]{:S(2)}) collective-permute-start(f32[24,128]{1,0:T(8,128)S(1)} %shard_map.76.b0), channel_id=1, source_target_pairs={{0,64},{32,96},{64,0},{96,32},{1,65},{33,97},{65,1},{97,33},{2,66}... | collective-permute-start | bytes 36872 | tf_op jit(solution)/shard_map/ppermute | solution.py:37
  50.6 5.0 %collective-permute-start.11 = (f32[24,128]{1,0:T(8,128)S(1)}, f32[24,128]{1,0:T(8,128)S(1)}, u32[]{:S(2)}, u32[]{:S(2)}) collective-permute-start(f32[24,128]{1,0:T(8,128)S(1)} %shard_map.76.b0), channel_id=1, source_target_pairs={{0,32},{32,64},{64,96},{96,0},{1,33},{33,65},{65,97},{97,1},{2,34}... | collective-permute-start | bytes 36872 | tf_op jit(solution)/shard_map/ppermute | solution.py:37
  55.6 2.2 %collective-permute-start.14 = (f32[24,128]{1,0:T(8,128)S(1)}, f32[24,128]{1,0:T(8,128)S(1)}, u32[]{:S(2)}, u32[]{:S(2)}) collective-permute-start(f32[24,128]{1,0:T(8,128)S(1)} %shard_map.77.b0), channel_id=1, source_target_pairs={{0,4},{4,0},{1,5},{5,1},{2,6},{6,2},{3,7},{7,3},{8,12},{12,8},{9,1... | collective-permute-start | bytes 36872 | tf_op jit(solution)/shard_map/ppermute | solution.py:41
  55.9 1.0 copy-start.1
  56.9 0.9 copy-start.3
  65.8 7.8 %collective-permute-start.21 = (f16[544,512]{1,0:T(8,128)(2,1)S(1)}, f16[544,512]{1,0:T(8,128)(2,1)S(1)}, u32[]{:S(2)}, u32[]{:S(2)}) collective-permute-start(f16[544,512]{1,0:T(8,128)(2,1)S(1)} %convert_element_type.117), channel_id=1, source_target_pairs={{0,4},{4,0},{1,5},{5,1},{2,6},{6,2},{3,7},{7,3},{8,12},{12,8},{9,1... | collective-permute-start | bytes 1671176 | tf_op jit(solution)/shard_map/ppermute | solution.py:41
  66.5 10.8 %collective-permute-start.17 = (f16[544,512]{1,0:T(8,128)(2,1)S(1)}, f16[544,512]{1,0:T(8,128)(2,1)S(1)}, u32[]{:S(2)}, u32[]{:S(2)}) collective-permute-start(f16[544,512]{1,0:T(8,128)(2,1)S(1)} %convert_element_type.100), channel_id=1, source_target_pairs={{0,1},{1,2},{2,3},{3,0},{4,12},{5,13},{6,14},{7,15},{8,9},{9,10},{... | collective-permute-start | bytes 1671176 | tf_op jit(solution)/shard_map/ppermute | solution.py:33
  68.5 10.8 %collective-permute-start.16 = (f16[544,512]{1,0:T(8,128)(2,1)S(1)}, f16[544,512]{1,0:T(8,128)(2,1)S(1)}, u32[]{:S(2)}, u32[]{:S(2)}) collective-permute-start(f16[544,512]{1,0:T(8,128)(2,1)S(1)} %convert_element_type.98), channel_id=1, source_target_pairs={{0,3},{1,0},{2,1},{3,2},{4,28},{5,29},{6,30},{7,31},{8,11},{9,8},{... | collective-permute-start | bytes 1671176 | tf_op jit(solution)/shard_map/ppermute | solution.py:33
  70.1 14.4 %collective-permute-start.15 = (f16[544,512]{1,0:T(8,128)(2,1)S(1)}, f16[544,512]{1,0:T(8,128)(2,1)S(1)}, u32[]{:S(2)}, u32[]{:S(2)}) collective-permute-start(f16[544,512]{1,0:T(8,128)(2,1)S(1)} %convert_element_type.96), channel_id=1, source_target_pairs={{0,2},{1,3},{2,0},{3,1},{4,20},{5,21},{6,22},{7,23},{8,10},{9,11},... | collective-permute-start | bytes 1671176 | tf_op jit(solution)/shard_map/ppermute | solution.py:33
  73.7 14.7 %collective-permute-start.22 = (f16[136,512]{1,0:T(8,128)(2,1)S(1)}, f16[136,512]{1,0:T(8,128)(2,1)S(1)}, u32[]{:S(2)}, u32[]{:S(2)}) collective-permute-start(f16[136,512]{1,0:T(8,128)(2,1)S(1)} %get-tuple-element.67), channel_id=1, source_target_pairs={{0,64},{32,96},{64,0},{96,32},{1,65},{33,97},{65,1},{97,33},{2,66}... | collective-permute-start | bytes 417800 | tf_op jit(solution)/shard_map/ppermute | solution.py:37
  75.2 15.9 %collective-permute-start.24 = (f16[136,512]{1,0:T(8,128)(2,1)S(1)}, f16[136,512]{1,0:T(8,128)(2,1)S(1)}, u32[]{:S(2)}, u32[]{:S(2)}) collective-permute-start(f16[136,512]{1,0:T(8,128)(2,1)S(1)} %get-tuple-element.68), channel_id=1, source_target_pairs={{0,32},{32,64},{64,96},{96,0},{1,33},{33,65},{65,97},{97,1},{2,34}... | collective-permute-start | bytes 417800 | tf_op jit(solution)/shard_map/ppermute | solution.py:37
  77.3 13.8 %collective-permute-start.23 = (f16[136,512]{1,0:T(8,128)(2,1)S(1)}, f16[136,512]{1,0:T(8,128)(2,1)S(1)}, u32[]{:S(2)}, u32[]{:S(2)}) collective-permute-start(f16[136,512]{1,0:T(8,128)(2,1)S(1)} %get-tuple-element.69), channel_id=1, source_target_pairs={{0,96},{32,0},{64,32},{96,64},{1,97},{33,1},{65,33},{97,65},{2,98}... | collective-permute-start | bytes 417800 | tf_op jit(solution)/shard_map/ppermute | solution.py:37
  84.8 7.1 %collective-permute-start.18 = (f16[136,512]{1,0:T(8,128)(2,1)S(1)}, f16[136,512]{1,0:T(8,128)(2,1)S(1)}, u32[]{:S(2)}, u32[]{:S(2)}) collective-permute-start(f16[136,512]{1,0:T(8,128)(2,1)S(1)} %get-tuple-element.64), channel_id=1, source_target_pairs={{0,16},{1,17},{2,18},{3,19},{4,6},{5,7},{6,4},{7,5},{8,24},{9,25},... | collective-permute-start | bytes 417800 | tf_op jit(solution)/shard_map/ppermute | solution.py:33
  87.8 6.3 %collective-permute-start.20 = (f16[136,512]{1,0:T(8,128)(2,1)S(1)}, f16[136,512]{1,0:T(8,128)(2,1)S(1)}, u32[]{:S(2)}, u32[]{:S(2)}) collective-permute-start(f16[136,512]{1,0:T(8,128)(2,1)S(1)} %get-tuple-element.65), channel_id=1, source_target_pairs={{0,8},{1,9},{2,10},{3,11},{4,5},{5,6},{6,7},{7,4},{8,16},{9,17},{1... | collective-permute-start | bytes 417800 | tf_op jit(solution)/shard_map/ppermute | solution.py:33
  88.4 5.7 %collective-permute-start.19 = (f16[136,512]{1,0:T(8,128)(2,1)S(1)}, f16[136,512]{1,0:T(8,128)(2,1)S(1)}, u32[]{:S(2)}, u32[]{:S(2)}) collective-permute-start(f16[136,512]{1,0:T(8,128)(2,1)S(1)} %get-tuple-element.66), channel_id=1, source_target_pairs={{0,24},{1,25},{2,26},{3,27},{4,7},{5,4},{6,5},{7,6},{8,0},{9,1},{1... | collective-permute-start | bytes 417800 | tf_op jit(solution)/shard_map/ppermute | solution.py:33

commit v8 on v7

--- a/solution.py
+++ b/solution.py
@@ -259,12 +259,12 @@
     return jnp.concatenate(pieces, axis=0)
 
 
-def middle_kernel(b0, b1, b2, b3, col_ref):
-    cs = (b0, b1, b2, b3)
-    lse, mean = merge([(rolled(c[0:8, :], d, 2), rolled(c[8:16, :], d, 2)) for d, c in enumerate(cs)])
+def middle_kernel(b0, b1, col_ref):
+    swapped = [jnp.concatenate([b1[k + 4 : k + 8, :], b1[k : k + 4, :]], axis=0) for k in (0, 8)]
+    lse, mean = merge([(b0[0:8, :], b0[8:16, :]), swapped])
     col_ref[0:8, :] = lse
     col_ref[8:16, :] = mean
-    col_ref[16:24, :] = greatest([c[16:24, :] for c in cs])
+    col_ref[16:24, :] = jnp.maximum(b0[16:24, :], b1[16:24, :])
 
 
 def pieces_of(value):
@@ -305,7 +305,7 @@
     return jnp.sum(jnp.sum(v, axis=0, keepdims=True), axis=1, keepdims=True)
 
 
-def end_kernel(s_ref, a_ref, b0, b1, row_ref, col_ref, codes_ref, unit_ref, back_ref, scr):
+def end_kernel(s_ref, a_ref, b0, b1, b2, b3, row_ref, col_ref, codes_ref, unit_ref, back_ref, scr):
     rs = [a_ref[40 * k : 40 * (k + 1), :] for k in range(16)]
     lse, mean = merge([(r[0:16, :], r[16:32, :]) for r in rs])
     scr[...] = lse + 1.0
@@ -315,11 +315,11 @@
     diagonal = total_of(sum(r[32:33, :] for r in rs)) * LN2
     text_peak = greatest([r[33:34, :] for r in rs])
     codes_ref[1:2, :] = encoded(total_of(lse) * LN2 - 2.0 * diagonal, 0.5 * LN2 * total_of(mean) - diagonal)
-    swapped = [jnp.concatenate([b1[k + 4 : k + 8, :], b1[k : k + 4, :]], axis=0) for k in (0, 8)]
-    lse, mean = merge([(b0[0:8, :], b0[8:16, :]), swapped])
+    cs = (b0, b1, b2, b3)
+    lse, mean = merge([(rolled(c[0:8, :], d, 2), rolled(c[8:16, :], d, 2)) for d, c in enumerate(cs)])
     for k in range(8):
         col_ref[:, 128 * k : 128 * (k + 1)] = lse[k : k + 1, :] + 1.0
-    image_peak = jnp.maximum(b0[16:17, :], b1[16:17, :])
+    image_peak = greatest([c[16:17, :] for c in cs])
     codes_ref[0:1, :] = encoded(total_of(lse) * LN2, 0.5 * LN2 * total_of(mean))
     scale = s_ref[0, 0] * LN2
     for k, top in enumerate((text_peak, image_peak)):
@@ -383,7 +383,7 @@
 def program(images, texts, log_scale):
     s2 = jnp.reshape(jnp.exp(log_scale) * LOG2E, (1, 1))
     own_images, own_texts = held(images, texts)
-    line = [own_images] + everyone(own_images, lambda v, d: turn(v, d, True))[1:]
+    line = [own_images] + everyone(images, lambda v, d: turn(v, d, True))[1:]
     line = joined(line)
     chunks = [line, None, None, None]
     for d in (1, 3):
@@ -393,20 +393,20 @@
         part = half(chunks[d], 256 * (d // 2))
         halves.append(turn(part, d, False))
     chunks[2] = joined(halves)
-    t0 = [own_texts] + everyone(own_texts, along_x)[1:]
+    t0 = [own_texts] + everyone(texts, along_x)[1:]
     t0 = joined(t0)
     t1 = other_core(t0)
     parts = []
     for k, im in (("0", chunks[0]), ("1", chunks[1]), ("2a", halves[0]), ("2b", halves[1]), ("3", chunks[3])):
         parts.append(logits_of(0 if k == "0" else 1, s2, im, t0, t1))
     cols = call(col_kernel, out((24, 128)), *[p[0] for p in parts], *[p[1] for p in parts])
+    other = other_core(cols)
     rows = call(
         row_kernel, jax.ShapeDtypeStruct((640, 128), F32), *[p[0] for p in parts], scratch=[pltpu.VMEM((40, 128), F32)]
     )
+    cols = call(middle_kernel, out((24, 128)), cols, other)
+    rows = lax.all_to_all(rows.reshape(16, 40, 128), ("y", "z"), 0, 0, tiled=True).reshape(640, 128)
     cols = everyone(cols, along_x)
-    rows = lax.all_to_all(rows.reshape(16, 40, 128), ("y", "z"), 0, 0, tiled=True).reshape(640, 128)
-    cols = call(middle_kernel, out((24, 128)), *cols)
-    cols = [cols, other_core(cols)]
     row_lse, col_lse, codes, unit, back = call(
         end_kernel,
         (out((16, 128)), out((1, 1024)), out((2, 512)), out((2, 128)), out((2, 512))),

time: 95.9 us -> 93.8 us (0.978)
  waiting for transfers between devices: 25.9 us -> 22.3 us
  starting transfers between devices: 40.3 us -> 41.7 us
    ppermute x9, waiting for transfers between devices: 10.3 us -> 6.74 us  [along_x(): return lax.ppermute(value, 'x', [(i, (i + shift) % 4) for i in range(4)])]
    all_to_all x1, starting transfers between devices: 3.55 us -> 4.81 us  [program(): lax.all_to_all(rows.reshape(16, 40, 128), ('y', 'z'), 0, 0, tiled=True)]
    ppermute x13, waiting for transfers between devices: 15.6 us -> 14.4 us  [turn(): return lax.ppermute(value, ('y', 'c', 'z'), pairs)]
    ppermute x3, waiting for transfers between devices: 0.01 us -> 1.17 us  [other_core(): return lax.ppermute(value, 'c', [(0, 1), (1, 0)])]
    unnamed x32 -> x34, local copies, waits for them, and re-layouts: 6.29 us -> 6.3 us
  transfers between devices with their start and end apart: 26 -> 26, of which waited for: 13 -> 12; matrix products, arithmetic and copies ran while one was open for 1% -> 1% of each run, Pallas kernels for 9% -> 10%
where the time goes in v8:
time: 93.8 us; the launch traced here: 93 us
  starting transfers between devices  41.7 us (44%)
  waiting for transfers between devices  22.3 us (24%)
  Pallas kernels  19.9 us (21%)
  local copies, waits for them, and re-layouts  6.3 us (7%)
  between operations  1.66 us (2%)
  other arithmetic  1.06 us (1%)
    ppermute x13, starting transfers between devices, turn(): return lax.ppermute(value, ('y', 'c', 'z'), pairs)  24.9 us
    pallas_call x22, Pallas kernels, call(): pl.pallas_call(kernel, out_shape=outs, in_specs=[pl.BlockSpec(memory_spac...  19 us
    ppermute x13, waiting for transfers between devices, turn(): return lax.ppermute(value, ('y', 'c', 'z'), pairs)  14.4 us
    ppermute x9, starting transfers between devices, along_x(): return lax.ppermute(value, 'x', [(i, (i + shift) % 4) for i in range(4)])  11.8 us
    ppermute x9, waiting for transfers between devices, along_x(): return lax.ppermute(value, 'x', [(i, (i + shift) % 4) for i in range(4)])  6.74 us
    unnamed x34, local copies, waits for them, and re-layouts  6.3 us
    all_to_all x1, starting transfers between devices, program(): lax.all_to_all(rows.reshape(16, 40, 128), ('y', 'z'), 0, 0, tiled=True)  4.81 us
  transfers between devices with their start and end apart: 26, of which 12 were waited for; matrix products, arithmetic and copies ran while one was open for 1% of the time, Pallas kernels for 10%

profile of v8, /device:TPU:0, one launch (start us, length us, event | category | flops | bytes accessed | tf_op | source)
XLA Modules:
  0.0 93.0 jit_solution(9326350076226109771)
XLA Ops:
  0.6 1.8 %collective-permute-start = (bf16[128,512]{1,0:T(8,128)(2,1)}, bf16[128,512]{1,0:T(8,128)(2,1)S(1)}, u32[]{:S(2)}, u32[]{:S(2)}) collective-permute-start(bf16[128,512]{1,0:T(8,128)(2,1)} %a_ref.1), channel_id=1, source_target_pairs={{0,8},{1,9},{2,10},{3,11},{4,5},{5,6},{6,7},{7,4},{8,16},{9,17},{1... | collective-permute-start | bytes 393224 | tf_op jit(solution)/shard_map/ppermute | solution.py:33
  2.4 1.5 %collective-permute-start.2 = (bf16[128,512]{1,0:T(8,128)(2,1)}, bf16[128,512]{1,0:T(8,128)(2,1)S(1)}, u32[]{:S(2)}, u32[]{:S(2)}) collective-permute-start(bf16[128,512]{1,0:T(8,128)(2,1)} %a_ref.1), channel_id=1, source_target_pairs={{0,24},{1,25},{2,26},{3,27},{4,7},{5,4},{6,5},{7,6},{8,0},{9,1},{1... | collective-permute-start | bytes 393224 | tf_op jit(solution)/shard_map/ppermute | solution.py:33
  3.9 2.1 %collective-permute-start.1 = (bf16[128,512]{1,0:T(8,128)(2,1)}, bf16[128,512]{1,0:T(8,128)(2,1)S(1)}, u32[]{:S(2)}, u32[]{:S(2)}) collective-permute-start(bf16[128,512]{1,0:T(8,128)(2,1)} %a_ref.1), channel_id=1, source_target_pairs={{0,16},{1,17},{2,18},{3,19},{4,6},{5,7},{6,4},{7,5},{8,24},{9,25},... | collective-permute-start | bytes 393224 | tf_op jit(solution)/shard_map/ppermute | solution.py:33
  6.0 1.0 %hold.1 = (bf16[128,512]{1,0:T(8,128)(2,1)S(1)}, bf16[128,512]{1,0:T(8,128)(2,1)S(1)}) custom-call(bf16[128,512]{1,0:T(8,128)(2,1)} %a_ref.1, bf16[128,512]{1,0:T(8,128)(2,1)} %b_ref.1), custom_call_target="tpu_custom_call" | custom-call | tf_op jit(solution)/shard_map/hold/pallas_call | solution.py:84
  7.1 0.5 collective-permute-done.2.refs_3_
  7.6 3.1 %collective-permute-done.1.refs_2_ = bf16[128,512]{1,0:T(8,128)(2,1)S(1)} collective-permute-done((bf16[128,512]{1,0:T(8,128)(2,1)}, bf16[128,512]{1,0:T(8,128)(2,1)S(1)}, u32[]{:S(2)}, u32[]{:S(2)}) %collective-permute-start.1) | collective-permute-done | bytes 131104 | tf_op jit(solution)/shard_map/ppermute | solution.py:33
  10.7 4.2 %collective-permute-start.9 = (bf16[512,512]{1,0:T(8,128)(2,1)S(1)}, bf16[512,512]{1,0:T(8,128)(2,1)S(1)}, u32[]{:S(2)}, u32[]{:S(2)}) collective-permute-start(bf16[512,512]{1,0:T(8,128)(2,1)S(1)} %shard_map.66.im_ref.i0), channel_id=1, source_target_pairs={{0,3},{1,0},{2,1},{3,2},{4,28},{5,29},{6,30},{7,31},{8,11},{9,8},{... | collective-permute-start | bytes 1572872 | tf_op jit(solution)/shard_map/ppermute | solution.py:33
  14.9 1.5 %collective-permute-start.3 = (bf16[128,512]{1,0:T(8,128)(2,1)S(1)}, bf16[128,512]{1,0:T(8,128)(2,1)S(1)}, u32[]{:S(2)}, u32[]{:S(2)}) collective-permute-start(bf16[128,512]{1,0:T(8,128)(2,1)S(1)} %copy-done.16), channel_id=1, source_target_pairs={{0,32},{32,64},{64,96},{96,0},{1,33},{33,65},{65,97},{97,1},{2,34}... | collective-permute-start | bytes 393224 | tf_op jit(solution)/shard_map/ppermute | solution.py:37
  16.4 1.7 %collective-permute-start.5 = (bf16[128,512]{1,0:T(8,128)(2,1)S(1)}, bf16[128,512]{1,0:T(8,128)(2,1)S(1)}, u32[]{:S(2)}, u32[]{:S(2)}) collective-permute-start(bf16[128,512]{1,0:T(8,128)(2,1)S(1)} %copy-done.16), channel_id=1, source_target_pairs={{0,96},{32,0},{64,32},{96,64},{1,97},{33,1},{65,33},{97,65},{2,98}... | collective-permute-start | bytes 393224 | tf_op jit(solution)/shard_map/ppermute | solution.py:37
  18.1 1.8 %collective-permute-start.4 = (bf16[128,512]{1,0:T(8,128)(2,1)S(1)}, bf16[128,512]{1,0:T(8,128)(2,1)S(1)}, u32[]{:S(2)}, u32[]{:S(2)}) collective-permute-start(bf16[128,512]{1,0:T(8,128)(2,1)S(1)} %copy-done.16), channel_id=1, source_target_pairs={{0,64},{32,96},{64,0},{96,32},{1,65},{33,97},{65,1},{97,33},{2,66}... | collective-permute-start | bytes 393224 | tf_op jit(solution)/shard_map/ppermute | solution.py:37
  19.9 2.5 %collective-permute-done.3.refs_1_ = bf16[128,512]{1,0:T(8,128)(2,1)S(1)} collective-permute-done((bf16[128,512]{1,0:T(8,128)(2,1)S(1)}, bf16[128,512]{1,0:T(8,128)(2,1)S(1)}, u32[]{:S(2)}, u32[]{:S(2)}) %collective-permute-start.3) | collective-permute-done | bytes 131104 | tf_op jit(solution)/shard_map/ppermute | solution.py:37
  22.5 2.1 %collective-permute-done.4.refs_2_ = bf16[128,512]{1,0:T(8,128)(2,1)S(1)} collective-permute-done((bf16[128,512]{1,0:T(8,128)(2,1)S(1)}, bf16[128,512]{1,0:T(8,128)(2,1)S(1)}, u32[]{:S(2)}, u32[]{:S(2)}) %collective-permute-start.4) | collective-permute-done | bytes 131104 | tf_op jit(solution)/shard_map/ppermute | solution.py:37
  24.8 3.3 %collective-permute-start.10 = (bf16[256,512]{1,0:T(8,128)(2,1)S(1)}, bf16[256,512]{1,0:T(8,128)(2,1)S(1)}, u32[]{:S(2)}, u32[]{:S(2)}) collective-permute-start(bf16[256,512]{1,0:T(8,128)(2,1)S(1)} %shard_map.72), channel_id=1, source_target_pairs={{0,3},{1,0},{2,1},{3,2},{4,28},{5,29},{6,30},{7,31},{8,11},{9,8},{... | collective-permute-start | bytes 786440 | tf_op jit(solution)/shard_map/ppermute | solution.py:33
  28.1 0.7 shard_map.70
  29.5 1.7 %shard_map.68 = (f32[16,128]{1,0:T(8,128)S(1)}, f32[8,1024]{1,0:T(8,128)S(1)}) custom-call(f32[1,1]{1,0:T(1,128)} %bitcast.s_ref, bf16[512,512]{1,0:T(8,128)(2,1)S(1)} %shard_map.66.im_ref.i0, bf16[512,512]{1,0:T(8,128)(2,1)S(1)} %shard_map.67.t0_ref, bf16[512,512]{1,0:T(8,128)(2,1)S(1)} %collective-permute-done.6.t1_ref), custom_call_target="tpu_custom_call" | custom-call | tf_op jit(solution)/shard_map/pallas_call | solution.py:56
  31.2 1.6 %shard_map.74 = (f32[16,128]{1,0:T(8,128)S(1)}, f32[8,1024]{1,0:T(8,128)S(1)}) custom-call(f32[1,1]{1,0:T(1,128)} %bitcast.s_ref, bf16[512,512]{1,0:T(8,128)(2,1)S(1)} %collective-permute-done.9.a_ref.im_ref.i3, bf16[512,512]{1,0:T(8,128)(2,1)S(1)} %shard_map.67.t0_ref, bf16[512,512]{1,0:T(8,128)(2,1)S(1)} %collective-permute-done.6.t1_ref), custom_call_target="tpu_custom_call" | custom-call | tf_op jit(solution)/shard_map/pallas_call | solution.py:56
  32.8 1.6 %shard_map.69 = (f32[16,128]{1,0:T(8,128)S(1)}, f32[8,1024]{1,0:T(8,128)S(1)}) custom-call(f32[1,1]{1,0:T(1,128)} %bitcast.s_ref, bf16[512,512]{1,0:T(8,128)(2,1)S(1)} %collective-permute-done.7.im_ref.a_ref.i1, bf16[512,512]{1,0:T(8,128)(2,1)S(1)} %shard_map.67.t0_ref, bf16[512,512]{1,0:T(8,128)(2,1)S(1)} %collective-permute-done.6.t1_ref), custom_call_target="tpu_custom_call" | custom-call | tf_op jit(solution)/shard_map/pallas_call | solution.py:56
  34.4 0.9 shard_map.73
  35.3 1.3 %collective-permute-done.8.im_ref.refs_0_ = bf16[256,512]{1,0:T(8,128)(2,1)S(1)} collective-permute-done((bf16[256,512]{1,0:T(8,128)(2,1)}, bf16[256,512]{1,0:T(8,128)(2,1)S(1)}, u32[]{:S(2)}, u32[]{:S(2)}) %collective-permute-start.8) | collective-permute-done | bytes 262176 | tf_op jit(solution)/shard_map/ppermute | solution.py:33
  36.6 0.9 shard_map.71
  37.5 0.8 shard_map.75
  38.4 4.8 %all-to-all-start = ((f32[16,40,128]{2,1,0:T(8,128)}), f32[16,40,128]{2,1,0:T(8,128)S(1)}, u32[]{:S(2)}, u32[]{:S(2)}) async-start(f32[16,40,128]{2,1,0:T(8,128)} %bitcast.1), calls=%async_computation | async-start | bytes 655360 | tf_op jit(solution)/shard_map/all_to_all | solution.py:408
  43.2 0.7 copy-done.5
  43.9 0.8 copy-done.7
  44.7 0.8 copy-done.9
  45.5 0.7 copy-done.11
  46.2 0.7 copy-done.13
  46.9 0.7 copy-done.15
  47.7 1.2 %collective-permute-done.11.b1 = f32[24,128]{1,0:T(8,128)S(1)} collective-permute-done((f32[24,128]{1,0:T(8,128)S(1)}, f32[24,128]{1,0:T(8,128)S(1)}, u32[]{:S(2)}, u32[]{:S(2)}) %collective-permute-start.11) | collective-permute-done | bytes 12320 | tf_op jit(solution)/shard_map/ppermute | solution.py:41
  48.9 1.6 %collective-permute-start.14 = (f32[24,128]{1,0:T(8,128)S(1)}, f32[24,128]{1,0:T(8,128)S(1)}, u32[]{:S(2)}, u32[]{:S(2)}) collective-permute-start(f32[24,128]{1,0:T(8,128)S(1)} %shard_map.77.b0), channel_id=1, source_target_pairs={{0,96},{32,0},{64,32},{96,64},{1,97},{33,1},{65,33},{97,65},{2,98}... | collective-permute-start | bytes 36872 | tf_op jit(solution)/shard_map/ppermute | solution.py:37
  50.5 0.8 collective-permute-start.13
  51.3 0.9 collective-permute-start.12
  52.2 0.9 %copy-done.1 = bf16[256,512]{1,0:T(8,128)(2,1)S(1)} copy-done((bf16[256,512]{1,0:T(8,128)(2,1)S(1)}, bf16[256,512]{1,0:T(8,128)(2,1)}, u32[]{:S(2)}) %copy-start.1) | copy-done | bytes 262168
  53.1 0.9 %copy-done.3 = bf16[256,512]{1,0:T(8,128)(2,1)S(1)} copy-done((bf16[256,512]{1,0:T(8,128)(2,1)S(1)}, bf16[256,512]{1,0:T(8,128)(2,1)}, u32[]{:S(2)}) %copy-start.3) | copy-done | bytes 262168
  54.1 1.6 %collective-permute-done.13.b2 = f32[24,128]{1,0:T(8,128)S(1)} collective-permute-done((f32[24,128]{1,0:T(8,128)S(1)}, f32[24,128]{1,0:T(8,128)S(1)}, u32[]{:S(2)}, u32[]{:S(2)}) %collective-permute-start.13) | collective-permute-done | bytes 12320 | tf_op jit(solution)/shard_map/ppermute | solution.py:37
  55.7 0.5 collective-permute-done.12.b1
  56.2 0.2 shard_map.78
  56.4 1.6 %shard_map.83 = (bf16[512,1024]{1,0:T(8,128)(2,1)S(1)}, f32[544,512]{1,0:T(8,128)S(1)}) custom-call(f32[1,1]{1,0:T(1,128)} %bitcast.s_ref, bf16[512,512]{1,0:T(8,128)(2,1)S(1)} %collective-permute-done.9.a_ref.im_ref.i3, f32[16,128]{1,0:T(8,128)S(1)} %get-tuple-element.46.row_ref, f32[1,1024]{1,0:T(1,128)S(1)} %get-tuple-element.47.col_ref, ...), custom_call_target="tpu_custom_call" | custom-call | tf_op jit(solution)/shard_map/pallas_call | solution.py:56
  58.0 1.6 %shard_map.82 = (bf16[512,1024]{1,0:T(8,128)(2,1)S(1)}, f32[544,512]{1,0:T(8,128)S(1)}) custom-call(f32[1,1]{1,0:T(1,128)} %bitcast.s_ref, bf16[512,512]{1,0:T(8,128)(2,1)S(1)} %collective-permute-done.7.im_ref.a_ref.i1, f32[16,128]{1,0:T(8,128)S(1)} %get-tuple-element.46.row_ref, f32[1,1024]{1,0:T(1,128)S(1)} %get-tuple-element.47.col_ref, ...), custom_call_target="tpu_custom_call" | custom-call | tf_op jit(solution)/shard_map/pallas_call | solution.py:56
  59.5 1.6 %shard_map.79 = (bf16[512,1024]{1,0:T(8,128)(2,1)S(1)}, f32[544,512]{1,0:T(8,128)S(1)}) custom-call(f32[1,1]{1,0:T(1,128)} %bitcast.s_ref, bf16[512,512]{1,0:T(8,128)(2,1)S(1)} %shard_map.66.im_ref.i0, f32[16,128]{1,0:T(8,128)S(1)} %get-tuple-element.46.row_ref, f32[1,1024]{1,0:T(1,128)S(1)} %get-tuple-element.47.col_ref, ...), custom_call_target="tpu_custom_call" | custom-call | tf_op jit(solution)/shard_map/pallas_call | solution.py:56
  61.1 1.6 %shard_map.81 = (bf16[512,1024]{1,0:T(8,128)(2,1)S(1)}, f32[544,512]{1,0:T(8,128)S(1)}) custom-call(f32[1,1]{1,0:T(1,128)} %bitcast.s_ref, bf16[512,512]{1,0:T(8,128)(2,1)S(1)} %shard_map.80.im_ref.i2, f32[16,128]{1,0:T(8,128)S(1)} %get-tuple-element.46.row_ref, f32[1,1024]{1,0:T(1,128)S(1)} %get-tuple-element.47.col_ref, ...), custom_call_target="tpu_custom_call" | custom-call | tf_op jit(solution)/shard_map/pallas_call | solution.py:56
  62.7 1.3 %shard_map.85 = f32[544,512]{1,0:T(8,128)S(1)} custom-call(bf16[512,1024]{1,0:T(8,128)(2,1)S(1)} %get-tuple-element.54.w0, bf16[512,1024]{1,0:T(8,128)(2,1)S(1)} %get-tuple-element.55.w1, bf16[512,1024]{1,0:T(8,128)(2,1)S(1)} %get-tuple-element.56.w2, bf16[512,1024]{1,0:T(8,128)(2,1)S(1)} %get-tuple-element.57.w3, bf16[512,512]{1,0:T(8,128)(2,1)S(1)} %shard_map.66.im_ref.i0, ...), custom_call_target="tpu_custom_call" | custom-call | tf_op jit(solution)/shard_map/pallas_call | solution.py:56
  64.0 0.1 convert_element_type.117
  64.2 0.1 convert_element_type.100
  64.3 2.0 %collective-permute-start.17 = (f16[544,512]{1,0:T(8,128)(2,1)S(1)}, f16[544,512]{1,0:T(8,128)(2,1)S(1)}, u32[]{:S(2)}, u32[]{:S(2)}) collective-permute-start(f16[544,512]{1,0:T(8,128)(2,1)S(1)} %convert_element_type.100), channel_id=1, source_target_pairs={{0,1},{1,2},{2,3},{3,0},{4,12},{5,13},{6,14},{7,15},{8,9},{9,10},{... | collective-permute-start | bytes 1671176 | tf_op jit(solution)/shard_map/ppermute | solution.py:33
  66.3 0.1 convert_element_type.98
  66.4 1.4 %collective-permute-start.16 = (f16[544,512]{1,0:T(8,128)(2,1)S(1)}, f16[544,512]{1,0:T(8,128)(2,1)S(1)}, u32[]{:S(2)}, u32[]{:S(2)}) collective-permute-start(f16[544,512]{1,0:T(8,128)(2,1)S(1)} %convert_element_type.98), channel_id=1, source_target_pairs={{0,3},{1,0},{2,1},{3,2},{4,28},{5,29},{6,30},{7,31},{8,11},{9,8},{... | collective-permute-start | bytes 1671176 | tf_op jit(solution)/shard_map/ppermute | solution.py:33
  67.8 0.1 convert_element_type.96
  67.9 2.3 %collective-permute-start.15 = (f16[544,512]{1,0:T(8,128)(2,1)S(1)}, f16[544,512]{1,0:T(8,128)(2,1)S(1)}, u32[]{:S(2)}, u32[]{:S(2)}) collective-permute-start(f16[544,512]{1,0:T(8,128)(2,1)S(1)} %convert_element_type.96), channel_id=1, source_target_pairs={{0,2},{1,3},{2,0},{3,1},{4,20},{5,21},{6,22},{7,23},{8,10},{9,11},... | collective-permute-start | bytes 1671176 | tf_op jit(solution)/shard_map/ppermute | solution.py:33
  70.2 1.3 %shard_map.84 = f32[544,512]{1,0:T(8,128)S(1)} custom-call(bf16[512,1024]{1,0:T(8,128)(2,1)S(1)} %get-tuple-element.54.w0, bf16[512,1024]{1,0:T(8,128)(2,1)S(1)} %get-tuple-element.55.w1, bf16[512,1024]{1,0:T(8,128)(2,1)S(1)} %get-tuple-element.56.w2, bf16[512,1024]{1,0:T(8,128)(2,1)S(1)} %get-tuple-element.57.w3, bf16[512,512]{1,0:T(8,128)(2,1)S(1)} %shard_map.66.im_ref.i0, ...), custom_call_target="tpu_custom_call" | custom-call | tf_op jit(solution)/shard_map/pallas_call | solution.py:56
  71.5 0.2 fusion.2
  71.7 1.6 %collective-permute-start.22 = (f16[136,512]{1,0:T(8,128)(2,1)S(1)}, f16[136,512]{1,0:T(8,128)(2,1)S(1)}, u32[]{:S(2)}, u32[]{:S(2)}) collective-permute-start(f16[136,512]{1,0:T(8,128)(2,1)S(1)} %get-tuple-element.67), channel_id=1, source_target_pairs={{0,64},{32,96},{64,0},{96,32},{1,65},{33,97},{65,1},{97,33},{2,66}... | collective-permute-start | bytes 417800 | tf_op jit(solution)/shard_map/ppermute | solution.py:37
  73.2 0.5 collective-permute-start.24
  73.7 1.4 %collective-permute-done.17 = f16[544,512]{1,0:T(8,128)(2,1)S(1)} collective-permute-done((f16[544,512]{1,0:T(8,128)(2,1)S(1)}, f16[544,512]{1,0:T(8,128)(2,1)S(1)}, u32[]{:S(2)}, u32[]{:S(2)}) %collective-permute-start.17) | collective-permute-done | bytes 557088 | tf_op jit(solution)/shard_map/ppermute | solution.py:33
  75.1 1.4 %collective-permute-start.23 = (f16[136,512]{1,0:T(8,128)(2,1)S(1)}, f16[136,512]{1,0:T(8,128)(2,1)S(1)}, u32[]{:S(2)}, u32[]{:S(2)}) collective-permute-start(f16[136,512]{1,0:T(8,128)(2,1)S(1)} %get-tuple-element.69), channel_id=1, source_target_pairs={{0,96},{32,0},{64,32},{96,64},{1,97},{33,1},{65,33},{97,65},{2,98}... | collective-permute-start | bytes 417800 | tf_op jit(solution)/shard_map/ppermute | solution.py:37
  76.5 5.9 %collective-permute-done.15 = f16[544,512]{1,0:T(8,128)(2,1)S(1)} collective-permute-done((f16[544,512]{1,0:T(8,128)(2,1)S(1)}, f16[544,512]{1,0:T(8,128)(2,1)S(1)}, u32[]{:S(2)}, u32[]{:S(2)}) %collective-permute-start.15) | collective-permute-done | bytes 557088 | tf_op jit(solution)/shard_map/ppermute | solution.py:33
  82.4 0.2 add_convert_fusion.2
  82.7 3.0 %collective-permute-start.18 = (f16[136,512]{1,0:T(8,128)(2,1)S(1)}, f16[136,512]{1,0:T(8,128)(2,1)S(1)}, u32[]{:S(2)}, u32[]{:S(2)}) collective-permute-start(f16[136,512]{1,0:T(8,128)(2,1)S(1)} %get-tuple-element.64), channel_id=1, source_target_pairs={{0,16},{1,17},{2,18},{3,19},{4,6},{5,7},{6,4},{7,5},{8,24},{9,25},... | collective-permute-start | bytes 417800 | tf_op jit(solution)/shard_map/ppermute | solution.py:33
  85.7 0.6 collective-permute-start.20
  86.3 2.7 %collective-permute-start.19 = (f16[136,512]{1,0:T(8,128)(2,1)S(1)}, f16[136,512]{1,0:T(8,128)(2,1)S(1)}, u32[]{:S(2)}, u32[]{:S(2)}) collective-permute-start(f16[136,512]{1,0:T(8,128)(2,1)S(1)} %get-tuple-element.66), channel_id=1, source_target_pairs={{0,24},{1,25},{2,26},{3,27},{4,7},{5,4},{6,5},{7,6},{8,0},{9,1},{1... | collective-permute-start | bytes 417800 | tf_op jit(solution)/shard_map/ppermute | solution.py:33
  89.1 0.7 shard_map.86
  89.8 2.2 %collective-permute-done.20 = f16[136,512]{1,0:T(8,128)(2,1)S(1)} collective-permute-done((f16[136,512]{1,0:T(8,128)(2,1)S(1)}, f16[136,512]{1,0:T(8,128)(2,1)S(1)}, u32[]{:S(2)}, u32[]{:S(2)}) %collective-permute-start.20) | collective-permute-done | bytes 139296 | tf_op jit(solution)/shard_map/ppermute | solution.py:33
  92.0 0.1 add_add_fusion.g_ref
  92.1 0.9 shard_map.87
  (53 shorter events, 0.7 us)
Async XLA Ops:
  0.6 14.3 %copy-start.16 = (bf16[128,512]{1,0:T(8,128)(2,1)S(1)}, bf16[128,512]{1,0:T(8,128)(2,1)}, u32[]{:S(2)}) copy-start(bf16[128,512]{1,0:T(8,128)(2,1)} %b_ref.1) | copy-start | bytes 393220
  0.6 6.5 %collective-permute-start = (bf16[128,512]{1,0:T(8,128)(2,1)}, bf16[128,512]{1,0:T(8,128)(2,1)S(1)}, u32[]{:S(2)}, u32[]{:S(2)}) collective-permute-start(bf16[128,512]{1,0:T(8,128)(2,1)} %a_ref.1), channel_id=1, source_target_pairs={{0,8},{1,9},{2,10},{3,11},{4,5},{5,6},{6,7},{7,4},{8,16},{9,17},{1... | collective-permute-start | bytes 393224 | tf_op jit(solution)/shard_map/ppermute | solution.py:33
  2.4 5.2 %collective-permute-start.2 = (bf16[128,512]{1,0:T(8,128)(2,1)}, bf16[128,512]{1,0:T(8,128)(2,1)S(1)}, u32[]{:S(2)}, u32[]{:S(2)}) collective-permute-start(bf16[128,512]{1,0:T(8,128)(2,1)} %a_ref.1), channel_id=1, source_target_pairs={{0,24},{1,25},{2,26},{3,27},{4,7},{5,4},{6,5},{7,6},{8,0},{9,1},{1... | collective-permute-start | bytes 393224 | tf_op jit(solution)/shard_map/ppermute | solution.py:33
  3.9 6.7 %collective-permute-start.1 = (bf16[128,512]{1,0:T(8,128)(2,1)}, bf16[128,512]{1,0:T(8,128)(2,1)S(1)}, u32[]{:S(2)}, u32[]{:S(2)}) collective-permute-start(bf16[128,512]{1,0:T(8,128)(2,1)} %a_ref.1), channel_id=1, source_target_pairs={{0,16},{1,17},{2,18},{3,19},{4,6},{5,7},{6,4},{7,5},{8,24},{9,25},... | collective-permute-start | bytes 393224 | tf_op jit(solution)/shard_map/ppermute | solution.py:33
  10.7 14.1 %collective-permute-start.9 = (bf16[512,512]{1,0:T(8,128)(2,1)S(1)}, bf16[512,512]{1,0:T(8,128)(2,1)S(1)}, u32[]{:S(2)}, u32[]{:S(2)}) collective-permute-start(bf16[512,512]{1,0:T(8,128)(2,1)S(1)} %shard_map.66.im_ref.i0), channel_id=1, source_target_pairs={{0,3},{1,0},{2,1},{3,2},{4,28},{5,29},{6,30},{7,31},{8,11},{9,8},{... | collective-permute-start | bytes 1572872 | tf_op jit(solution)/shard_map/ppermute | solution.py:33
  14.9 13.2 %collective-permute-start.7 = (bf16[512,512]{1,0:T(8,128)(2,1)S(1)}, bf16[512,512]{1,0:T(8,128)(2,1)S(1)}, u32[]{:S(2)}, u32[]{:S(2)}) collective-permute-start(bf16[512,512]{1,0:T(8,128)(2,1)S(1)} %shard_map.66.im_ref.i0), channel_id=1, source_target_pairs={{0,1},{1,2},{2,3},{3,0},{4,12},{5,13},{6,14},{7,15},{8,9},{9,10},{... | collective-permute-start | bytes 1572872 | tf_op jit(solution)/shard_map/ppermute | solution.py:33
  14.9 7.6 %collective-permute-start.3 = (bf16[128,512]{1,0:T(8,128)(2,1)S(1)}, bf16[128,512]{1,0:T(8,128)(2,1)S(1)}, u32[]{:S(2)}, u32[]{:S(2)}) collective-permute-start(bf16[128,512]{1,0:T(8,128)(2,1)S(1)} %copy-done.16), channel_id=1, source_target_pairs={{0,32},{32,64},{64,96},{96,0},{1,33},{33,65},{65,97},{97,1},{2,34}... | collective-permute-start | bytes 393224 | tf_op jit(solution)/shard_map/ppermute | solution.py:37
  16.4 6.1 %collective-permute-start.5 = (bf16[128,512]{1,0:T(8,128)(2,1)S(1)}, bf16[128,512]{1,0:T(8,128)(2,1)S(1)}, u32[]{:S(2)}, u32[]{:S(2)}) collective-permute-start(bf16[128,512]{1,0:T(8,128)(2,1)S(1)} %copy-done.16), channel_id=1, source_target_pairs={{0,96},{32,0},{64,32},{96,64},{1,97},{33,1},{65,33},{97,65},{2,98}... | collective-permute-start | bytes 393224 | tf_op jit(solution)/shard_map/ppermute | solution.py:37
  18.1 6.5 %collective-permute-start.4 = (bf16[128,512]{1,0:T(8,128)(2,1)S(1)}, bf16[128,512]{1,0:T(8,128)(2,1)S(1)}, u32[]{:S(2)}, u32[]{:S(2)}) collective-permute-start(bf16[128,512]{1,0:T(8,128)(2,1)S(1)} %copy-done.16), channel_id=1, source_target_pairs={{0,64},{32,96},{64,0},{96,32},{1,65},{33,97},{65,1},{97,33},{2,66}... | collective-permute-start | bytes 393224 | tf_op jit(solution)/shard_map/ppermute | solution.py:37
  24.6 4.8 %collective-permute-start.6 = (bf16[512,512]{1,0:T(8,128)(2,1)S(1)}, bf16[512,512]{1,0:T(8,128)(2,1)S(1)}, u32[]{:S(2)}, u32[]{:S(2)}) collective-permute-start(bf16[512,512]{1,0:T(8,128)(2,1)S(1)} %shard_map.67.t0_ref), channel_id=1, source_target_pairs={{0,4},{4,0},{1,5},{5,1},{2,6},{6,2},{3,7},{7,3},{8,12},{12,8},{9,1... | collective-permute-start | bytes 1572872 | tf_op jit(solution)/shard_map/ppermute | solution.py:41
  24.8 9.6 %collective-permute-start.10 = (bf16[256,512]{1,0:T(8,128)(2,1)S(1)}, bf16[256,512]{1,0:T(8,128)(2,1)S(1)}, u32[]{:S(2)}, u32[]{:S(2)}) collective-permute-start(bf16[256,512]{1,0:T(8,128)(2,1)S(1)} %shard_map.72), channel_id=1, source_target_pairs={{0,3},{1,0},{2,1},{3,2},{4,28},{5,29},{6,30},{7,31},{8,11},{9,8},{... | collective-permute-start | bytes 786440 | tf_op jit(solution)/shard_map/ppermute | solution.py:33
  28.8 7.8 %collective-permute-start.8 = (bf16[256,512]{1,0:T(8,128)(2,1)}, bf16[256,512]{1,0:T(8,128)(2,1)S(1)}, u32[]{:S(2)}, u32[]{:S(2)}) collective-permute-start(bf16[256,512]{1,0:T(8,128)(2,1)} %shard_map.70), channel_id=1, source_target_pairs={{0,1},{1,2},{2,3},{3,0},{4,12},{5,13},{6,14},{7,15},{8,9},{9,10},{... | collective-permute-start | bytes 786440 | tf_op jit(solution)/shard_map/ppermute | solution.py:33
  34.4 3.1 %copy-start.4 = (f32[8,1024]{1,0:T(8,128)}, f32[8,1024]{1,0:T(8,128)S(1)}, u32[]{:S(2)}) copy-start(f32[8,1024]{1,0:T(8,128)S(1)} %get-tuple-element.42.c1) | copy-start | bytes 98308
  34.4 3.1 %copy-start.10 = (f32[16,128]{1,0:T(8,128)}, f32[16,128]{1,0:T(8,128)S(1)}, u32[]{:S(2)}) copy-start(f32[16,128]{1,0:T(8,128)S(1)} %get-tuple-element.37.r1) | copy-start | bytes 24580
  34.4 3.1 %copy-start = (bf16[256,512]{1,0:T(8,128)(2,1)}, bf16[256,512]{1,0:T(8,128)(2,1)S(1)}, u32[]{:S(2)}) copy-start(bf16[256,512]{1,0:T(8,128)(2,1)S(1)} %collective-permute-done.10.im_ref.refs_1_) | copy-start | bytes 786436
  35.3 3.0 %copy-start.12 = (f32[16,128]{1,0:T(8,128)}, f32[16,128]{1,0:T(8,128)S(1)}, u32[]{:S(2)}) copy-start(f32[16,128]{1,0:T(8,128)S(1)} %get-tuple-element.39.r3) | copy-start | bytes 24580
  35.3 3.0 %copy-start.6 = (f32[8,1024]{1,0:T(8,128)}, f32[8,1024]{1,0:T(8,128)S(1)}, u32[]{:S(2)}) copy-start(f32[8,1024]{1,0:T(8,128)S(1)} %get-tuple-element.44.c3) | copy-start | bytes 98308
  36.6 1.8 %copy-start.2 = (bf16[256,512]{1,0:T(8,128)(2,1)}, bf16[256,512]{1,0:T(8,128)(2,1)S(1)}, u32[]{:S(2)}) copy-start(bf16[256,512]{1,0:T(8,128)(2,1)S(1)} %collective-permute-done.8.im_ref.refs_0_) | copy-start | bytes 786436
  37.5 0.8 copy-start.14
  37.5 0.8 copy-start.8
  38.4 17.8 %all-to-all-start = ((f32[16,40,128]{2,1,0:T(8,128)}), f32[16,40,128]{2,1,0:T(8,128)S(1)}, u32[]{:S(2)}, u32[]{:S(2)}) async-start(f32[16,40,128]{2,1,0:T(8,128)} %bitcast.1), calls=%async_computation | async-start | bytes 655360 | tf_op jit(solution)/shard_map/all_to_all | solution.py:408
  43.2 0.8 copy-start.5
  43.9 0.8 copy-start.7
  44.7 0.8 copy-start.9
  45.5 0.7 copy-start.11
  46.2 0.7 copy-start.13
  46.9 0.7 copy-start.15
  47.6 1.3 %collective-permute-start.11 = (f32[24,128]{1,0:T(8,128)S(1)}, f32[24,128]{1,0:T(8,128)S(1)}, u32[]{:S(2)}, u32[]{:S(2)}) collective-permute-start(f32[24,128]{1,0:T(8,128)S(1)} %shard_map.76.b0), channel_id=1, source_target_pairs={{0,4},{4,0},{1,5},{5,1},{2,6},{6,2},{3,7},{7,3},{8,12},{12,8},{9,1... | collective-permute-start | bytes 36872 | tf_op jit(solution)/shard_map/ppermute | solution.py:41
  48.9 5.2 %collective-permute-start.14 = (f32[24,128]{1,0:T(8,128)S(1)}, f32[24,128]{1,0:T(8,128)S(1)}, u32[]{:S(2)}, u32[]{:S(2)}) collective-permute-start(f32[24,128]{1,0:T(8,128)S(1)} %shard_map.77.b0), channel_id=1, source_target_pairs={{0,96},{32,0},{64,32},{96,64},{1,97},{33,1},{65,33},{97,65},{2,98}... | collective-permute-start | bytes 36872 | tf_op jit(solution)/shard_map/ppermute | solution.py:37
  50.5 5.2 %collective-permute-start.13 = (f32[24,128]{1,0:T(8,128)S(1)}, f32[24,128]{1,0:T(8,128)S(1)}, u32[]{:S(2)}, u32[]{:S(2)}) collective-permute-start(f32[24,128]{1,0:T(8,128)S(1)} %shard_map.77.b0), channel_id=1, source_target_pairs={{0,64},{32,96},{64,0},{96,32},{1,65},{33,97},{65,1},{97,33},{2,66}... | collective-permute-start | bytes 36872 | tf_op jit(solution)/shard_map/ppermute | solution.py:37
  51.3 4.9 %collective-permute-start.12 = (f32[24,128]{1,0:T(8,128)S(1)}, f32[24,128]{1,0:T(8,128)S(1)}, u32[]{:S(2)}, u32[]{:S(2)}) collective-permute-start(f32[24,128]{1,0:T(8,128)S(1)} %shard_map.77.b0), channel_id=1, source_target_pairs={{0,32},{32,64},{64,96},{96,0},{1,33},{33,65},{65,97},{97,1},{2,34}... | collective-permute-start | bytes 36872 | tf_op jit(solution)/shard_map/ppermute | solution.py:37
  52.2 0.9 %copy-start.1 = (bf16[256,512]{1,0:T(8,128)(2,1)S(1)}, bf16[256,512]{1,0:T(8,128)(2,1)}, u32[]{:S(2)}) copy-start(bf16[256,512]{1,0:T(8,128)(2,1)} %copy-done) | copy-start | bytes 786436
  53.1 0.9 %copy-start.3 = (bf16[256,512]{1,0:T(8,128)(2,1)S(1)}, bf16[256,512]{1,0:T(8,128)(2,1)}, u32[]{:S(2)}) copy-start(bf16[256,512]{1,0:T(8,128)(2,1)} %copy-done.2) | copy-start | bytes 786436
  64.1 7.4 %collective-permute-start.21 = (f16[544,512]{1,0:T(8,128)(2,1)S(1)}, f16[544,512]{1,0:T(8,128)(2,1)S(1)}, u32[]{:S(2)}, u32[]{:S(2)}) collective-permute-start(f16[544,512]{1,0:T(8,128)(2,1)S(1)} %convert_element_type.117), channel_id=1, source_target_pairs={{0,4},{4,0},{1,5},{5,1},{2,6},{6,2},{3,7},{7,3},{8,12},{12,8},{9,1... | collective-permute-start | bytes 1671176 | tf_op jit(solution)/shard_map/ppermute | solution.py:41
  64.3 10.8 %collective-permute-start.17 = (f16[544,512]{1,0:T(8,128)(2,1)S(1)}, f16[544,512]{1,0:T(8,128)(2,1)S(1)}, u32[]{:S(2)}, u32[]{:S(2)}) collective-permute-start(f16[544,512]{1,0:T(8,128)(2,1)S(1)} %convert_element_type.100), channel_id=1, source_target_pairs={{0,1},{1,2},{2,3},{3,0},{4,12},{5,13},{6,14},{7,15},{8,9},{9,10},{... | collective-permute-start | bytes 1671176 | tf_op jit(solution)/shard_map/ppermute | solution.py:33
  66.4 10.1 %collective-permute-start.16 = (f16[544,512]{1,0:T(8,128)(2,1)S(1)}, f16[544,512]{1,0:T(8,128)(2,1)S(1)}, u32[]{:S(2)}, u32[]{:S(2)}) collective-permute-start(f16[544,512]{1,0:T(8,128)(2,1)S(1)} %convert_element_type.98), channel_id=1, source_target_pairs={{0,3},{1,0},{2,1},{3,2},{4,28},{5,29},{6,30},{7,31},{8,11},{9,8},{... | collective-permute-start | bytes 1671176 | tf_op jit(solution)/shard_map/ppermute | solution.py:33
  67.9 14.5 %collective-permute-start.15 = (f16[544,512]{1,0:T(8,128)(2,1)S(1)}, f16[544,512]{1,0:T(8,128)(2,1)S(1)}, u32[]{:S(2)}, u32[]{:S(2)}) collective-permute-start(f16[544,512]{1,0:T(8,128)(2,1)S(1)} %convert_element_type.96), channel_id=1, source_target_pairs={{0,2},{1,3},{2,0},{3,1},{4,20},{5,21},{6,22},{7,23},{8,10},{9,11},... | collective-permute-start | bytes 1671176 | tf_op jit(solution)/shard_map/ppermute | solution.py:33
  71.7 14.6 %collective-permute-start.22 = (f16[136,512]{1,0:T(8,128)(2,1)S(1)}, f16[136,512]{1,0:T(8,128)(2,1)S(1)}, u32[]{:S(2)}, u32[]{:S(2)}) collective-permute-start(f16[136,512]{1,0:T(8,128)(2,1)S(1)} %get-tuple-element.67), channel_id=1, source_target_pairs={{0,64},{32,96},{64,0},{96,32},{1,65},{33,97},{65,1},{97,33},{2,66}... | collective-permute-start | bytes 417800 | tf_op jit(solution)/shard_map/ppermute | solution.py:37
  73.2 15.7 %collective-permute-start.24 = (f16[136,512]{1,0:T(8,128)(2,1)S(1)}, f16[136,512]{1,0:T(8,128)(2,1)S(1)}, u32[]{:S(2)}, u32[]{:S(2)}) collective-permute-start(f16[136,512]{1,0:T(8,128)(2,1)S(1)} %get-tuple-element.68), channel_id=1, source_target_pairs={{0,32},{32,64},{64,96},{96,0},{1,33},{33,65},{65,97},{97,1},{2,34}... | collective-permute-start | bytes 417800 | tf_op jit(solution)/shard_map/ppermute | solution.py:37
  75.1 13.8 %collective-permute-start.23 = (f16[136,512]{1,0:T(8,128)(2,1)S(1)}, f16[136,512]{1,0:T(8,128)(2,1)S(1)}, u32[]{:S(2)}, u32[]{:S(2)}) collective-permute-start(f16[136,512]{1,0:T(8,128)(2,1)S(1)} %get-tuple-element.69), channel_id=1, source_target_pairs={{0,96},{32,0},{64,32},{96,64},{1,97},{33,1},{65,33},{97,65},{2,98}... | collective-permute-start | bytes 417800 | tf_op jit(solution)/shard_map/ppermute | solution.py:37
  82.7 7.1 %collective-permute-start.18 = (f16[136,512]{1,0:T(8,128)(2,1)S(1)}, f16[136,512]{1,0:T(8,128)(2,1)S(1)}, u32[]{:S(2)}, u32[]{:S(2)}) collective-permute-start(f16[136,512]{1,0:T(8,128)(2,1)S(1)} %get-tuple-element.64), channel_id=1, source_target_pairs={{0,16},{1,17},{2,18},{3,19},{4,6},{5,7},{6,4},{7,5},{8,24},{9,25},... | collective-permute-start | bytes 417800 | tf_op jit(solution)/shard_map/ppermute | solution.py:33
  85.7 6.3 %collective-permute-start.20 = (f16[136,512]{1,0:T(8,128)(2,1)S(1)}, f16[136,512]{1,0:T(8,128)(2,1)S(1)}, u32[]{:S(2)}, u32[]{:S(2)}) collective-permute-start(f16[136,512]{1,0:T(8,128)(2,1)S(1)} %get-tuple-element.65), channel_id=1, source_target_pairs={{0,8},{1,9},{2,10},{3,11},{4,5},{5,6},{6,7},{7,4},{8,16},{9,17},{1... | collective-permute-start | bytes 417800 | tf_op jit(solution)/shard_map/ppermute | solution.py:33
  86.3 5.7 %collective-permute-start.19 = (f16[136,512]{1,0:T(8,128)(2,1)S(1)}, f16[136,512]{1,0:T(8,128)(2,1)S(1)}, u32[]{:S(2)}, u32[]{:S(2)}) collective-permute-start(f16[136,512]{1,0:T(8,128)(2,1)S(1)} %get-tuple-element.66), channel_id=1, source_target_pairs={{0,24},{1,25},{2,26},{3,27},{4,7},{5,4},{6,5},{7,6},{8,0},{9,1},{1... | collective-permute-start | bytes 417800 | tf_op jit(solution)/shard_map/ppermute | solution.py:33
